TPU v7x, 128 devices: a whole 4x4x4 slice. The times are simulated.
128 devices in a mesh: samp: 16 (over z, y_lo, core), var: 8 (over x, y_hi).
Axes of the slice: x: 4, y: 4 (y_hi: 2, y_lo: 2; y = y_hi * 2 + y_lo), z: 4, core: 2. Of those that a mesh axis runs over, the one named last changes fastest.
Arguments:
- hap_words: int32 [2, 1024, 1024], P(None, 'samp', 'var'), may hold values from 0 to 1073741823
- total_counts: int32 [30720, 8192], P('samp', 'var'), may hold values from 0 to 4999
- allele_one: int32 [30720, 8192], P('samp', 'var'), may hold values from 0 to 299
- allele_two: int32 [30720, 8192], P('samp', 'var'), may hold values from 0 to 299
Outputs:
- z_total: float32 [1024, 8192], P('samp', 'var')
- z_allelic: float32 [1024, 8192], P('samp', 'var')
Inputs may be any that keep to these rules, and one draw needn't show every extreme that they name: Bit k, for k below 30, of hap_words[c, j, v] is haplotype c of sample 30 * j + k at variant v; higher bits are zero.
All inputs are finite; a program needn't handle non-finite values.
Results may differ from a plain program's by a relative error of at most 0.0003.
The roundings to bfloat16 on the way count: a program that leaves them out, or rounds other values in their place, can miss the bound.
Values sent between devices are 32-bit elements; how exact they have to be, the bound alone decides.
No kernel may reach another device: no remote copies, remote signals or barrier semaphores. Data moves between devices by JAX's collectives and lax.ppermute only.
A program may use at most 192 MiB of HBM per device.

v0:
```python
import jax
import jax.numpy as jnp
from jax import lax
from jax.experimental import pallas as pl
from jax.experimental.pallas import tpu as pltpu
from jax.sharding import PartitionSpec as P

BITS = 30
HALF = BITS // 2
LANES = 128
CHUNKS = (512, 512)
MIB = 1024 * 1024

CORE, SIDE_Y, SIDE_A, SIDE_B = 1, 2, 4, 12
MARGIN_ORDER = (CORE, SIDE_Y, SIDE_A, SIDE_B)
ORDERS = ((SIDE_Y, SIDE_A, SIDE_B), (SIDE_A, SIDE_B, SIDE_Y), (SIDE_B, SIDE_Y, SIDE_A))


def swap(array, axis, flip):
    size = lax.axis_size(axis)
    return lax.ppermute(array, axis, [(d, d ^ flip) for d in range(size)])


def place_of(relative, order):
    bits = {
        SIDE_Y: (relative >> 1) & 1,
        SIDE_A: ((relative >> 2) ^ (relative >> 3)) & 1,
        SIDE_B: (relative >> 3) & 1,
    }
    place = relative & 1
    for side in order:
        place = 2 * place + bits[side]
    return place


def unpack_kernel(where_ref, own_ref, twin_ref, *refs):
    far_refs, (dosage_ref, phase_ref, mixed_ref, margin_ref) = refs[:-4], refs[-4:]
    samp, var = where_ref[0], where_ref[1]
    low = (1 << HALF) - 1
    words, block = own_ref.shape[1:]
    rows = block // 2
    samples = float(words * BITS)
    one, zero = jnp.bfloat16(1), jnp.bfloat16(0)
    pieces = [(0, own_ref, 0), (1, twin_ref, 0)]
    for step, far_ref in enumerate(far_refs):
        pieces += [(2 * step + 2 + twin, far_ref, 2 * twin) for twin in range(2)]
    for flip, word_ref, spot in pieces:
        source = var ^ flip
        first, second = word_ref[spot], word_ref[spot + 1]
        ones = lax.population_count(first) + lax.population_count(second)
        mixed = lax.population_count(first ^ second)
        margin_ref[pl.ds(source, 1), 0:1, :] = (
            jnp.sum(ones.astype(jnp.float32), axis=0, keepdims=True) - samples
        )[None]
        margin_ref[pl.ds(source, 1), 1:2, :] = (
            samples - jnp.sum(mixed.astype(jnp.float32), axis=0, keepdims=True)
        )[None]
        turned = [
            jnp.concatenate([w & low, (w >> HALF) & low], axis=0).T.astype(jnp.int16)
            for w in (first, second)
        ]
        for part in range(2):
            relative = (2 * source + part) ^ samp
            starts = [pl.multiple_of(place_of(relative, order) * rows, rows) for order in ORDERS]
            mine = [t[part * rows : (part + 1) * rows] for t in turned]
            for bit in range(HALF):
                mask = jnp.int16(1 << bit)
                hap_one = jnp.where((mine[0] & mask) != 0, one, zero)
                hap_two = jnp.where((mine[1] & mask) != 0, one, zero)
                phase = hap_one - hap_two
                lanes = slice(bit * 2 * words, (bit + 1) * 2 * words)
                dosage_ref[pl.ds(starts[0], rows), lanes] = (hap_one + hap_two) - one
                phase_ref[pl.ds(starts[1], rows), lanes] = phase
                mixed_ref[pl.ds(starts[2], rows), lanes] = phase * phase


def unpack(where, own, twin, far):
    _, words, block = own.shape
    count = 2 + 2 * len(far)
    variants, samples = count * block, words * BITS
    design = jax.ShapeDtypeStruct((variants, samples), jnp.bfloat16)
    return pl.pallas_call(
        unpack_kernel,
        out_shape=(design,) * 3 + (jax.ShapeDtypeStruct((count, 2, block), jnp.float32),),
        in_specs=[pl.BlockSpec(memory_space=pltpu.SMEM)]
        + [pl.BlockSpec(memory_space=pltpu.VMEM)] * (2 + len(far)),
        cost_estimate=pl.CostEstimate(
            flops=6_000_000_000, bytes_accessed=6 * variants * samples, transcendentals=0
        ),
        compiler_params=pltpu.CompilerParams(vmem_limit_bytes=8 * MIB),
        name="unpack",
    )(where, own, twin, *far)


def feature_kernel(total_ref, one_ref, two_ref, *refs):
    total_out, weighted_out, weight_out, margin_ref = refs[-4:]
    words = total_ref.shape[0] // BITS

    def step(bit, sums):
        log_sum, log_sq = sums
        for half in range(2):
            rows = pl.ds(bit + half * HALF, words, stride=BITS)
            spot = pl.ds(pl.multiple_of((2 * bit + half) * words, words), words)
            log_total = jnp.log(total_ref[rows, :].astype(jnp.float32) + 1.0)
            one_plus = one_ref[rows, :].astype(jnp.float32) + 1.0
            two_plus = two_ref[rows, :].astype(jnp.float32) + 1.0
            log_ratio = jnp.log(one_plus / two_plus)
            weight = (one_plus * two_plus) / (one_plus + two_plus)
            total_out[0, spot, :] = log_total.astype(jnp.bfloat16)
            weighted_out[0, spot, :] = (weight * log_ratio).astype(jnp.bfloat16)
            weight_out[0, spot, :] = weight.astype(jnp.bfloat16)
            folded = log_total.reshape(words // 8, 8, LANES)
            log_sum = log_sum + jnp.sum(folded, axis=0)
            log_sq = log_sq + jnp.sum(folded * folded, axis=0)
        return log_sum, log_sq

    blank = jnp.zeros((8, LANES), jnp.float32)
    log_sum, log_sq = lax.fori_loop(0, HALF, step, (blank, blank))
    margin_ref[0:1, :] = jnp.sum(log_sum, axis=0, keepdims=True)
    margin_ref[1:2, :] = jnp.sum(log_sq, axis=0, keepdims=True)


def features(total_counts, allele_one, allele_two, first, width, after):
    samples = total_counts.shape[0]
    counts = pl.BlockSpec((samples, LANES), lambda i: (0, first // LANES + i))
    feature = jax.ShapeDtypeStruct((width // LANES, samples, LANES), jnp.bfloat16)
    return pl.pallas_call(
        feature_kernel,
        grid=(width // LANES,),
        out_shape=(feature,) * 3 + (jax.ShapeDtypeStruct((2, width), jnp.float32),),
        in_specs=[counts] * 3 + [pl.BlockSpec(memory_space=pl.ANY)] * len(after),
        out_specs=(pl.BlockSpec((1, samples, LANES), lambda i: (i, 0, 0)),) * 3
        + (pl.BlockSpec((2, LANES), lambda i: (0, i)),),
        cost_estimate=pl.CostEstimate(
            flops=12_000_000 * width, bytes_accessed=18 * samples * width, transcendentals=0
        ),
        compiler_params=pltpu.CompilerParams(vmem_limit_bytes=46 * MIB),
        name="features",
    )(total_counts, allele_one, allele_two, *after)


def cross_kernel(design_ref, feature_ref, *refs):
    keep_ref, send_ref = refs[-2:]
    kept = keep_ref.shape[0]
    for pair in range(feature_ref.shape[0] // 2):
        right = jnp.concatenate([feature_ref[2 * pair], feature_ref[2 * pair + 1]], axis=1)
        lanes = slice(pair * 2 * LANES, (pair + 1) * 2 * LANES)
        for part, out_ref in ((1, send_ref), (0, keep_ref)):
            out_ref[:, lanes] = jnp.dot(
                design_ref[part * kept : (part + 1) * kept, :],
                right,
                preferred_element_type=jnp.float32,
            )


def cross(design, feature, after):
    variants, samples = design.shape
    width = feature.shape[0] * LANES
    part = jax.ShapeDtypeStruct((variants // 2, width), jnp.float32)
    return pl.pallas_call(
        cross_kernel,
        out_shape=(part, part),
        in_specs=[pl.BlockSpec(memory_space=pltpu.VMEM)] * 2
        + [pl.BlockSpec(memory_space=pl.ANY)] * len(after),
        cost_estimate=pl.CostEstimate(
            flops=2 * variants * samples * width,
            bytes_accessed=2 * (variants + width) * samples,
            transcendentals=0,
        ),
        compiler_params=pltpu.CompilerParams(vmem_limit_bytes=8 * MIB),
        name="cross",
    )(design, feature, *after)


def fold_kernel(left_ref, right_ref, keep_ref, send_ref):
    half = keep_ref.shape[0]
    keep_ref[...] = left_ref[:half] + right_ref[:half]
    send_ref[...] = left_ref[half:] + right_ref[half:]


def fold(left, right):
    rows, width = left.shape
    part = jax.ShapeDtypeStruct((rows // 2, width), jnp.float32)
    return pl.pallas_call(
        fold_kernel,
        out_shape=(part, part),
        cost_estimate=pl.CostEstimate(
            flops=rows * width, bytes_accessed=12 * rows * width, transcendentals=0
        ),
        compiler_params=pltpu.CompilerParams(vmem_limit_bytes=8 * MIB),
        name="fold",
    )(left, right)


def finish(pair_sums, dos_margin, gene_margin, sample_count):
    dos_sum, dos_sq = (dos_margin[0], dos_margin[1])
    gene_sum, gene_sq = (gene_margin[0], gene_margin[1])
    dosage_var = dos_sq - dos_sum * dos_sum / sample_count
    gene_var = gene_sq - gene_sum * gene_sum / sample_count
    covariance = pair_sums[0] - dos_sum[:, None] * gene_sum[None, :] / sample_count
    z_total = (
        jnp.sqrt(sample_count)
        * covariance
        / jnp.sqrt((dosage_var[:, None] + 1.0) * (gene_var[None, :] + 1.0))
    )
    z_allelic = pair_sums[1] / jnp.sqrt(pair_sums[2] + 1.0)
    return (z_total, z_allelic)


def per_device(hap_words, total_counts, allele_one, allele_two):
    samp, var = lax.axis_index("samp"), lax.axis_index("var")
    twin = swap(hap_words, "var", 1)
    counts = (total_counts, allele_one, allele_two)
    starts = [sum(CHUNKS[:chunk]) for chunk in range(len(CHUNKS))]
    made = []
    for chunk, (start, width) in enumerate(zip(starts, CHUNKS)):
        made.append(features(*counts, start, width, () if chunk == 0 else (twin,)))
    pair = jnp.concatenate([hap_words, twin], axis=0)
    far = []
    for flip in (2, 4, 6):
        far.append(swap(pair, "var", flip))
    *designs, dos_part = unpack(jnp.stack([samp, var]).astype(jnp.int32), hap_words, twin, far)
    sums, first_sends = [], [()] * 3
    for feature in made:
        folded = []
        for index in range(3):
            keep, send = cross(designs[index], feature[index], first_sends[index])
            got = swap(send, "samp", CORE)
            folded.append(fold(keep, got))
        first_sends = [(send,) for _, send in folded]
        for step in range(3):
            got = []
            for index in range(3):
                got.append(swap(folded[index][1], "samp", ORDERS[index][step]))
            if step < 2:
                folded = [fold(folded[i][0], got[i]) for i in range(3)]
            else:
                sums.append([folded[i][0] + got[i] for i in range(3)])
    gene_parts = [parts[3] for parts in made]
    variants = designs[0].shape[0]
    genes = total_counts.shape[1]
    dos_part = jnp.moveaxis(dos_part, 1, 0).reshape(2, variants)
    margins = jnp.concatenate([*gene_parts, dos_part], axis=1)
    margins, *_ = lax.optimization_barrier((margins, *first_sends))
    for side in MARGIN_ORDER:
        got = swap(margins, "samp", side)
        margins = margins + got
    own = variants // lax.axis_size("samp")
    dos_margin = lax.dynamic_slice_in_dim(margins[:, genes:], samp * own, own, 1)
    sample_count = jnp.float32(total_counts.shape[0] * lax.axis_size("samp"))
    outs, first = [], 0
    for pair_sums, width in zip(sums, CHUNKS):
        outs.append(finish(pair_sums, dos_margin, margins[:, first : first + width], sample_count))
        first += width
    return tuple(jnp.concatenate(parts, axis=1) for parts in zip(*outs))


def solution(mesh):
    in_specs = (P(None, "samp", "var"), P("samp", "var"), P("samp", "var"), P("samp", "var"))
    out_specs = (P("samp", "var"), P("samp", "var"))

    return jax.shard_map(
        per_device, mesh=mesh, in_specs=in_specs, out_specs=out_specs, check_vma=False
    )
```

profile of v0, /device:TPU:0, one launch (start us, length us, event | category | flops | bytes accessed | tf_op | source)
XLA Modules:
  0.0 133.9 jit_solution(13413718947332981653)
XLA Ops:
  0.6 3.4 %collective-permute-start = (s32[2,64,128]{2,1,0:T(8,128)}, s32[2,64,128]{2,1,0:T(8,128)S(1)}, u32[]{:S(2)}, u32[]{:S(2)}) collective-permute-start(s32[2,64,128]{2,1,0:T(8,128)} %own_ref.1), channel_id=1, source_target_pairs={{0,1},{1,0},{2,3},{3,2},{4,5},{5,4},{6,7},{7,6},{8,9},{9,8},{10,11... | collective-permute-start | bytes 196616 | tf_op jit(solution)/shard_map/ppermute | solution.py:21
  4.0 0.9 constant_dynamic-update-slice_fusion.1
  4.9 1.8 %collective-permute-done.twin_ref.refs_0_ = s32[2,64,128]{2,1,0:T(8,128)S(1)} collective-permute-done((s32[2,64,128]{2,1,0:T(8,128)}, s32[2,64,128]{2,1,0:T(8,128)S(1)}, u32[]{:S(2)}, u32[]{:S(2)}) %collective-permute-start) | collective-permute-done | bytes 65568 | tf_op jit(solution)/shard_map/ppermute | solution.py:21
  6.7 1.7 %collective-permute-start.1 = (s32[4,64,128]{2,1,0:T(8,128)S(1)}, s32[4,64,128]{2,1,0:T(8,128)S(1)}, u32[]{:S(2)}, u32[]{:S(2)}) collective-permute-start(s32[4,64,128]{2,1,0:T(8,128)S(1)} %constant_dynamic-update-slice_fusion), channel_id=1, source_target_pairs={{0,2},{1,3},{2,0},{3,1},{4,6},{5,7},{6,4},{7,5},{8,10},{9,11},{10,... | collective-permute-start | bytes 393224 | tf_op jit(solution)/shard_map/ppermute | solution.py:21
  8.4 2.7 %collective-permute-start.2 = (s32[4,64,128]{2,1,0:T(8,128)S(1)}, s32[4,64,128]{2,1,0:T(8,128)S(1)}, u32[]{:S(2)}, u32[]{:S(2)}) collective-permute-start(s32[4,64,128]{2,1,0:T(8,128)S(1)} %constant_dynamic-update-slice_fusion), channel_id=1, source_target_pairs={{0,4},{1,5},{2,6},{3,7},{4,0},{5,1},{6,2},{7,3},{8,12},{9,13},{10,... | collective-permute-start | bytes 393224 | tf_op jit(solution)/shard_map/ppermute | solution.py:21
  11.1 0.4 collective-permute-start.3
  11.5 6.5 %features.2 = (bf16[4,1920,128]{2,1,0:T(8,128)(2,1)S(1)}, bf16[4,1920,128]{2,1,0:T(8,128)(2,1)S(1)}, bf16[4,1920,128]{2,1,0:T(8,128)(2,1)S(1)}, f32[2,512]{1,0:T(2,128)S(1)}) custom-call(s32[1920,1024]{1,0:T(8,128)} %total_ref.3, s32[1920,1024]{1,0:T(8,128)} %one_ref.3, s32[1920,1024]{1,0:T(8,128)} %two_ref.3), custom_call_target="tpu_custom_call" | custom-call | flops 6144000000 | bytes 17694720 | tf_op jit(solution)/shard_map/features/pallas_call | solution.py:127
  18.0 1.3 copy-done.1
  19.3 1.3 copy-done.3
  20.7 2.9 %unpack.1 = (bf16[1024,1920]{1,0:T(8,128)(2,1)S(1)}, bf16[1024,1920]{1,0:T(8,128)(2,1)S(1)}, bf16[1024,1920]{1,0:T(8,128)(2,1)S(1)}, f32[8,2,128]{2,1,0:T(2,128)S(1)}) custom-call(s32[2]{0:T(128)S(1)} %pad_add_fusion.where_ref, s32[2,64,128]{2,1,0:T(8,128)S(1)} %copy-done, s32[2,64,128]{2,1,0:T(8,128)S(1)} %collective-permute-done.twin_ref.refs_0_, ...), custom_call_target="tpu_custom_call" | custom-call | flops 6000000000 | bytes 11796480 | tf_op jit(solution)/shard_map/unpack/pallas_call | solution.py:82
  23.6 3.4 %cross.8 = (f32[512,512]{1,0:T(8,128)S(1)}, f32[512,512]{1,0:T(8,128)}) custom-call(bf16[1024,1920]{1,0:T(8,128)(2,1)S(1)} %get-tuple-element.80.design_ref, bf16[4,1920,128]{2,1,0:T(8,128)(2,1)S(1)} %copy-done.4), custom_call_target="tpu_custom_call" | custom-call | flops 2013265920 | bytes 5898240 | tf_op jit(solution)/shard_map/cross/pallas_call | solution.py:160
  27.1 1.9 %copy-done.10 = bf16[1024,1920]{1,0:T(8,128)(2,1)} copy-done((bf16[1024,1920]{1,0:T(8,128)(2,1)}, bf16[1024,1920]{1,0:T(8,128)(2,1)S(1)}, u32[]{:S(2)}) %copy-start.10) | copy-done | bytes 3932184
  29.0 2.3 %cross.10 = (f32[512,512]{1,0:T(8,128)S(1)}, f32[512,512]{1,0:T(8,128)S(1)}) custom-call(bf16[1024,1920]{1,0:T(8,128)(2,1)S(1)} %get-tuple-element.89.design_ref, bf16[4,1920,128]{2,1,0:T(8,128)(2,1)S(1)} %copy-done.2), custom_call_target="tpu_custom_call" | custom-call | flops 2013265920 | bytes 5898240 | tf_op jit(solution)/shard_map/cross/pallas_call | solution.py:160
  31.3 0.6 collective-permute-start.11
  31.9 2.3 %cross.6 = (f32[512,512]{1,0:T(8,128)S(1)}, f32[512,512]{1,0:T(8,128)S(1)}) custom-call(bf16[1024,1920]{1,0:T(8,128)(2,1)S(1)} %get-tuple-element.63.design_ref, bf16[4,1920,128]{2,1,0:T(8,128)(2,1)S(1)} %get-tuple-element.64.feature_ref), custom_call_target="tpu_custom_call" | custom-call | flops 2013265920 | bytes 5898240 | tf_op jit(solution)/shard_map/cross/pallas_call | solution.py:160
  34.4 6.5 %features.3 = (bf16[4,1920,128]{2,1,0:T(8,128)(2,1)S(1)}, bf16[4,1920,128]{2,1,0:T(8,128)(2,1)S(1)}, bf16[4,1920,128]{2,1,0:T(8,128)(2,1)S(1)}, f32[2,512]{1,0:T(2,128)S(1)}) custom-call(s32[1920,1024]{1,0:T(8,128)} %total_ref.3, s32[1920,1024]{1,0:T(8,128)} %one_ref.3, s32[1920,1024]{1,0:T(8,128)} %two_ref.3, ...), custom_call_target="tpu_custom_call" | custom-call | flops 6144000000 | bytes 17694720 | tf_op jit(solution)/shard_map/features/pallas_call | solution.py:127
  40.9 0.1 fold.22
  41.0 2.1 %collective-permute-start.20 = (f32[256,512]{1,0:T(8,128)S(1)}, f32[256,512]{1,0:T(8,128)S(1)}, u32[]{:S(2)}, u32[]{:S(2)}) collective-permute-start(f32[256,512]{1,0:T(8,128)S(1)} %get-tuple-element.85.refs_0_), channel_id=1, source_target_pairs={{0,32},{8,40},{16,48},{24,56},{32,0},{40,8},{48,16},{56,24},{64,96... | collective-permute-start | bytes 1572872 | tf_op jit(solution)/shard_map/ppermute | solution.py:21
  43.1 2.1 %copy-done.11 = bf16[1024,1920]{1,0:T(8,128)(2,1)S(1)} copy-done((bf16[1024,1920]{1,0:T(8,128)(2,1)S(1)}, bf16[1024,1920]{1,0:T(8,128)(2,1)}, u32[]{:S(2)}) %copy-start.11) | copy-done | bytes 3932184
  45.3 2.3 %cross.9 = (f32[512,512]{1,0:T(8,128)S(1)}, f32[512,512]{1,0:T(8,128)S(1)}) custom-call(bf16[1024,1920]{1,0:T(8,128)(2,1)S(1)} %copy-done.11, bf16[4,1920,128]{2,1,0:T(8,128)(2,1)S(1)} %get-tuple-element.81.feature_ref, f32[256,512]{1,0:T(8,128)S(1)} %get-tuple-element.85.refs_0_), custom_call_target="tpu_custom_call" | custom-call | flops 2013265920 | bytes 5898240 | tf_op jit(solution)/shard_map/cross/pallas_call | solution.py:160
  47.6 0.5 collective-permute-start.10
  48.1 0.1 fold.24
  48.2 2.3 %cross.11 = (f32[512,512]{1,0:T(8,128)S(1)}, f32[512,512]{1,0:T(8,128)S(1)}) custom-call(bf16[1024,1920]{1,0:T(8,128)(2,1)S(1)} %copy-done.9, bf16[4,1920,128]{2,1,0:T(8,128)(2,1)S(1)} %get-tuple-element.90.feature_ref, f32[256,512]{1,0:T(8,128)S(1)} %get-tuple-element.94.refs_0_), custom_call_target="tpu_custom_call" | custom-call | flops 2013265920 | bytes 5898240 | tf_op jit(solution)/shard_map/cross/pallas_call | solution.py:160
  50.5 0.4 collective-permute-start.12
  50.9 0.1 fold.18
  51.0 2.3 %cross.7 = (f32[512,512]{1,0:T(8,128)S(1)}, f32[512,512]{1,0:T(8,128)S(1)}) custom-call(bf16[1024,1920]{1,0:T(8,128)(2,1)S(1)} %copy-done.7, bf16[4,1920,128]{2,1,0:T(8,128)(2,1)S(1)} %get-tuple-element.76.feature_ref, f32[256,512]{1,0:T(8,128)S(1)} %get-tuple-element.68.refs_0_), custom_call_target="tpu_custom_call" | custom-call | flops 2013265920 | bytes 5898240 | tf_op jit(solution)/shard_map/cross/pallas_call | solution.py:160
  53.4 0.3 collective-permute-start.8
  53.7 2.5 %collective-permute-start.23 = (f32[256,512]{1,0:T(8,128)S(1)}, f32[256,512]{1,0:T(8,128)S(1)}, u32[]{:S(2)}, u32[]{:S(2)}) collective-permute-start(f32[256,512]{1,0:T(8,128)S(1)} %get-tuple-element.94.refs_0_), channel_id=1, source_target_pairs={{0,96},{8,104},{16,112},{24,120},{32,64},{40,72},{48,80},{56,88},{... | collective-permute-start | bytes 1572872 | tf_op jit(solution)/shard_map/ppermute | solution.py:21
  56.2 1.6 %collective-permute-start.5 = (f32[256,512]{1,0:T(8,128)S(1)}, f32[256,512]{1,0:T(8,128)S(1)}, u32[]{:S(2)}, u32[]{:S(2)}) collective-permute-start(f32[256,512]{1,0:T(8,128)S(1)} %get-tuple-element.68.refs_0_), channel_id=1, source_target_pairs={{0,16},{8,24},{16,0},{24,8},{32,48},{40,56},{48,32},{56,40},{64,80... | collective-permute-start | bytes 1572872 | tf_op jit(solution)/shard_map/ppermute | solution.py:21
  57.8 11.2 %collective-permute-done.23.right_ref = f32[256,512]{1,0:T(8,128)S(1)} collective-permute-done((f32[256,512]{1,0:T(8,128)S(1)}, f32[256,512]{1,0:T(8,128)S(1)}, u32[]{:S(2)}, u32[]{:S(2)}) %collective-permute-start.23) | collective-permute-done | bytes 524320 | tf_op jit(solution)/shard_map/ppermute | solution.py:21
  69.0 2.5 %collective-permute-start.21 = (f32[128,512]{1,0:T(8,128)S(1)}, f32[128,512]{1,0:T(8,128)S(1)}, u32[]{:S(2)}, u32[]{:S(2)}) collective-permute-start(f32[128,512]{1,0:T(8,128)S(1)} %get-tuple-element.106), channel_id=1, source_target_pairs={{0,96},{8,104},{16,112},{24,120},{32,64},{40,72},{48,80},{56,88},{... | collective-permute-start | bytes 786440 | tf_op jit(solution)/shard_map/ppermute | solution.py:21
  71.6 1.6 %collective-permute-start.24 = (f32[128,512]{1,0:T(8,128)S(1)}, f32[128,512]{1,0:T(8,128)S(1)}, u32[]{:S(2)}, u32[]{:S(2)}) collective-permute-start(f32[128,512]{1,0:T(8,128)S(1)} %get-tuple-element.111), channel_id=1, source_target_pairs={{0,16},{8,24},{16,0},{24,8},{32,48},{40,56},{48,32},{56,40},{64,80... | collective-permute-start | bytes 786440 | tf_op jit(solution)/shard_map/ppermute | solution.py:21
  73.3 4.6 %collective-permute-done.21.right_ref = f32[128,512]{1,0:T(8,128)S(1)} collective-permute-done((f32[128,512]{1,0:T(8,128)S(1)}, f32[128,512]{1,0:T(8,128)S(1)}, u32[]{:S(2)}, u32[]{:S(2)}) %collective-permute-start.21) | collective-permute-done | bytes 262176 | tf_op jit(solution)/shard_map/ppermute | solution.py:21
  77.9 1.2 collective-permute-done.24.right_ref
  79.1 1.6 %collective-permute-start.22 = (f32[64,512]{1,0:T(8,128)S(1)}, f32[64,512]{1,0:T(8,128)}, u32[]{:S(2)}, u32[]{:S(2)}) collective-permute-start(f32[64,512]{1,0:T(8,128)S(1)} %get-tuple-element.108), channel_id=1, source_target_pairs={{0,16},{8,24},{16,0},{24,8},{32,48},{40,56},{48,32},{56,40},{64,80... | collective-permute-start | bytes 393224 | tf_op jit(solution)/shard_map/ppermute | solution.py:21
  80.6 0.7 fold.31
  81.3 1.0 collective-permute-start.25
  82.3 0.9 fold.23
  83.2 0.9 fold.25
  84.1 0.1 fold.21
  84.3 1.2 collective-permute-done.13
  85.5 0.5 collective-permute-start.14
  86.1 1.1 collective-permute-start.26
  87.1 2.2 %collective-permute-done.14 = f32[2,2048]{1,0:T(2,128)S(1)} collective-permute-done((f32[2,2048]{1,0:T(2,128)S(1)}, f32[2,2048]{1,0:T(2,128)S(1)}, u32[]{:S(2)}, u32[]{:S(2)}) %collective-permute-start.14) | collective-permute-done | bytes 16416 | tf_op jit(solution)/shard_map/ppermute | solution.py:21
  89.3 2.5 %collective-permute-start.29 = (f32[256,512]{1,0:T(8,128)}, f32[256,512]{1,0:T(8,128)S(1)}, u32[]{:S(2)}, u32[]{:S(2)}) collective-permute-start(f32[256,512]{1,0:T(8,128)} %get-tuple-element.97), channel_id=1, source_target_pairs={{0,96},{8,104},{16,112},{24,120},{32,64},{40,72},{48,80},{56,88},{... | collective-permute-start | bytes 1572872 | tf_op jit(solution)/shard_map/ppermute | solution.py:21
  92.0 8.4 %collective-permute-done.15 = f32[2,2048]{1,0:T(2,128)} collective-permute-done((f32[2,2048]{1,0:T(2,128)S(1)}, f32[2,2048]{1,0:T(2,128)}, u32[]{:S(2)}, u32[]{:S(2)}) %collective-permute-start.15) | collective-permute-done | bytes 16416 | tf_op jit(solution)/shard_map/ppermute | solution.py:21
  100.4 2.5 %collective-permute-start.7 = (f32[64,512]{1,0:T(8,128)S(1)}, f32[64,512]{1,0:T(8,128)S(1)}, u32[]{:S(2)}, u32[]{:S(2)}) collective-permute-start(f32[64,512]{1,0:T(8,128)S(1)} %get-tuple-element.72), channel_id=1, source_target_pairs={{0,96},{8,104},{16,112},{24,120},{32,64},{40,72},{48,80},{56,88},{... | collective-permute-start | bytes 393224 | tf_op jit(solution)/shard_map/ppermute | solution.py:21
  103.0 0.7 add.61
  103.7 1.6 %collective-permute-start.17 = (f32[256,512]{1,0:T(8,128)}, f32[256,512]{1,0:T(8,128)S(1)}, u32[]{:S(2)}, u32[]{:S(2)}) collective-permute-start(f32[256,512]{1,0:T(8,128)} %copy-done.5), channel_id=1, source_target_pairs={{0,16},{8,24},{16,0},{24,8},{32,48},{40,56},{48,32},{56,40},{64,80... | collective-permute-start | bytes 1572872 | tf_op jit(solution)/shard_map/ppermute | solution.py:21
  105.4 0.7 collective-permute-start.16
  106.1 1.0 rsqrt_multiply_fusion.1
  107.1 3.2 %collective-permute-done.16 = f32[2,2048]{1,0:T(2,128)S(1)} collective-permute-done((f32[2,2048]{1,0:T(2,128)S(1)}, f32[2,2048]{1,0:T(2,128)S(1)}, u32[]{:S(2)}, u32[]{:S(2)}) %collective-permute-start.16) | collective-permute-done | bytes 16416 | tf_op jit(solution)/shard_map/ppermute | solution.py:21
  110.4 0.8 collective-permute-start.27
  111.3 0.5 collective-permute-start.30
  111.9 6.9 %collective-permute-done.17.right_ref = f32[256,512]{1,0:T(8,128)S(1)} collective-permute-done((f32[256,512]{1,0:T(8,128)}, f32[256,512]{1,0:T(8,128)S(1)}, u32[]{:S(2)}, u32[]{:S(2)}) %collective-permute-start.17) | collective-permute-done | bytes 524320 | tf_op jit(solution)/shard_map/ppermute | solution.py:21
  119.0 1.6 %collective-permute-start.28 = (f32[64,512]{1,0:T(8,128)S(1)}, f32[64,512]{1,0:T(8,128)S(1)}, u32[]{:S(2)}, u32[]{:S(2)}) collective-permute-start(f32[64,512]{1,0:T(8,128)S(1)} %get-tuple-element.118), channel_id=1, source_target_pairs={{0,16},{8,24},{16,0},{24,8},{32,48},{40,56},{48,32},{56,40},{64,80... | collective-permute-start | bytes 393224 | tf_op jit(solution)/shard_map/ppermute | solution.py:21
  120.7 2.8 %collective-permute-done.30.right_ref = f32[128,512]{1,0:T(8,128)S(1)} collective-permute-done((f32[128,512]{1,0:T(8,128)S(1)}, f32[128,512]{1,0:T(8,128)S(1)}, u32[]{:S(2)}, u32[]{:S(2)}) %collective-permute-start.30) | collective-permute-done | bytes 262176 | tf_op jit(solution)/shard_map/ppermute | solution.py:21
  123.6 3.1 %collective-permute-done.18.right_ref = f32[128,512]{1,0:T(8,128)S(1)} collective-permute-done((f32[128,512]{1,0:T(8,128)S(1)}, f32[128,512]{1,0:T(8,128)S(1)}, u32[]{:S(2)}, u32[]{:S(2)}) %collective-permute-start.18) | collective-permute-done | bytes 262176 | tf_op jit(solution)/shard_map/ppermute | solution.py:21
  126.8 0.8 collective-permute-start.19
  127.6 1.0 collective-permute-done.31
  128.6 0.7 pad_maximum_fusion.1
  129.4 3.7 %collective-permute-done.19 = f32[64,512]{1,0:T(8,128)S(1)} collective-permute-done((f32[64,512]{1,0:T(8,128)S(1)}, f32[64,512]{1,0:T(8,128)S(1)}, u32[]{:S(2)}, u32[]{:S(2)}) %collective-permute-start.19) | collective-permute-done | bytes 131104 | tf_op jit(solution)/shard_map/ppermute | solution.py:21
  133.0 0.1 rsqrt_multiply_fusion.3
  133.2 0.7 pad_maximum_fusion
  (69 shorter events, 1.3 us)
Async XLA Ops:
  0.6 6.1 %collective-permute-start = (s32[2,64,128]{2,1,0:T(8,128)}, s32[2,64,128]{2,1,0:T(8,128)S(1)}, u32[]{:S(2)}, u32[]{:S(2)}) collective-permute-start(s32[2,64,128]{2,1,0:T(8,128)} %own_ref.1), channel_id=1, source_target_pairs={{0,1},{1,0},{2,3},{3,2},{4,5},{5,4},{6,7},{7,6},{8,9},{9,8},{10,11... | collective-permute-start | bytes 196616 | tf_op jit(solution)/shard_map/ppermute | solution.py:21
  6.7 14.0 %copy-start = (s32[2,64,128]{2,1,0:T(8,128)S(1)}, s32[2,64,128]{2,1,0:T(8,128)}, u32[]{:S(2)}) copy-start(s32[2,64,128]{2,1,0:T(8,128)} %own_ref.1) | copy-start | bytes 196612
  6.7 14.0 %collective-permute-start.1 = (s32[4,64,128]{2,1,0:T(8,128)S(1)}, s32[4,64,128]{2,1,0:T(8,128)S(1)}, u32[]{:S(2)}, u32[]{:S(2)}) collective-permute-start(s32[4,64,128]{2,1,0:T(8,128)S(1)} %constant_dynamic-update-slice_fusion), channel_id=1, source_target_pairs={{0,2},{1,3},{2,0},{3,1},{4,6},{5,7},{6,4},{7,5},{8,10},{9,11},{10,... | collective-permute-start | bytes 393224 | tf_op jit(solution)/shard_map/ppermute | solution.py:21
  8.4 12.3 %collective-permute-start.2 = (s32[4,64,128]{2,1,0:T(8,128)S(1)}, s32[4,64,128]{2,1,0:T(8,128)S(1)}, u32[]{:S(2)}, u32[]{:S(2)}) collective-permute-start(s32[4,64,128]{2,1,0:T(8,128)S(1)} %constant_dynamic-update-slice_fusion), channel_id=1, source_target_pairs={{0,4},{1,5},{2,6},{3,7},{4,0},{5,1},{6,2},{7,3},{8,12},{9,13},{10,... | collective-permute-start | bytes 393224 | tf_op jit(solution)/shard_map/ppermute | solution.py:21
  11.1 9.6 %collective-permute-start.3 = (s32[4,64,128]{2,1,0:T(8,128)S(1)}, s32[4,64,128]{2,1,0:T(8,128)S(1)}, u32[]{:S(2)}, u32[]{:S(2)}) collective-permute-start(s32[4,64,128]{2,1,0:T(8,128)S(1)} %constant_dynamic-update-slice_fusion), channel_id=1, source_target_pairs={{0,6},{1,7},{2,4},{3,5},{4,2},{5,3},{6,0},{7,1},{8,14},{9,15},{10,... | collective-permute-start | bytes 393224 | tf_op jit(solution)/shard_map/ppermute | solution.py:21
  18.0 1.3 copy-start.1
  19.3 1.3 copy-start.3
  20.7 2.9 %copy-start.4 = (bf16[4,1920,128]{2,1,0:T(8,128)(2,1)S(1)}, bf16[4,1920,128]{2,1,0:T(8,128)(2,1)}, u32[]{:S(2)}) copy-start(bf16[4,1920,128]{2,1,0:T(8,128)(2,1)} %copy-done.3) | copy-start | bytes 5898244
  23.6 7.7 %copy-start.8 = (bf16[1024,1920]{1,0:T(8,128)(2,1)}, bf16[1024,1920]{1,0:T(8,128)(2,1)S(1)}, u32[]{:S(2)}) copy-start(bf16[1024,1920]{1,0:T(8,128)(2,1)S(1)} %get-tuple-element.89.design_ref) | copy-start | bytes 11796484
  23.6 8.3 %copy-start.6 = (bf16[1024,1920]{1,0:T(8,128)(2,1)}, bf16[1024,1920]{1,0:T(8,128)(2,1)S(1)}, u32[]{:S(2)}) copy-start(bf16[1024,1920]{1,0:T(8,128)(2,1)S(1)} %get-tuple-element.63.design_ref) | copy-start | bytes 11796484
  23.6 5.4 %copy-start.2 = (bf16[4,1920,128]{2,1,0:T(8,128)(2,1)S(1)}, bf16[4,1920,128]{2,1,0:T(8,128)(2,1)}, u32[]{:S(2)}) copy-start(bf16[4,1920,128]{2,1,0:T(8,128)(2,1)} %copy-done.1) | copy-start | bytes 5898244
  27.1 1.9 %copy-start.10 = (bf16[1024,1920]{1,0:T(8,128)(2,1)}, bf16[1024,1920]{1,0:T(8,128)(2,1)S(1)}, u32[]{:S(2)}) copy-start(bf16[1024,1920]{1,0:T(8,128)(2,1)S(1)} %get-tuple-element.80.design_ref) | copy-start | bytes 11796484
  29.0 11.9 %collective-permute-start.9 = (f32[512,512]{1,0:T(8,128)}, f32[512,512]{1,0:T(8,128)S(1)}, u32[]{:S(2)}, u32[]{:S(2)}) collective-permute-start(f32[512,512]{1,0:T(8,128)} %get-tuple-element.84), channel_id=1, source_target_pairs={{0,8},{8,0},{16,24},{24,16},{32,40},{40,32},{48,56},{56,48},{64,72... | collective-permute-start | bytes 3145736 | tf_op jit(solution)/shard_map/ppermute | solution.py:21
  31.3 16.7 %collective-permute-start.11 = (f32[512,512]{1,0:T(8,128)S(1)}, f32[512,512]{1,0:T(8,128)S(1)}, u32[]{:S(2)}, u32[]{:S(2)}) collective-permute-start(f32[512,512]{1,0:T(8,128)S(1)} %get-tuple-element.93), channel_id=1, source_target_pairs={{0,8},{8,0},{16,24},{24,16},{32,40},{40,32},{48,56},{56,48},{64,72... | collective-permute-start | bytes 3145736 | tf_op jit(solution)/shard_map/ppermute | solution.py:21
  34.2 16.7 %collective-permute-start.4 = (f32[512,512]{1,0:T(8,128)S(1)}, f32[512,512]{1,0:T(8,128)S(1)}, u32[]{:S(2)}, u32[]{:S(2)}) collective-permute-start(f32[512,512]{1,0:T(8,128)S(1)} %get-tuple-element.66), channel_id=1, source_target_pairs={{0,8},{8,0},{16,24},{24,16},{32,40},{40,32},{48,56},{56,48},{64,72... | collective-permute-start | bytes 3145736 | tf_op jit(solution)/shard_map/ppermute | solution.py:21
  41.0 15.1 %collective-permute-start.20 = (f32[256,512]{1,0:T(8,128)S(1)}, f32[256,512]{1,0:T(8,128)S(1)}, u32[]{:S(2)}, u32[]{:S(2)}) collective-permute-start(f32[256,512]{1,0:T(8,128)S(1)} %get-tuple-element.85.refs_0_), channel_id=1, source_target_pairs={{0,32},{8,40},{16,48},{24,56},{32,0},{40,8},{48,16},{56,24},{64,96... | collective-permute-start | bytes 1572872 | tf_op jit(solution)/shard_map/ppermute | solution.py:21
  43.1 2.1 %copy-start.11 = (bf16[1024,1920]{1,0:T(8,128)(2,1)S(1)}, bf16[1024,1920]{1,0:T(8,128)(2,1)}, u32[]{:S(2)}) copy-start(bf16[1024,1920]{1,0:T(8,128)(2,1)} %copy-done.10) | copy-start | bytes 11796484
  45.3 2.9 %copy-start.9 = (bf16[1024,1920]{1,0:T(8,128)(2,1)S(1)}, bf16[1024,1920]{1,0:T(8,128)(2,1)}, u32[]{:S(2)}) copy-start(bf16[1024,1920]{1,0:T(8,128)(2,1)} %copy-done.8) | copy-start | bytes 11796484
  47.6 33.7 %collective-permute-start.10 = (f32[512,512]{1,0:T(8,128)S(1)}, f32[512,512]{1,0:T(8,128)S(1)}, u32[]{:S(2)}, u32[]{:S(2)}) collective-permute-start(f32[512,512]{1,0:T(8,128)S(1)} %get-tuple-element.87), channel_id=1, source_target_pairs={{0,8},{8,0},{16,24},{24,16},{32,40},{40,32},{48,56},{56,48},{64,72... | collective-permute-start | bytes 3145736 | tf_op jit(solution)/shard_map/ppermute | solution.py:21
  48.2 2.9 %copy-start.7 = (bf16[1024,1920]{1,0:T(8,128)(2,1)S(1)}, bf16[1024,1920]{1,0:T(8,128)(2,1)}, u32[]{:S(2)}) copy-start(bf16[1024,1920]{1,0:T(8,128)(2,1)} %copy-done.6) | copy-start | bytes 11796484
  50.5 32.7 %collective-permute-start.12 = (f32[512,512]{1,0:T(8,128)S(1)}, f32[512,512]{1,0:T(8,128)S(1)}, u32[]{:S(2)}, u32[]{:S(2)}) collective-permute-start(f32[512,512]{1,0:T(8,128)S(1)} %get-tuple-element.96), channel_id=1, source_target_pairs={{0,8},{8,0},{16,24},{24,16},{32,40},{40,32},{48,56},{56,48},{64,72... | collective-permute-start | bytes 3145736 | tf_op jit(solution)/shard_map/ppermute | solution.py:21
  53.4 30.8 %collective-permute-start.8 = (f32[512,512]{1,0:T(8,128)S(1)}, f32[512,512]{1,0:T(8,128)S(1)}, u32[]{:S(2)}, u32[]{:S(2)}) collective-permute-start(f32[512,512]{1,0:T(8,128)S(1)} %get-tuple-element.78), channel_id=1, source_target_pairs={{0,8},{8,0},{16,24},{24,16},{32,40},{40,32},{48,56},{56,48},{64,72... | collective-permute-start | bytes 3145736 | tf_op jit(solution)/shard_map/ppermute | solution.py:21
  53.7 15.4 %collective-permute-start.23 = (f32[256,512]{1,0:T(8,128)S(1)}, f32[256,512]{1,0:T(8,128)S(1)}, u32[]{:S(2)}, u32[]{:S(2)}) collective-permute-start(f32[256,512]{1,0:T(8,128)S(1)} %get-tuple-element.94.refs_0_), channel_id=1, source_target_pairs={{0,96},{8,104},{16,112},{24,120},{32,64},{40,72},{48,80},{56,88},{... | collective-permute-start | bytes 1572872 | tf_op jit(solution)/shard_map/ppermute | solution.py:21
  56.2 15.4 %collective-permute-start.5 = (f32[256,512]{1,0:T(8,128)S(1)}, f32[256,512]{1,0:T(8,128)S(1)}, u32[]{:S(2)}, u32[]{:S(2)}) collective-permute-start(f32[256,512]{1,0:T(8,128)S(1)} %get-tuple-element.68.refs_0_), channel_id=1, source_target_pairs={{0,16},{8,24},{16,0},{24,8},{32,48},{40,56},{48,32},{56,40},{64,80... | collective-permute-start | bytes 1572872 | tf_op jit(solution)/shard_map/ppermute | solution.py:21
  69.0 8.9 %collective-permute-start.21 = (f32[128,512]{1,0:T(8,128)S(1)}, f32[128,512]{1,0:T(8,128)S(1)}, u32[]{:S(2)}, u32[]{:S(2)}) collective-permute-start(f32[128,512]{1,0:T(8,128)S(1)} %get-tuple-element.106), channel_id=1, source_target_pairs={{0,96},{8,104},{16,112},{24,120},{32,64},{40,72},{48,80},{56,88},{... | collective-permute-start | bytes 786440 | tf_op jit(solution)/shard_map/ppermute | solution.py:21
  71.6 7.5 %collective-permute-start.24 = (f32[128,512]{1,0:T(8,128)S(1)}, f32[128,512]{1,0:T(8,128)S(1)}, u32[]{:S(2)}, u32[]{:S(2)}) collective-permute-start(f32[128,512]{1,0:T(8,128)S(1)} %get-tuple-element.111), channel_id=1, source_target_pairs={{0,16},{8,24},{16,0},{24,8},{32,48},{40,56},{48,32},{56,40},{64,80... | collective-permute-start | bytes 786440 | tf_op jit(solution)/shard_map/ppermute | solution.py:21
  77.9 14.0 %collective-permute-start.6 = (f32[128,512]{1,0:T(8,128)S(1)}, f32[128,512]{1,0:T(8,128)S(1)}, u32[]{:S(2)}, u32[]{:S(2)}) collective-permute-start(f32[128,512]{1,0:T(8,128)S(1)} %get-tuple-element.70), channel_id=1, source_target_pairs={{0,32},{8,40},{16,48},{24,56},{32,0},{40,8},{48,16},{56,24},{64,96... | collective-permute-start | bytes 786440 | tf_op jit(solution)/shard_map/ppermute | solution.py:21
  79.1 24.6 %collective-permute-start.22 = (f32[64,512]{1,0:T(8,128)S(1)}, f32[64,512]{1,0:T(8,128)}, u32[]{:S(2)}, u32[]{:S(2)}) collective-permute-start(f32[64,512]{1,0:T(8,128)S(1)} %get-tuple-element.108), channel_id=1, source_target_pairs={{0,16},{8,24},{16,0},{24,8},{32,48},{40,56},{48,32},{56,40},{64,80... | collective-permute-start | bytes 393224 | tf_op jit(solution)/shard_map/ppermute | solution.py:21
  81.3 24.0 %collective-permute-start.25 = (f32[64,512]{1,0:T(8,128)}, f32[64,512]{1,0:T(8,128)}, u32[]{:S(2)}, u32[]{:S(2)}) collective-permute-start(f32[64,512]{1,0:T(8,128)} %get-tuple-element.113), channel_id=1, source_target_pairs={{0,32},{8,40},{16,48},{24,56},{32,0},{40,8},{48,16},{56,24},{64,96... | collective-permute-start | bytes 393224 | tf_op jit(solution)/shard_map/ppermute | solution.py:21
  84.2 2.9 %copy-start.5 = (f32[256,512]{1,0:T(8,128)}, f32[256,512]{1,0:T(8,128)S(1)}, u32[]{:S(2)}) copy-start(f32[256,512]{1,0:T(8,128)S(1)} %get-tuple-element.79) | copy-start | bytes 1572868
  84.2 1.3 collective-permute-start.13
  85.5 3.8 %collective-permute-start.14 = (f32[2,2048]{1,0:T(2,128)S(1)}, f32[2,2048]{1,0:T(2,128)S(1)}, u32[]{:S(2)}, u32[]{:S(2)}) collective-permute-start(f32[2,2048]{1,0:T(2,128)S(1)} %add.59), channel_id=1, source_target_pairs={{0,16},{8,24},{16,0},{24,8},{32,48},{40,56},{48,32},{56,40},{64,80... | collective-permute-start | bytes 49160 | tf_op jit(solution)/shard_map/ppermute | solution.py:21
  86.1 24.3 %collective-permute-start.26 = (f32[256,512]{1,0:T(8,128)}, f32[256,512]{1,0:T(8,128)S(1)}, u32[]{:S(2)}, u32[]{:S(2)}) collective-permute-start(f32[256,512]{1,0:T(8,128)} %get-tuple-element.88), channel_id=1, source_target_pairs={{0,32},{8,40},{16,48},{24,56},{32,0},{40,8},{48,16},{56,24},{64,96... | collective-permute-start | bytes 1572872 | tf_op jit(solution)/shard_map/ppermute | solution.py:21
  89.3 21.9 %collective-permute-start.29 = (f32[256,512]{1,0:T(8,128)}, f32[256,512]{1,0:T(8,128)S(1)}, u32[]{:S(2)}, u32[]{:S(2)}) collective-permute-start(f32[256,512]{1,0:T(8,128)} %get-tuple-element.97), channel_id=1, source_target_pairs={{0,96},{8,104},{16,112},{24,120},{32,64},{40,72},{48,80},{56,88},{... | collective-permute-start | bytes 1572872 | tf_op jit(solution)/shard_map/ppermute | solution.py:21
  91.9 8.6 %collective-permute-start.15 = (f32[2,2048]{1,0:T(2,128)S(1)}, f32[2,2048]{1,0:T(2,128)}, u32[]{:S(2)}, u32[]{:S(2)}) collective-permute-start(f32[2,2048]{1,0:T(2,128)S(1)} %add.60), channel_id=1, source_target_pairs={{0,32},{8,40},{16,48},{24,56},{32,0},{40,8},{48,16},{56,24},{64,96... | collective-permute-start | bytes 49160 | tf_op jit(solution)/shard_map/ppermute | solution.py:21
  100.4 28.9 %collective-permute-start.7 = (f32[64,512]{1,0:T(8,128)S(1)}, f32[64,512]{1,0:T(8,128)S(1)}, u32[]{:S(2)}, u32[]{:S(2)}) collective-permute-start(f32[64,512]{1,0:T(8,128)S(1)} %get-tuple-element.72), channel_id=1, source_target_pairs={{0,96},{8,104},{16,112},{24,120},{32,64},{40,72},{48,80},{56,88},{... | collective-permute-start | bytes 393224 | tf_op jit(solution)/shard_map/ppermute | solution.py:21
  103.7 15.1 %collective-permute-start.17 = (f32[256,512]{1,0:T(8,128)}, f32[256,512]{1,0:T(8,128)S(1)}, u32[]{:S(2)}, u32[]{:S(2)}) collective-permute-start(f32[256,512]{1,0:T(8,128)} %copy-done.5), channel_id=1, source_target_pairs={{0,16},{8,24},{16,0},{24,8},{32,48},{40,56},{48,32},{56,40},{64,80... | collective-permute-start | bytes 1572872 | tf_op jit(solution)/shard_map/ppermute | solution.py:21
  105.4 5.0 %collective-permute-start.16 = (f32[2,2048]{1,0:T(2,128)S(1)}, f32[2,2048]{1,0:T(2,128)S(1)}, u32[]{:S(2)}, u32[]{:S(2)}) collective-permute-start(f32[2,2048]{1,0:T(2,128)S(1)} %add.61), channel_id=1, source_target_pairs={{0,96},{8,104},{16,112},{24,120},{32,64},{40,72},{48,80},{56,88},{... | collective-permute-start | bytes 49160 | tf_op jit(solution)/shard_map/ppermute | solution.py:21
  110.4 8.6 %collective-permute-start.27 = (f32[128,512]{1,0:T(8,128)S(1)}, f32[128,512]{1,0:T(8,128)S(1)}, u32[]{:S(2)}, u32[]{:S(2)}) collective-permute-start(f32[128,512]{1,0:T(8,128)S(1)} %get-tuple-element.116), channel_id=1, source_target_pairs={{0,96},{8,104},{16,112},{24,120},{32,64},{40,72},{48,80},{56,88},{... | collective-permute-start | bytes 786440 | tf_op jit(solution)/shard_map/ppermute | solution.py:21
  111.3 12.2 %collective-permute-start.30 = (f32[128,512]{1,0:T(8,128)S(1)}, f32[128,512]{1,0:T(8,128)S(1)}, u32[]{:S(2)}, u32[]{:S(2)}) collective-permute-start(f32[128,512]{1,0:T(8,128)S(1)} %get-tuple-element.121), channel_id=1, source_target_pairs={{0,16},{8,24},{16,0},{24,8},{32,48},{40,56},{48,32},{56,40},{64,80... | collective-permute-start | bytes 786440 | tf_op jit(solution)/shard_map/ppermute | solution.py:21
  118.9 7.9 %collective-permute-start.18 = (f32[128,512]{1,0:T(8,128)S(1)}, f32[128,512]{1,0:T(8,128)S(1)}, u32[]{:S(2)}, u32[]{:S(2)}) collective-permute-start(f32[128,512]{1,0:T(8,128)S(1)} %get-tuple-element.101), channel_id=1, source_target_pairs={{0,32},{8,40},{16,48},{24,56},{32,0},{40,8},{48,16},{56,24},{64,96... | collective-permute-start | bytes 786440 | tf_op jit(solution)/shard_map/ppermute | solution.py:21
  119.0 8.5 %collective-permute-start.28 = (f32[64,512]{1,0:T(8,128)S(1)}, f32[64,512]{1,0:T(8,128)S(1)}, u32[]{:S(2)}, u32[]{:S(2)}) collective-permute-start(f32[64,512]{1,0:T(8,128)S(1)} %get-tuple-element.118), channel_id=1, source_target_pairs={{0,16},{8,24},{16,0},{24,8},{32,48},{40,56},{48,32},{56,40},{64,80... | collective-permute-start | bytes 393224 | tf_op jit(solution)/shard_map/ppermute | solution.py:21
  123.5 5.0 %collective-permute-start.31 = (f32[64,512]{1,0:T(8,128)S(1)}, f32[64,512]{1,0:T(8,128)S(1)}, u32[]{:S(2)}, u32[]{:S(2)}) collective-permute-start(f32[64,512]{1,0:T(8,128)S(1)} %get-tuple-element.123), channel_id=1, source_target_pairs={{0,32},{8,40},{16,48},{24,56},{32,0},{40,8},{48,16},{56,24},{64,96... | collective-permute-start | bytes 393224 | tf_op jit(solution)/shard_map/ppermute | solution.py:21
  126.8 6.3 %collective-permute-start.19 = (f32[64,512]{1,0:T(8,128)S(1)}, f32[64,512]{1,0:T(8,128)S(1)}, u32[]{:S(2)}, u32[]{:S(2)}) collective-permute-start(f32[64,512]{1,0:T(8,128)S(1)} %get-tuple-element.103), channel_id=1, source_target_pairs={{0,96},{8,104},{16,112},{24,120},{32,64},{40,72},{48,80},{56,88},{... | collective-permute-start | bytes 393224 | tf_op jit(solution)/shard_map/ppermute | solution.py:21
where the time goes:
time: 134 us
  waiting for transfers between devices  51.3 us (38%)
  starting transfers between devices  36 us (27%)
  Pallas kernels  34.4 us (26%)
  local copies, waits for them, and re-layouts  7.62 us (6%)
  other arithmetic  3.49 us (3%)
    ppermute x32, waiting for transfers between devices, swap(): return lax.ppermute(array, axis, [(d, d ^ flip) for d in range(size)])  51.3 us
    ppermute x32, starting transfers between devices, swap(): return lax.ppermute(array, axis, [(d, d ^ flip) for d in range(size)])  36 us
    pallas_call x6, Pallas kernels, cross(): pl.pallas_call(cross_kernel, out_shape=(part, part), in_specs=[pl.BlockSp...  15.1 us
    pallas_call x2, Pallas kernels, features(): pl.pallas_call(feature_kernel, grid=(width // LANES,), out_shape=(feature...  13.1 us
    unnamed x25, local copies, waits for them, and re-layouts  7.54 us
    pallas_call x18, Pallas kernels, fold(): pl.pallas_call(fold_kernel, out_shape=(part, part), cost_estimate=pl.Cost...  3.44 us
    pallas_call x1, Pallas kernels, unpack(): pl.pallas_call(unpack_kernel, out_shape=(design,) * 3 + (jax.ShapeDtypeSt...  2.86 us
  transfers between devices with their start and end apart: 32, of which 13 were waited for; matrix products, arithmetic and copies ran while one was open for 3% of the time, Pallas kernels for 21%

commit v1 on v0

v1 whole, which is shorter than its diff:
```python
import functools

import jax
import jax.numpy as jnp
from jax import lax
from jax.experimental import pallas as pl
from jax.experimental.pallas import tpu as pltpu
from jax.sharding import PartitionSpec as P

BITS = 30
HALF = BITS // 2
LANES = 128
MIB = 1024 * 1024
MADE = (2, 6)
CHUNKS = (2, 4, 2)
GROUPS = ((0, 1), (2,))
DOS_CHUNK = 1
EXTRA = 8

CORE, SIDE_Y, SIDE_A, SIDE_B = 1, 2, 4, 12
ORDERS = ((SIDE_Y, SIDE_A, SIDE_B), (SIDE_A, SIDE_B, SIDE_Y), (SIDE_B, SIDE_Y, SIDE_A))


def swap(array, axis, flip):
    size = lax.axis_size(axis)
    return lax.ppermute(array, axis, [(d, d ^ flip) for d in range(size)])


def place_of(relative, order):
    bits = {
        SIDE_Y: (relative >> 1) & 1,
        SIDE_A: ((relative >> 2) ^ (relative >> 3)) & 1,
        SIDE_B: (relative >> 3) & 1,
    }
    place = relative & 1
    for side in order:
        place = 2 * place + bits[side]
    return place


def whole(count):
    return [pl.BlockSpec(memory_space=pltpu.VMEM)] * count


def params(mib):
    return pltpu.CompilerParams(vmem_limit_bytes=mib * MIB)


def unpack_kernel(where_ref, own_ref, twin_ref, *refs):
    far_refs, (dosage_ref, phase_ref, mixed_ref, margin_ref) = refs[:-4], refs[-4:]
    samp, var = where_ref[0], where_ref[1]
    low = (1 << HALF) - 1
    words, block = own_ref.shape[1:]
    rows = block // 2
    samples = float(words * BITS)
    one, zero = jnp.bfloat16(1), jnp.bfloat16(0)
    pieces = [(0, own_ref, 0), (1, twin_ref, 0)]
    for step, far_ref in enumerate(far_refs):
        pieces += [(2 * step + 2 + twin, far_ref, 2 * twin) for twin in range(2)]
    for flip, word_ref, spot in pieces:
        source = var ^ flip
        first, second = word_ref[spot], word_ref[spot + 1]
        ones = lax.population_count(first) + lax.population_count(second)
        mixed = lax.population_count(first ^ second)
        margin_ref[pl.ds(source, 1), 0:1, :] = (
            jnp.sum(ones.astype(jnp.float32), axis=0, keepdims=True) - samples
        )[None]
        margin_ref[pl.ds(source, 1), 1:2, :] = (
            samples - jnp.sum(mixed.astype(jnp.float32), axis=0, keepdims=True)
        )[None]
        turned = [
            jnp.concatenate([w & low, (w >> HALF) & low], axis=0).T.astype(jnp.int16)
            for w in (first, second)
        ]
        for part in range(2):
            relative = (2 * source + part) ^ samp
            starts = [pl.multiple_of(place_of(relative, order) * rows, rows) for order in ORDERS]
            mine = [t[part * rows : (part + 1) * rows] for t in turned]
            for bit in range(HALF):
                mask = jnp.int16(1 << bit)
                hap_one = jnp.where((mine[0] & mask) != 0, one, zero)
                hap_two = jnp.where((mine[1] & mask) != 0, one, zero)
                phase = hap_one - hap_two
                lanes = slice(bit * 2 * words, (bit + 1) * 2 * words)
                dosage_ref[pl.ds(starts[0], rows), lanes] = (hap_one + hap_two) - one
                phase_ref[pl.ds(starts[1], rows), lanes] = phase
                mixed_ref[pl.ds(starts[2], rows), lanes] = phase * phase


def unpack(where, own, twin, far):
    _, words, block = own.shape
    count = 2 + 2 * len(far)
    variants, samples = count * block, words * BITS
    design = jax.ShapeDtypeStruct((variants, samples), jnp.bfloat16)
    return pl.pallas_call(
        unpack_kernel,
        out_shape=(design,) * 3 + (jax.ShapeDtypeStruct((count, 2, block), jnp.float32),),
        in_specs=[pl.BlockSpec(memory_space=pltpu.SMEM)] + whole(2 + len(far)),
        cost_estimate=pl.CostEstimate(
            flops=6_000_000_000, bytes_accessed=6 * variants * samples, transcendentals=0
        ),
        compiler_params=params(8),
        name="unpack",
    )(where, own, twin, *far)


def feature_kernel(first, total_hbm, one_hbm, two_hbm, *refs):
    total_out, weighted_out, weight_out, margin_ref, buffer, sems = refs[-6:]
    blocks, samples = total_out.shape[:2]
    words = samples // BITS

    def copies(block):
        lanes = pl.ds((first + block) * LANES, LANES)
        return [
            pltpu.make_async_copy(ref.at[:, lanes], buffer.at[spot, block], sems.at[spot, block])
            for spot, ref in enumerate((total_hbm, one_hbm, two_hbm))
        ]

    for block in range(blocks):
        for copy in copies(block):
            copy.start()
    for block in range(blocks):
        for copy in copies(block):
            copy.wait()

        def step(bit, sums, block=block):
            log_sum, log_sq = sums
            for half in range(2):
                rows = pl.ds(bit + half * HALF, words, stride=BITS)
                spot = pl.ds(pl.multiple_of((2 * bit + half) * words, words), words)
                log_total = jnp.log(buffer[0, block, rows, :].astype(jnp.float32) + 1.0)
                one_plus = buffer[1, block, rows, :].astype(jnp.float32) + 1.0
                two_plus = buffer[2, block, rows, :].astype(jnp.float32) + 1.0
                log_ratio = jnp.log(one_plus / two_plus)
                weight = (one_plus * two_plus) / (one_plus + two_plus)
                total_out[block, spot, :] = log_total.astype(jnp.bfloat16)
                weighted_out[block, spot, :] = (weight * log_ratio).astype(jnp.bfloat16)
                weight_out[block, spot, :] = weight.astype(jnp.bfloat16)
                folded = log_total.reshape(words // 8, 8, LANES)
                log_sum = log_sum + jnp.sum(folded, axis=0)
                log_sq = log_sq + jnp.sum(folded * folded, axis=0)
            return log_sum, log_sq

        blank = jnp.zeros((8, LANES), jnp.float32)
        sums = lax.fori_loop(0, HALF, step, (blank, blank), unroll=3)
        for kind in range(2):
            margin_ref[kind : kind + 1, block * LANES : (block + 1) * LANES] = jnp.sum(
                sums[kind], axis=0, keepdims=True
            )


def features(total_counts, allele_one, allele_two, first, blocks, after):
    samples = total_counts.shape[0]
    width = blocks * LANES
    feature = jax.ShapeDtypeStruct((blocks, samples, LANES), jnp.bfloat16)
    return pl.pallas_call(
        functools.partial(feature_kernel, first),
        out_shape=(feature,) * 3 + (jax.ShapeDtypeStruct((2, width), jnp.float32),),
        in_specs=[pl.BlockSpec(memory_space=pltpu.HBM)] * 3
        + [pl.BlockSpec(memory_space=pl.ANY)] * len(after),
        out_specs=tuple(whole(4)),
        scratch_shapes=[
            pltpu.VMEM((3, blocks, samples, LANES), jnp.int32),
            pltpu.SemaphoreType.DMA((3, blocks)),
        ],
        cost_estimate=pl.CostEstimate(
            flops=12_000_000 * width, bytes_accessed=18 * samples * width, transcendentals=0
        ),
        compiler_params=params(44),
        name="features",
    )(total_counts, allele_one, allele_two, *after)


def cross_kernel(spots, margins, design_ref, *refs):
    keep_ref, send_ref = refs[-2:]
    calls = 1 + max(call for call, _ in spots)
    feature_refs, margin_refs = refs[:calls], refs[calls : calls + margins]
    kept = design_ref.shape[0] // 2
    for pair in range(len(spots) // 2):
        right = jnp.concatenate(
            [feature_refs[call][block] for call, block in spots[2 * pair : 2 * pair + 2]], axis=1
        )
        lanes = slice(pair * 2 * LANES, (pair + 1) * 2 * LANES)
        for part, out_ref in ((1, send_ref), (0, keep_ref)):
            out_ref[:kept, lanes] = jnp.dot(
                design_ref[part * kept : (part + 1) * kept, :],
                right,
                preferred_element_type=jnp.float32,
            )
    if margins:
        blank = jnp.zeros((EXTRA - 2, LANES), jnp.float32)
        for place, (call, block) in enumerate(spots):
            gene = margin_refs[call][:, block * LANES : (block + 1) * LANES]
            rest = blank
            if margins > calls:
                dos_ref = margin_refs[calls]
                picked = [
                    dos_ref[spot // 2, spot % 2 : spot % 2 + 1, :]
                    for spot in range(place, 2 * dos_ref.shape[0], len(spots))
                ]
                rest = jnp.concatenate([*picked, blank[len(picked) :]], axis=0)
            rows = jnp.concatenate([gene, rest], axis=0)
            lanes = slice(place * LANES, (place + 1) * LANES)
            keep_ref[kept:, lanes] = rows
            send_ref[kept:, lanes] = rows


def cross(design, features_of, spots, margins, after):
    variants, samples = design.shape
    width = len(spots) * LANES
    rows = variants // 2 + (EXTRA if margins else 0)
    part = jax.ShapeDtypeStruct((rows, width), jnp.float32)
    return pl.pallas_call(
        functools.partial(cross_kernel, spots, len(margins)),
        out_shape=(part, part),
        in_specs=whole(1 + len(features_of) + len(margins))
        + [pl.BlockSpec(memory_space=pl.ANY)] * len(after),
        cost_estimate=pl.CostEstimate(
            flops=2 * variants * samples * width,
            bytes_accessed=2 * (variants + width) * samples,
            transcendentals=0,
        ),
        compiler_params=params(8),
        name="cross",
    )(design, *features_of, *margins, *after)


def fold_kernel(extra, *refs):
    keep_ref, send_ref = refs[-2:]
    count = (len(refs) - 2) // 2
    half = keep_ref.shape[0] - extra
    first = 0
    for left_ref, right_ref in zip(refs[:count], refs[count : 2 * count]):
        lanes = slice(first, first + left_ref.shape[1])
        first += left_ref.shape[1]
        keep_ref[:half, lanes] = left_ref[:half] + right_ref[:half]
        send_ref[:half, lanes] = left_ref[half : 2 * half] + right_ref[half : 2 * half]
        if extra:
            margin = left_ref[2 * half :] + right_ref[2 * half :]
            keep_ref[half:, lanes] = margin
            send_ref[half:, lanes] = margin


def fold(lefts, rights, extra):
    half = (lefts[0].shape[0] - extra) // 2
    width = sum(left.shape[1] for left in lefts)
    part = jax.ShapeDtypeStruct((half + extra, width), jnp.float32)
    return pl.pallas_call(
        functools.partial(fold_kernel, extra),
        out_shape=(part, part),
        in_specs=whole(2 * len(lefts)),
        cost_estimate=pl.CostEstimate(
            flops=2 * half * width, bytes_accessed=24 * half * width, transcendentals=0
        ),
        compiler_params=params(8),
        name="fold",
    )(*lefts, *rights)


def finish_kernel(sample_count, dos_first, dos_blocks, where_ref, *refs):
    left_refs, right_refs, (total_ref, allelic_ref) = refs[:3], refs[3:6], refs[6:]
    own = total_ref.shape[0]
    samp = where_ref[0]
    margin = left_refs[0][own:, :] + right_refs[0][own:, :]
    columns = []
    for kind in range(2):
        picked = jnp.zeros((1, LANES), jnp.float32)
        for source in range(lax.axis_size("var")):
            spot = 2 * source + kind
            row, block = 2 + spot // dos_blocks, dos_first + spot % dos_blocks
            row_now = margin[row : row + 1, block * LANES : (block + 1) * LANES]
            picked = jnp.where(samp >> 1 == source, row_now, picked)
        turned = jnp.broadcast_to(picked, (LANES, LANES)).T
        columns.append(jnp.where(samp & 1 == 0, turned[:own], turned[own:]))
    dos_sum, dos_sq = columns
    dosage_var = dos_sq - dos_sum * dos_sum / sample_count
    scale = jnp.sqrt(jnp.float32(sample_count))
    for block in range(total_ref.shape[1] // LANES):
        lanes = slice(block * LANES, (block + 1) * LANES)
        gene_sum, gene_sq = margin[0:1, lanes], margin[1:2, lanes]
        gene_var = gene_sq - gene_sum * gene_sum / sample_count
        pair_sums = [
            left_ref[:own, lanes] + right_ref[:own, lanes]
            for left_ref, right_ref in zip(left_refs, right_refs)
        ]
        covariance = pair_sums[0] - dos_sum * gene_sum / sample_count
        total_ref[:, lanes] = (
            scale * covariance / jnp.sqrt((dosage_var + 1.0) * (gene_var + 1.0))
        )
        allelic_ref[:, lanes] = pair_sums[1] / jnp.sqrt(pair_sums[2] + 1.0)


def finish(where, lefts, rights, sample_count):
    own, width = lefts[1].shape
    dos_first = sum(CHUNKS[:DOS_CHUNK])
    out = jax.ShapeDtypeStruct((own, width), jnp.float32)
    return pl.pallas_call(
        functools.partial(finish_kernel, sample_count, dos_first, CHUNKS[DOS_CHUNK]),
        out_shape=(out, out),
        in_specs=[pl.BlockSpec(memory_space=pltpu.SMEM)] + whole(6),
        compiler_params=params(8),
        name="finish",
    )(where, *lefts, *rights)


def per_device(hap_words, total_counts, allele_one, allele_two):
    where = jnp.stack([lax.axis_index("samp"), lax.axis_index("var")]).astype(jnp.int32)
    twin = swap(hap_words, "var", 1)
    counts = (total_counts, allele_one, allele_two)
    made = []
    for call, blocks in enumerate(MADE):
        first = sum(MADE[:call])
        made.append(features(*counts, first, blocks, (twin,) if call else ()))
    pair = jnp.concatenate([hap_words, twin], axis=0)
    far = []
    for flip in (2, 4, 6):
        far.append(swap(pair, "var", flip))
    *designs, dos_part = unpack(where, hap_words, twin, far)
    spots = [(call, block) for call, blocks in enumerate(MADE) for block in range(blocks)]
    extras = (EXTRA, 0, 0)
    lefts = [[] for _ in range(3)]
    rights = [[] for _ in range(3)]
    waits = [()] * 3
    for chunk, blocks in enumerate(CHUNKS):
        first = sum(CHUNKS[:chunk])
        mine = spots[first : first + blocks]
        calls = 1 + max(call for call, _ in mine)
        for index in range(3):
            margins = [made[call][3] for call in range(calls)] if index == 0 else []
            if margins and chunk == DOS_CHUNK:
                margins.append(dos_part)
            keep, send = cross(
                designs[index],
                [made[call][index] for call in range(calls)],
                mine,
                margins,
                waits[index],
            )
            got = swap(send, "samp", CORE)
            keep, send = fold([keep], [got], extras[index])
            waits[index] = (send,)
            lefts[index].append(keep)
            rights[index].append(swap(send, "samp", ORDERS[index][0]))
    for groups, step in ((GROUPS, 1), ((range(len(GROUPS)),), 2)):
        new_lefts = [[] for _ in range(3)]
        new_rights = [[] for _ in range(3)]
        for group in groups:
            for index in range(3):
                keep, send = fold(
                    [lefts[index][g] for g in group],
                    [rights[index][g] for g in group],
                    extras[index],
                )
                new_lefts[index].append(keep)
                new_rights[index].append(swap(send, "samp", ORDERS[index][step]))
        lefts, rights = new_lefts, new_rights
    sample_count = float(total_counts.shape[0] * lax.axis_size("samp"))
    return finish(
        where, [left[0] for left in lefts], [right[0] for right in rights], sample_count
    )


def solution(mesh):
    in_specs = (P(None, "samp", "var"), P("samp", "var"), P("samp", "var"), P("samp", "var"))
    out_specs = (P("samp", "var"), P("samp", "var"))

    return jax.shard_map(
        per_device, mesh=mesh, in_specs=in_specs, out_specs=out_specs, check_vma=False
    )
```

time: 134 us -> 127 us (0.948)
  starting transfers between devices: 36 us -> 30.2 us
  waiting for transfers between devices: 51.3 us -> 46.9 us
  local copies, waits for them, and re-layouts: 7.62 us -> 11.5 us
  other arithmetic: 3.49 us -> 0.07 us
  Pallas kernels: 34.4 us -> 36.6 us
    ppermute x32 -> x31, starting transfers between devices: 36 us -> 30.2 us  [swap(): return lax.ppermute(array, axis, [(d, d ^ flip) for d in range(size)])]
    ppermute x32 -> x31, waiting for transfers between devices: 51.3 us -> 46.9 us  [swap(): return lax.ppermute(array, axis, [(d, d ^ flip) for d in range(size)])]
    unnamed x25 -> x47, local copies, waits for them, and re-layouts: 7.54 us -> 11.5 us
    pallas_call x26 -> x30, Pallas kernels: 31.6 us -> 33.7 us  [the longest x9 16.9 us: cross(): pl.pallas_call(functools.partial(cross_kernel, spots, len(margins)), out_...]
    concatenate x3 -> x0, other arithmetic: 1.45 us -> none  [the longest x2 1.44 us: per_device(): return tuple((jnp.concatenate(parts, axis=1) for parts in zip(*outs)))]
  transfers between devices with their start and end apart: 32 -> 31, of which waited for: 13 -> 10; matrix products, arithmetic and copies ran while one was open for 3% -> 1% of each run, Pallas kernels for 21% -> 24%
where the time goes in v1:
time: 127 us; the launch traced here: 126 us
  waiting for transfers between devices  46.9 us (37%)
  Pallas kernels  36.6 us (29%)
  starting transfers between devices  30.2 us (24%)
  local copies, waits for them, and re-layouts  11.5 us (9%)
    ppermute x31, waiting for transfers between devices, swap(): return lax.ppermute(array, axis, [(d, d ^ flip) for d in range(size)])  46.9 us
    ppermute x31, starting transfers between devices, swap(): return lax.ppermute(array, axis, [(d, d ^ flip) for d in range(size)])  30.2 us
    pallas_call x9, Pallas kernels, cross(): pl.pallas_call(functools.partial(cross_kernel, spots, len(margins)), out_...  16.9 us
    unnamed x47, local copies, waits for them, and re-layouts  11.5 us
    pallas_call x2, Pallas kernels, features(): pl.pallas_call(functools.partial(feature_kernel, first), out_shape=(featu...  10.8 us
    pallas_call x18, Pallas kernels, fold(): pl.pallas_call(functools.partial(fold_kernel, extra), out_shape=(part, pa...  4.41 us
    pallas_call x1, Pallas kernels, unpack(): pl.pallas_call(unpack_kernel, out_shape=(design,) * 3 + (jax.ShapeDtypeSt...  2.86 us
  transfers between devices with their start and end apart: 31, of which 10 were waited for; matrix products, arithmetic and copies ran while one was open for 1% of the time, Pallas kernels for 24%

profile of v1, /device:TPU:0, one launch (start us, length us, event | category | flops | bytes accessed | tf_op | source)
XLA Modules:
  0.0 126.3 jit_solution(6282085652919092904)
XLA Ops:
  0.6 3.4 %collective-permute-start = (s32[2,64,128]{2,1,0:T(8,128)}, s32[2,64,128]{2,1,0:T(8,128)S(1)}, u32[]{:S(2)}, u32[]{:S(2)}) collective-permute-start(s32[2,64,128]{2,1,0:T(8,128)} %own_ref.1), channel_id=1, source_target_pairs={{0,1},{1,0},{2,3},{3,2},{4,5},{5,4},{6,7},{7,6},{8,9},{9,8},{10,11... | collective-permute-start | bytes 196616 | tf_op jit(solution)/shard_map/ppermute | solution.py:26
  4.0 0.9 constant_dynamic-update-slice_fusion.1
  4.9 1.8 %collective-permute-done.twin_ref.refs_0_ = s32[2,64,128]{2,1,0:T(8,128)S(1)} collective-permute-done((s32[2,64,128]{2,1,0:T(8,128)}, s32[2,64,128]{2,1,0:T(8,128)S(1)}, u32[]{:S(2)}, u32[]{:S(2)}) %collective-permute-start) | collective-permute-done | bytes 65568 | tf_op jit(solution)/shard_map/ppermute | solution.py:26
  6.7 1.7 %collective-permute-start.1 = (s32[4,64,128]{2,1,0:T(8,128)S(1)}, s32[4,64,128]{2,1,0:T(8,128)S(1)}, u32[]{:S(2)}, u32[]{:S(2)}) collective-permute-start(s32[4,64,128]{2,1,0:T(8,128)S(1)} %constant_dynamic-update-slice_fusion), channel_id=1, source_target_pairs={{0,2},{1,3},{2,0},{3,1},{4,6},{5,7},{6,4},{7,5},{8,10},{9,11},{10,... | collective-permute-start | bytes 393224 | tf_op jit(solution)/shard_map/ppermute | solution.py:26
  8.4 2.7 %collective-permute-start.2 = (s32[4,64,128]{2,1,0:T(8,128)S(1)}, s32[4,64,128]{2,1,0:T(8,128)S(1)}, u32[]{:S(2)}, u32[]{:S(2)}) collective-permute-start(s32[4,64,128]{2,1,0:T(8,128)S(1)} %constant_dynamic-update-slice_fusion), channel_id=1, source_target_pairs={{0,4},{1,5},{2,6},{3,7},{4,0},{5,1},{6,2},{7,3},{8,12},{9,13},{10,... | collective-permute-start | bytes 393224 | tf_op jit(solution)/shard_map/ppermute | solution.py:26
  11.1 0.4 collective-permute-start.3
  11.5 3.6 %features.2 = (bf16[2,1920,128]{2,1,0:T(8,128)(2,1)S(1)}, bf16[2,1920,128]{2,1,0:T(8,128)(2,1)S(1)}, bf16[2,1920,128]{2,1,0:T(8,128)(2,1)S(1)}, f32[2,256]{1,0:T(2,128)S(1)}) custom-call(s32[1920,1024]{1,0:T(8,128)} %total_hbm.3, s32[1920,1024]{1,0:T(8,128)} %one_hbm.3, s32[1920,1024]{1,0:T(8,128)} %two_hbm.3), custom_call_target="tpu_custom_call" | custom-call | flops 3072000000 | bytes 8847360 | tf_op jit(solution)/shard_map/features/pallas_call | solution.py:156
  15.1 1.0 copy-done
  16.0 0.9 copy-done.4
  17.0 1.0 copy-done.7
  18.0 0.7 copy-done.17
  18.7 0.7 copy-done.19
  19.3 0.6 copy-done.21
  20.0 0.9 copy-done.18
  20.9 0.9 copy-done.20
  21.8 0.9 copy-done.22
  22.7 2.9 %unpack.1 = (bf16[1024,1920]{1,0:T(8,128)(2,1)S(1)}, bf16[1024,1920]{1,0:T(8,128)(2,1)S(1)}, bf16[1024,1920]{1,0:T(8,128)(2,1)S(1)}, f32[8,2,128]{2,1,0:T(2,128)S(1)}) custom-call(s32[2]{0:T(128)S(1)} %pad_add_fusion.where_ref, s32[2,64,128]{2,1,0:T(8,128)S(1)} %copy-done.16, s32[2,64,128]{2,1,0:T(8,128)S(1)} %collective-permute-done.twin_ref.refs_0_, ...), custom_call_target="tpu_custom_call" | custom-call | flops 6000000000 | bytes 11796480 | tf_op jit(solution)/shard_map/unpack/pallas_call | solution.py:95
  25.6 2.1 %cross.15 = (f32[512,256]{1,0:T(8,128)S(1)}, f32[512,256]{1,0:T(8,128)}) custom-call(bf16[1024,1920]{1,0:T(8,128)(2,1)S(1)} %get-tuple-element.111.design_ref, bf16[2,1920,128]{2,1,0:T(8,128)(2,1)S(1)} %copy-done.8), custom_call_target="tpu_custom_call" | custom-call | flops 1006632960 | bytes 4915200 | tf_op jit(solution)/shard_map/cross/pallas_call | solution.py:213
  27.6 2.1 %cross.12 = (f32[512,256]{1,0:T(8,128)S(1)}, f32[512,256]{1,0:T(8,128)}) custom-call(bf16[1024,1920]{1,0:T(8,128)(2,1)S(1)} %get-tuple-element.91.design_ref, bf16[2,1920,128]{2,1,0:T(8,128)(2,1)S(1)} %copy-done.5), custom_call_target="tpu_custom_call" | custom-call | flops 1006632960 | bytes 4915200 | tf_op jit(solution)/shard_map/cross/pallas_call | solution.py:213
  29.7 0.5 collective-permute-start.12
  30.2 2.1 %cross.9 = (f32[520,256]{1,0:T(8,128)S(1)}, f32[520,256]{1,0:T(8,128)}) custom-call(bf16[1024,1920]{1,0:T(8,128)(2,1)S(1)} %get-tuple-element.68.design_ref, bf16[2,1920,128]{2,1,0:T(8,128)(2,1)S(1)} %copy-done.1, f32[2,256]{1,0:T(2,128)S(1)} %get-tuple-element.70.refs_1_.refs_2_), custom_call_target="tpu_custom_call" | custom-call | flops 1006632960 | bytes 4915200 | tf_op jit(solution)/shard_map/cross/pallas_call | solution.py:213
  32.3 0.8 copy-done.10
  33.1 7.2 %features.3 = (bf16[6,1920,128]{2,1,0:T(8,128)(2,1)S(1)}, bf16[6,1920,128]{2,1,0:T(8,128)(2,1)S(1)}, bf16[6,1920,128]{2,1,0:T(8,128)(2,1)S(1)}, f32[2,768]{1,0:T(2,128)S(1)}) custom-call(s32[1920,1024]{1,0:T(8,128)} %total_hbm.3, s32[1920,1024]{1,0:T(8,128)} %one_hbm.3, s32[1920,1024]{1,0:T(8,128)} %two_hbm.3, ...), custom_call_target="tpu_custom_call" | custom-call | flops 9216000000 | bytes 26542080 | tf_op jit(solution)/shard_map/features/pallas_call | solution.py:156
  40.4 1.0 copy-done.11
  41.4 1.1 fold.18
  42.5 1.2 copy-done.2
  43.7 2.3 %cross.10 = (f32[520,512]{1,0:T(8,128)S(1)}, f32[520,512]{1,0:T(8,128)S(1)}) custom-call(bf16[1024,1920]{1,0:T(8,128)(2,1)S(1)} %get-tuple-element.68.design_ref, bf16[2,1920,128]{2,1,0:T(8,128)(2,1)S(1)} %copy-done.2, bf16[6,1920,128]{2,1,0:T(8,128)(2,1)S(1)} %get-tuple-element.74.refs_1_, f32[2,256]{1,0:T(2,128)S(1)} %get-tuple-element.70.refs_1_.refs_2_, ...), custom_call_target="tpu_custom_call" | custom-call | flops 2013265920 | bytes 5898240 | tf_op jit(solution)/shard_map/cross/pallas_call | solution.py:213
  46.1 0.6 collective-permute-start.5
  46.7 1.1 fold.30
  47.8 2.3 %cross.16 = (f32[512,512]{1,0:T(8,128)S(1)}, f32[512,512]{1,0:T(8,128)S(1)}) custom-call(bf16[1024,1920]{1,0:T(8,128)(2,1)S(1)} %get-tuple-element.111.design_ref, bf16[2,1920,128]{2,1,0:T(8,128)(2,1)S(1)} %copy-done.9, bf16[6,1920,128]{2,1,0:T(8,128)(2,1)S(1)} %get-tuple-element.116.refs_1_, f32[256,256]{1,0:T(8,128)S(1)} %get-tuple-element.117.refs_2_), custom_call_target="tpu_custom_call" | custom-call | flops 2013265920 | bytes 5898240 | tf_op jit(solution)/shard_map/cross/pallas_call | solution.py:213
  50.1 0.3 collective-permute-start.21
  50.4 1.1 fold.24
  51.6 2.3 %cross.13 = (f32[512,512]{1,0:T(8,128)S(1)}, f32[512,512]{1,0:T(8,128)S(1)}) custom-call(bf16[1024,1920]{1,0:T(8,128)(2,1)S(1)} %get-tuple-element.91.design_ref, bf16[2,1920,128]{2,1,0:T(8,128)(2,1)S(1)} %copy-done.6, bf16[6,1920,128]{2,1,0:T(8,128)(2,1)S(1)} %get-tuple-element.96.refs_1_, f32[256,256]{1,0:T(8,128)S(1)} %get-tuple-element.97.refs_2_), custom_call_target="tpu_custom_call" | custom-call | flops 2013265920 | bytes 5898240 | tf_op jit(solution)/shard_map/cross/pallas_call | solution.py:213
  53.9 0.6 collective-permute-start.13
  54.5 0.2 fold.19
  54.6 1.3 cross.11
  55.9 0.1 collective-permute-start.8
  56.0 4.2 %collective-permute-start.22 = (f32[256,256]{1,0:T(8,128)S(1)}, f32[256,256]{1,0:T(8,128)S(1)}, u32[]{:S(2)}, u32[]{:S(2)}) collective-permute-start(f32[256,256]{1,0:T(8,128)S(1)} %get-tuple-element.117.refs_2_), channel_id=1, source_target_pairs={{0,96},{8,104},{16,112},{24,120},{32,64},{40,72},{48,80},{56,88},{... | collective-permute-start | bytes 786440 | tf_op jit(solution)/shard_map/ppermute | solution.py:26
  60.2 1.6 %collective-permute-start.6 = (f32[264,256]{1,0:T(8,128)S(1)}, f32[264,256]{1,0:T(8,128)S(1)}, u32[]{:S(2)}, u32[]{:S(2)}) collective-permute-start(f32[264,256]{1,0:T(8,128)S(1)} %get-tuple-element.77.refs_5_), channel_id=1, source_target_pairs={{0,16},{8,24},{16,0},{24,8},{32,48},{40,56},{48,32},{56,40},{64,80... | collective-permute-start | bytes 811016 | tf_op jit(solution)/shard_map/ppermute | solution.py:26
  61.8 0.1 fold.31
  61.9 1.3 cross.17
  63.2 3.9 %collective-permute-done.22.refs_2_ = f32[256,256]{1,0:T(8,128)S(1)} collective-permute-done((f32[256,256]{1,0:T(8,128)S(1)}, f32[256,256]{1,0:T(8,128)S(1)}, u32[]{:S(2)}, u32[]{:S(2)}) %collective-permute-start.22) | collective-permute-done | bytes 262176 | tf_op jit(solution)/shard_map/ppermute | solution.py:26
  67.1 3.0 %collective-permute-start.23 = (f32[256,512]{1,0:T(8,128)S(1)}, f32[256,512]{1,0:T(8,128)S(1)}, u32[]{:S(2)}, u32[]{:S(2)}) collective-permute-start(f32[256,512]{1,0:T(8,128)S(1)} %get-tuple-element.121.refs_2_), channel_id=1, source_target_pairs={{0,96},{8,104},{16,112},{24,120},{32,64},{40,72},{48,80},{56,88},{... | collective-permute-start | bytes 1572872 | tf_op jit(solution)/shard_map/ppermute | solution.py:26
  70.0 1.6 %collective-permute-start.7 = (f32[264,512]{1,0:T(8,128)S(1)}, f32[264,512]{1,0:T(8,128)S(1)}, u32[]{:S(2)}, u32[]{:S(2)}) collective-permute-start(f32[264,512]{1,0:T(8,128)S(1)} %get-tuple-element.81.refs_4_), channel_id=1, source_target_pairs={{0,16},{8,24},{16,0},{24,8},{32,48},{40,56},{48,32},{56,40},{64,80... | collective-permute-start | bytes 1622024 | tf_op jit(solution)/shard_map/ppermute | solution.py:26
  71.7 1.3 cross.14
  73.3 0.6 collective-permute-start.9
  73.8 8.2 %collective-permute-done.23.refs_3_ = f32[256,512]{1,0:T(8,128)S(1)} collective-permute-done((f32[256,512]{1,0:T(8,128)S(1)}, f32[256,512]{1,0:T(8,128)S(1)}, u32[]{:S(2)}, u32[]{:S(2)}) %collective-permute-start.23) | collective-permute-done | bytes 524320 | tf_op jit(solution)/shard_map/ppermute | solution.py:26
  82.0 3.2 %collective-permute-done.7.refs_3_ = f32[264,512]{1,0:T(8,128)S(1)} collective-permute-done((f32[264,512]{1,0:T(8,128)S(1)}, f32[264,512]{1,0:T(8,128)S(1)}, u32[]{:S(2)}, u32[]{:S(2)}) %collective-permute-start.7) | collective-permute-done | bytes 540704 | tf_op jit(solution)/shard_map/ppermute | solution.py:26
  85.2 0.3 collective-permute-start.25
  85.6 0.8 collective-permute-start.10
  86.6 7.0 %collective-permute-done.14.refs_2_ = f32[256,256]{1,0:T(8,128)S(1)} collective-permute-done((f32[256,256]{1,0:T(8,128)S(1)}, f32[256,256]{1,0:T(8,128)S(1)}, u32[]{:S(2)}, u32[]{:S(2)}) %collective-permute-start.14) | collective-permute-done | bytes 262176 | tf_op jit(solution)/shard_map/ppermute | solution.py:26
  93.6 0.5 collective-permute-start.26
  94.2 1.4 %collective-permute-start.18 = (f32[128,768]{1,0:T(8,128)S(1)}, f32[128,768]{1,0:T(8,128)S(1)}, u32[]{:S(2)}, u32[]{:S(2)}) collective-permute-start(f32[128,768]{1,0:T(8,128)S(1)} %get-tuple-element.108), channel_id=1, source_target_pairs={{0,96},{8,104},{16,112},{24,120},{32,64},{40,72},{48,80},{56,88},{... | collective-permute-start | bytes 1179656 | tf_op jit(solution)/shard_map/ppermute | solution.py:26
  95.6 1.5 %collective-permute-start.11 = (f32[136,256]{1,0:T(8,128)S(1)}, f32[136,256]{1,0:T(8,128)S(1)}, u32[]{:S(2)}, u32[]{:S(2)}) collective-permute-start(f32[136,256]{1,0:T(8,128)S(1)} %get-tuple-element.89), channel_id=1, source_target_pairs={{0,32},{8,40},{16,48},{24,56},{32,0},{40,8},{48,16},{56,24},{64,96... | collective-permute-start | bytes 417800 | tf_op jit(solution)/shard_map/ppermute | solution.py:26
  97.1 11.0 %collective-permute-done.17.refs_1_ = f32[256,256]{1,0:T(8,128)S(1)} collective-permute-done((f32[256,256]{1,0:T(8,128)S(1)}, f32[256,256]{1,0:T(8,128)S(1)}, u32[]{:S(2)}, u32[]{:S(2)}) %collective-permute-start.17) | collective-permute-done | bytes 262176 | tf_op jit(solution)/shard_map/ppermute | solution.py:26
  108.1 0.5 collective-permute-start.27
  108.7 1.9 %collective-permute-done.11.refs_3_ = f32[136,256]{1,0:T(8,128)S(1)} collective-permute-done((f32[136,256]{1,0:T(8,128)S(1)}, f32[136,256]{1,0:T(8,128)S(1)}, u32[]{:S(2)}, u32[]{:S(2)}) %collective-permute-start.11) | collective-permute-done | bytes 139296 | tf_op jit(solution)/shard_map/ppermute | solution.py:26
  110.6 0.3 collective-permute-start.19
  110.9 3.0 %collective-permute-start.28 = (f32[72,1024]{1,0:T(8,128)S(1)}, f32[72,1024]{1,0:T(8,128)S(1)}, u32[]{:S(2)}, u32[]{:S(2)}) collective-permute-start(f32[72,1024]{1,0:T(8,128)S(1)} %get-tuple-element.131), channel_id=1, source_target_pairs={{0,96},{8,104},{16,112},{24,120},{32,64},{40,72},{48,80},{56,88},{... | collective-permute-start | bytes 884744 | tf_op jit(solution)/shard_map/ppermute | solution.py:26
  114.1 4.0 %collective-permute-done.19.refs_3_ = f32[128,256]{1,0:T(8,128)S(1)} collective-permute-done((f32[128,256]{1,0:T(8,128)S(1)}, f32[128,256]{1,0:T(8,128)S(1)}, u32[]{:S(2)}, u32[]{:S(2)}) %collective-permute-start.19) | collective-permute-done | bytes 131104 | tf_op jit(solution)/shard_map/ppermute | solution.py:26
  118.2 0.6 collective-permute-start.29
  118.8 2.6 %collective-permute-done.30.refs_5_ = f32[64,1024]{1,0:T(8,128)S(1)} collective-permute-done((f32[64,1024]{1,0:T(8,128)S(1)}, f32[64,1024]{1,0:T(8,128)S(1)}, u32[]{:S(2)}, u32[]{:S(2)}) %collective-permute-start.30) | collective-permute-done | bytes 262176 | tf_op jit(solution)/shard_map/ppermute | solution.py:26
  121.3 3.3 %collective-permute-done.29.refs_4_ = f32[64,1024]{1,0:T(8,128)S(1)} collective-permute-done((f32[64,1024]{1,0:T(8,128)S(1)}, f32[64,1024]{1,0:T(8,128)S(1)}, u32[]{:S(2)}, u32[]{:S(2)}) %collective-permute-start.29) | collective-permute-done | bytes 262176 | tf_op jit(solution)/shard_map/ppermute | solution.py:26
  124.7 1.6 %finish.1 = (f32[64,1024]{1,0:T(8,128)}, f32[64,1024]{1,0:T(8,128)}) custom-call(s32[2]{0:T(128)S(1)} %pad_add_fusion.where_ref, f32[72,1024]{1,0:T(8,128)S(1)} %get-tuple-element.90.refs_0_, f32[64,1024]{1,0:T(8,128)S(1)} %get-tuple-element.110.refs_1_, f32[64,1024]{1,0:T(8,128)S(1)} %get-tuple-element.130.refs_2_, ...), custom_call_target="tpu_custom_call" | custom-call | tf_op jit(solution)/shard_map/finish/pallas_call | solution.py:297
  (78 shorter events, 1.4 us)
Async XLA Ops:
  0.6 6.1 %collective-permute-start = (s32[2,64,128]{2,1,0:T(8,128)}, s32[2,64,128]{2,1,0:T(8,128)S(1)}, u32[]{:S(2)}, u32[]{:S(2)}) collective-permute-start(s32[2,64,128]{2,1,0:T(8,128)} %own_ref.1), channel_id=1, source_target_pairs={{0,1},{1,0},{2,3},{3,2},{4,5},{5,4},{6,7},{7,6},{8,9},{9,8},{10,11... | collective-permute-start | bytes 196616 | tf_op jit(solution)/shard_map/ppermute | solution.py:26
  6.7 13.3 %copy-start.16 = (s32[2,64,128]{2,1,0:T(8,128)S(1)}, s32[2,64,128]{2,1,0:T(8,128)}, u32[]{:S(2)}) copy-start(s32[2,64,128]{2,1,0:T(8,128)} %own_ref.1) | copy-start | bytes 196612
  6.7 11.3 %collective-permute-start.1 = (s32[4,64,128]{2,1,0:T(8,128)S(1)}, s32[4,64,128]{2,1,0:T(8,128)S(1)}, u32[]{:S(2)}, u32[]{:S(2)}) collective-permute-start(s32[4,64,128]{2,1,0:T(8,128)S(1)} %constant_dynamic-update-slice_fusion), channel_id=1, source_target_pairs={{0,2},{1,3},{2,0},{3,1},{4,6},{5,7},{6,4},{7,5},{8,10},{9,11},{10,... | collective-permute-start | bytes 393224 | tf_op jit(solution)/shard_map/ppermute | solution.py:26
  8.4 10.3 %collective-permute-start.2 = (s32[4,64,128]{2,1,0:T(8,128)S(1)}, s32[4,64,128]{2,1,0:T(8,128)S(1)}, u32[]{:S(2)}, u32[]{:S(2)}) collective-permute-start(s32[4,64,128]{2,1,0:T(8,128)S(1)} %constant_dynamic-update-slice_fusion), channel_id=1, source_target_pairs={{0,4},{1,5},{2,6},{3,7},{4,0},{5,1},{6,2},{7,3},{8,12},{9,13},{10,... | collective-permute-start | bytes 393224 | tf_op jit(solution)/shard_map/ppermute | solution.py:26
  11.1 8.2 %collective-permute-start.3 = (s32[4,64,128]{2,1,0:T(8,128)S(1)}, s32[4,64,128]{2,1,0:T(8,128)S(1)}, u32[]{:S(2)}, u32[]{:S(2)}) collective-permute-start(s32[4,64,128]{2,1,0:T(8,128)S(1)} %constant_dynamic-update-slice_fusion), channel_id=1, source_target_pairs={{0,6},{1,7},{2,4},{3,5},{4,2},{5,3},{6,0},{7,1},{8,14},{9,15},{10,... | collective-permute-start | bytes 393224 | tf_op jit(solution)/shard_map/ppermute | solution.py:26
  15.1 1.0 copy-start
  16.0 1.0 copy-start.4
  17.0 1.0 copy-start.7
  18.0 7.6 %copy-start.8 = (bf16[2,1920,128]{2,1,0:T(8,128)(2,1)S(1)}, bf16[2,1920,128]{2,1,0:T(8,128)(2,1)}, u32[]{:S(2)}) copy-start(bf16[2,1920,128]{2,1,0:T(8,128)(2,1)} %copy-done.7) | copy-start | bytes 2949124
  18.0 0.7 copy-start.17
  18.7 0.7 copy-start.19
  19.3 0.6 copy-start.21
  20.0 0.9 copy-start.18
  20.9 0.9 copy-start.20
  21.8 0.9 copy-start.22
  25.6 2.1 %copy-start.5 = (bf16[2,1920,128]{2,1,0:T(8,128)(2,1)S(1)}, bf16[2,1920,128]{2,1,0:T(8,128)(2,1)}, u32[]{:S(2)}) copy-start(bf16[2,1920,128]{2,1,0:T(8,128)(2,1)} %copy-done.4) | copy-start | bytes 2949124
  25.6 4.6 %copy-start.1 = (bf16[2,1920,128]{2,1,0:T(8,128)(2,1)S(1)}, bf16[2,1920,128]{2,1,0:T(8,128)(2,1)}, u32[]{:S(2)}) copy-start(bf16[2,1920,128]{2,1,0:T(8,128)(2,1)} %copy-done) | copy-start | bytes 2949124
  27.6 4.6 %copy-start.14 = (f32[512,256]{1,0:T(8,128)}, f32[512,256]{1,0:T(8,128)S(1)}, u32[]{:S(2)}) copy-start(f32[512,256]{1,0:T(8,128)S(1)} %get-tuple-element.113.refs_0_) | copy-start | bytes 1572868
  27.6 19.0 %collective-permute-start.20 = (f32[512,256]{1,0:T(8,128)}, f32[512,256]{1,0:T(8,128)}, u32[]{:S(2)}, u32[]{:S(2)}) collective-permute-start(f32[512,256]{1,0:T(8,128)} %get-tuple-element.114), channel_id=1, source_target_pairs={{0,8},{8,0},{16,24},{24,16},{32,40},{40,32},{48,56},{56,48},{64,72... | collective-permute-start | bytes 1572872 | tf_op jit(solution)/shard_map/ppermute | solution.py:26
  29.7 3.4 %copy-start.12 = (f32[512,256]{1,0:T(8,128)}, f32[512,256]{1,0:T(8,128)S(1)}, u32[]{:S(2)}) copy-start(f32[512,256]{1,0:T(8,128)S(1)} %get-tuple-element.93.refs_0_) | copy-start | bytes 1572868
  29.7 20.7 %collective-permute-start.12 = (f32[512,256]{1,0:T(8,128)}, f32[512,256]{1,0:T(8,128)}, u32[]{:S(2)}, u32[]{:S(2)}) collective-permute-start(f32[512,256]{1,0:T(8,128)} %get-tuple-element.94), channel_id=1, source_target_pairs={{0,8},{8,0},{16,24},{24,16},{32,40},{40,32},{48,56},{56,48},{64,72... | collective-permute-start | bytes 1572872 | tf_op jit(solution)/shard_map/ppermute | solution.py:26
  32.3 0.9 copy-start.10
  33.1 7.2 %collective-permute-start.4 = (f32[520,256]{1,0:T(8,128)}, f32[520,256]{1,0:T(8,128)}, u32[]{:S(2)}, u32[]{:S(2)}) collective-permute-start(f32[520,256]{1,0:T(8,128)} %get-tuple-element.72), channel_id=1, source_target_pairs={{0,8},{8,0},{16,24},{24,16},{32,40},{40,32},{48,56},{56,48},{64,72... | collective-permute-start | bytes 1597448 | tf_op jit(solution)/shard_map/ppermute | solution.py:26
  40.4 1.0 copy-start.11
  42.5 1.2 copy-start.2
  43.7 2.9 %copy-start.15 = (f32[512,256]{1,0:T(8,128)S(1)}, f32[512,256]{1,0:T(8,128)}, u32[]{:S(2)}) copy-start(f32[512,256]{1,0:T(8,128)} %copy-done.14) | copy-start | bytes 1572868
  43.7 4.0 %copy-start.9 = (bf16[2,1920,128]{2,1,0:T(8,128)(2,1)S(1)}, bf16[2,1920,128]{2,1,0:T(8,128)(2,1)}, u32[]{:S(2)}) copy-start(bf16[2,1920,128]{2,1,0:T(8,128)(2,1)} %copy-done.7) | copy-start | bytes 2949124
  46.1 8.4 %collective-permute-start.5 = (f32[520,512]{1,0:T(8,128)S(1)}, f32[520,512]{1,0:T(8,128)S(1)}, u32[]{:S(2)}, u32[]{:S(2)}) collective-permute-start(f32[520,512]{1,0:T(8,128)S(1)} %get-tuple-element.79), channel_id=1, source_target_pairs={{0,8},{8,0},{16,24},{24,16},{32,40},{40,32},{48,56},{56,48},{64,72... | collective-permute-start | bytes 3194888 | tf_op jit(solution)/shard_map/ppermute | solution.py:26
  47.8 2.7 %copy-start.13 = (f32[512,256]{1,0:T(8,128)S(1)}, f32[512,256]{1,0:T(8,128)}, u32[]{:S(2)}) copy-start(f32[512,256]{1,0:T(8,128)} %copy-done.12) | copy-start | bytes 1572868
  47.8 3.8 %copy-start.6 = (bf16[2,1920,128]{2,1,0:T(8,128)(2,1)S(1)}, bf16[2,1920,128]{2,1,0:T(8,128)(2,1)}, u32[]{:S(2)}) copy-start(bf16[2,1920,128]{2,1,0:T(8,128)(2,1)} %copy-done.4) | copy-start | bytes 2949124
  50.1 11.6 %collective-permute-start.21 = (f32[512,512]{1,0:T(8,128)S(1)}, f32[512,512]{1,0:T(8,128)S(1)}, u32[]{:S(2)}, u32[]{:S(2)}) collective-permute-start(f32[512,512]{1,0:T(8,128)S(1)} %get-tuple-element.119), channel_id=1, source_target_pairs={{0,8},{8,0},{16,24},{24,16},{32,40},{40,32},{48,56},{56,48},{64,72... | collective-permute-start | bytes 3145736 | tf_op jit(solution)/shard_map/ppermute | solution.py:26
  51.5 3.1 %copy-start.3 = (bf16[2,1920,128]{2,1,0:T(8,128)(2,1)S(1)}, bf16[2,1920,128]{2,1,0:T(8,128)(2,1)}, u32[]{:S(2)}) copy-start(bf16[2,1920,128]{2,1,0:T(8,128)(2,1)} %copy-done) | copy-start | bytes 2949124
  53.9 16.1 %collective-permute-start.13 = (f32[512,512]{1,0:T(8,128)S(1)}, f32[512,512]{1,0:T(8,128)S(1)}, u32[]{:S(2)}, u32[]{:S(2)}) collective-permute-start(f32[512,512]{1,0:T(8,128)S(1)} %get-tuple-element.99), channel_id=1, source_target_pairs={{0,8},{8,0},{16,24},{24,16},{32,40},{40,32},{48,56},{56,48},{64,72... | collective-permute-start | bytes 3145736 | tf_op jit(solution)/shard_map/ppermute | solution.py:26
  55.9 17.2 %collective-permute-start.8 = (f32[520,256]{1,0:T(8,128)S(1)}, f32[520,256]{1,0:T(8,128)S(1)}, u32[]{:S(2)}, u32[]{:S(2)}) collective-permute-start(f32[520,256]{1,0:T(8,128)S(1)} %get-tuple-element.84), channel_id=1, source_target_pairs={{0,8},{8,0},{16,24},{24,16},{32,40},{40,32},{48,56},{56,48},{64,72... | collective-permute-start | bytes 1597448 | tf_op jit(solution)/shard_map/ppermute | solution.py:26
  56.0 11.1 %collective-permute-start.22 = (f32[256,256]{1,0:T(8,128)S(1)}, f32[256,256]{1,0:T(8,128)S(1)}, u32[]{:S(2)}, u32[]{:S(2)}) collective-permute-start(f32[256,256]{1,0:T(8,128)S(1)} %get-tuple-element.117.refs_2_), channel_id=1, source_target_pairs={{0,96},{8,104},{16,112},{24,120},{32,64},{40,72},{48,80},{56,88},{... | collective-permute-start | bytes 786440 | tf_op jit(solution)/shard_map/ppermute | solution.py:26
  60.2 12.8 %collective-permute-start.6 = (f32[264,256]{1,0:T(8,128)S(1)}, f32[264,256]{1,0:T(8,128)S(1)}, u32[]{:S(2)}, u32[]{:S(2)}) collective-permute-start(f32[264,256]{1,0:T(8,128)S(1)} %get-tuple-element.77.refs_5_), channel_id=1, source_target_pairs={{0,16},{8,24},{16,0},{24,8},{32,48},{40,56},{48,32},{56,40},{64,80... | collective-permute-start | bytes 811016 | tf_op jit(solution)/shard_map/ppermute | solution.py:26
  63.1 10.1 %collective-permute-start.24 = (f32[512,256]{1,0:T(8,128)S(1)}, f32[512,256]{1,0:T(8,128)S(1)}, u32[]{:S(2)}, u32[]{:S(2)}) collective-permute-start(f32[512,256]{1,0:T(8,128)S(1)} %get-tuple-element.124), channel_id=1, source_target_pairs={{0,8},{8,0},{16,24},{24,16},{32,40},{40,32},{48,56},{56,48},{64,72... | collective-permute-start | bytes 1572872 | tf_op jit(solution)/shard_map/ppermute | solution.py:26
  67.1 14.9 %collective-permute-start.23 = (f32[256,512]{1,0:T(8,128)S(1)}, f32[256,512]{1,0:T(8,128)S(1)}, u32[]{:S(2)}, u32[]{:S(2)}) collective-permute-start(f32[256,512]{1,0:T(8,128)S(1)} %get-tuple-element.121.refs_2_), channel_id=1, source_target_pairs={{0,96},{8,104},{16,112},{24,120},{32,64},{40,72},{48,80},{56,88},{... | collective-permute-start | bytes 1572872 | tf_op jit(solution)/shard_map/ppermute | solution.py:26
  70.0 15.1 %collective-permute-start.7 = (f32[264,512]{1,0:T(8,128)S(1)}, f32[264,512]{1,0:T(8,128)S(1)}, u32[]{:S(2)}, u32[]{:S(2)}) collective-permute-start(f32[264,512]{1,0:T(8,128)S(1)} %get-tuple-element.81.refs_4_), channel_id=1, source_target_pairs={{0,16},{8,24},{16,0},{24,8},{32,48},{40,56},{48,32},{56,40},{64,80... | collective-permute-start | bytes 1622024 | tf_op jit(solution)/shard_map/ppermute | solution.py:26
  73.0 12.6 %collective-permute-start.16 = (f32[512,256]{1,0:T(8,128)S(1)}, f32[512,256]{1,0:T(8,128)S(1)}, u32[]{:S(2)}, u32[]{:S(2)}) collective-permute-start(f32[512,256]{1,0:T(8,128)S(1)} %get-tuple-element.104), channel_id=1, source_target_pairs={{0,8},{8,0},{16,24},{24,16},{32,40},{40,32},{48,56},{56,48},{64,72... | collective-permute-start | bytes 1572872 | tf_op jit(solution)/shard_map/ppermute | solution.py:26
  73.1 20.5 %collective-permute-start.15 = (f32[256,512]{1,0:T(8,128)S(1)}, f32[256,512]{1,0:T(8,128)S(1)}, u32[]{:S(2)}, u32[]{:S(2)}) collective-permute-start(f32[256,512]{1,0:T(8,128)S(1)} %get-tuple-element.101.refs_2_), channel_id=1, source_target_pairs={{0,32},{8,40},{16,48},{24,56},{32,0},{40,8},{48,16},{56,24},{64,96... | collective-permute-start | bytes 1572872 | tf_op jit(solution)/shard_map/ppermute | solution.py:26
  73.3 20.9 %collective-permute-start.9 = (f32[264,256]{1,0:T(8,128)S(1)}, f32[264,256]{1,0:T(8,128)S(1)}, u32[]{:S(2)}, u32[]{:S(2)}) collective-permute-start(f32[264,256]{1,0:T(8,128)S(1)} %get-tuple-element.86), channel_id=1, source_target_pairs={{0,16},{8,24},{16,0},{24,8},{32,48},{40,56},{48,32},{56,40},{64,80... | collective-permute-start | bytes 811016 | tf_op jit(solution)/shard_map/ppermute | solution.py:26
  82.0 11.6 %collective-permute-start.14 = (f32[256,256]{1,0:T(8,128)S(1)}, f32[256,256]{1,0:T(8,128)S(1)}, u32[]{:S(2)}, u32[]{:S(2)}) collective-permute-start(f32[256,256]{1,0:T(8,128)S(1)} %get-tuple-element.97.refs_2_), channel_id=1, source_target_pairs={{0,32},{8,40},{16,48},{24,56},{32,0},{40,8},{48,16},{56,24},{64,96... | collective-permute-start | bytes 786440 | tf_op jit(solution)/shard_map/ppermute | solution.py:26
  85.2 10.4 %collective-permute-start.25 = (f32[256,256]{1,0:T(8,128)S(1)}, f32[256,256]{1,0:T(8,128)S(1)}, u32[]{:S(2)}, u32[]{:S(2)}) collective-permute-start(f32[256,256]{1,0:T(8,128)S(1)} %get-tuple-element.126), channel_id=1, source_target_pairs={{0,96},{8,104},{16,112},{24,120},{32,64},{40,72},{48,80},{56,88},{... | collective-permute-start | bytes 786440 | tf_op jit(solution)/shard_map/ppermute | solution.py:26
  85.6 25.3 %collective-permute-start.10 = (f32[136,768]{1,0:T(8,128)S(1)}, f32[136,768]{1,0:T(8,128)S(1)}, u32[]{:S(2)}, u32[]{:S(2)}) collective-permute-start(f32[136,768]{1,0:T(8,128)S(1)} %get-tuple-element.88), channel_id=1, source_target_pairs={{0,32},{8,40},{16,48},{24,56},{32,0},{40,8},{48,16},{56,24},{64,96... | collective-permute-start | bytes 1253384 | tf_op jit(solution)/shard_map/ppermute | solution.py:26
  93.6 14.6 %collective-permute-start.17 = (f32[256,256]{1,0:T(8,128)S(1)}, f32[256,256]{1,0:T(8,128)S(1)}, u32[]{:S(2)}, u32[]{:S(2)}) collective-permute-start(f32[256,256]{1,0:T(8,128)S(1)} %get-tuple-element.106), channel_id=1, source_target_pairs={{0,32},{8,40},{16,48},{24,56},{32,0},{40,8},{48,16},{56,24},{64,96... | collective-permute-start | bytes 786440 | tf_op jit(solution)/shard_map/ppermute | solution.py:26
  93.6 20.4 %collective-permute-start.26 = (f32[128,768]{1,0:T(8,128)S(1)}, f32[128,768]{1,0:T(8,128)S(1)}, u32[]{:S(2)}, u32[]{:S(2)}) collective-permute-start(f32[128,768]{1,0:T(8,128)S(1)} %get-tuple-element.128), channel_id=1, source_target_pairs={{0,16},{8,24},{16,0},{24,8},{32,48},{40,56},{48,32},{56,40},{64,80... | collective-permute-start | bytes 1179656 | tf_op jit(solution)/shard_map/ppermute | solution.py:26
  94.2 24.0 %collective-permute-start.18 = (f32[128,768]{1,0:T(8,128)S(1)}, f32[128,768]{1,0:T(8,128)S(1)}, u32[]{:S(2)}, u32[]{:S(2)}) collective-permute-start(f32[128,768]{1,0:T(8,128)S(1)} %get-tuple-element.108), channel_id=1, source_target_pairs={{0,96},{8,104},{16,112},{24,120},{32,64},{40,72},{48,80},{56,88},{... | collective-permute-start | bytes 1179656 | tf_op jit(solution)/shard_map/ppermute | solution.py:26
  95.6 15.0 %collective-permute-start.11 = (f32[136,256]{1,0:T(8,128)S(1)}, f32[136,256]{1,0:T(8,128)S(1)}, u32[]{:S(2)}, u32[]{:S(2)}) collective-permute-start(f32[136,256]{1,0:T(8,128)S(1)} %get-tuple-element.89), channel_id=1, source_target_pairs={{0,32},{8,40},{16,48},{24,56},{32,0},{40,8},{48,16},{56,24},{64,96... | collective-permute-start | bytes 417800 | tf_op jit(solution)/shard_map/ppermute | solution.py:26
  108.1 5.8 %collective-permute-start.27 = (f32[128,256]{1,0:T(8,128)S(1)}, f32[128,256]{1,0:T(8,128)S(1)}, u32[]{:S(2)}, u32[]{:S(2)}) collective-permute-start(f32[128,256]{1,0:T(8,128)S(1)} %get-tuple-element.129), channel_id=1, source_target_pairs={{0,16},{8,24},{16,0},{24,8},{32,48},{40,56},{48,32},{56,40},{64,80... | collective-permute-start | bytes 393224 | tf_op jit(solution)/shard_map/ppermute | solution.py:26
  110.6 7.6 %collective-permute-start.19 = (f32[128,256]{1,0:T(8,128)S(1)}, f32[128,256]{1,0:T(8,128)S(1)}, u32[]{:S(2)}, u32[]{:S(2)}) collective-permute-start(f32[128,256]{1,0:T(8,128)S(1)} %get-tuple-element.109), channel_id=1, source_target_pairs={{0,96},{8,104},{16,112},{24,120},{32,64},{40,72},{48,80},{56,88},{... | collective-permute-start | bytes 393224 | tf_op jit(solution)/shard_map/ppermute | solution.py:26
  110.9 13.7 %collective-permute-start.28 = (f32[72,1024]{1,0:T(8,128)S(1)}, f32[72,1024]{1,0:T(8,128)S(1)}, u32[]{:S(2)}, u32[]{:S(2)}) collective-permute-start(f32[72,1024]{1,0:T(8,128)S(1)} %get-tuple-element.131), channel_id=1, source_target_pairs={{0,96},{8,104},{16,112},{24,120},{32,64},{40,72},{48,80},{56,88},{... | collective-permute-start | bytes 884744 | tf_op jit(solution)/shard_map/ppermute | solution.py:26
  114.0 7.3 %collective-permute-start.30 = (f32[64,1024]{1,0:T(8,128)S(1)}, f32[64,1024]{1,0:T(8,128)S(1)}, u32[]{:S(2)}, u32[]{:S(2)}) collective-permute-start(f32[64,1024]{1,0:T(8,128)S(1)} %get-tuple-element.133), channel_id=1, source_target_pairs={{0,32},{8,40},{16,48},{24,56},{32,0},{40,8},{48,16},{56,24},{64,96... | collective-permute-start | bytes 786440 | tf_op jit(solution)/shard_map/ppermute | solution.py:26
  118.2 6.5 %collective-permute-start.29 = (f32[64,1024]{1,0:T(8,128)S(1)}, f32[64,1024]{1,0:T(8,128)S(1)}, u32[]{:S(2)}, u32[]{:S(2)}) collective-permute-start(f32[64,1024]{1,0:T(8,128)S(1)} %get-tuple-element.132), channel_id=1, source_target_pairs={{0,16},{8,24},{16,0},{24,8},{32,48},{40,56},{48,32},{56,40},{64,80... | collective-permute-start | bytes 786440 | tf_op jit(solution)/shard_map/ppermute | solution.py:26

commit v2 on v1

v2 whole, which is shorter than its diff:
```python
import functools

import jax
import jax.numpy as jnp
from jax import lax
from jax.experimental import pallas as pl
from jax.experimental.pallas import tpu as pltpu
from jax.sharding import PartitionSpec as P

BITS = 30
HALF = BITS // 2
LANES = 128
MIB = 1024 * 1024
MADE = (2, 6)
CHUNKS = (4, 4)
DOS_CHUNK = 0
EXTRA = 8

CORE, SIDE_Y, SIDE_A, SIDE_B = 1, 2, 4, 12
ORDERS = ((SIDE_Y, SIDE_A, SIDE_B), (SIDE_A, SIDE_B, SIDE_Y), (SIDE_B, SIDE_Y, SIDE_A))
TURNED = ((1, 1),)
FAR = (4, 2, 6)


def swap(array, axis, flip):
    size = lax.axis_size(axis)
    return lax.ppermute(array, axis, [(d, d ^ flip) for d in range(size)])


def place_of(relative, order):
    bits = {
        SIDE_Y: (relative >> 1) & 1,
        SIDE_A: ((relative >> 2) ^ (relative >> 3)) & 1,
        SIDE_B: (relative >> 3) & 1,
    }
    first, second, third = order
    return 8 * bits[first] + 4 * (relative & 1) + 2 * bits[second] + bits[third]


def sides(index, chunk):
    first, second, third = ORDERS[index]
    return (first, third, second) if (index, chunk) in TURNED else (first, second, third)


def whole(count):
    return [pl.BlockSpec(memory_space=pltpu.VMEM)] * count


def params(mib):
    return pltpu.CompilerParams(vmem_limit_bytes=mib * MIB)


def unpack_kernel(where_ref, *refs):
    word_refs, (dosage_ref, phase_ref, mixed_ref, margin_ref) = refs[:-4], refs[-4:]
    samp, var = where_ref[0], where_ref[1]
    low = (1 << HALF) - 1
    words, block = word_refs[0].shape[1:]
    rows = block // 2
    samples = float(words * BITS)
    one, zero = jnp.bfloat16(1), jnp.bfloat16(0)
    pieces = [
        (flip + twin, word_ref, 2 * twin)
        for flip, word_ref in zip((0, *FAR), word_refs)
        for twin in range(2)
    ]
    for flip, word_ref, spot in pieces:
        source = var ^ flip
        first, second = word_ref[spot], word_ref[spot + 1]
        ones = lax.population_count(first) + lax.population_count(second)
        mixed = lax.population_count(first ^ second)
        margin_ref[pl.ds(source, 1), 0:1, :] = (
            jnp.sum(ones.astype(jnp.float32), axis=0, keepdims=True) - samples
        )[None]
        margin_ref[pl.ds(source, 1), 1:2, :] = (
            samples - jnp.sum(mixed.astype(jnp.float32), axis=0, keepdims=True)
        )[None]
        turned = [
            jnp.concatenate([w & low, (w >> HALF) & low], axis=0).T.astype(jnp.int16)
            for w in (first, second)
        ]
        for part in range(2):
            relative = (2 * source + part) ^ samp
            starts = [pl.multiple_of(place_of(relative, order) * rows, rows) for order in ORDERS]
            mine = [t[part * rows : (part + 1) * rows] for t in turned]
            for bit in range(HALF):
                mask = jnp.int16(1 << bit)
                hap_one = jnp.where((mine[0] & mask) != 0, one, zero)
                hap_two = jnp.where((mine[1] & mask) != 0, one, zero)
                phase = hap_one - hap_two
                lanes = slice(bit * 2 * words, (bit + 1) * 2 * words)
                dosage_ref[pl.ds(starts[0], rows), lanes] = (hap_one + hap_two) - one
                phase_ref[pl.ds(starts[1], rows), lanes] = phase
                mixed_ref[pl.ds(starts[2], rows), lanes] = phase * phase


def unpack(where, pairs):
    _, words, block = pairs[0].shape
    count = 2 * len(pairs)
    variants, samples = count * block, words * BITS
    design = jax.ShapeDtypeStruct((variants, samples), jnp.bfloat16)
    return pl.pallas_call(
        unpack_kernel,
        out_shape=(design,) * 3 + (jax.ShapeDtypeStruct((count, 2, block), jnp.float32),),
        in_specs=[pl.BlockSpec(memory_space=pltpu.SMEM)] + whole(len(pairs)),
        cost_estimate=pl.CostEstimate(
            flops=6_000_000_000, bytes_accessed=6 * variants * samples, transcendentals=0
        ),
        compiler_params=params(8),
        name="unpack",
    )(where, *pairs)


def pair_kernel(own_ref, twin_ref, pair_ref):
    pair_ref[:2] = own_ref[...]
    pair_ref[2:] = twin_ref[...]


def paired(own, twin):
    _, words, block = own.shape
    return pl.pallas_call(
        pair_kernel,
        out_shape=jax.ShapeDtypeStruct((4, words, block), own.dtype),
        in_specs=whole(2),
        compiler_params=params(8),
        name="paired",
    )(own, twin)


def feature_kernel(first, total_hbm, one_hbm, two_hbm, *refs):
    total_out, weighted_out, weight_out, margin_ref, buffer, sems = refs[-6:]
    blocks, samples = total_out.shape[:2]
    words = samples // BITS

    def copies(block):
        lanes = pl.ds((first + block) * LANES, LANES)
        return [
            pltpu.make_async_copy(ref.at[:, lanes], buffer.at[spot, block], sems.at[spot, block])
            for spot, ref in enumerate((total_hbm, one_hbm, two_hbm))
        ]

    for block in range(blocks):
        for copy in copies(block):
            copy.start()
    for block in range(blocks):
        for copy in copies(block):
            copy.wait()

        def step(bit, sums, block=block):
            log_sum, log_sq = sums
            for half in range(2):
                rows = pl.ds(bit + half * HALF, words, stride=BITS)
                spot = pl.ds(pl.multiple_of((2 * bit + half) * words, words), words)
                log_total = jnp.log(buffer[0, block, rows, :].astype(jnp.float32) + 1.0)
                one_plus = buffer[1, block, rows, :].astype(jnp.float32) + 1.0
                two_plus = buffer[2, block, rows, :].astype(jnp.float32) + 1.0
                log_ratio = jnp.log(one_plus / two_plus)
                weight = (one_plus * two_plus) / (one_plus + two_plus)
                total_out[block, spot, :] = log_total.astype(jnp.bfloat16)
                weighted_out[block, spot, :] = (weight * log_ratio).astype(jnp.bfloat16)
                weight_out[block, spot, :] = weight.astype(jnp.bfloat16)
                folded = log_total.reshape(words // 8, 8, LANES)
                log_sum = log_sum + jnp.sum(folded, axis=0)
                log_sq = log_sq + jnp.sum(folded * folded, axis=0)
            return log_sum, log_sq

        blank = jnp.zeros((8, LANES), jnp.float32)
        sums = lax.fori_loop(0, HALF, step, (blank, blank), unroll=3)
        for kind in range(2):
            margin_ref[kind : kind + 1, block * LANES : (block + 1) * LANES] = jnp.sum(
                sums[kind], axis=0, keepdims=True
            )


def features(total_counts, allele_one, allele_two, first, blocks, after):
    samples = total_counts.shape[0]
    width = blocks * LANES
    feature = jax.ShapeDtypeStruct((blocks, samples, LANES), jnp.bfloat16)
    return pl.pallas_call(
        functools.partial(feature_kernel, first),
        out_shape=(feature,) * 3 + (jax.ShapeDtypeStruct((2, width), jnp.float32),),
        in_specs=[pl.BlockSpec(memory_space=pltpu.HBM)] * 3
        + [pl.BlockSpec(memory_space=pl.ANY)] * len(after),
        out_specs=tuple(whole(4)),
        scratch_shapes=[
            pltpu.VMEM((3, blocks, samples, LANES), jnp.int32),
            pltpu.SemaphoreType.DMA((3, blocks)),
        ],
        cost_estimate=pl.CostEstimate(
            flops=12_000_000 * width, bytes_accessed=18 * samples * width, transcendentals=0
        ),
        compiler_params=params(44),
        name="features",
    )(total_counts, allele_one, allele_two, *after)


def cross_kernel(spots, part, margins, design_ref, *refs):
    keep_ref, send_ref = refs[-2:]
    calls = 1 + max(call for call, _ in spots)
    feature_refs, margin_refs = refs[:calls], refs[calls : calls + margins]
    half = design_ref.shape[0] // 2
    kept = half // 2
    for pair in range(len(spots) // 2):
        right = jnp.concatenate(
            [feature_refs[call][block] for call, block in spots[2 * pair : 2 * pair + 2]], axis=1
        )
        lanes = slice(pair * 2 * LANES, (pair + 1) * 2 * LANES)
        product = jnp.dot(
            design_ref[part * half : (part + 1) * half, :],
            right,
            preferred_element_type=jnp.float32,
        )
        keep_ref[:kept, lanes] = product[:kept]
        send_ref[:kept, lanes] = product[kept:]
    if margins:
        blank = jnp.zeros((EXTRA - 2, LANES), jnp.float32)
        for place, (call, block) in enumerate(spots):
            gene = margin_refs[call][:, block * LANES : (block + 1) * LANES]
            rest = blank
            if margins > calls:
                dos_ref = margin_refs[calls]
                picked = [
                    dos_ref[spot // 2, spot % 2 : spot % 2 + 1, :]
                    for spot in range(place, 2 * dos_ref.shape[0], len(spots))
                ]
                rest = jnp.concatenate([*picked, blank[len(picked) :]], axis=0)
            rows = jnp.concatenate([gene, rest], axis=0)
            lanes = slice(place * LANES, (place + 1) * LANES)
            keep_ref[kept:, lanes] = rows
            send_ref[kept:, lanes] = rows


def cross(design, features_of, spots, part, margins):
    variants, samples = design.shape
    width = len(spots) * LANES
    rows = variants // 4 + (EXTRA if margins else 0)
    out = jax.ShapeDtypeStruct((rows, width), jnp.float32)
    return pl.pallas_call(
        functools.partial(cross_kernel, spots, part, len(margins)),
        out_shape=(out, out),
        in_specs=whole(1 + len(features_of) + len(margins)),
        cost_estimate=pl.CostEstimate(
            flops=variants * samples * width,
            bytes_accessed=2 * (variants + width) * samples,
            transcendentals=0,
        ),
        compiler_params=params(8),
        name="cross",
    )(design, *features_of, *margins)


def meet_kernel(left_ref, right_ref, out_ref):
    out_ref[...] = left_ref[...] + right_ref[...]


def meet(left, right):
    return pl.pallas_call(
        meet_kernel,
        out_shape=jax.ShapeDtypeStruct(left.shape, left.dtype),
        in_specs=whole(2),
        compiler_params=params(8),
        name="meet",
    )(left, right)


def fold_kernel(turned, count, *refs):
    keep_ref, send_ref = refs[-2:]
    terms, margins = refs[:count], refs[count:-2]
    half = min(term.shape[0] for term in terms) // 2 // 64 * 64
    quarter = half // 2
    if turned:
        keep_spots = ((0, quarter), (2 * quarter, quarter))
        send_spots = ((quarter, quarter), (3 * quarter, quarter))
    else:
        keep_spots, send_spots = ((0, half),), ((half, half),)
    for out_ref, spots in ((send_ref, send_spots), (keep_ref, keep_spots)):
        at = 0
        for first, rows in spots:
            total = terms[0][first : first + rows]
            for term in terms[1:]:
                total = total + term[first : first + rows]
            out_ref[at : at + rows] = total
            at += rows
        if margins:
            start = margins[0].shape[0] - EXTRA
            total = margins[0][start:]
            for margin in margins[1:]:
                total = total + margin[margin.shape[0] - EXTRA :]
            out_ref[half:] = total


def fold(terms, margins, turned):
    rows, width = min(term.shape for term in terms)
    half = rows // 2 // 64 * 64
    out = jax.ShapeDtypeStruct((half + (EXTRA if margins else 0), width), jnp.float32)
    return pl.pallas_call(
        functools.partial(fold_kernel, turned, len(terms)),
        out_shape=(out, out),
        in_specs=whole(len(terms) + len(margins)),
        compiler_params=params(8),
        name="fold",
    )(*terms, *margins)


def finish_kernel(sample_count, where_ref, *refs):
    total_ref, allelic_ref = refs[-2:]
    own = total_ref.shape[0]
    samp = where_ref[0]
    chunks = len(CHUNKS)
    couples = [refs[at : at + 2] for at in range(0, 6 * chunks, 2)]
    pair_of = [couples[index * chunks : (index + 1) * chunks] for index in range(3)]
    margins = [left[own:, :] + right[own:, :] for left, right in pair_of[0]]
    columns = []
    for kind in range(2):
        picked = jnp.zeros((1, LANES), jnp.float32)
        for source in range(lax.axis_size("var")):
            spot = 2 * source + kind
            row, block = 2 + spot // CHUNKS[DOS_CHUNK], spot % CHUNKS[DOS_CHUNK]
            row_now = margins[DOS_CHUNK][row : row + 1, block * LANES : (block + 1) * LANES]
            picked = jnp.where(samp >> 1 == source, row_now, picked)
        turned = jnp.broadcast_to(picked, (LANES, LANES)).T
        columns.append(jnp.where(samp & 1 == 0, turned[:own], turned[own:]))
    dos_sum, dos_sq = columns
    dosage_var = dos_sq - dos_sum * dos_sum / sample_count
    scale = jnp.sqrt(jnp.float32(sample_count))
    first = 0
    for chunk, blocks in enumerate(CHUNKS):
        for block in range(blocks):
            lanes = slice(block * LANES, (block + 1) * LANES)
            spot = slice((first + block) * LANES, (first + block + 1) * LANES)
            gene_sum, gene_sq = margins[chunk][0:1, lanes], margins[chunk][1:2, lanes]
            gene_var = gene_sq - gene_sum * gene_sum / sample_count
            pair_sums = [
                pair_of[index][chunk][0][:own, lanes] + pair_of[index][chunk][1][:own, lanes]
                for index in range(3)
            ]
            covariance = pair_sums[0] - dos_sum * gene_sum / sample_count
            total_ref[:, spot] = (
                scale * covariance / jnp.sqrt((dosage_var + 1.0) * (gene_var + 1.0))
            )
            allelic_ref[:, spot] = pair_sums[1] / jnp.sqrt(pair_sums[2] + 1.0)
        first += blocks


def finish(where, parts, own, width, sample_count):
    out = jax.ShapeDtypeStruct((own, width), jnp.float32)
    return pl.pallas_call(
        functools.partial(finish_kernel, sample_count),
        out_shape=(out, out),
        in_specs=[pl.BlockSpec(memory_space=pltpu.SMEM)] + whole(len(parts)),
        compiler_params=params(8),
        name="finish",
    )(where, *parts)


def per_device(hap_words, total_counts, allele_one, allele_two):
    where = jnp.stack([lax.axis_index("samp"), lax.axis_index("var")]).astype(jnp.int32)
    twin = swap(hap_words, "var", 1)
    counts = (total_counts, allele_one, allele_two)
    made = []
    for call, blocks in enumerate(MADE):
        after = (twin,) if call else ()
        made.append(features(*counts, sum(MADE[:call]), blocks, after))
    pairs = [paired(hap_words, twin)]
    for flip in FAR:
        pairs.append(swap(pairs[0], "var", flip))
    *designs, dos_part = unpack(where, pairs)
    spots = [(call, block) for call, blocks in enumerate(MADE) for block in range(blocks)]
    kept, cored, sent, came = {}, {}, {}, {}
    for part, chunk, index in items():
        first = sum(CHUNKS[:chunk])
        mine = spots[first : first + CHUNKS[chunk]]
        calls = 1 + max(call for call, _ in mine)
        margins = []
        if index == 0 and part == 1:
            margins = [made[call][3] for call in range(calls)]
            margins += [dos_part] if chunk == DOS_CHUNK else []
        features_of = [made[call][index] for call in range(calls)]
        keep, send = cross(designs[index], features_of, mine, part, margins)
        got = swap(send, "samp", CORE)
        if part == 0:
            kept[chunk, index], cored[chunk, index] = keep, got
        else:
            sent[chunk, index] = meet(keep, got)
            came[chunk, index] = swap(sent[chunk, index], "samp", sides(index, chunk)[0])
    cells = [(chunk, index) for chunk in range(len(CHUNKS)) for index in range(3)]
    for chunk, index in cells:
        cell = chunk, index
        margins = [sent[cell], came[cell]] if index == 0 else []
        keep, send = fold(
            [kept[cell], cored[cell], came[cell]], margins, cell[::-1] in TURNED
        )
        kept[cell], came[cell] = keep, swap(send, "samp", sides(index, chunk)[1])
    for chunk, index in cells:
        cell = chunk, index
        margins = [kept[cell], came[cell]] if index == 0 else []
        keep, send = fold([kept[cell], came[cell]], margins, False)
        kept[cell], came[cell] = keep, swap(send, "samp", sides(index, chunk)[2])
    sample_count = float(total_counts.shape[0] * lax.axis_size("samp"))
    own = designs[0].shape[0] // lax.axis_size("samp")
    parts = []
    for index in range(3):
        for chunk in range(len(CHUNKS)):
            parts += [kept[chunk, index], came[chunk, index]]
    return finish(where, parts, own, total_counts.shape[1], sample_count)


def items():
    return [
        (part, chunk, index)
        for part in (1, 0)
        for chunk in range(len(CHUNKS))
        for index in range(3)
    ]


def solution(mesh):
    in_specs = (P(None, "samp", "var"), P("samp", "var"), P("samp", "var"), P("samp", "var"))
    out_specs = (P("samp", "var"), P("samp", "var"))

    return jax.shard_map(
        per_device, mesh=mesh, in_specs=in_specs, out_specs=out_specs, check_vma=False
    )
```

time: 127 us -> 99.4 us (0.78)
  local copies, waits for them, and re-layouts: 11.5 us -> 0.01 us
  waiting for transfers between devices: 46.9 us -> 37 us
  Pallas kernels: 36.6 us -> 31.5 us
    unnamed x47 -> x2, local copies, waits for them, and re-layouts: 11.5 us -> 0.01 us
    ppermute x31 -> x34, waiting for transfers between devices: 46.9 us -> 37 us  [swap(): return lax.ppermute(array, axis, [(d, d ^ flip) for d in range(size)])]
    pallas_call x28 -> x32, Pallas kernels: 22.9 us -> 17.8 us  [the longest x12 15.1 us: cross(): pl.pallas_call(functools.partial(cross_kernel, spots, part, len(margins))...]
    ppermute x31 -> x34, starting transfers between devices: 30.2 us -> 29.7 us  [swap(): return lax.ppermute(array, axis, [(d, d ^ flip) for d in range(size)])]
  transfers between devices with their start and end apart: 31 -> 34, of which waited for: 10 -> 9; matrix products, arithmetic and copies ran while one was open for 1% -> 0% of each run, Pallas kernels for 24% -> 26%
where the time goes in v2:
time: 99.4 us; the launch traced here: 99.2 us
  waiting for transfers between devices  37 us (37%)
  Pallas kernels  31.5 us (32%)
  starting transfers between devices  29.7 us (30%)
    ppermute x34, waiting for transfers between devices, swap(): return lax.ppermute(array, axis, [(d, d ^ flip) for d in range(size)])  37 us
    ppermute x34, starting transfers between devices, swap(): return lax.ppermute(array, axis, [(d, d ^ flip) for d in range(size)])  29.7 us
    pallas_call x12, Pallas kernels, cross(): pl.pallas_call(functools.partial(cross_kernel, spots, part, len(margins))...  15.1 us
    pallas_call x2, Pallas kernels, features(): pl.pallas_call(functools.partial(feature_kernel, first), out_shape=(featu...  10.8 us
    pallas_call x1, Pallas kernels, unpack(): pl.pallas_call(unpack_kernel, out_shape=(design,) * 3 + (jax.ShapeDtypeSt...  2.87 us
  transfers between devices with their start and end apart: 34, of which 9 were waited for; matrix products, arithmetic and copies ran while one was open for 0% of the time, Pallas kernels for 26%

profile of v2, /device:TPU:0, one launch (start us, length us, event | category | flops | bytes accessed | tf_op | source)
XLA Modules:
  0.0 99.2 jit_solution(14747828562409718509)
XLA Ops:
  0.6 3.4 %collective-permute-start = (s32[2,64,128]{2,1,0:T(8,128)}, s32[2,64,128]{2,1,0:T(8,128)S(1)}, u32[]{:S(2)}, u32[]{:S(2)}) collective-permute-start(s32[2,64,128]{2,1,0:T(8,128)} %own_ref.1), channel_id=1, source_target_pairs={{0,1},{1,0},{2,3},{3,2},{4,5},{5,4},{6,7},{7,6},{8,9},{9,8},{10,11... | collective-permute-start | bytes 196616 | tf_op jit(solution)/shard_map/ppermute | solution.py:27
  4.0 3.6 %features.2 = (bf16[2,1920,128]{2,1,0:T(8,128)(2,1)S(1)}, bf16[2,1920,128]{2,1,0:T(8,128)(2,1)S(1)}, bf16[2,1920,128]{2,1,0:T(8,128)(2,1)S(1)}, f32[2,256]{1,0:T(2,128)S(1)}) custom-call(s32[1920,1024]{1,0:T(8,128)} %total_hbm.3, s32[1920,1024]{1,0:T(8,128)} %one_hbm.3, s32[1920,1024]{1,0:T(8,128)} %two_hbm.3), custom_call_target="tpu_custom_call" | custom-call | flops 3072000000 | bytes 8847360 | tf_op jit(solution)/shard_map/features/pallas_call | solution.py:178
  7.6 0.1 pad_add_fusion.where_ref
  7.7 3.1 %collective-permute-start.1 = (s32[4,64,128]{2,1,0:T(8,128)S(1)}, s32[4,64,128]{2,1,0:T(8,128)S(1)}, u32[]{:S(2)}, u32[]{:S(2)}) collective-permute-start(s32[4,64,128]{2,1,0:T(8,128)S(1)} %paired.1.refs_0_), channel_id=1, source_target_pairs={{0,4},{1,5},{2,6},{3,7},{4,0},{5,1},{6,2},{7,3},{8,12},{9,13},{10,... | collective-permute-start | bytes 393224 | tf_op jit(solution)/shard_map/ppermute | solution.py:27
  10.8 0.6 collective-permute-start.2
  11.4 0.6 collective-permute-start.3
  12.0 7.2 %features.3 = (bf16[6,1920,128]{2,1,0:T(8,128)(2,1)S(1)}, bf16[6,1920,128]{2,1,0:T(8,128)(2,1)S(1)}, bf16[6,1920,128]{2,1,0:T(8,128)(2,1)S(1)}, f32[2,768]{1,0:T(2,128)S(1)}) custom-call(s32[1920,1024]{1,0:T(8,128)} %total_hbm.3, s32[1920,1024]{1,0:T(8,128)} %one_hbm.3, s32[1920,1024]{1,0:T(8,128)} %two_hbm.3, ...), custom_call_target="tpu_custom_call" | custom-call | flops 9216000000 | bytes 26542080 | tf_op jit(solution)/shard_map/features/pallas_call | solution.py:178
  19.2 2.9 %unpack.1 = (bf16[1024,1920]{1,0:T(8,128)(2,1)S(1)}, bf16[1024,1920]{1,0:T(8,128)(2,1)S(1)}, bf16[1024,1920]{1,0:T(8,128)(2,1)S(1)}, f32[8,2,128]{2,1,0:T(2,128)S(1)}) custom-call(s32[2]{0:T(128)S(1)} %pad_add_fusion.where_ref, s32[4,64,128]{2,1,0:T(8,128)S(1)} %paired.1.refs_0_, s32[4,64,128]{2,1,0:T(8,128)S(1)} %collective-permute-done.1.refs_1_, ...), custom_call_target="tpu_custom_call" | custom-call | flops 6000000000 | bytes 11796480 | tf_op jit(solution)/shard_map/unpack/pallas_call | solution.py:101
  22.1 1.3 %cross.23 = (f32[256,512]{1,0:T(8,128)S(1)}, f32[256,512]{1,0:T(8,128)S(1)}) custom-call(bf16[1024,1920]{1,0:T(8,128)(2,1)S(1)} %get-tuple-element.103.design_ref, bf16[2,1920,128]{2,1,0:T(8,128)(2,1)S(1)} %get-tuple-element.104.refs_0_, bf16[6,1920,128]{2,1,0:T(8,128)(2,1)S(1)} %get-tuple-element.105.refs_1_), custom_call_target="tpu_custom_call" | custom-call | flops 1006632960 | bytes 5898240 | tf_op jit(solution)/shard_map/cross/pallas_call | solution.py:237
  23.4 0.1 collective-permute-start.30
  23.5 1.3 %cross.22 = (f32[256,512]{1,0:T(8,128)S(1)}, f32[256,512]{1,0:T(8,128)S(1)}) custom-call(bf16[1024,1920]{1,0:T(8,128)(2,1)S(1)} %get-tuple-element.103.design_ref, bf16[2,1920,128]{2,1,0:T(8,128)(2,1)S(1)} %get-tuple-element.104.refs_0_, bf16[6,1920,128]{2,1,0:T(8,128)(2,1)S(1)} %get-tuple-element.105.refs_1_), custom_call_target="tpu_custom_call" | custom-call | flops 1006632960 | bytes 5898240 | tf_op jit(solution)/shard_map/cross/pallas_call | solution.py:237
  24.7 0.6 collective-permute-start.29
  25.3 1.3 %cross.21 = (f32[256,512]{1,0:T(8,128)S(1)}, f32[256,512]{1,0:T(8,128)S(1)}) custom-call(bf16[1024,1920]{1,0:T(8,128)(2,1)S(1)} %get-tuple-element.103.design_ref, bf16[2,1920,128]{2,1,0:T(8,128)(2,1)S(1)} %get-tuple-element.104.refs_0_, bf16[6,1920,128]{2,1,0:T(8,128)(2,1)S(1)} %get-tuple-element.105.refs_1_), custom_call_target="tpu_custom_call" | custom-call | flops 1006632960 | bytes 5898240 | tf_op jit(solution)/shard_map/cross/pallas_call | solution.py:237
  26.6 0.1 collective-permute-start.25
  26.7 1.3 %cross.20 = (f32[256,512]{1,0:T(8,128)S(1)}, f32[256,512]{1,0:T(8,128)S(1)}) custom-call(bf16[1024,1920]{1,0:T(8,128)(2,1)S(1)} %get-tuple-element.103.design_ref, bf16[2,1920,128]{2,1,0:T(8,128)(2,1)S(1)} %get-tuple-element.104.refs_0_, bf16[6,1920,128]{2,1,0:T(8,128)(2,1)S(1)} %get-tuple-element.105.refs_1_), custom_call_target="tpu_custom_call" | custom-call | flops 1006632960 | bytes 5898240 | tf_op jit(solution)/shard_map/cross/pallas_call | solution.py:237
  27.9 0.6 collective-permute-start.24
  28.5 1.3 %cross.19 = (f32[256,512]{1,0:T(8,128)S(1)}, f32[256,512]{1,0:T(8,128)S(1)}) custom-call(bf16[1024,1920]{1,0:T(8,128)(2,1)S(1)} %get-tuple-element.84.design_ref, bf16[2,1920,128]{2,1,0:T(8,128)(2,1)S(1)} %get-tuple-element.85.refs_0_, bf16[6,1920,128]{2,1,0:T(8,128)(2,1)S(1)} %get-tuple-element.86.refs_1_), custom_call_target="tpu_custom_call" | custom-call | flops 1006632960 | bytes 5898240 | tf_op jit(solution)/shard_map/cross/pallas_call | solution.py:237
  29.8 0.1 collective-permute-start.20
  29.9 1.3 %cross.18 = (f32[256,512]{1,0:T(8,128)S(1)}, f32[256,512]{1,0:T(8,128)S(1)}) custom-call(bf16[1024,1920]{1,0:T(8,128)(2,1)S(1)} %get-tuple-element.84.design_ref, bf16[2,1920,128]{2,1,0:T(8,128)(2,1)S(1)} %get-tuple-element.85.refs_0_, bf16[6,1920,128]{2,1,0:T(8,128)(2,1)S(1)} %get-tuple-element.86.refs_1_), custom_call_target="tpu_custom_call" | custom-call | flops 1006632960 | bytes 5898240 | tf_op jit(solution)/shard_map/cross/pallas_call | solution.py:237
  31.1 1.3 %cross.15 = (f32[264,512]{1,0:T(8,128)S(1)}, f32[264,512]{1,0:T(8,128)S(1)}) custom-call(bf16[1024,1920]{1,0:T(8,128)(2,1)S(1)} %get-tuple-element.62.design_ref, bf16[2,1920,128]{2,1,0:T(8,128)(2,1)S(1)} %get-tuple-element.63.refs_0_, bf16[6,1920,128]{2,1,0:T(8,128)(2,1)S(1)} %get-tuple-element.64.refs_1_, f32[2,256]{1,0:T(2,128)S(1)} %get-tuple-element.67.refs_2_, ...), custom_call_target="tpu_custom_call" | custom-call | flops 1006632960 | bytes 5898240 | tf_op jit(solution)/shard_map/cross/pallas_call | solution.py:237
  32.4 0.6 collective-permute-start.19
  33.0 0.3 collective-permute-start.10
  33.3 1.3 %cross.17 = (f32[256,512]{1,0:T(8,128)S(1)}, f32[256,512]{1,0:T(8,128)S(1)}) custom-call(bf16[1024,1920]{1,0:T(8,128)(2,1)S(1)} %get-tuple-element.84.design_ref, bf16[2,1920,128]{2,1,0:T(8,128)(2,1)S(1)} %get-tuple-element.85.refs_0_, bf16[6,1920,128]{2,1,0:T(8,128)(2,1)S(1)} %get-tuple-element.86.refs_1_), custom_call_target="tpu_custom_call" | custom-call | flops 1006632960 | bytes 5898240 | tf_op jit(solution)/shard_map/cross/pallas_call | solution.py:237
  34.5 0.3 collective-permute-start.15
  34.8 1.3 %cross.13 = (f32[264,512]{1,0:T(8,128)S(1)}, f32[264,512]{1,0:T(8,128)S(1)}) custom-call(bf16[1024,1920]{1,0:T(8,128)(2,1)S(1)} %get-tuple-element.62.design_ref, bf16[2,1920,128]{2,1,0:T(8,128)(2,1)S(1)} %get-tuple-element.63.refs_0_, bf16[6,1920,128]{2,1,0:T(8,128)(2,1)S(1)} %get-tuple-element.64.refs_1_, f32[2,256]{1,0:T(2,128)S(1)} %get-tuple-element.67.refs_2_, ...), custom_call_target="tpu_custom_call" | custom-call | flops 1006632960 | bytes 5898240 | tf_op jit(solution)/shard_map/cross/pallas_call | solution.py:237
  36.1 0.4 collective-permute-start.5
  36.5 1.3 %cross.16 = (f32[256,512]{1,0:T(8,128)S(1)}, f32[256,512]{1,0:T(8,128)S(1)}) custom-call(bf16[1024,1920]{1,0:T(8,128)(2,1)S(1)} %get-tuple-element.84.design_ref, bf16[2,1920,128]{2,1,0:T(8,128)(2,1)S(1)} %get-tuple-element.85.refs_0_, bf16[6,1920,128]{2,1,0:T(8,128)(2,1)S(1)} %get-tuple-element.86.refs_1_), custom_call_target="tpu_custom_call" | custom-call | flops 1006632960 | bytes 5898240 | tf_op jit(solution)/shard_map/cross/pallas_call | solution.py:237
  37.8 0.3 collective-permute-start.14
  38.1 1.3 %cross.14 = (f32[256,512]{1,0:T(8,128)S(1)}, f32[256,512]{1,0:T(8,128)S(1)}) custom-call(bf16[1024,1920]{1,0:T(8,128)(2,1)S(1)} %get-tuple-element.62.design_ref, bf16[2,1920,128]{2,1,0:T(8,128)(2,1)S(1)} %get-tuple-element.63.refs_0_, bf16[6,1920,128]{2,1,0:T(8,128)(2,1)S(1)} %get-tuple-element.64.refs_1_), custom_call_target="tpu_custom_call" | custom-call | flops 1006632960 | bytes 5898240 | tf_op jit(solution)/shard_map/cross/pallas_call | solution.py:237
  39.3 0.4 collective-permute-start.9
  39.7 1.3 %cross.12 = (f32[256,512]{1,0:T(8,128)S(1)}, f32[256,512]{1,0:T(8,128)S(1)}) custom-call(bf16[1024,1920]{1,0:T(8,128)(2,1)S(1)} %get-tuple-element.62.design_ref, bf16[2,1920,128]{2,1,0:T(8,128)(2,1)S(1)} %get-tuple-element.63.refs_0_, bf16[6,1920,128]{2,1,0:T(8,128)(2,1)S(1)} %get-tuple-element.64.refs_1_), custom_call_target="tpu_custom_call" | custom-call | flops 1006632960 | bytes 5898240 | tf_op jit(solution)/shard_map/cross/pallas_call | solution.py:237
  41.0 0.3 collective-permute-start.4
  41.3 0.1 meet.11
  41.4 4.1 %collective-permute-start.31 = (f32[256,512]{1,0:T(8,128)S(1)}, f32[256,512]{1,0:T(8,128)S(1)}, u32[]{:S(2)}, u32[]{:S(2)}) collective-permute-start(f32[256,512]{1,0:T(8,128)S(1)} %meet.11), channel_id=1, source_target_pairs={{0,96},{8,104},{16,112},{24,120},{32,64},{40,72},{48,80},{56,88},{... | collective-permute-start | bytes 1572872 | tf_op jit(solution)/shard_map/ppermute | solution.py:27
  45.5 0.1 meet.7.refs_3_
  45.6 0.8 collective-permute-start.11
  46.4 1.4 %collective-permute-start.6 = (f32[264,512]{1,0:T(8,128)S(1)}, f32[264,512]{1,0:T(8,128)S(1)}, u32[]{:S(2)}, u32[]{:S(2)}) collective-permute-start(f32[264,512]{1,0:T(8,128)S(1)} %meet.6.refs_3_), channel_id=1, source_target_pairs={{0,16},{8,24},{16,0},{24,8},{32,48},{40,56},{48,32},{56,40},{64,80... | collective-permute-start | bytes 1622024 | tf_op jit(solution)/shard_map/ppermute | solution.py:27
  47.9 0.1 collective-permute-start.26
  48.1 0.1 collective-permute-start.21
  48.2 10.0 %collective-permute-done.31.refs_2_ = f32[256,512]{1,0:T(8,128)S(1)} collective-permute-done((f32[256,512]{1,0:T(8,128)S(1)}, f32[256,512]{1,0:T(8,128)S(1)}, u32[]{:S(2)}, u32[]{:S(2)}) %collective-permute-start.31) | collective-permute-done | bytes 524320 | tf_op jit(solution)/shard_map/ppermute | solution.py:27
  58.3 0.1 fold.22
  58.4 2.4 %collective-permute-done.11.refs_2_.refs_4_ = f32[264,512]{1,0:T(8,128)S(1)} collective-permute-done((f32[264,512]{1,0:T(8,128)S(1)}, f32[264,512]{1,0:T(8,128)S(1)}, u32[]{:S(2)}, u32[]{:S(2)}) %collective-permute-start.11) | collective-permute-done | bytes 540704 | tf_op jit(solution)/shard_map/ppermute | solution.py:27
  60.8 0.7 collective-permute-start.32
  61.5 0.1 fold.14
  61.6 10.8 %collective-permute-done.6.refs_2_.refs_4_ = f32[264,512]{1,0:T(8,128)S(1)} collective-permute-done((f32[264,512]{1,0:T(8,128)S(1)}, f32[264,512]{1,0:T(8,128)S(1)}, u32[]{:S(2)}, u32[]{:S(2)}) %collective-permute-start.6) | collective-permute-done | bytes 540704 | tf_op jit(solution)/shard_map/ppermute | solution.py:27
  72.4 0.1 fold.12
  72.5 2.1 %collective-permute-start.7 = (f32[136,512]{1,0:T(8,128)S(1)}, f32[136,512]{1,0:T(8,128)S(1)}, u32[]{:S(2)}, u32[]{:S(2)}) collective-permute-start(f32[136,512]{1,0:T(8,128)S(1)} %get-tuple-element.73), channel_id=1, source_target_pairs={{0,32},{8,40},{16,48},{24,56},{32,0},{40,8},{48,16},{56,24},{64,96... | collective-permute-start | bytes 835592 | tf_op jit(solution)/shard_map/ppermute | solution.py:27
  74.6 0.1 fold.20
  74.7 0.8 collective-permute-start.27
  75.5 0.1 fold.18
  75.6 1.4 %collective-permute-start.22 = (f32[128,512]{1,0:T(8,128)S(1)}, f32[128,512]{1,0:T(8,128)S(1)}, u32[]{:S(2)}, u32[]{:S(2)}) collective-permute-start(f32[128,512]{1,0:T(8,128)S(1)} %get-tuple-element.100), channel_id=1, source_target_pairs={{0,16},{8,24},{16,0},{24,8},{32,48},{40,56},{48,32},{56,40},{64,80... | collective-permute-start | bytes 786440 | tf_op jit(solution)/shard_map/ppermute | solution.py:27
  77.0 0.1 fold.16
  77.1 0.9 collective-permute-done.32.refs_1_
  78.0 3.9 %collective-permute-done.12.refs_1_.refs_3_ = f32[136,512]{1,0:T(8,128)S(1)} collective-permute-done((f32[136,512]{1,0:T(8,128)S(1)}, f32[136,512]{1,0:T(8,128)S(1)}, u32[]{:S(2)}, u32[]{:S(2)}) %collective-permute-start.12) | collective-permute-done | bytes 278560 | tf_op jit(solution)/shard_map/ppermute | solution.py:27
  81.9 4.5 %collective-permute-done.7.refs_1_.refs_3_ = f32[136,512]{1,0:T(8,128)S(1)} collective-permute-done((f32[136,512]{1,0:T(8,128)S(1)}, f32[136,512]{1,0:T(8,128)S(1)}, u32[]{:S(2)}, u32[]{:S(2)}) %collective-permute-start.7) | collective-permute-done | bytes 278560 | tf_op jit(solution)/shard_map/ppermute | solution.py:27
  86.5 2.4 %collective-permute-start.13 = (f32[72,512]{1,0:T(8,128)S(1)}, f32[72,512]{1,0:T(8,128)S(1)}, u32[]{:S(2)}, u32[]{:S(2)}) collective-permute-start(f32[72,512]{1,0:T(8,128)S(1)} %get-tuple-element.83), channel_id=1, source_target_pairs={{0,96},{8,104},{16,112},{24,120},{32,64},{40,72},{48,80},{56,88},{... | collective-permute-start | bytes 442376 | tf_op jit(solution)/shard_map/ppermute | solution.py:27
  89.0 0.9 collective-permute-start.8
  89.9 0.1 collective-permute-start.28
  90.0 2.5 %collective-permute-start.23 = (f32[64,512]{1,0:T(8,128)S(1)}, f32[64,512]{1,0:T(8,128)S(1)}, u32[]{:S(2)}, u32[]{:S(2)}) collective-permute-start(f32[64,512]{1,0:T(8,128)S(1)} %get-tuple-element.102), channel_id=1, source_target_pairs={{0,96},{8,104},{16,112},{24,120},{32,64},{40,72},{48,80},{56,88},{... | collective-permute-start | bytes 393224 | tf_op jit(solution)/shard_map/ppermute | solution.py:27
  92.6 0.8 collective-permute-start.18
  93.3 1.6 %collective-permute-done.28.refs_9_ = f32[64,512]{1,0:T(8,128)S(1)} collective-permute-done((f32[64,512]{1,0:T(8,128)S(1)}, f32[64,512]{1,0:T(8,128)S(1)}, u32[]{:S(2)}, u32[]{:S(2)}) %collective-permute-start.28) | collective-permute-done | bytes 131104 | tf_op jit(solution)/shard_map/ppermute | solution.py:27
  94.9 2.4 %collective-permute-done.23.refs_7_ = f32[64,512]{1,0:T(8,128)S(1)} collective-permute-done((f32[64,512]{1,0:T(8,128)S(1)}, f32[64,512]{1,0:T(8,128)S(1)}, u32[]{:S(2)}, u32[]{:S(2)}) %collective-permute-start.23) | collective-permute-done | bytes 131104 | tf_op jit(solution)/shard_map/ppermute | solution.py:27
  97.3 0.3 collective-permute-done.18.refs_5_
  97.6 1.6 %finish.1 = (f32[64,1024]{1,0:T(8,128)}, f32[64,1024]{1,0:T(8,128)}) custom-call(s32[2]{0:T(128)S(1)} %pad_add_fusion.where_ref, f32[72,512]{1,0:T(8,128)S(1)} %get-tuple-element.74.refs_0_, f32[72,512]{1,0:T(8,128)S(1)} %collective-permute-done.8.refs_1_, f32[72,512]{1,0:T(8,128)S(1)} %get-tuple-element.82.refs_2_, ...), custom_call_target="tpu_custom_call" | custom-call | tf_op jit(solution)/shard_map/finish/pallas_call | solution.py:346
  (42 shorter events, 0.5 us)
Async XLA Ops:
  0.6 7.1 %collective-permute-start = (s32[2,64,128]{2,1,0:T(8,128)}, s32[2,64,128]{2,1,0:T(8,128)S(1)}, u32[]{:S(2)}, u32[]{:S(2)}) collective-permute-start(s32[2,64,128]{2,1,0:T(8,128)} %own_ref.1), channel_id=1, source_target_pairs={{0,1},{1,0},{2,3},{3,2},{4,5},{5,4},{6,7},{7,6},{8,9},{9,8},{10,11... | collective-permute-start | bytes 196616 | tf_op jit(solution)/shard_map/ppermute | solution.py:27
  4.0 3.7 %copy-start = (s32[2,64,128]{2,1,0:T(8,128)S(1)}, s32[2,64,128]{2,1,0:T(8,128)}, u32[]{:S(2)}) copy-start(s32[2,64,128]{2,1,0:T(8,128)} %own_ref.1) | copy-start | bytes 196612
  7.7 11.5 %collective-permute-start.1 = (s32[4,64,128]{2,1,0:T(8,128)S(1)}, s32[4,64,128]{2,1,0:T(8,128)S(1)}, u32[]{:S(2)}, u32[]{:S(2)}) collective-permute-start(s32[4,64,128]{2,1,0:T(8,128)S(1)} %paired.1.refs_0_), channel_id=1, source_target_pairs={{0,4},{1,5},{2,6},{3,7},{4,0},{5,1},{6,2},{7,3},{8,12},{9,13},{10,... | collective-permute-start | bytes 393224 | tf_op jit(solution)/shard_map/ppermute | solution.py:27
  10.8 8.4 %collective-permute-start.2 = (s32[4,64,128]{2,1,0:T(8,128)S(1)}, s32[4,64,128]{2,1,0:T(8,128)S(1)}, u32[]{:S(2)}, u32[]{:S(2)}) collective-permute-start(s32[4,64,128]{2,1,0:T(8,128)S(1)} %paired.1.refs_0_), channel_id=1, source_target_pairs={{0,2},{1,3},{2,0},{3,1},{4,6},{5,7},{6,4},{7,5},{8,10},{9,11},{10,... | collective-permute-start | bytes 393224 | tf_op jit(solution)/shard_map/ppermute | solution.py:27
  11.4 7.8 %collective-permute-start.3 = (s32[4,64,128]{2,1,0:T(8,128)S(1)}, s32[4,64,128]{2,1,0:T(8,128)S(1)}, u32[]{:S(2)}, u32[]{:S(2)}) collective-permute-start(s32[4,64,128]{2,1,0:T(8,128)S(1)} %paired.1.refs_0_), channel_id=1, source_target_pairs={{0,6},{1,7},{2,4},{3,5},{4,2},{5,3},{6,0},{7,1},{8,14},{9,15},{10,... | collective-permute-start | bytes 393224 | tf_op jit(solution)/shard_map/ppermute | solution.py:27
  23.4 9.0 %collective-permute-start.30 = (f32[256,512]{1,0:T(8,128)S(1)}, f32[256,512]{1,0:T(8,128)S(1)}, u32[]{:S(2)}, u32[]{:S(2)}) collective-permute-start(f32[256,512]{1,0:T(8,128)S(1)} %get-tuple-element.117), channel_id=1, source_target_pairs={{0,8},{8,0},{16,24},{24,16},{32,40},{40,32},{48,56},{56,48},{64,72... | collective-permute-start | bytes 1572872 | tf_op jit(solution)/shard_map/ppermute | solution.py:27
  24.7 8.2 %collective-permute-start.29 = (f32[256,512]{1,0:T(8,128)S(1)}, f32[256,512]{1,0:T(8,128)S(1)}, u32[]{:S(2)}, u32[]{:S(2)}) collective-permute-start(f32[256,512]{1,0:T(8,128)S(1)} %get-tuple-element.115), channel_id=1, source_target_pairs={{0,8},{8,0},{16,24},{24,16},{32,40},{40,32},{48,56},{56,48},{64,72... | collective-permute-start | bytes 1572872 | tf_op jit(solution)/shard_map/ppermute | solution.py:27
  26.6 8.0 %collective-permute-start.25 = (f32[256,512]{1,0:T(8,128)S(1)}, f32[256,512]{1,0:T(8,128)S(1)}, u32[]{:S(2)}, u32[]{:S(2)}) collective-permute-start(f32[256,512]{1,0:T(8,128)S(1)} %get-tuple-element.109), channel_id=1, source_target_pairs={{0,8},{8,0},{16,24},{24,16},{32,40},{40,32},{48,56},{56,48},{64,72... | collective-permute-start | bytes 1572872 | tf_op jit(solution)/shard_map/ppermute | solution.py:27
  27.9 8.2 %collective-permute-start.24 = (f32[256,512]{1,0:T(8,128)S(1)}, f32[256,512]{1,0:T(8,128)S(1)}, u32[]{:S(2)}, u32[]{:S(2)}) collective-permute-start(f32[256,512]{1,0:T(8,128)S(1)} %get-tuple-element.107), channel_id=1, source_target_pairs={{0,8},{8,0},{16,24},{24,16},{32,40},{40,32},{48,56},{56,48},{64,72... | collective-permute-start | bytes 1572872 | tf_op jit(solution)/shard_map/ppermute | solution.py:27
  29.8 8.0 %collective-permute-start.20 = (f32[256,512]{1,0:T(8,128)S(1)}, f32[256,512]{1,0:T(8,128)S(1)}, u32[]{:S(2)}, u32[]{:S(2)}) collective-permute-start(f32[256,512]{1,0:T(8,128)S(1)} %get-tuple-element.98), channel_id=1, source_target_pairs={{0,8},{8,0},{16,24},{24,16},{32,40},{40,32},{48,56},{56,48},{64,72... | collective-permute-start | bytes 1572872 | tf_op jit(solution)/shard_map/ppermute | solution.py:27
  32.4 6.9 %collective-permute-start.19 = (f32[256,512]{1,0:T(8,128)S(1)}, f32[256,512]{1,0:T(8,128)S(1)}, u32[]{:S(2)}, u32[]{:S(2)}) collective-permute-start(f32[256,512]{1,0:T(8,128)S(1)} %get-tuple-element.96), channel_id=1, source_target_pairs={{0,8},{8,0},{16,24},{24,16},{32,40},{40,32},{48,56},{56,48},{64,72... | collective-permute-start | bytes 1572872 | tf_op jit(solution)/shard_map/ppermute | solution.py:27
  33.0 8.4 %collective-permute-start.10 = (f32[264,512]{1,0:T(8,128)S(1)}, f32[264,512]{1,0:T(8,128)S(1)}, u32[]{:S(2)}, u32[]{:S(2)}) collective-permute-start(f32[264,512]{1,0:T(8,128)S(1)} %get-tuple-element.79), channel_id=1, source_target_pairs={{0,8},{8,0},{16,24},{24,16},{32,40},{40,32},{48,56},{56,48},{64,72... | collective-permute-start | bytes 1622024 | tf_op jit(solution)/shard_map/ppermute | solution.py:27
  34.5 6.4 %collective-permute-start.15 = (f32[256,512]{1,0:T(8,128)S(1)}, f32[256,512]{1,0:T(8,128)S(1)}, u32[]{:S(2)}, u32[]{:S(2)}) collective-permute-start(f32[256,512]{1,0:T(8,128)S(1)} %get-tuple-element.90), channel_id=1, source_target_pairs={{0,8},{8,0},{16,24},{24,16},{32,40},{40,32},{48,56},{56,48},{64,72... | collective-permute-start | bytes 1572872 | tf_op jit(solution)/shard_map/ppermute | solution.py:27
  36.1 9.4 %collective-permute-start.5 = (f32[264,512]{1,0:T(8,128)S(1)}, f32[264,512]{1,0:T(8,128)S(1)}, u32[]{:S(2)}, u32[]{:S(2)}) collective-permute-start(f32[264,512]{1,0:T(8,128)S(1)} %get-tuple-element.71), channel_id=1, source_target_pairs={{0,8},{8,0},{16,24},{24,16},{32,40},{40,32},{48,56},{56,48},{64,72... | collective-permute-start | bytes 1622024 | tf_op jit(solution)/shard_map/ppermute | solution.py:27
  37.8 8.6 %collective-permute-start.14 = (f32[256,512]{1,0:T(8,128)S(1)}, f32[256,512]{1,0:T(8,128)S(1)}, u32[]{:S(2)}, u32[]{:S(2)}) collective-permute-start(f32[256,512]{1,0:T(8,128)S(1)} %get-tuple-element.88), channel_id=1, source_target_pairs={{0,8},{8,0},{16,24},{24,16},{32,40},{40,32},{48,56},{56,48},{64,72... | collective-permute-start | bytes 1572872 | tf_op jit(solution)/shard_map/ppermute | solution.py:27
  39.3 8.5 %collective-permute-start.9 = (f32[256,512]{1,0:T(8,128)S(1)}, f32[256,512]{1,0:T(8,128)S(1)}, u32[]{:S(2)}, u32[]{:S(2)}) collective-permute-start(f32[256,512]{1,0:T(8,128)S(1)} %get-tuple-element.77), channel_id=1, source_target_pairs={{0,8},{8,0},{16,24},{24,16},{32,40},{40,32},{48,56},{56,48},{64,72... | collective-permute-start | bytes 1572872 | tf_op jit(solution)/shard_map/ppermute | solution.py:27
  41.0 7.1 %collective-permute-start.4 = (f32[256,512]{1,0:T(8,128)S(1)}, f32[256,512]{1,0:T(8,128)S(1)}, u32[]{:S(2)}, u32[]{:S(2)}) collective-permute-start(f32[256,512]{1,0:T(8,128)S(1)} %get-tuple-element.66), channel_id=1, source_target_pairs={{0,8},{8,0},{16,24},{24,16},{32,40},{40,32},{48,56},{56,48},{64,72... | collective-permute-start | bytes 1572872 | tf_op jit(solution)/shard_map/ppermute | solution.py:27
  41.4 16.9 %collective-permute-start.31 = (f32[256,512]{1,0:T(8,128)S(1)}, f32[256,512]{1,0:T(8,128)S(1)}, u32[]{:S(2)}, u32[]{:S(2)}) collective-permute-start(f32[256,512]{1,0:T(8,128)S(1)} %meet.11), channel_id=1, source_target_pairs={{0,96},{8,104},{16,112},{24,120},{32,64},{40,72},{48,80},{56,88},{... | collective-permute-start | bytes 1572872 | tf_op jit(solution)/shard_map/ppermute | solution.py:27
  45.6 15.2 %collective-permute-start.11 = (f32[264,512]{1,0:T(8,128)S(1)}, f32[264,512]{1,0:T(8,128)S(1)}, u32[]{:S(2)}, u32[]{:S(2)}) collective-permute-start(f32[264,512]{1,0:T(8,128)S(1)} %meet.7.refs_3_), channel_id=1, source_target_pairs={{0,16},{8,24},{16,0},{24,8},{32,48},{40,56},{48,32},{56,40},{64,80... | collective-permute-start | bytes 1622024 | tf_op jit(solution)/shard_map/ppermute | solution.py:27
  46.4 26.0 %collective-permute-start.6 = (f32[264,512]{1,0:T(8,128)S(1)}, f32[264,512]{1,0:T(8,128)S(1)}, u32[]{:S(2)}, u32[]{:S(2)}) collective-permute-start(f32[264,512]{1,0:T(8,128)S(1)} %meet.6.refs_3_), channel_id=1, source_target_pairs={{0,16},{8,24},{16,0},{24,8},{32,48},{40,56},{48,32},{56,40},{64,80... | collective-permute-start | bytes 1622024 | tf_op jit(solution)/shard_map/ppermute | solution.py:27
  47.9 24.6 %collective-permute-start.26 = (f32[256,512]{1,0:T(8,128)S(1)}, f32[256,512]{1,0:T(8,128)S(1)}, u32[]{:S(2)}, u32[]{:S(2)}) collective-permute-start(f32[256,512]{1,0:T(8,128)S(1)} %meet.10), channel_id=1, source_target_pairs={{0,96},{8,104},{16,112},{24,120},{32,64},{40,72},{48,80},{56,88},{... | collective-permute-start | bytes 1572872 | tf_op jit(solution)/shard_map/ppermute | solution.py:27
  48.1 26.6 %collective-permute-start.21 = (f32[256,512]{1,0:T(8,128)S(1)}, f32[256,512]{1,0:T(8,128)S(1)}, u32[]{:S(2)}, u32[]{:S(2)}) collective-permute-start(f32[256,512]{1,0:T(8,128)S(1)} %meet.9), channel_id=1, source_target_pairs={{0,32},{8,40},{16,48},{24,56},{32,0},{40,8},{48,16},{56,24},{64,96... | collective-permute-start | bytes 1572872 | tf_op jit(solution)/shard_map/ppermute | solution.py:27
  58.3 17.3 %collective-permute-start.16 = (f32[256,512]{1,0:T(8,128)S(1)}, f32[256,512]{1,0:T(8,128)S(1)}, u32[]{:S(2)}, u32[]{:S(2)}) collective-permute-start(f32[256,512]{1,0:T(8,128)S(1)} %meet.8), channel_id=1, source_target_pairs={{0,32},{8,40},{16,48},{24,56},{32,0},{40,8},{48,16},{56,24},{64,96... | collective-permute-start | bytes 1572872 | tf_op jit(solution)/shard_map/ppermute | solution.py:27
  60.8 17.2 %collective-permute-start.32 = (f32[128,512]{1,0:T(8,128)S(1)}, f32[128,512]{1,0:T(8,128)S(1)}, u32[]{:S(2)}, u32[]{:S(2)}) collective-permute-start(f32[128,512]{1,0:T(8,128)S(1)} %get-tuple-element.119), channel_id=1, source_target_pairs={{0,16},{8,24},{16,0},{24,8},{32,48},{40,56},{48,32},{56,40},{64,80... | collective-permute-start | bytes 786440 | tf_op jit(solution)/shard_map/ppermute | solution.py:27
  72.4 9.5 %collective-permute-start.12 = (f32[136,512]{1,0:T(8,128)S(1)}, f32[136,512]{1,0:T(8,128)S(1)}, u32[]{:S(2)}, u32[]{:S(2)}) collective-permute-start(f32[136,512]{1,0:T(8,128)S(1)} %get-tuple-element.81), channel_id=1, source_target_pairs={{0,32},{8,40},{16,48},{24,56},{32,0},{40,8},{48,16},{56,24},{64,96... | collective-permute-start | bytes 835592 | tf_op jit(solution)/shard_map/ppermute | solution.py:27
  72.5 14.0 %collective-permute-start.7 = (f32[136,512]{1,0:T(8,128)S(1)}, f32[136,512]{1,0:T(8,128)S(1)}, u32[]{:S(2)}, u32[]{:S(2)}) collective-permute-start(f32[136,512]{1,0:T(8,128)S(1)} %get-tuple-element.73), channel_id=1, source_target_pairs={{0,32},{8,40},{16,48},{24,56},{32,0},{40,8},{48,16},{56,24},{64,96... | collective-permute-start | bytes 835592 | tf_op jit(solution)/shard_map/ppermute | solution.py:27
  74.7 14.3 %collective-permute-start.27 = (f32[128,512]{1,0:T(8,128)S(1)}, f32[128,512]{1,0:T(8,128)S(1)}, u32[]{:S(2)}, u32[]{:S(2)}) collective-permute-start(f32[128,512]{1,0:T(8,128)S(1)} %get-tuple-element.111), channel_id=1, source_target_pairs={{0,16},{8,24},{16,0},{24,8},{32,48},{40,56},{48,32},{56,40},{64,80... | collective-permute-start | bytes 786440 | tf_op jit(solution)/shard_map/ppermute | solution.py:27
  75.6 14.3 %collective-permute-start.22 = (f32[128,512]{1,0:T(8,128)S(1)}, f32[128,512]{1,0:T(8,128)S(1)}, u32[]{:S(2)}, u32[]{:S(2)}) collective-permute-start(f32[128,512]{1,0:T(8,128)S(1)} %get-tuple-element.100), channel_id=1, source_target_pairs={{0,16},{8,24},{16,0},{24,8},{32,48},{40,56},{48,32},{56,40},{64,80... | collective-permute-start | bytes 786440 | tf_op jit(solution)/shard_map/ppermute | solution.py:27
  78.0 12.0 %collective-permute-start.17 = (f32[128,512]{1,0:T(8,128)S(1)}, f32[128,512]{1,0:T(8,128)S(1)}, u32[]{:S(2)}, u32[]{:S(2)}) collective-permute-start(f32[128,512]{1,0:T(8,128)S(1)} %get-tuple-element.92), channel_id=1, source_target_pairs={{0,96},{8,104},{16,112},{24,120},{32,64},{40,72},{48,80},{56,88},{... | collective-permute-start | bytes 786440 | tf_op jit(solution)/shard_map/ppermute | solution.py:27
  81.9 10.7 %collective-permute-start.33 = (f32[64,512]{1,0:T(8,128)S(1)}, f32[64,512]{1,0:T(8,128)S(1)}, u32[]{:S(2)}, u32[]{:S(2)}) collective-permute-start(f32[64,512]{1,0:T(8,128)S(1)} %get-tuple-element.121), channel_id=1, source_target_pairs={{0,32},{8,40},{16,48},{24,56},{32,0},{40,8},{48,16},{56,24},{64,96... | collective-permute-start | bytes 393224 | tf_op jit(solution)/shard_map/ppermute | solution.py:27
  86.5 11.2 %collective-permute-start.13 = (f32[72,512]{1,0:T(8,128)S(1)}, f32[72,512]{1,0:T(8,128)S(1)}, u32[]{:S(2)}, u32[]{:S(2)}) collective-permute-start(f32[72,512]{1,0:T(8,128)S(1)} %get-tuple-element.83), channel_id=1, source_target_pairs={{0,96},{8,104},{16,112},{24,120},{32,64},{40,72},{48,80},{56,88},{... | collective-permute-start | bytes 442376 | tf_op jit(solution)/shard_map/ppermute | solution.py:27
  89.0 8.7 %collective-permute-start.8 = (f32[72,512]{1,0:T(8,128)S(1)}, f32[72,512]{1,0:T(8,128)S(1)}, u32[]{:S(2)}, u32[]{:S(2)}) collective-permute-start(f32[72,512]{1,0:T(8,128)S(1)} %get-tuple-element.75), channel_id=1, source_target_pairs={{0,96},{8,104},{16,112},{24,120},{32,64},{40,72},{48,80},{56,88},{... | collective-permute-start | bytes 442376 | tf_op jit(solution)/shard_map/ppermute | solution.py:27
  89.9 5.0 %collective-permute-start.28 = (f32[64,512]{1,0:T(8,128)S(1)}, f32[64,512]{1,0:T(8,128)S(1)}, u32[]{:S(2)}, u32[]{:S(2)}) collective-permute-start(f32[64,512]{1,0:T(8,128)S(1)} %get-tuple-element.113), channel_id=1, source_target_pairs={{0,32},{8,40},{16,48},{24,56},{32,0},{40,8},{48,16},{56,24},{64,96... | collective-permute-start | bytes 393224 | tf_op jit(solution)/shard_map/ppermute | solution.py:27
  90.0 7.3 %collective-permute-start.23 = (f32[64,512]{1,0:T(8,128)S(1)}, f32[64,512]{1,0:T(8,128)S(1)}, u32[]{:S(2)}, u32[]{:S(2)}) collective-permute-start(f32[64,512]{1,0:T(8,128)S(1)} %get-tuple-element.102), channel_id=1, source_target_pairs={{0,96},{8,104},{16,112},{24,120},{32,64},{40,72},{48,80},{56,88},{... | collective-permute-start | bytes 393224 | tf_op jit(solution)/shard_map/ppermute | solution.py:27
  92.6 5.0 %collective-permute-start.18 = (f32[64,512]{1,0:T(8,128)S(1)}, f32[64,512]{1,0:T(8,128)S(1)}, u32[]{:S(2)}, u32[]{:S(2)}) collective-permute-start(f32[64,512]{1,0:T(8,128)S(1)} %get-tuple-element.94), channel_id=1, source_target_pairs={{0,16},{8,24},{16,0},{24,8},{32,48},{40,56},{48,32},{56,40},{64,80... | collective-permute-start | bytes 393224 | tf_op jit(solution)/shard_map/ppermute | solution.py:27

commit v3 on v2

--- a/solution.py
+++ b/solution.py
@@ -18,7 +18,40 @@
 
 CORE, SIDE_Y, SIDE_A, SIDE_B = 1, 2, 4, 12
 ORDERS = ((SIDE_Y, SIDE_A, SIDE_B), (SIDE_A, SIDE_B, SIDE_Y), (SIDE_B, SIDE_Y, SIDE_A))
-TURNED = ((1, 1),)
+TURNED = ()
+SENDING, KEEPING, FIRST, SECOND, THIRD = "sending", "keeping", "first", "second", "third"
+PLAN = (
+    (SENDING, 1, 1),
+    (SENDING, 0, 0),
+    (SENDING, 2, 0),
+    (FIRST, 1, 1),
+    (FIRST, 0, 0),
+    (FIRST, 2, 0),
+    (SENDING, 1, 0),
+    (SENDING, 0, 1),
+    (SENDING, 2, 1),
+    (FIRST, 1, 0),
+    (FIRST, 0, 1),
+    (KEEPING, 1, 0),
+    (FIRST, 2, 1),
+    (KEEPING, 0, 0),
+    (KEEPING, 1, 1),
+    (KEEPING, 0, 1),
+    (KEEPING, 2, 0),
+    (SECOND, 0, 0),
+    (SECOND, 1, 1),
+    (SECOND, 2, 0),
+    (KEEPING, 2, 1),
+    (SECOND, 0, 1),
+    (SECOND, 2, 1),
+    (SECOND, 1, 0),
+    (THIRD, 0, 0),
+    (THIRD, 1, 1),
+    (THIRD, 2, 0),
+    (THIRD, 0, 1),
+    (THIRD, 2, 1),
+    (THIRD, 1, 0),
+)
 FAR = (4, 2, 6)
 
 
@@ -365,52 +398,40 @@
         pairs.append(swap(pairs[0], "var", flip))
     *designs, dos_part = unpack(where, pairs)
     spots = [(call, block) for call, blocks in enumerate(MADE) for block in range(blocks)]
-    kept, cored, sent, came = {}, {}, {}, {}
-    for part, chunk, index in items():
-        first = sum(CHUNKS[:chunk])
-        mine = spots[first : first + CHUNKS[chunk]]
-        calls = 1 + max(call for call, _ in mine)
-        margins = []
-        if index == 0 and part == 1:
-            margins = [made[call][3] for call in range(calls)]
-            margins += [dos_part] if chunk == DOS_CHUNK else []
-        features_of = [made[call][index] for call in range(calls)]
-        keep, send = cross(designs[index], features_of, mine, part, margins)
-        got = swap(send, "samp", CORE)
-        if part == 0:
-            kept[chunk, index], cored[chunk, index] = keep, got
+    kept, sent, came = {}, {}, {}
+    for kind, index, chunk in PLAN:
+        cell = index, chunk
+        if kind in (SENDING, KEEPING):
+            first = sum(CHUNKS[:chunk])
+            mine = spots[first : first + CHUNKS[chunk]]
+            calls = 1 + max(call for call, _ in mine)
+            margins = []
+            if index == 0 and kind == SENDING:
+                margins = [made[call][3] for call in range(calls)]
+                margins += [dos_part] if chunk == DOS_CHUNK else []
+            features_of = [made[call][index] for call in range(calls)]
+            part = int(kind == SENDING)
+            keep, send = cross(designs[index], features_of, mine, part, margins)
+        elif kind == FIRST:
+            keep, send = None, meet(kept[SENDING, cell], came[SENDING, cell])
+            sent[cell] = send
+        elif kind == SECOND:
+            terms = [kept[KEEPING, cell], came[KEEPING, cell], came[FIRST, cell]]
+            margins = [sent[cell], came[FIRST, cell]] if index == 0 else []
+            keep, send = fold(terms, margins, cell in TURNED)
         else:
-            sent[chunk, index] = meet(keep, got)
-            came[chunk, index] = swap(sent[chunk, index], "samp", sides(index, chunk)[0])
-    cells = [(chunk, index) for chunk in range(len(CHUNKS)) for index in range(3)]
-    for chunk, index in cells:
-        cell = chunk, index
-        margins = [sent[cell], came[cell]] if index == 0 else []
-        keep, send = fold(
-            [kept[cell], cored[cell], came[cell]], margins, cell[::-1] in TURNED
-        )
-        kept[cell], came[cell] = keep, swap(send, "samp", sides(index, chunk)[1])
-    for chunk, index in cells:
-        cell = chunk, index
-        margins = [kept[cell], came[cell]] if index == 0 else []
-        keep, send = fold([kept[cell], came[cell]], margins, False)
-        kept[cell], came[cell] = keep, swap(send, "samp", sides(index, chunk)[2])
+            terms = [kept[SECOND, cell], came[SECOND, cell]]
+            keep, send = fold(terms, terms if index == 0 else [], False)
+        at = (FIRST, SECOND, THIRD).index(kind) if kind in (FIRST, SECOND, THIRD) else None
+        side = CORE if at is None else sides(index, chunk)[at]
+        kept[kind, cell], came[kind, cell] = keep, swap(send, "samp", side)
     sample_count = float(total_counts.shape[0] * lax.axis_size("samp"))
     own = designs[0].shape[0] // lax.axis_size("samp")
     parts = []
     for index in range(3):
         for chunk in range(len(CHUNKS)):
-            parts += [kept[chunk, index], came[chunk, index]]
+            parts += [kept[THIRD, (index, chunk)], came[THIRD, (index, chunk)]]
     return finish(where, parts, own, total_counts.shape[1], sample_count)
-
-
-def items():
-    return [
-        (part, chunk, index)
-        for part in (1, 0)
-        for chunk in range(len(CHUNKS))
-        for index in range(3)
-    ]
 
 
 def solution(mesh):

time: 99.4 us -> 98.2 us (0.988)
  waiting for transfers between devices: 37 us -> 35.8 us
    ppermute x34, waiting for transfers between devices: 37 us -> 35.8 us  [swap(): return lax.ppermute(array, axis, [(d, d ^ flip) for d in range(size)])]
where the time goes in v3:
time: 98.2 us; the launch traced here: 98.1 us
  waiting for transfers between devices  35.8 us (36%)
  Pallas kernels  31.5 us (32%)
  starting transfers between devices  29.8 us (30%)
  between operations  0.99 us (1%)
    ppermute x34, waiting for transfers between devices, swap(): return lax.ppermute(array, axis, [(d, d ^ flip) for d in range(size)])  35.8 us
    ppermute x34, starting transfers between devices, swap(): return lax.ppermute(array, axis, [(d, d ^ flip) for d in range(size)])  29.8 us
    pallas_call x12, Pallas kernels, cross(): pl.pallas_call(functools.partial(cross_kernel, spots, part, len(margins))...  15.1 us
    pallas_call x2, Pallas kernels, features(): pl.pallas_call(functools.partial(feature_kernel, first), out_shape=(featu...  10.8 us
    pallas_call x1, Pallas kernels, unpack(): pl.pallas_call(unpack_kernel, out_shape=(design,) * 3 + (jax.ShapeDtypeSt...  2.87 us
  transfers between devices with their start and end apart: 34, of which 9 were waited for; matrix products, arithmetic and copies ran while one was open for 0% of the time, Pallas kernels for 26%

profile of v3, /device:TPU:0, one launch (start us, length us, event | category | flops | bytes accessed | tf_op | source)
XLA Modules:
  0.0 98.1 jit_solution(1438016305184224830)
XLA Ops:
  0.6 3.4 %collective-permute-start = (s32[2,64,128]{2,1,0:T(8,128)}, s32[2,64,128]{2,1,0:T(8,128)S(1)}, u32[]{:S(2)}, u32[]{:S(2)}) collective-permute-start(s32[2,64,128]{2,1,0:T(8,128)} %own_ref.1), channel_id=1, source_target_pairs={{0,1},{1,0},{2,3},{3,2},{4,5},{5,4},{6,7},{7,6},{8,9},{9,8},{10,11... | collective-permute-start | bytes 196616 | tf_op jit(solution)/shard_map/ppermute | solution.py:60
  4.0 3.6 %features.2 = (bf16[2,1920,128]{2,1,0:T(8,128)(2,1)S(1)}, bf16[2,1920,128]{2,1,0:T(8,128)(2,1)S(1)}, bf16[2,1920,128]{2,1,0:T(8,128)(2,1)S(1)}, f32[2,256]{1,0:T(2,128)S(1)}) custom-call(s32[1920,1024]{1,0:T(8,128)} %total_hbm.3, s32[1920,1024]{1,0:T(8,128)} %one_hbm.3, s32[1920,1024]{1,0:T(8,128)} %two_hbm.3), custom_call_target="tpu_custom_call" | custom-call | flops 3072000000 | bytes 8847360 | tf_op jit(solution)/shard_map/features/pallas_call | solution.py:211
  7.6 0.1 pad_add_fusion.where_ref
  7.7 3.1 %collective-permute-start.1 = (s32[4,64,128]{2,1,0:T(8,128)S(1)}, s32[4,64,128]{2,1,0:T(8,128)S(1)}, u32[]{:S(2)}, u32[]{:S(2)}) collective-permute-start(s32[4,64,128]{2,1,0:T(8,128)S(1)} %paired.1.refs_0_), channel_id=1, source_target_pairs={{0,4},{1,5},{2,6},{3,7},{4,0},{5,1},{6,2},{7,3},{8,12},{9,13},{10,... | collective-permute-start | bytes 393224 | tf_op jit(solution)/shard_map/ppermute | solution.py:60
  10.8 0.6 collective-permute-start.2
  11.4 0.6 collective-permute-start.3
  12.0 7.2 %features.3 = (bf16[6,1920,128]{2,1,0:T(8,128)(2,1)S(1)}, bf16[6,1920,128]{2,1,0:T(8,128)(2,1)S(1)}, bf16[6,1920,128]{2,1,0:T(8,128)(2,1)S(1)}, f32[2,768]{1,0:T(2,128)S(1)}) custom-call(s32[1920,1024]{1,0:T(8,128)} %total_hbm.3, s32[1920,1024]{1,0:T(8,128)} %one_hbm.3, s32[1920,1024]{1,0:T(8,128)} %two_hbm.3, ...), custom_call_target="tpu_custom_call" | custom-call | flops 9216000000 | bytes 26542080 | tf_op jit(solution)/shard_map/features/pallas_call | solution.py:211
  19.2 2.9 %unpack.1 = (bf16[1024,1920]{1,0:T(8,128)(2,1)S(1)}, bf16[1024,1920]{1,0:T(8,128)(2,1)S(1)}, bf16[1024,1920]{1,0:T(8,128)(2,1)S(1)}, f32[8,2,128]{2,1,0:T(2,128)S(1)}) custom-call(s32[2]{0:T(128)S(1)} %pad_add_fusion.where_ref, s32[4,64,128]{2,1,0:T(8,128)S(1)} %paired.1.refs_0_, s32[4,64,128]{2,1,0:T(8,128)S(1)} %collective-permute-done.1.refs_1_, ...), custom_call_target="tpu_custom_call" | custom-call | flops 6000000000 | bytes 11796480 | tf_op jit(solution)/shard_map/unpack/pallas_call | solution.py:134
  22.1 1.3 %cross.23 = (f32[256,512]{1,0:T(8,128)S(1)}, f32[256,512]{1,0:T(8,128)S(1)}) custom-call(bf16[1024,1920]{1,0:T(8,128)(2,1)S(1)} %get-tuple-element.103.design_ref, bf16[2,1920,128]{2,1,0:T(8,128)(2,1)S(1)} %get-tuple-element.104.refs_0_, bf16[6,1920,128]{2,1,0:T(8,128)(2,1)S(1)} %get-tuple-element.105.refs_1_), custom_call_target="tpu_custom_call" | custom-call | flops 1006632960 | bytes 5898240 | tf_op jit(solution)/shard_map/cross/pallas_call | solution.py:270
  23.4 0.1 collective-permute-start.30
  23.5 1.3 %cross.22 = (f32[256,512]{1,0:T(8,128)S(1)}, f32[256,512]{1,0:T(8,128)S(1)}) custom-call(bf16[1024,1920]{1,0:T(8,128)(2,1)S(1)} %get-tuple-element.103.design_ref, bf16[2,1920,128]{2,1,0:T(8,128)(2,1)S(1)} %get-tuple-element.104.refs_0_, bf16[6,1920,128]{2,1,0:T(8,128)(2,1)S(1)} %get-tuple-element.105.refs_1_), custom_call_target="tpu_custom_call" | custom-call | flops 1006632960 | bytes 5898240 | tf_op jit(solution)/shard_map/cross/pallas_call | solution.py:270
  24.7 0.6 collective-permute-start.29
  25.3 1.3 %cross.21 = (f32[256,512]{1,0:T(8,128)S(1)}, f32[256,512]{1,0:T(8,128)S(1)}) custom-call(bf16[1024,1920]{1,0:T(8,128)(2,1)S(1)} %get-tuple-element.103.design_ref, bf16[2,1920,128]{2,1,0:T(8,128)(2,1)S(1)} %get-tuple-element.104.refs_0_, bf16[6,1920,128]{2,1,0:T(8,128)(2,1)S(1)} %get-tuple-element.105.refs_1_), custom_call_target="tpu_custom_call" | custom-call | flops 1006632960 | bytes 5898240 | tf_op jit(solution)/shard_map/cross/pallas_call | solution.py:270
  26.6 0.1 collective-permute-start.25
  26.7 1.3 %cross.20 = (f32[256,512]{1,0:T(8,128)S(1)}, f32[256,512]{1,0:T(8,128)S(1)}) custom-call(bf16[1024,1920]{1,0:T(8,128)(2,1)S(1)} %get-tuple-element.103.design_ref, bf16[2,1920,128]{2,1,0:T(8,128)(2,1)S(1)} %get-tuple-element.104.refs_0_, bf16[6,1920,128]{2,1,0:T(8,128)(2,1)S(1)} %get-tuple-element.105.refs_1_), custom_call_target="tpu_custom_call" | custom-call | flops 1006632960 | bytes 5898240 | tf_op jit(solution)/shard_map/cross/pallas_call | solution.py:270
  27.9 0.6 collective-permute-start.24
  28.5 1.3 %cross.19 = (f32[256,512]{1,0:T(8,128)S(1)}, f32[256,512]{1,0:T(8,128)S(1)}) custom-call(bf16[1024,1920]{1,0:T(8,128)(2,1)S(1)} %get-tuple-element.84.design_ref, bf16[2,1920,128]{2,1,0:T(8,128)(2,1)S(1)} %get-tuple-element.85.refs_0_, bf16[6,1920,128]{2,1,0:T(8,128)(2,1)S(1)} %get-tuple-element.86.refs_1_), custom_call_target="tpu_custom_call" | custom-call | flops 1006632960 | bytes 5898240 | tf_op jit(solution)/shard_map/cross/pallas_call | solution.py:270
  29.8 0.1 collective-permute-start.20
  29.9 1.3 %cross.18 = (f32[256,512]{1,0:T(8,128)S(1)}, f32[256,512]{1,0:T(8,128)S(1)}) custom-call(bf16[1024,1920]{1,0:T(8,128)(2,1)S(1)} %get-tuple-element.84.design_ref, bf16[2,1920,128]{2,1,0:T(8,128)(2,1)S(1)} %get-tuple-element.85.refs_0_, bf16[6,1920,128]{2,1,0:T(8,128)(2,1)S(1)} %get-tuple-element.86.refs_1_), custom_call_target="tpu_custom_call" | custom-call | flops 1006632960 | bytes 5898240 | tf_op jit(solution)/shard_map/cross/pallas_call | solution.py:270
  31.1 1.3 %cross.15 = (f32[264,512]{1,0:T(8,128)S(1)}, f32[264,512]{1,0:T(8,128)S(1)}) custom-call(bf16[1024,1920]{1,0:T(8,128)(2,1)S(1)} %get-tuple-element.62.design_ref, bf16[2,1920,128]{2,1,0:T(8,128)(2,1)S(1)} %get-tuple-element.63.refs_0_, bf16[6,1920,128]{2,1,0:T(8,128)(2,1)S(1)} %get-tuple-element.64.refs_1_, f32[2,256]{1,0:T(2,128)S(1)} %get-tuple-element.67.refs_2_, ...), custom_call_target="tpu_custom_call" | custom-call | flops 1006632960 | bytes 5898240 | tf_op jit(solution)/shard_map/cross/pallas_call | solution.py:270
  32.4 0.6 collective-permute-start.19
  33.0 0.3 collective-permute-start.10
  33.3 1.3 %cross.17 = (f32[256,512]{1,0:T(8,128)S(1)}, f32[256,512]{1,0:T(8,128)S(1)}) custom-call(bf16[1024,1920]{1,0:T(8,128)(2,1)S(1)} %get-tuple-element.84.design_ref, bf16[2,1920,128]{2,1,0:T(8,128)(2,1)S(1)} %get-tuple-element.85.refs_0_, bf16[6,1920,128]{2,1,0:T(8,128)(2,1)S(1)} %get-tuple-element.86.refs_1_), custom_call_target="tpu_custom_call" | custom-call | flops 1006632960 | bytes 5898240 | tf_op jit(solution)/shard_map/cross/pallas_call | solution.py:270
  34.5 0.3 collective-permute-start.15
  34.8 1.3 %cross.13 = (f32[264,512]{1,0:T(8,128)S(1)}, f32[264,512]{1,0:T(8,128)S(1)}) custom-call(bf16[1024,1920]{1,0:T(8,128)(2,1)S(1)} %get-tuple-element.62.design_ref, bf16[2,1920,128]{2,1,0:T(8,128)(2,1)S(1)} %get-tuple-element.63.refs_0_, bf16[6,1920,128]{2,1,0:T(8,128)(2,1)S(1)} %get-tuple-element.64.refs_1_, f32[2,256]{1,0:T(2,128)S(1)} %get-tuple-element.67.refs_2_, ...), custom_call_target="tpu_custom_call" | custom-call | flops 1006632960 | bytes 5898240 | tf_op jit(solution)/shard_map/cross/pallas_call | solution.py:270
  36.1 0.4 collective-permute-start.5
  36.5 1.3 %cross.16 = (f32[256,512]{1,0:T(8,128)S(1)}, f32[256,512]{1,0:T(8,128)S(1)}) custom-call(bf16[1024,1920]{1,0:T(8,128)(2,1)S(1)} %get-tuple-element.84.design_ref, bf16[2,1920,128]{2,1,0:T(8,128)(2,1)S(1)} %get-tuple-element.85.refs_0_, bf16[6,1920,128]{2,1,0:T(8,128)(2,1)S(1)} %get-tuple-element.86.refs_1_), custom_call_target="tpu_custom_call" | custom-call | flops 1006632960 | bytes 5898240 | tf_op jit(solution)/shard_map/cross/pallas_call | solution.py:270
  37.8 0.3 collective-permute-start.14
  38.1 1.3 %cross.14 = (f32[256,512]{1,0:T(8,128)S(1)}, f32[256,512]{1,0:T(8,128)S(1)}) custom-call(bf16[1024,1920]{1,0:T(8,128)(2,1)S(1)} %get-tuple-element.62.design_ref, bf16[2,1920,128]{2,1,0:T(8,128)(2,1)S(1)} %get-tuple-element.63.refs_0_, bf16[6,1920,128]{2,1,0:T(8,128)(2,1)S(1)} %get-tuple-element.64.refs_1_), custom_call_target="tpu_custom_call" | custom-call | flops 1006632960 | bytes 5898240 | tf_op jit(solution)/shard_map/cross/pallas_call | solution.py:270
  39.3 0.4 collective-permute-start.9
  39.7 1.3 %cross.12 = (f32[256,512]{1,0:T(8,128)S(1)}, f32[256,512]{1,0:T(8,128)S(1)}) custom-call(bf16[1024,1920]{1,0:T(8,128)(2,1)S(1)} %get-tuple-element.62.design_ref, bf16[2,1920,128]{2,1,0:T(8,128)(2,1)S(1)} %get-tuple-element.63.refs_0_, bf16[6,1920,128]{2,1,0:T(8,128)(2,1)S(1)} %get-tuple-element.64.refs_1_), custom_call_target="tpu_custom_call" | custom-call | flops 1006632960 | bytes 5898240 | tf_op jit(solution)/shard_map/cross/pallas_call | solution.py:270
  41.0 0.3 collective-permute-start.4
  41.3 0.1 meet.11
  41.4 4.1 %collective-permute-start.31 = (f32[256,512]{1,0:T(8,128)S(1)}, f32[256,512]{1,0:T(8,128)S(1)}, u32[]{:S(2)}, u32[]{:S(2)}) collective-permute-start(f32[256,512]{1,0:T(8,128)S(1)} %meet.11), channel_id=1, source_target_pairs={{0,96},{8,104},{16,112},{24,120},{32,64},{40,72},{48,80},{56,88},{... | collective-permute-start | bytes 1572872 | tf_op jit(solution)/shard_map/ppermute | solution.py:60
  45.6 0.8 collective-permute-start.11
  46.4 1.4 %collective-permute-start.6 = (f32[264,512]{1,0:T(8,128)S(1)}, f32[264,512]{1,0:T(8,128)S(1)}, u32[]{:S(2)}, u32[]{:S(2)}) collective-permute-start(f32[264,512]{1,0:T(8,128)S(1)} %meet.6.refs_3_), channel_id=1, source_target_pairs={{0,16},{8,24},{16,0},{24,8},{32,48},{40,56},{48,32},{56,40},{64,80... | collective-permute-start | bytes 1622024 | tf_op jit(solution)/shard_map/ppermute | solution.py:60
  47.9 0.1 collective-permute-start.26
  48.1 0.1 collective-permute-start.21
  48.2 10.0 %collective-permute-done.31.refs_2_ = f32[256,512]{1,0:T(8,128)S(1)} collective-permute-done((f32[256,512]{1,0:T(8,128)S(1)}, f32[256,512]{1,0:T(8,128)S(1)}, u32[]{:S(2)}, u32[]{:S(2)}) %collective-permute-start.31) | collective-permute-done | bytes 524320 | tf_op jit(solution)/shard_map/ppermute | solution.py:60
  58.3 0.1 fold.22
  58.4 2.4 %collective-permute-done.11.refs_2_.refs_4_ = f32[264,512]{1,0:T(8,128)S(1)} collective-permute-done((f32[264,512]{1,0:T(8,128)S(1)}, f32[264,512]{1,0:T(8,128)S(1)}, u32[]{:S(2)}, u32[]{:S(2)}) %collective-permute-start.11) | collective-permute-done | bytes 540704 | tf_op jit(solution)/shard_map/ppermute | solution.py:60
  60.8 0.7 collective-permute-start.32
  61.5 0.1 fold.14
  61.6 10.8 %collective-permute-done.6.refs_2_.refs_4_ = f32[264,512]{1,0:T(8,128)S(1)} collective-permute-done((f32[264,512]{1,0:T(8,128)S(1)}, f32[264,512]{1,0:T(8,128)S(1)}, u32[]{:S(2)}, u32[]{:S(2)}) %collective-permute-start.6) | collective-permute-done | bytes 540704 | tf_op jit(solution)/shard_map/ppermute | solution.py:60
  72.4 0.1 fold.12
  72.5 2.1 %collective-permute-start.7 = (f32[136,512]{1,0:T(8,128)S(1)}, f32[136,512]{1,0:T(8,128)S(1)}, u32[]{:S(2)}, u32[]{:S(2)}) collective-permute-start(f32[136,512]{1,0:T(8,128)S(1)} %get-tuple-element.73), channel_id=1, source_target_pairs={{0,32},{8,40},{16,48},{24,56},{32,0},{40,8},{48,16},{56,24},{64,96... | collective-permute-start | bytes 835592 | tf_op jit(solution)/shard_map/ppermute | solution.py:60
  74.6 0.1 fold.20
  74.7 0.8 collective-permute-start.27
  75.5 0.1 fold.18
  75.6 1.5 %collective-permute-start.22 = (f32[128,512]{1,0:T(8,128)S(1)}, f32[128,512]{1,0:T(8,128)S(1)}, u32[]{:S(2)}, u32[]{:S(2)}) collective-permute-start(f32[128,512]{1,0:T(8,128)S(1)} %get-tuple-element.100), channel_id=1, source_target_pairs={{0,96},{8,104},{16,112},{24,120},{32,64},{40,72},{48,80},{56,88},{... | collective-permute-start | bytes 786440 | tf_op jit(solution)/shard_map/ppermute | solution.py:60
  77.1 0.1 fold.16
  77.2 0.8 collective-permute-done.32.refs_1_
  78.0 1.0 %collective-permute-start.17 = (f32[128,512]{1,0:T(8,128)S(1)}, f32[128,512]{1,0:T(8,128)S(1)}, u32[]{:S(2)}, u32[]{:S(2)}) collective-permute-start(f32[128,512]{1,0:T(8,128)S(1)} %get-tuple-element.92), channel_id=1, source_target_pairs={{0,96},{8,104},{16,112},{24,120},{32,64},{40,72},{48,80},{56,88},{... | collective-permute-start | bytes 786440 | tf_op jit(solution)/shard_map/ppermute | solution.py:60
  79.1 2.8 %collective-permute-done.12.refs_1_.refs_3_ = f32[136,512]{1,0:T(8,128)S(1)} collective-permute-done((f32[136,512]{1,0:T(8,128)S(1)}, f32[136,512]{1,0:T(8,128)S(1)}, u32[]{:S(2)}, u32[]{:S(2)}) %collective-permute-start.12) | collective-permute-done | bytes 278560 | tf_op jit(solution)/shard_map/ppermute | solution.py:60
  81.9 4.5 %collective-permute-done.7.refs_1_.refs_3_ = f32[136,512]{1,0:T(8,128)S(1)} collective-permute-done((f32[136,512]{1,0:T(8,128)S(1)}, f32[136,512]{1,0:T(8,128)S(1)}, u32[]{:S(2)}, u32[]{:S(2)}) %collective-permute-start.7) | collective-permute-done | bytes 278560 | tf_op jit(solution)/shard_map/ppermute | solution.py:60
  86.5 2.4 %collective-permute-start.13 = (f32[72,512]{1,0:T(8,128)S(1)}, f32[72,512]{1,0:T(8,128)S(1)}, u32[]{:S(2)}, u32[]{:S(2)}) collective-permute-start(f32[72,512]{1,0:T(8,128)S(1)} %get-tuple-element.83), channel_id=1, source_target_pairs={{0,96},{8,104},{16,112},{24,120},{32,64},{40,72},{48,80},{56,88},{... | collective-permute-start | bytes 442376 | tf_op jit(solution)/shard_map/ppermute | solution.py:60
  89.0 0.9 collective-permute-start.8
  89.9 0.1 collective-permute-start.28
  90.0 1.0 %collective-permute-start.23 = (f32[64,512]{1,0:T(8,128)S(1)}, f32[64,512]{1,0:T(8,128)S(1)}, u32[]{:S(2)}, u32[]{:S(2)}) collective-permute-start(f32[64,512]{1,0:T(8,128)S(1)} %get-tuple-element.102), channel_id=1, source_target_pairs={{0,16},{8,24},{16,0},{24,8},{32,48},{40,56},{48,32},{56,40},{64,80... | collective-permute-start | bytes 393224 | tf_op jit(solution)/shard_map/ppermute | solution.py:60
  91.1 1.1 %collective-permute-start.18 = (f32[64,512]{1,0:T(8,128)S(1)}, f32[64,512]{1,0:T(8,128)S(1)}, u32[]{:S(2)}, u32[]{:S(2)}) collective-permute-start(f32[64,512]{1,0:T(8,128)S(1)} %get-tuple-element.94), channel_id=1, source_target_pairs={{0,16},{8,24},{16,0},{24,8},{32,48},{40,56},{48,32},{56,40},{64,80... | collective-permute-start | bytes 393224 | tf_op jit(solution)/shard_map/ppermute | solution.py:60
  92.3 2.7 %collective-permute-done.28.refs_9_ = f32[64,512]{1,0:T(8,128)S(1)} collective-permute-done((f32[64,512]{1,0:T(8,128)S(1)}, f32[64,512]{1,0:T(8,128)S(1)}, u32[]{:S(2)}, u32[]{:S(2)}) %collective-permute-start.28) | collective-permute-done | bytes 131104 | tf_op jit(solution)/shard_map/ppermute | solution.py:60
  94.9 0.1 collective-permute-done.23.refs_7_
  95.1 1.4 %collective-permute-done.18.refs_5_ = f32[64,512]{1,0:T(8,128)S(1)} collective-permute-done((f32[64,512]{1,0:T(8,128)S(1)}, f32[64,512]{1,0:T(8,128)S(1)}, u32[]{:S(2)}, u32[]{:S(2)}) %collective-permute-start.18) | collective-permute-done | bytes 131104 | tf_op jit(solution)/shard_map/ppermute | solution.py:60
  96.5 1.6 %finish.1 = (f32[64,1024]{1,0:T(8,128)}, f32[64,1024]{1,0:T(8,128)}) custom-call(s32[2]{0:T(128)S(1)} %pad_add_fusion.where_ref, f32[72,512]{1,0:T(8,128)S(1)} %get-tuple-element.74.refs_0_, f32[72,512]{1,0:T(8,128)S(1)} %collective-permute-done.8.refs_1_, f32[72,512]{1,0:T(8,128)S(1)} %get-tuple-element.82.refs_2_, ...), custom_call_target="tpu_custom_call" | custom-call | tf_op jit(solution)/shard_map/finish/pallas_call | solution.py:379
  (42 shorter events, 0.6 us)
Async XLA Ops:
  0.6 7.1 %collective-permute-start = (s32[2,64,128]{2,1,0:T(8,128)}, s32[2,64,128]{2,1,0:T(8,128)S(1)}, u32[]{:S(2)}, u32[]{:S(2)}) collective-permute-start(s32[2,64,128]{2,1,0:T(8,128)} %own_ref.1), channel_id=1, source_target_pairs={{0,1},{1,0},{2,3},{3,2},{4,5},{5,4},{6,7},{7,6},{8,9},{9,8},{10,11... | collective-permute-start | bytes 196616 | tf_op jit(solution)/shard_map/ppermute | solution.py:60
  4.0 3.7 %copy-start = (s32[2,64,128]{2,1,0:T(8,128)S(1)}, s32[2,64,128]{2,1,0:T(8,128)}, u32[]{:S(2)}) copy-start(s32[2,64,128]{2,1,0:T(8,128)} %own_ref.1) | copy-start | bytes 196612
  7.7 11.5 %collective-permute-start.1 = (s32[4,64,128]{2,1,0:T(8,128)S(1)}, s32[4,64,128]{2,1,0:T(8,128)S(1)}, u32[]{:S(2)}, u32[]{:S(2)}) collective-permute-start(s32[4,64,128]{2,1,0:T(8,128)S(1)} %paired.1.refs_0_), channel_id=1, source_target_pairs={{0,4},{1,5},{2,6},{3,7},{4,0},{5,1},{6,2},{7,3},{8,12},{9,13},{10,... | collective-permute-start | bytes 393224 | tf_op jit(solution)/shard_map/ppermute | solution.py:60
  10.8 8.4 %collective-permute-start.2 = (s32[4,64,128]{2,1,0:T(8,128)S(1)}, s32[4,64,128]{2,1,0:T(8,128)S(1)}, u32[]{:S(2)}, u32[]{:S(2)}) collective-permute-start(s32[4,64,128]{2,1,0:T(8,128)S(1)} %paired.1.refs_0_), channel_id=1, source_target_pairs={{0,2},{1,3},{2,0},{3,1},{4,6},{5,7},{6,4},{7,5},{8,10},{9,11},{10,... | collective-permute-start | bytes 393224 | tf_op jit(solution)/shard_map/ppermute | solution.py:60
  11.4 7.8 %collective-permute-start.3 = (s32[4,64,128]{2,1,0:T(8,128)S(1)}, s32[4,64,128]{2,1,0:T(8,128)S(1)}, u32[]{:S(2)}, u32[]{:S(2)}) collective-permute-start(s32[4,64,128]{2,1,0:T(8,128)S(1)} %paired.1.refs_0_), channel_id=1, source_target_pairs={{0,6},{1,7},{2,4},{3,5},{4,2},{5,3},{6,0},{7,1},{8,14},{9,15},{10,... | collective-permute-start | bytes 393224 | tf_op jit(solution)/shard_map/ppermute | solution.py:60
  23.4 9.0 %collective-permute-start.30 = (f32[256,512]{1,0:T(8,128)S(1)}, f32[256,512]{1,0:T(8,128)S(1)}, u32[]{:S(2)}, u32[]{:S(2)}) collective-permute-start(f32[256,512]{1,0:T(8,128)S(1)} %get-tuple-element.117), channel_id=1, source_target_pairs={{0,8},{8,0},{16,24},{24,16},{32,40},{40,32},{48,56},{56,48},{64,72... | collective-permute-start | bytes 1572872 | tf_op jit(solution)/shard_map/ppermute | solution.py:60
  24.7 8.2 %collective-permute-start.29 = (f32[256,512]{1,0:T(8,128)S(1)}, f32[256,512]{1,0:T(8,128)S(1)}, u32[]{:S(2)}, u32[]{:S(2)}) collective-permute-start(f32[256,512]{1,0:T(8,128)S(1)} %get-tuple-element.115), channel_id=1, source_target_pairs={{0,8},{8,0},{16,24},{24,16},{32,40},{40,32},{48,56},{56,48},{64,72... | collective-permute-start | bytes 1572872 | tf_op jit(solution)/shard_map/ppermute | solution.py:60
  26.6 8.0 %collective-permute-start.25 = (f32[256,512]{1,0:T(8,128)S(1)}, f32[256,512]{1,0:T(8,128)S(1)}, u32[]{:S(2)}, u32[]{:S(2)}) collective-permute-start(f32[256,512]{1,0:T(8,128)S(1)} %get-tuple-element.109), channel_id=1, source_target_pairs={{0,8},{8,0},{16,24},{24,16},{32,40},{40,32},{48,56},{56,48},{64,72... | collective-permute-start | bytes 1572872 | tf_op jit(solution)/shard_map/ppermute | solution.py:60
  27.9 8.2 %collective-permute-start.24 = (f32[256,512]{1,0:T(8,128)S(1)}, f32[256,512]{1,0:T(8,128)S(1)}, u32[]{:S(2)}, u32[]{:S(2)}) collective-permute-start(f32[256,512]{1,0:T(8,128)S(1)} %get-tuple-element.107), channel_id=1, source_target_pairs={{0,8},{8,0},{16,24},{24,16},{32,40},{40,32},{48,56},{56,48},{64,72... | collective-permute-start | bytes 1572872 | tf_op jit(solution)/shard_map/ppermute | solution.py:60
  29.8 8.0 %collective-permute-start.20 = (f32[256,512]{1,0:T(8,128)S(1)}, f32[256,512]{1,0:T(8,128)S(1)}, u32[]{:S(2)}, u32[]{:S(2)}) collective-permute-start(f32[256,512]{1,0:T(8,128)S(1)} %get-tuple-element.98), channel_id=1, source_target_pairs={{0,8},{8,0},{16,24},{24,16},{32,40},{40,32},{48,56},{56,48},{64,72... | collective-permute-start | bytes 1572872 | tf_op jit(solution)/shard_map/ppermute | solution.py:60
  32.4 6.9 %collective-permute-start.19 = (f32[256,512]{1,0:T(8,128)S(1)}, f32[256,512]{1,0:T(8,128)S(1)}, u32[]{:S(2)}, u32[]{:S(2)}) collective-permute-start(f32[256,512]{1,0:T(8,128)S(1)} %get-tuple-element.96), channel_id=1, source_target_pairs={{0,8},{8,0},{16,24},{24,16},{32,40},{40,32},{48,56},{56,48},{64,72... | collective-permute-start | bytes 1572872 | tf_op jit(solution)/shard_map/ppermute | solution.py:60
  33.0 8.4 %collective-permute-start.10 = (f32[264,512]{1,0:T(8,128)S(1)}, f32[264,512]{1,0:T(8,128)S(1)}, u32[]{:S(2)}, u32[]{:S(2)}) collective-permute-start(f32[264,512]{1,0:T(8,128)S(1)} %get-tuple-element.79), channel_id=1, source_target_pairs={{0,8},{8,0},{16,24},{24,16},{32,40},{40,32},{48,56},{56,48},{64,72... | collective-permute-start | bytes 1622024 | tf_op jit(solution)/shard_map/ppermute | solution.py:60
  34.5 6.4 %collective-permute-start.15 = (f32[256,512]{1,0:T(8,128)S(1)}, f32[256,512]{1,0:T(8,128)S(1)}, u32[]{:S(2)}, u32[]{:S(2)}) collective-permute-start(f32[256,512]{1,0:T(8,128)S(1)} %get-tuple-element.90), channel_id=1, source_target_pairs={{0,8},{8,0},{16,24},{24,16},{32,40},{40,32},{48,56},{56,48},{64,72... | collective-permute-start | bytes 1572872 | tf_op jit(solution)/shard_map/ppermute | solution.py:60
  36.1 9.4 %collective-permute-start.5 = (f32[264,512]{1,0:T(8,128)S(1)}, f32[264,512]{1,0:T(8,128)S(1)}, u32[]{:S(2)}, u32[]{:S(2)}) collective-permute-start(f32[264,512]{1,0:T(8,128)S(1)} %get-tuple-element.71), channel_id=1, source_target_pairs={{0,8},{8,0},{16,24},{24,16},{32,40},{40,32},{48,56},{56,48},{64,72... | collective-permute-start | bytes 1622024 | tf_op jit(solution)/shard_map/ppermute | solution.py:60
  37.8 8.6 %collective-permute-start.14 = (f32[256,512]{1,0:T(8,128)S(1)}, f32[256,512]{1,0:T(8,128)S(1)}, u32[]{:S(2)}, u32[]{:S(2)}) collective-permute-start(f32[256,512]{1,0:T(8,128)S(1)} %get-tuple-element.88), channel_id=1, source_target_pairs={{0,8},{8,0},{16,24},{24,16},{32,40},{40,32},{48,56},{56,48},{64,72... | collective-permute-start | bytes 1572872 | tf_op jit(solution)/shard_map/ppermute | solution.py:60
  39.3 8.5 %collective-permute-start.9 = (f32[256,512]{1,0:T(8,128)S(1)}, f32[256,512]{1,0:T(8,128)S(1)}, u32[]{:S(2)}, u32[]{:S(2)}) collective-permute-start(f32[256,512]{1,0:T(8,128)S(1)} %get-tuple-element.77), channel_id=1, source_target_pairs={{0,8},{8,0},{16,24},{24,16},{32,40},{40,32},{48,56},{56,48},{64,72... | collective-permute-start | bytes 1572872 | tf_op jit(solution)/shard_map/ppermute | solution.py:60
  41.0 7.1 %collective-permute-start.4 = (f32[256,512]{1,0:T(8,128)S(1)}, f32[256,512]{1,0:T(8,128)S(1)}, u32[]{:S(2)}, u32[]{:S(2)}) collective-permute-start(f32[256,512]{1,0:T(8,128)S(1)} %get-tuple-element.66), channel_id=1, source_target_pairs={{0,8},{8,0},{16,24},{24,16},{32,40},{40,32},{48,56},{56,48},{64,72... | collective-permute-start | bytes 1572872 | tf_op jit(solution)/shard_map/ppermute | solution.py:60
  41.4 16.9 %collective-permute-start.31 = (f32[256,512]{1,0:T(8,128)S(1)}, f32[256,512]{1,0:T(8,128)S(1)}, u32[]{:S(2)}, u32[]{:S(2)}) collective-permute-start(f32[256,512]{1,0:T(8,128)S(1)} %meet.11), channel_id=1, source_target_pairs={{0,96},{8,104},{16,112},{24,120},{32,64},{40,72},{48,80},{56,88},{... | collective-permute-start | bytes 1572872 | tf_op jit(solution)/shard_map/ppermute | solution.py:60
  45.6 15.2 %collective-permute-start.11 = (f32[264,512]{1,0:T(8,128)S(1)}, f32[264,512]{1,0:T(8,128)S(1)}, u32[]{:S(2)}, u32[]{:S(2)}) collective-permute-start(f32[264,512]{1,0:T(8,128)S(1)} %meet.7.refs_3_), channel_id=1, source_target_pairs={{0,16},{8,24},{16,0},{24,8},{32,48},{40,56},{48,32},{56,40},{64,80... | collective-permute-start | bytes 1622024 | tf_op jit(solution)/shard_map/ppermute | solution.py:60
  46.4 26.0 %collective-permute-start.6 = (f32[264,512]{1,0:T(8,128)S(1)}, f32[264,512]{1,0:T(8,128)S(1)}, u32[]{:S(2)}, u32[]{:S(2)}) collective-permute-start(f32[264,512]{1,0:T(8,128)S(1)} %meet.6.refs_3_), channel_id=1, source_target_pairs={{0,16},{8,24},{16,0},{24,8},{32,48},{40,56},{48,32},{56,40},{64,80... | collective-permute-start | bytes 1622024 | tf_op jit(solution)/shard_map/ppermute | solution.py:60
  47.9 24.6 %collective-permute-start.26 = (f32[256,512]{1,0:T(8,128)S(1)}, f32[256,512]{1,0:T(8,128)S(1)}, u32[]{:S(2)}, u32[]{:S(2)}) collective-permute-start(f32[256,512]{1,0:T(8,128)S(1)} %meet.10), channel_id=1, source_target_pairs={{0,96},{8,104},{16,112},{24,120},{32,64},{40,72},{48,80},{56,88},{... | collective-permute-start | bytes 1572872 | tf_op jit(solution)/shard_map/ppermute | solution.py:60
  48.1 26.6 %collective-permute-start.21 = (f32[256,512]{1,0:T(8,128)S(1)}, f32[256,512]{1,0:T(8,128)S(1)}, u32[]{:S(2)}, u32[]{:S(2)}) collective-permute-start(f32[256,512]{1,0:T(8,128)S(1)} %meet.9), channel_id=1, source_target_pairs={{0,32},{8,40},{16,48},{24,56},{32,0},{40,8},{48,16},{56,24},{64,96... | collective-permute-start | bytes 1572872 | tf_op jit(solution)/shard_map/ppermute | solution.py:60
  58.3 17.3 %collective-permute-start.16 = (f32[256,512]{1,0:T(8,128)S(1)}, f32[256,512]{1,0:T(8,128)S(1)}, u32[]{:S(2)}, u32[]{:S(2)}) collective-permute-start(f32[256,512]{1,0:T(8,128)S(1)} %meet.8), channel_id=1, source_target_pairs={{0,32},{8,40},{16,48},{24,56},{32,0},{40,8},{48,16},{56,24},{64,96... | collective-permute-start | bytes 1572872 | tf_op jit(solution)/shard_map/ppermute | solution.py:60
  60.8 17.2 %collective-permute-start.32 = (f32[128,512]{1,0:T(8,128)S(1)}, f32[128,512]{1,0:T(8,128)S(1)}, u32[]{:S(2)}, u32[]{:S(2)}) collective-permute-start(f32[128,512]{1,0:T(8,128)S(1)} %get-tuple-element.119), channel_id=1, source_target_pairs={{0,16},{8,24},{16,0},{24,8},{32,48},{40,56},{48,32},{56,40},{64,80... | collective-permute-start | bytes 786440 | tf_op jit(solution)/shard_map/ppermute | solution.py:60
  72.4 9.5 %collective-permute-start.12 = (f32[136,512]{1,0:T(8,128)S(1)}, f32[136,512]{1,0:T(8,128)S(1)}, u32[]{:S(2)}, u32[]{:S(2)}) collective-permute-start(f32[136,512]{1,0:T(8,128)S(1)} %get-tuple-element.81), channel_id=1, source_target_pairs={{0,32},{8,40},{16,48},{24,56},{32,0},{40,8},{48,16},{56,24},{64,96... | collective-permute-start | bytes 835592 | tf_op jit(solution)/shard_map/ppermute | solution.py:60
  72.5 14.0 %collective-permute-start.7 = (f32[136,512]{1,0:T(8,128)S(1)}, f32[136,512]{1,0:T(8,128)S(1)}, u32[]{:S(2)}, u32[]{:S(2)}) collective-permute-start(f32[136,512]{1,0:T(8,128)S(1)} %get-tuple-element.73), channel_id=1, source_target_pairs={{0,32},{8,40},{16,48},{24,56},{32,0},{40,8},{48,16},{56,24},{64,96... | collective-permute-start | bytes 835592 | tf_op jit(solution)/shard_map/ppermute | solution.py:60
  74.7 14.3 %collective-permute-start.27 = (f32[128,512]{1,0:T(8,128)S(1)}, f32[128,512]{1,0:T(8,128)S(1)}, u32[]{:S(2)}, u32[]{:S(2)}) collective-permute-start(f32[128,512]{1,0:T(8,128)S(1)} %get-tuple-element.111), channel_id=1, source_target_pairs={{0,16},{8,24},{16,0},{24,8},{32,48},{40,56},{48,32},{56,40},{64,80... | collective-permute-start | bytes 786440 | tf_op jit(solution)/shard_map/ppermute | solution.py:60
  75.6 14.3 %collective-permute-start.22 = (f32[128,512]{1,0:T(8,128)S(1)}, f32[128,512]{1,0:T(8,128)S(1)}, u32[]{:S(2)}, u32[]{:S(2)}) collective-permute-start(f32[128,512]{1,0:T(8,128)S(1)} %get-tuple-element.100), channel_id=1, source_target_pairs={{0,96},{8,104},{16,112},{24,120},{32,64},{40,72},{48,80},{56,88},{... | collective-permute-start | bytes 786440 | tf_op jit(solution)/shard_map/ppermute | solution.py:60
  78.0 12.0 %collective-permute-start.17 = (f32[128,512]{1,0:T(8,128)S(1)}, f32[128,512]{1,0:T(8,128)S(1)}, u32[]{:S(2)}, u32[]{:S(2)}) collective-permute-start(f32[128,512]{1,0:T(8,128)S(1)} %get-tuple-element.92), channel_id=1, source_target_pairs={{0,96},{8,104},{16,112},{24,120},{32,64},{40,72},{48,80},{56,88},{... | collective-permute-start | bytes 786440 | tf_op jit(solution)/shard_map/ppermute | solution.py:60
  81.9 9.2 %collective-permute-start.33 = (f32[64,512]{1,0:T(8,128)S(1)}, f32[64,512]{1,0:T(8,128)S(1)}, u32[]{:S(2)}, u32[]{:S(2)}) collective-permute-start(f32[64,512]{1,0:T(8,128)S(1)} %get-tuple-element.121), channel_id=1, source_target_pairs={{0,32},{8,40},{16,48},{24,56},{32,0},{40,8},{48,16},{56,24},{64,96... | collective-permute-start | bytes 393224 | tf_op jit(solution)/shard_map/ppermute | solution.py:60
  86.5 10.0 %collective-permute-start.13 = (f32[72,512]{1,0:T(8,128)S(1)}, f32[72,512]{1,0:T(8,128)S(1)}, u32[]{:S(2)}, u32[]{:S(2)}) collective-permute-start(f32[72,512]{1,0:T(8,128)S(1)} %get-tuple-element.83), channel_id=1, source_target_pairs={{0,96},{8,104},{16,112},{24,120},{32,64},{40,72},{48,80},{56,88},{... | collective-permute-start | bytes 442376 | tf_op jit(solution)/shard_map/ppermute | solution.py:60
  89.0 7.5 %collective-permute-start.8 = (f32[72,512]{1,0:T(8,128)S(1)}, f32[72,512]{1,0:T(8,128)S(1)}, u32[]{:S(2)}, u32[]{:S(2)}) collective-permute-start(f32[72,512]{1,0:T(8,128)S(1)} %get-tuple-element.75), channel_id=1, source_target_pairs={{0,96},{8,104},{16,112},{24,120},{32,64},{40,72},{48,80},{56,88},{... | collective-permute-start | bytes 442376 | tf_op jit(solution)/shard_map/ppermute | solution.py:60
  89.9 5.0 %collective-permute-start.28 = (f32[64,512]{1,0:T(8,128)S(1)}, f32[64,512]{1,0:T(8,128)S(1)}, u32[]{:S(2)}, u32[]{:S(2)}) collective-permute-start(f32[64,512]{1,0:T(8,128)S(1)} %get-tuple-element.113), channel_id=1, source_target_pairs={{0,32},{8,40},{16,48},{24,56},{32,0},{40,8},{48,16},{56,24},{64,96... | collective-permute-start | bytes 393224 | tf_op jit(solution)/shard_map/ppermute | solution.py:60
  90.0 5.0 %collective-permute-start.23 = (f32[64,512]{1,0:T(8,128)S(1)}, f32[64,512]{1,0:T(8,128)S(1)}, u32[]{:S(2)}, u32[]{:S(2)}) collective-permute-start(f32[64,512]{1,0:T(8,128)S(1)} %get-tuple-element.102), channel_id=1, source_target_pairs={{0,16},{8,24},{16,0},{24,8},{32,48},{40,56},{48,32},{56,40},{64,80... | collective-permute-start | bytes 393224 | tf_op jit(solution)/shard_map/ppermute | solution.py:60
  91.1 5.4 %collective-permute-start.18 = (f32[64,512]{1,0:T(8,128)S(1)}, f32[64,512]{1,0:T(8,128)S(1)}, u32[]{:S(2)}, u32[]{:S(2)}) collective-permute-start(f32[64,512]{1,0:T(8,128)S(1)} %get-tuple-element.94), channel_id=1, source_target_pairs={{0,16},{8,24},{16,0},{24,8},{32,48},{40,56},{48,32},{56,40},{64,80... | collective-permute-start | bytes 393224 | tf_op jit(solution)/shard_map/ppermute | solution.py:60

commit v4 on v3

--- a/solution.py
+++ b/solution.py
@@ -13,7 +13,7 @@
 MIB = 1024 * 1024
 MADE = (2, 6)
 CHUNKS = (4, 4)
-DOS_CHUNK = 0
+RIDE = (0, 0)
 EXTRA = 8
 
 CORE, SIDE_Y, SIDE_A, SIDE_B = 1, 2, 4, 12
@@ -21,36 +21,36 @@
 TURNED = ()
 SENDING, KEEPING, FIRST, SECOND, THIRD = "sending", "keeping", "first", "second", "third"
 PLAN = (
-    (SENDING, 1, 1),
-    (SENDING, 0, 0),
-    (SENDING, 2, 0),
-    (FIRST, 1, 1),
-    (FIRST, 0, 0),
-    (FIRST, 2, 0),
     (SENDING, 1, 0),
     (SENDING, 0, 1),
     (SENDING, 2, 1),
     (FIRST, 1, 0),
     (FIRST, 0, 1),
+    (FIRST, 2, 1),
+    (SENDING, 1, 1),
+    (SENDING, 0, 0),
+    (SENDING, 2, 0),
+    (FIRST, 1, 1),
+    (FIRST, 2, 0),
+    (FIRST, 0, 0),
     (KEEPING, 1, 0),
-    (FIRST, 2, 1),
+    (KEEPING, 2, 0),
+    (KEEPING, 2, 1),
+    (KEEPING, 0, 1),
+    (SECOND, 2, 1),
+    (SECOND, 0, 1),
+    (SECOND, 1, 0),
     (KEEPING, 0, 0),
     (KEEPING, 1, 1),
-    (KEEPING, 0, 1),
-    (KEEPING, 2, 0),
     (SECOND, 0, 0),
+    (SECOND, 2, 0),
     (SECOND, 1, 1),
-    (SECOND, 2, 0),
-    (KEEPING, 2, 1),
-    (SECOND, 0, 1),
-    (SECOND, 2, 1),
-    (SECOND, 1, 0),
-    (THIRD, 0, 0),
-    (THIRD, 1, 1),
-    (THIRD, 2, 0),
-    (THIRD, 0, 1),
     (THIRD, 2, 1),
     (THIRD, 1, 0),
+    (THIRD, 0, 1),
+    (THIRD, 0, 0),
+    (THIRD, 2, 0),
+    (THIRD, 1, 1),
 )
 FAR = (4, 2, 6)
 
@@ -115,12 +115,18 @@
             relative = (2 * source + part) ^ samp
             starts = [pl.multiple_of(place_of(relative, order) * rows, rows) for order in ORDERS]
             mine = [t[part * rows : (part + 1) * rows] for t in turned]
-            for bit in range(HALF):
+            wide = [jnp.concatenate([m, m], axis=1) for m in mine]
+            lane = lax.broadcasted_iota(jnp.int32, wide[0].shape, 1)
+            for bit in range(0, HALF, 2):
+                both = min(2, HALF - bit)
+                used = wide if both == 2 else mine
                 mask = jnp.int16(1 << bit)
-                hap_one = jnp.where((mine[0] & mask) != 0, one, zero)
-                hap_two = jnp.where((mine[1] & mask) != 0, one, zero)
+                if both == 2:
+                    mask = jnp.where(lane < 2 * words, 1 << bit, 2 << bit).astype(jnp.int16)
+                hap_one = jnp.where((used[0] & mask) != 0, one, zero)
+                hap_two = jnp.where((used[1] & mask) != 0, one, zero)
                 phase = hap_one - hap_two
-                lanes = slice(bit * 2 * words, (bit + 1) * 2 * words)
+                lanes = slice(bit * 2 * words, (bit + both) * 2 * words)
                 dosage_ref[pl.ds(starts[0], rows), lanes] = (hap_one + hap_two) - one
                 phase_ref[pl.ds(starts[1], rows), lanes] = phase
                 mixed_ref[pl.ds(starts[2], rows), lanes] = phase * phase
@@ -224,6 +230,23 @@
         compiler_params=params(44),
         name="features",
     )(total_counts, allele_one, allele_two, *after)
+
+
+def margin_rows(place, margin_refs):
+    *gene_refs, dos_ref = margin_refs
+    rows, first = [], 0
+    for blocks in CHUNKS:
+        call = 0
+        at = first + place
+        while at >= MADE[call]:
+            at -= MADE[call]
+            call += 1
+        rows.append(gene_refs[call][:, at * LANES : (at + 1) * LANES])
+        first += blocks
+    stride = CHUNKS[RIDE[1]]
+    for spot in range(place, 2 * dos_ref.shape[0], stride):
+        rows.append(dos_ref[spot // 2, spot % 2 : spot % 2 + 1, :])
+    return jnp.concatenate(rows, axis=0)
 
 
 def cross_kernel(spots, part, margins, design_ref, *refs):
@@ -245,18 +268,8 @@
         keep_ref[:kept, lanes] = product[:kept]
         send_ref[:kept, lanes] = product[kept:]
     if margins:
-        blank = jnp.zeros((EXTRA - 2, LANES), jnp.float32)
-        for place, (call, block) in enumerate(spots):
-            gene = margin_refs[call][:, block * LANES : (block + 1) * LANES]
-            rest = blank
-            if margins > calls:
-                dos_ref = margin_refs[calls]
-                picked = [
-                    dos_ref[spot // 2, spot % 2 : spot % 2 + 1, :]
-                    for spot in range(place, 2 * dos_ref.shape[0], len(spots))
-                ]
-                rest = jnp.concatenate([*picked, blank[len(picked) :]], axis=0)
-            rows = jnp.concatenate([gene, rest], axis=0)
+        for place in range(len(spots)):
+            rows = margin_rows(place, margin_refs)
             lanes = slice(place * LANES, (place + 1) * LANES)
             keep_ref[kept:, lanes] = rows
             send_ref[kept:, lanes] = rows
@@ -335,32 +348,35 @@
 
 
 def finish_kernel(sample_count, where_ref, *refs):
-    total_ref, allelic_ref = refs[-2:]
+    total_hbm, allelic_hbm, total_ref, allelic_ref, sems = refs[-5:]
     own = total_ref.shape[0]
     samp = where_ref[0]
     chunks = len(CHUNKS)
     couples = [refs[at : at + 2] for at in range(0, 6 * chunks, 2)]
     pair_of = [couples[index * chunks : (index + 1) * chunks] for index in range(3)]
-    margins = [left[own:, :] + right[own:, :] for left, right in pair_of[0]]
+    left, right = pair_of[RIDE[0]][RIDE[1]]
+    margin = left[own:, :] + right[own:, :]
+    stride = CHUNKS[RIDE[1]]
     columns = []
     for kind in range(2):
         picked = jnp.zeros((1, LANES), jnp.float32)
         for source in range(lax.axis_size("var")):
             spot = 2 * source + kind
-            row, block = 2 + spot // CHUNKS[DOS_CHUNK], spot % CHUNKS[DOS_CHUNK]
-            row_now = margins[DOS_CHUNK][row : row + 1, block * LANES : (block + 1) * LANES]
+            row, block = 2 * chunks + spot // stride, spot % stride
+            row_now = margin[row : row + 1, block * LANES : (block + 1) * LANES]
             picked = jnp.where(samp >> 1 == source, row_now, picked)
         turned = jnp.broadcast_to(picked, (LANES, LANES)).T
         columns.append(jnp.where(samp & 1 == 0, turned[:own], turned[own:]))
     dos_sum, dos_sq = columns
     dosage_var = dos_sq - dos_sum * dos_sum / sample_count
     scale = jnp.sqrt(jnp.float32(sample_count))
-    first = 0
+    first, copies = 0, []
     for chunk, blocks in enumerate(CHUNKS):
         for block in range(blocks):
             lanes = slice(block * LANES, (block + 1) * LANES)
             spot = slice((first + block) * LANES, (first + block + 1) * LANES)
-            gene_sum, gene_sq = margins[chunk][0:1, lanes], margins[chunk][1:2, lanes]
+            gene_sum = margin[2 * chunk : 2 * chunk + 1, lanes]
+            gene_sq = margin[2 * chunk + 1 : 2 * chunk + 2, lanes]
             gene_var = gene_sq - gene_sum * gene_sum / sample_count
             pair_sums = [
                 pair_of[index][chunk][0][:own, lanes] + pair_of[index][chunk][1][:own, lanes]
@@ -371,7 +387,14 @@
                 scale * covariance / jnp.sqrt((dosage_var + 1.0) * (gene_var + 1.0))
             )
             allelic_ref[:, spot] = pair_sums[1] / jnp.sqrt(pair_sums[2] + 1.0)
+        lanes = pl.ds(first * LANES, blocks * LANES)
+        for which, (ref, hbm) in enumerate(((total_ref, total_hbm), (allelic_ref, allelic_hbm))):
+            copy = pltpu.make_async_copy(ref.at[:, lanes], hbm.at[:, lanes], sems.at[which, chunk])
+            copy.start()
+            copies.append(copy)
         first += blocks
+    for copy in copies:
+        copy.wait()
 
 
 def finish(where, parts, own, width, sample_count):
@@ -380,6 +403,12 @@
         functools.partial(finish_kernel, sample_count),
         out_shape=(out, out),
         in_specs=[pl.BlockSpec(memory_space=pltpu.SMEM)] + whole(len(parts)),
+        out_specs=(pl.BlockSpec(memory_space=pl.ANY),) * 2,
+        scratch_shapes=[
+            pltpu.VMEM((own, width), jnp.float32),
+            pltpu.VMEM((own, width), jnp.float32),
+            pltpu.SemaphoreType.DMA((2, len(CHUNKS))),
+        ],
         compiler_params=params(8),
         name="finish",
     )(where, *parts)
@@ -406,9 +435,8 @@
             mine = spots[first : first + CHUNKS[chunk]]
             calls = 1 + max(call for call, _ in mine)
             margins = []
-            if index == 0 and kind == SENDING:
-                margins = [made[call][3] for call in range(calls)]
-                margins += [dos_part] if chunk == DOS_CHUNK else []
+            if cell == RIDE and kind == SENDING:
+                margins = [*(parts[3] for parts in made), dos_part]
             features_of = [made[call][index] for call in range(calls)]
             part = int(kind == SENDING)
             keep, send = cross(designs[index], features_of, mine, part, margins)
@@ -417,11 +445,11 @@
             sent[cell] = send
         elif kind == SECOND:
             terms = [kept[KEEPING, cell], came[KEEPING, cell], came[FIRST, cell]]
-            margins = [sent[cell], came[FIRST, cell]] if index == 0 else []
+            margins = [sent[cell], came[FIRST, cell]] if cell == RIDE else []
             keep, send = fold(terms, margins, cell in TURNED)
         else:
             terms = [kept[SECOND, cell], came[SECOND, cell]]
-            keep, send = fold(terms, terms if index == 0 else [], False)
+            keep, send = fold(terms, terms if cell == RIDE else [], False)
         at = (FIRST, SECOND, THIRD).index(kind) if kind in (FIRST, SECOND, THIRD) else None
         side = CORE if at is None else sides(index, chunk)[at]
         kept[kind, cell], came[kind, cell] = keep, swap(send, "samp", side)

time: 98.2 us -> 96 us (0.978)
  waiting for transfers between devices: 35.8 us -> 27.5 us
  starting transfers between devices: 29.8 us -> 35.8 us
    ppermute x34, waiting for transfers between devices: 35.8 us -> 27.5 us  [swap(): return lax.ppermute(array, axis, [(d, d ^ flip) for d in range(size)])]
    ppermute x34, starting transfers between devices: 29.8 us -> 35.8 us  [swap(): return lax.ppermute(array, axis, [(d, d ^ flip) for d in range(size)])]
  transfers between devices with their start and end apart: 34 -> 34, of which waited for: 9 -> 9; matrix products, arithmetic and copies ran while one was open for 0% -> 0% of each run, Pallas kernels for 26% -> 27%
where the time goes in v4:
time: 96 us; the launch traced here: 95.6 us
  starting transfers between devices  35.8 us (37%)
  Pallas kernels  31.1 us (32%)
  waiting for transfers between devices  27.5 us (29%)
  between operations  1.13 us (1%)
    ppermute x34, starting transfers between devices, swap(): return lax.ppermute(array, axis, [(d, d ^ flip) for d in range(size)])  35.8 us
    ppermute x34, waiting for transfers between devices, swap(): return lax.ppermute(array, axis, [(d, d ^ flip) for d in range(size)])  27.5 us
    pallas_call x12, Pallas kernels, cross(): pl.pallas_call(functools.partial(cross_kernel, spots, part, len(margins))...  15.1 us
    pallas_call x2, Pallas kernels, features(): pl.pallas_call(functools.partial(feature_kernel, first), out_shape=(featu...  10.8 us
    pallas_call x1, Pallas kernels, unpack(): pl.pallas_call(unpack_kernel, out_shape=(design,) * 3 + (jax.ShapeDtypeSt...  2.43 us
  transfers between devices with their start and end apart: 34, of which 9 were waited for; matrix products, arithmetic and copies ran while one was open for 0% of the time, Pallas kernels for 27%

profile of v4, /device:TPU:0, one launch (start us, length us, event | category | flops | bytes accessed | tf_op | source)
XLA Modules:
  0.0 95.6 jit_solution(12292928703298226192)
XLA Ops:
  0.6 3.4 %collective-permute-start = (s32[2,64,128]{2,1,0:T(8,128)}, s32[2,64,128]{2,1,0:T(8,128)S(1)}, u32[]{:S(2)}, u32[]{:S(2)}) collective-permute-start(s32[2,64,128]{2,1,0:T(8,128)} %own_ref.1), channel_id=1, source_target_pairs={{0,1},{1,0},{2,3},{3,2},{4,5},{5,4},{6,7},{7,6},{8,9},{9,8},{10,11... | collective-permute-start | bytes 196616 | tf_op jit(solution)/shard_map/ppermute | solution.py:60
  4.0 3.6 %features.2 = (bf16[2,1920,128]{2,1,0:T(8,128)(2,1)S(1)}, bf16[2,1920,128]{2,1,0:T(8,128)(2,1)S(1)}, bf16[2,1920,128]{2,1,0:T(8,128)(2,1)S(1)}, f32[2,256]{1,0:T(2,128)S(1)}) custom-call(s32[1920,1024]{1,0:T(8,128)} %total_hbm.3, s32[1920,1024]{1,0:T(8,128)} %one_hbm.3, s32[1920,1024]{1,0:T(8,128)} %two_hbm.3), custom_call_target="tpu_custom_call" | custom-call | flops 3072000000 | bytes 8847360 | tf_op jit(solution)/shard_map/features/pallas_call | solution.py:217
  7.6 0.1 pad_add_fusion.where_ref
  7.7 3.1 %collective-permute-start.1 = (s32[4,64,128]{2,1,0:T(8,128)S(1)}, s32[4,64,128]{2,1,0:T(8,128)S(1)}, u32[]{:S(2)}, u32[]{:S(2)}) collective-permute-start(s32[4,64,128]{2,1,0:T(8,128)S(1)} %paired.1.refs_0_), channel_id=1, source_target_pairs={{0,4},{1,5},{2,6},{3,7},{4,0},{5,1},{6,2},{7,3},{8,12},{9,13},{10,... | collective-permute-start | bytes 393224 | tf_op jit(solution)/shard_map/ppermute | solution.py:60
  10.8 0.6 collective-permute-start.2
  11.4 0.6 collective-permute-start.3
  12.0 7.2 %features.3 = (bf16[6,1920,128]{2,1,0:T(8,128)(2,1)S(1)}, bf16[6,1920,128]{2,1,0:T(8,128)(2,1)S(1)}, bf16[6,1920,128]{2,1,0:T(8,128)(2,1)S(1)}, f32[2,768]{1,0:T(2,128)S(1)}) custom-call(s32[1920,1024]{1,0:T(8,128)} %total_hbm.3, s32[1920,1024]{1,0:T(8,128)} %one_hbm.3, s32[1920,1024]{1,0:T(8,128)} %two_hbm.3, ...), custom_call_target="tpu_custom_call" | custom-call | flops 9216000000 | bytes 26542080 | tf_op jit(solution)/shard_map/features/pallas_call | solution.py:217
  19.2 2.4 %unpack.1 = (bf16[1024,1920]{1,0:T(8,128)(2,1)S(1)}, bf16[1024,1920]{1,0:T(8,128)(2,1)S(1)}, bf16[1024,1920]{1,0:T(8,128)(2,1)S(1)}, f32[8,2,128]{2,1,0:T(2,128)S(1)}) custom-call(s32[2]{0:T(128)S(1)} %pad_add_fusion.where_ref, s32[4,64,128]{2,1,0:T(8,128)S(1)} %paired.1.refs_0_, s32[4,64,128]{2,1,0:T(8,128)S(1)} %collective-permute-done.1.refs_1_, ...), custom_call_target="tpu_custom_call" | custom-call | flops 6000000000 | bytes 11796480 | tf_op jit(solution)/shard_map/unpack/pallas_call | solution.py:140
  21.7 1.3 %cross.23 = (f32[256,512]{1,0:T(8,128)S(1)}, f32[256,512]{1,0:T(8,128)S(1)}) custom-call(bf16[1024,1920]{1,0:T(8,128)(2,1)S(1)} %get-tuple-element.103.design_ref, bf16[2,1920,128]{2,1,0:T(8,128)(2,1)S(1)} %get-tuple-element.104.refs_0_, bf16[6,1920,128]{2,1,0:T(8,128)(2,1)S(1)} %get-tuple-element.105.refs_1_), custom_call_target="tpu_custom_call" | custom-call | flops 1006632960 | bytes 5898240 | tf_op jit(solution)/shard_map/cross/pallas_call | solution.py:283
  22.9 0.1 collective-permute-start.30
  23.0 1.3 %cross.22 = (f32[256,512]{1,0:T(8,128)S(1)}, f32[256,512]{1,0:T(8,128)S(1)}) custom-call(bf16[1024,1920]{1,0:T(8,128)(2,1)S(1)} %get-tuple-element.103.design_ref, bf16[2,1920,128]{2,1,0:T(8,128)(2,1)S(1)} %get-tuple-element.104.refs_0_, bf16[6,1920,128]{2,1,0:T(8,128)(2,1)S(1)} %get-tuple-element.105.refs_1_), custom_call_target="tpu_custom_call" | custom-call | flops 1006632960 | bytes 5898240 | tf_op jit(solution)/shard_map/cross/pallas_call | solution.py:283
  24.3 0.6 collective-permute-start.29
  24.9 1.3 %cross.21 = (f32[256,512]{1,0:T(8,128)S(1)}, f32[256,512]{1,0:T(8,128)S(1)}) custom-call(bf16[1024,1920]{1,0:T(8,128)(2,1)S(1)} %get-tuple-element.103.design_ref, bf16[2,1920,128]{2,1,0:T(8,128)(2,1)S(1)} %get-tuple-element.104.refs_0_, bf16[6,1920,128]{2,1,0:T(8,128)(2,1)S(1)} %get-tuple-element.105.refs_1_), custom_call_target="tpu_custom_call" | custom-call | flops 1006632960 | bytes 5898240 | tf_op jit(solution)/shard_map/cross/pallas_call | solution.py:283
  26.1 0.1 collective-permute-start.25
  26.2 1.3 %cross.20 = (f32[256,512]{1,0:T(8,128)S(1)}, f32[256,512]{1,0:T(8,128)S(1)}) custom-call(bf16[1024,1920]{1,0:T(8,128)(2,1)S(1)} %get-tuple-element.103.design_ref, bf16[2,1920,128]{2,1,0:T(8,128)(2,1)S(1)} %get-tuple-element.104.refs_0_, bf16[6,1920,128]{2,1,0:T(8,128)(2,1)S(1)} %get-tuple-element.105.refs_1_), custom_call_target="tpu_custom_call" | custom-call | flops 1006632960 | bytes 5898240 | tf_op jit(solution)/shard_map/cross/pallas_call | solution.py:283
  27.5 0.6 collective-permute-start.24
  28.1 1.3 %cross.19 = (f32[256,512]{1,0:T(8,128)S(1)}, f32[256,512]{1,0:T(8,128)S(1)}) custom-call(bf16[1024,1920]{1,0:T(8,128)(2,1)S(1)} %get-tuple-element.84.design_ref, bf16[2,1920,128]{2,1,0:T(8,128)(2,1)S(1)} %get-tuple-element.85.refs_0_, bf16[6,1920,128]{2,1,0:T(8,128)(2,1)S(1)} %get-tuple-element.86.refs_1_), custom_call_target="tpu_custom_call" | custom-call | flops 1006632960 | bytes 5898240 | tf_op jit(solution)/shard_map/cross/pallas_call | solution.py:283
  29.3 0.1 collective-permute-start.20
  29.4 1.3 %cross.18 = (f32[256,512]{1,0:T(8,128)S(1)}, f32[256,512]{1,0:T(8,128)S(1)}) custom-call(bf16[1024,1920]{1,0:T(8,128)(2,1)S(1)} %get-tuple-element.84.design_ref, bf16[2,1920,128]{2,1,0:T(8,128)(2,1)S(1)} %get-tuple-element.85.refs_0_, bf16[6,1920,128]{2,1,0:T(8,128)(2,1)S(1)} %get-tuple-element.86.refs_1_), custom_call_target="tpu_custom_call" | custom-call | flops 1006632960 | bytes 5898240 | tf_op jit(solution)/shard_map/cross/pallas_call | solution.py:283
  30.7 1.3 %cross.13 = (f32[264,512]{1,0:T(8,128)S(1)}, f32[264,512]{1,0:T(8,128)S(1)}) custom-call(bf16[1024,1920]{1,0:T(8,128)(2,1)S(1)} %get-tuple-element.62.design_ref, bf16[2,1920,128]{2,1,0:T(8,128)(2,1)S(1)} %get-tuple-element.63.refs_0_, bf16[6,1920,128]{2,1,0:T(8,128)(2,1)S(1)} %get-tuple-element.64.refs_1_, f32[2,256]{1,0:T(2,128)S(1)} %get-tuple-element.67.refs_2_, ...), custom_call_target="tpu_custom_call" | custom-call | flops 1006632960 | bytes 5898240 | tf_op jit(solution)/shard_map/cross/pallas_call | solution.py:283
  32.0 0.6 collective-permute-start.19
  32.5 0.3 collective-permute-start.5
  32.8 1.3 %cross.17 = (f32[256,512]{1,0:T(8,128)S(1)}, f32[256,512]{1,0:T(8,128)S(1)}) custom-call(bf16[1024,1920]{1,0:T(8,128)(2,1)S(1)} %get-tuple-element.84.design_ref, bf16[2,1920,128]{2,1,0:T(8,128)(2,1)S(1)} %get-tuple-element.85.refs_0_, bf16[6,1920,128]{2,1,0:T(8,128)(2,1)S(1)} %get-tuple-element.86.refs_1_), custom_call_target="tpu_custom_call" | custom-call | flops 1006632960 | bytes 5898240 | tf_op jit(solution)/shard_map/cross/pallas_call | solution.py:283
  34.1 0.3 collective-permute-start.15
  34.4 1.3 %cross.16 = (f32[256,512]{1,0:T(8,128)S(1)}, f32[256,512]{1,0:T(8,128)S(1)}) custom-call(bf16[1024,1920]{1,0:T(8,128)(2,1)S(1)} %get-tuple-element.84.design_ref, bf16[2,1920,128]{2,1,0:T(8,128)(2,1)S(1)} %get-tuple-element.85.refs_0_, bf16[6,1920,128]{2,1,0:T(8,128)(2,1)S(1)} %get-tuple-element.86.refs_1_), custom_call_target="tpu_custom_call" | custom-call | flops 1006632960 | bytes 5898240 | tf_op jit(solution)/shard_map/cross/pallas_call | solution.py:283
  35.7 0.4 collective-permute-start.14
  36.0 1.3 %cross.15 = (f32[256,512]{1,0:T(8,128)S(1)}, f32[256,512]{1,0:T(8,128)S(1)}) custom-call(bf16[1024,1920]{1,0:T(8,128)(2,1)S(1)} %get-tuple-element.62.design_ref, bf16[2,1920,128]{2,1,0:T(8,128)(2,1)S(1)} %get-tuple-element.63.refs_0_, bf16[6,1920,128]{2,1,0:T(8,128)(2,1)S(1)} %get-tuple-element.64.refs_1_), custom_call_target="tpu_custom_call" | custom-call | flops 1006632960 | bytes 5898240 | tf_op jit(solution)/shard_map/cross/pallas_call | solution.py:283
  37.3 0.3 collective-permute-start.10
  37.6 1.3 %cross.14 = (f32[256,512]{1,0:T(8,128)S(1)}, f32[256,512]{1,0:T(8,128)S(1)}) custom-call(bf16[1024,1920]{1,0:T(8,128)(2,1)S(1)} %get-tuple-element.62.design_ref, bf16[2,1920,128]{2,1,0:T(8,128)(2,1)S(1)} %get-tuple-element.63.refs_0_, bf16[6,1920,128]{2,1,0:T(8,128)(2,1)S(1)} %get-tuple-element.64.refs_1_), custom_call_target="tpu_custom_call" | custom-call | flops 1006632960 | bytes 5898240 | tf_op jit(solution)/shard_map/cross/pallas_call | solution.py:283
  38.9 0.4 collective-permute-start.9
  39.3 1.3 %cross.12 = (f32[256,512]{1,0:T(8,128)S(1)}, f32[256,512]{1,0:T(8,128)S(1)}) custom-call(bf16[1024,1920]{1,0:T(8,128)(2,1)S(1)} %get-tuple-element.62.design_ref, bf16[2,1920,128]{2,1,0:T(8,128)(2,1)S(1)} %get-tuple-element.63.refs_0_, bf16[6,1920,128]{2,1,0:T(8,128)(2,1)S(1)} %get-tuple-element.64.refs_1_), custom_call_target="tpu_custom_call" | custom-call | flops 1006632960 | bytes 5898240 | tf_op jit(solution)/shard_map/cross/pallas_call | solution.py:283
  40.5 0.3 collective-permute-start.4
  40.9 4.1 %collective-permute-start.31 = (f32[256,512]{1,0:T(8,128)S(1)}, f32[256,512]{1,0:T(8,128)S(1)}, u32[]{:S(2)}, u32[]{:S(2)}) collective-permute-start(f32[256,512]{1,0:T(8,128)S(1)} %meet.11), channel_id=1, source_target_pairs={{0,96},{8,104},{16,112},{24,120},{32,64},{40,72},{48,80},{56,88},{... | collective-permute-start | bytes 1572872 | tf_op jit(solution)/shard_map/ppermute | solution.py:60
  45.1 0.8 collective-permute-start.6
  45.9 0.1 collective-permute-start.26
  46.1 0.1 collective-permute-start.21
  46.3 2.1 %collective-permute-start.16 = (f32[256,512]{1,0:T(8,128)S(1)}, f32[256,512]{1,0:T(8,128)S(1)}, u32[]{:S(2)}, u32[]{:S(2)}) collective-permute-start(f32[256,512]{1,0:T(8,128)S(1)} %meet.8), channel_id=1, source_target_pairs={{0,32},{8,40},{16,48},{24,56},{32,0},{40,8},{48,16},{56,24},{64,96... | collective-permute-start | bytes 1572872 | tf_op jit(solution)/shard_map/ppermute | solution.py:60
  48.4 9.4 %collective-permute-done.31.refs_2_ = f32[256,512]{1,0:T(8,128)S(1)} collective-permute-done((f32[256,512]{1,0:T(8,128)S(1)}, f32[256,512]{1,0:T(8,128)S(1)}, u32[]{:S(2)}, u32[]{:S(2)}) %collective-permute-start.31) | collective-permute-done | bytes 524320 | tf_op jit(solution)/shard_map/ppermute | solution.py:60
  57.8 0.7 collective-permute-start.11
  58.5 0.1 fold.22
  58.6 0.8 collective-permute-done.6.refs_2_.refs_4_
  59.4 0.7 collective-permute-start.32
  60.0 0.1 fold.12
  60.1 8.5 %collective-permute-done.26.refs_2_ = f32[256,512]{1,0:T(8,128)S(1)} collective-permute-done((f32[256,512]{1,0:T(8,128)S(1)}, f32[256,512]{1,0:T(8,128)S(1)}, u32[]{:S(2)}, u32[]{:S(2)}) %collective-permute-start.26) | collective-permute-done | bytes 524320 | tf_op jit(solution)/shard_map/ppermute | solution.py:60
  68.6 0.1 fold.20
  68.7 0.8 collective-permute-start.27
  69.5 0.1 fold.18
  69.6 1.4 %collective-permute-done.16.refs_2_ = f32[256,512]{1,0:T(8,128)S(1)} collective-permute-done((f32[256,512]{1,0:T(8,128)S(1)}, f32[256,512]{1,0:T(8,128)S(1)}, u32[]{:S(2)}, u32[]{:S(2)}) %collective-permute-start.16) | collective-permute-done | bytes 524320 | tf_op jit(solution)/shard_map/ppermute | solution.py:60
  71.0 3.2 %collective-permute-start.22 = (f32[128,512]{1,0:T(8,128)S(1)}, f32[128,512]{1,0:T(8,128)S(1)}, u32[]{:S(2)}, u32[]{:S(2)}) collective-permute-start(f32[128,512]{1,0:T(8,128)S(1)} %get-tuple-element.100), channel_id=1, source_target_pairs={{0,96},{8,104},{16,112},{24,120},{32,64},{40,72},{48,80},{56,88},{... | collective-permute-start | bytes 786440 | tf_op jit(solution)/shard_map/ppermute | solution.py:60
  74.2 0.1 fold.16
  74.3 1.5 %collective-permute-start.17 = (f32[128,512]{1,0:T(8,128)S(1)}, f32[128,512]{1,0:T(8,128)S(1)}, u32[]{:S(2)}, u32[]{:S(2)}) collective-permute-start(f32[128,512]{1,0:T(8,128)S(1)} %get-tuple-element.92), channel_id=1, source_target_pairs={{0,96},{8,104},{16,112},{24,120},{32,64},{40,72},{48,80},{56,88},{... | collective-permute-start | bytes 786440 | tf_op jit(solution)/shard_map/ppermute | solution.py:60
  75.8 0.1 fold.14
  75.9 2.3 %collective-permute-done.32.refs_1_ = f32[128,512]{1,0:T(8,128)S(1)} collective-permute-done((f32[128,512]{1,0:T(8,128)S(1)}, f32[128,512]{1,0:T(8,128)S(1)}, u32[]{:S(2)}, u32[]{:S(2)}) %collective-permute-start.32) | collective-permute-done | bytes 262176 | tf_op jit(solution)/shard_map/ppermute | solution.py:60
  78.3 2.1 %collective-permute-start.33 = (f32[64,512]{1,0:T(8,128)S(1)}, f32[64,512]{1,0:T(8,128)S(1)}, u32[]{:S(2)}, u32[]{:S(2)}) collective-permute-start(f32[64,512]{1,0:T(8,128)S(1)} %get-tuple-element.121), channel_id=1, source_target_pairs={{0,32},{8,40},{16,48},{24,56},{32,0},{40,8},{48,16},{56,24},{64,96... | collective-permute-start | bytes 393224 | tf_op jit(solution)/shard_map/ppermute | solution.py:60
  80.4 1.8 %collective-permute-done.27.refs_1_ = f32[128,512]{1,0:T(8,128)S(1)} collective-permute-done((f32[128,512]{1,0:T(8,128)S(1)}, f32[128,512]{1,0:T(8,128)S(1)}, u32[]{:S(2)}, u32[]{:S(2)}) %collective-permute-start.27) | collective-permute-done | bytes 262176 | tf_op jit(solution)/shard_map/ppermute | solution.py:60
  82.2 2.7 %collective-permute-start.8 = (f32[72,512]{1,0:T(8,128)S(1)}, f32[72,512]{1,0:T(8,128)S(1)}, u32[]{:S(2)}, u32[]{:S(2)}) collective-permute-start(f32[72,512]{1,0:T(8,128)S(1)} %get-tuple-element.75), channel_id=1, source_target_pairs={{0,96},{8,104},{16,112},{24,120},{32,64},{40,72},{48,80},{56,88},{... | collective-permute-start | bytes 442376 | tf_op jit(solution)/shard_map/ppermute | solution.py:60
  84.9 0.1 collective-permute-start.28
  85.0 0.3 collective-permute-done.17.refs_1_
  85.3 2.0 %collective-permute-start.23 = (f32[64,512]{1,0:T(8,128)S(1)}, f32[64,512]{1,0:T(8,128)S(1)}, u32[]{:S(2)}, u32[]{:S(2)}) collective-permute-start(f32[64,512]{1,0:T(8,128)S(1)} %get-tuple-element.102), channel_id=1, source_target_pairs={{0,16},{8,24},{16,0},{24,8},{32,48},{40,56},{48,32},{56,40},{64,80... | collective-permute-start | bytes 393224 | tf_op jit(solution)/shard_map/ppermute | solution.py:60
  87.4 0.1 collective-permute-start.18
  87.5 3.3 %collective-permute-start.13 = (f32[64,512]{1,0:T(8,128)S(1)}, f32[64,512]{1,0:T(8,128)S(1)}, u32[]{:S(2)}, u32[]{:S(2)}) collective-permute-start(f32[64,512]{1,0:T(8,128)S(1)} %get-tuple-element.83), channel_id=1, source_target_pairs={{0,96},{8,104},{16,112},{24,120},{32,64},{40,72},{48,80},{56,88},{... | collective-permute-start | bytes 393224 | tf_op jit(solution)/shard_map/ppermute | solution.py:60
  90.8 1.6 %collective-permute-done.18.refs_5_ = f32[64,512]{1,0:T(8,128)S(1)} collective-permute-done((f32[64,512]{1,0:T(8,128)S(1)}, f32[64,512]{1,0:T(8,128)S(1)}, u32[]{:S(2)}, u32[]{:S(2)}) %collective-permute-start.18) | collective-permute-done | bytes 131104 | tf_op jit(solution)/shard_map/ppermute | solution.py:60
  92.4 1.4 %collective-permute-done.13.refs_3_ = f32[64,512]{1,0:T(8,128)S(1)} collective-permute-done((f32[64,512]{1,0:T(8,128)S(1)}, f32[64,512]{1,0:T(8,128)S(1)}, u32[]{:S(2)}, u32[]{:S(2)}) %collective-permute-start.13) | collective-permute-done | bytes 131104 | tf_op jit(solution)/shard_map/ppermute | solution.py:60
  93.8 1.6 %finish.1 = (f32[64,1024]{1,0:T(8,128)}, f32[64,1024]{1,0:T(8,128)}) custom-call(s32[2]{0:T(128)S(1)} %pad_add_fusion.where_ref, f32[72,512]{1,0:T(8,128)S(1)} %get-tuple-element.74.refs_0_, f32[72,512]{1,0:T(8,128)S(1)} %collective-permute-done.8.refs_1_, f32[64,512]{1,0:T(8,128)S(1)} %get-tuple-element.82.refs_2_, ...), custom_call_target="tpu_custom_call" | custom-call | tf_op jit(solution)/shard_map/finish/pallas_call | solution.py:402
  (42 shorter events, 0.6 us)
Async XLA Ops:
  0.6 7.1 %collective-permute-start = (s32[2,64,128]{2,1,0:T(8,128)}, s32[2,64,128]{2,1,0:T(8,128)S(1)}, u32[]{:S(2)}, u32[]{:S(2)}) collective-permute-start(s32[2,64,128]{2,1,0:T(8,128)} %own_ref.1), channel_id=1, source_target_pairs={{0,1},{1,0},{2,3},{3,2},{4,5},{5,4},{6,7},{7,6},{8,9},{9,8},{10,11... | collective-permute-start | bytes 196616 | tf_op jit(solution)/shard_map/ppermute | solution.py:60
  4.0 3.7 %copy-start = (s32[2,64,128]{2,1,0:T(8,128)S(1)}, s32[2,64,128]{2,1,0:T(8,128)}, u32[]{:S(2)}) copy-start(s32[2,64,128]{2,1,0:T(8,128)} %own_ref.1) | copy-start | bytes 196612
  7.7 11.5 %collective-permute-start.1 = (s32[4,64,128]{2,1,0:T(8,128)S(1)}, s32[4,64,128]{2,1,0:T(8,128)S(1)}, u32[]{:S(2)}, u32[]{:S(2)}) collective-permute-start(s32[4,64,128]{2,1,0:T(8,128)S(1)} %paired.1.refs_0_), channel_id=1, source_target_pairs={{0,4},{1,5},{2,6},{3,7},{4,0},{5,1},{6,2},{7,3},{8,12},{9,13},{10,... | collective-permute-start | bytes 393224 | tf_op jit(solution)/shard_map/ppermute | solution.py:60
  10.8 8.4 %collective-permute-start.2 = (s32[4,64,128]{2,1,0:T(8,128)S(1)}, s32[4,64,128]{2,1,0:T(8,128)S(1)}, u32[]{:S(2)}, u32[]{:S(2)}) collective-permute-start(s32[4,64,128]{2,1,0:T(8,128)S(1)} %paired.1.refs_0_), channel_id=1, source_target_pairs={{0,2},{1,3},{2,0},{3,1},{4,6},{5,7},{6,4},{7,5},{8,10},{9,11},{10,... | collective-permute-start | bytes 393224 | tf_op jit(solution)/shard_map/ppermute | solution.py:60
  11.4 7.8 %collective-permute-start.3 = (s32[4,64,128]{2,1,0:T(8,128)S(1)}, s32[4,64,128]{2,1,0:T(8,128)S(1)}, u32[]{:S(2)}, u32[]{:S(2)}) collective-permute-start(s32[4,64,128]{2,1,0:T(8,128)S(1)} %paired.1.refs_0_), channel_id=1, source_target_pairs={{0,6},{1,7},{2,4},{3,5},{4,2},{5,3},{6,0},{7,1},{8,14},{9,15},{10,... | collective-permute-start | bytes 393224 | tf_op jit(solution)/shard_map/ppermute | solution.py:60
  22.9 9.0 %collective-permute-start.30 = (f32[256,512]{1,0:T(8,128)S(1)}, f32[256,512]{1,0:T(8,128)S(1)}, u32[]{:S(2)}, u32[]{:S(2)}) collective-permute-start(f32[256,512]{1,0:T(8,128)S(1)} %get-tuple-element.117), channel_id=1, source_target_pairs={{0,8},{8,0},{16,24},{24,16},{32,40},{40,32},{48,56},{56,48},{64,72... | collective-permute-start | bytes 1572872 | tf_op jit(solution)/shard_map/ppermute | solution.py:60
  24.3 8.2 %collective-permute-start.29 = (f32[256,512]{1,0:T(8,128)S(1)}, f32[256,512]{1,0:T(8,128)S(1)}, u32[]{:S(2)}, u32[]{:S(2)}) collective-permute-start(f32[256,512]{1,0:T(8,128)S(1)} %get-tuple-element.115), channel_id=1, source_target_pairs={{0,8},{8,0},{16,24},{24,16},{32,40},{40,32},{48,56},{56,48},{64,72... | collective-permute-start | bytes 1572872 | tf_op jit(solution)/shard_map/ppermute | solution.py:60
  26.1 8.0 %collective-permute-start.25 = (f32[256,512]{1,0:T(8,128)S(1)}, f32[256,512]{1,0:T(8,128)S(1)}, u32[]{:S(2)}, u32[]{:S(2)}) collective-permute-start(f32[256,512]{1,0:T(8,128)S(1)} %get-tuple-element.109), channel_id=1, source_target_pairs={{0,8},{8,0},{16,24},{24,16},{32,40},{40,32},{48,56},{56,48},{64,72... | collective-permute-start | bytes 1572872 | tf_op jit(solution)/shard_map/ppermute | solution.py:60
  27.5 8.2 %collective-permute-start.24 = (f32[256,512]{1,0:T(8,128)S(1)}, f32[256,512]{1,0:T(8,128)S(1)}, u32[]{:S(2)}, u32[]{:S(2)}) collective-permute-start(f32[256,512]{1,0:T(8,128)S(1)} %get-tuple-element.107), channel_id=1, source_target_pairs={{0,8},{8,0},{16,24},{24,16},{32,40},{40,32},{48,56},{56,48},{64,72... | collective-permute-start | bytes 1572872 | tf_op jit(solution)/shard_map/ppermute | solution.py:60
  29.3 8.0 %collective-permute-start.20 = (f32[256,512]{1,0:T(8,128)S(1)}, f32[256,512]{1,0:T(8,128)S(1)}, u32[]{:S(2)}, u32[]{:S(2)}) collective-permute-start(f32[256,512]{1,0:T(8,128)S(1)} %get-tuple-element.98), channel_id=1, source_target_pairs={{0,8},{8,0},{16,24},{24,16},{32,40},{40,32},{48,56},{56,48},{64,72... | collective-permute-start | bytes 1572872 | tf_op jit(solution)/shard_map/ppermute | solution.py:60
  32.0 6.9 %collective-permute-start.19 = (f32[256,512]{1,0:T(8,128)S(1)}, f32[256,512]{1,0:T(8,128)S(1)}, u32[]{:S(2)}, u32[]{:S(2)}) collective-permute-start(f32[256,512]{1,0:T(8,128)S(1)} %get-tuple-element.96), channel_id=1, source_target_pairs={{0,8},{8,0},{16,24},{24,16},{32,40},{40,32},{48,56},{56,48},{64,72... | collective-permute-start | bytes 1572872 | tf_op jit(solution)/shard_map/ppermute | solution.py:60
  32.5 8.4 %collective-permute-start.5 = (f32[264,512]{1,0:T(8,128)S(1)}, f32[264,512]{1,0:T(8,128)S(1)}, u32[]{:S(2)}, u32[]{:S(2)}) collective-permute-start(f32[264,512]{1,0:T(8,128)S(1)} %get-tuple-element.71), channel_id=1, source_target_pairs={{0,8},{8,0},{16,24},{24,16},{32,40},{40,32},{48,56},{56,48},{64,72... | collective-permute-start | bytes 1622024 | tf_op jit(solution)/shard_map/ppermute | solution.py:60
  34.1 6.4 %collective-permute-start.15 = (f32[256,512]{1,0:T(8,128)S(1)}, f32[256,512]{1,0:T(8,128)S(1)}, u32[]{:S(2)}, u32[]{:S(2)}) collective-permute-start(f32[256,512]{1,0:T(8,128)S(1)} %get-tuple-element.90), channel_id=1, source_target_pairs={{0,8},{8,0},{16,24},{24,16},{32,40},{40,32},{48,56},{56,48},{64,72... | collective-permute-start | bytes 1572872 | tf_op jit(solution)/shard_map/ppermute | solution.py:60
  35.7 9.4 %collective-permute-start.14 = (f32[256,512]{1,0:T(8,128)S(1)}, f32[256,512]{1,0:T(8,128)S(1)}, u32[]{:S(2)}, u32[]{:S(2)}) collective-permute-start(f32[256,512]{1,0:T(8,128)S(1)} %get-tuple-element.88), channel_id=1, source_target_pairs={{0,8},{8,0},{16,24},{24,16},{32,40},{40,32},{48,56},{56,48},{64,72... | collective-permute-start | bytes 1572872 | tf_op jit(solution)/shard_map/ppermute | solution.py:60
  37.3 8.6 %collective-permute-start.10 = (f32[256,512]{1,0:T(8,128)S(1)}, f32[256,512]{1,0:T(8,128)S(1)}, u32[]{:S(2)}, u32[]{:S(2)}) collective-permute-start(f32[256,512]{1,0:T(8,128)S(1)} %get-tuple-element.79), channel_id=1, source_target_pairs={{0,8},{8,0},{16,24},{24,16},{32,40},{40,32},{48,56},{56,48},{64,72... | collective-permute-start | bytes 1572872 | tf_op jit(solution)/shard_map/ppermute | solution.py:60
  38.9 7.2 %collective-permute-start.9 = (f32[256,512]{1,0:T(8,128)S(1)}, f32[256,512]{1,0:T(8,128)S(1)}, u32[]{:S(2)}, u32[]{:S(2)}) collective-permute-start(f32[256,512]{1,0:T(8,128)S(1)} %get-tuple-element.77), channel_id=1, source_target_pairs={{0,8},{8,0},{16,24},{24,16},{32,40},{40,32},{48,56},{56,48},{64,72... | collective-permute-start | bytes 1572872 | tf_op jit(solution)/shard_map/ppermute | solution.py:60
  40.5 5.7 %collective-permute-start.4 = (f32[256,512]{1,0:T(8,128)S(1)}, f32[256,512]{1,0:T(8,128)S(1)}, u32[]{:S(2)}, u32[]{:S(2)}) collective-permute-start(f32[256,512]{1,0:T(8,128)S(1)} %get-tuple-element.66), channel_id=1, source_target_pairs={{0,8},{8,0},{16,24},{24,16},{32,40},{40,32},{48,56},{56,48},{64,72... | collective-permute-start | bytes 1572872 | tf_op jit(solution)/shard_map/ppermute | solution.py:60
  40.9 16.9 %collective-permute-start.31 = (f32[256,512]{1,0:T(8,128)S(1)}, f32[256,512]{1,0:T(8,128)S(1)}, u32[]{:S(2)}, u32[]{:S(2)}) collective-permute-start(f32[256,512]{1,0:T(8,128)S(1)} %meet.11), channel_id=1, source_target_pairs={{0,96},{8,104},{16,112},{24,120},{32,64},{40,72},{48,80},{56,88},{... | collective-permute-start | bytes 1572872 | tf_op jit(solution)/shard_map/ppermute | solution.py:60
  45.1 14.3 %collective-permute-start.6 = (f32[264,512]{1,0:T(8,128)S(1)}, f32[264,512]{1,0:T(8,128)S(1)}, u32[]{:S(2)}, u32[]{:S(2)}) collective-permute-start(f32[264,512]{1,0:T(8,128)S(1)} %meet.6.refs_3_), channel_id=1, source_target_pairs={{0,16},{8,24},{16,0},{24,8},{32,48},{40,56},{48,32},{56,40},{64,80... | collective-permute-start | bytes 1622024 | tf_op jit(solution)/shard_map/ppermute | solution.py:60
  45.9 22.7 %collective-permute-start.26 = (f32[256,512]{1,0:T(8,128)S(1)}, f32[256,512]{1,0:T(8,128)S(1)}, u32[]{:S(2)}, u32[]{:S(2)}) collective-permute-start(f32[256,512]{1,0:T(8,128)S(1)} %meet.10), channel_id=1, source_target_pairs={{0,96},{8,104},{16,112},{24,120},{32,64},{40,72},{48,80},{56,88},{... | collective-permute-start | bytes 1572872 | tf_op jit(solution)/shard_map/ppermute | solution.py:60
  46.1 22.7 %collective-permute-start.21 = (f32[256,512]{1,0:T(8,128)S(1)}, f32[256,512]{1,0:T(8,128)S(1)}, u32[]{:S(2)}, u32[]{:S(2)}) collective-permute-start(f32[256,512]{1,0:T(8,128)S(1)} %meet.9), channel_id=1, source_target_pairs={{0,32},{8,40},{16,48},{24,56},{32,0},{40,8},{48,16},{56,24},{64,96... | collective-permute-start | bytes 1572872 | tf_op jit(solution)/shard_map/ppermute | solution.py:60
  46.3 24.7 %collective-permute-start.16 = (f32[256,512]{1,0:T(8,128)S(1)}, f32[256,512]{1,0:T(8,128)S(1)}, u32[]{:S(2)}, u32[]{:S(2)}) collective-permute-start(f32[256,512]{1,0:T(8,128)S(1)} %meet.8), channel_id=1, source_target_pairs={{0,32},{8,40},{16,48},{24,56},{32,0},{40,8},{48,16},{56,24},{64,96... | collective-permute-start | bytes 1572872 | tf_op jit(solution)/shard_map/ppermute | solution.py:60
  57.8 16.5 %collective-permute-start.11 = (f32[256,512]{1,0:T(8,128)S(1)}, f32[256,512]{1,0:T(8,128)S(1)}, u32[]{:S(2)}, u32[]{:S(2)}) collective-permute-start(f32[256,512]{1,0:T(8,128)S(1)} %meet.7), channel_id=1, source_target_pairs={{0,16},{8,24},{16,0},{24,8},{32,48},{40,56},{48,32},{56,40},{64,80... | collective-permute-start | bytes 1572872 | tf_op jit(solution)/shard_map/ppermute | solution.py:60
  59.4 18.9 %collective-permute-start.32 = (f32[128,512]{1,0:T(8,128)S(1)}, f32[128,512]{1,0:T(8,128)S(1)}, u32[]{:S(2)}, u32[]{:S(2)}) collective-permute-start(f32[128,512]{1,0:T(8,128)S(1)} %get-tuple-element.119), channel_id=1, source_target_pairs={{0,16},{8,24},{16,0},{24,8},{32,48},{40,56},{48,32},{56,40},{64,80... | collective-permute-start | bytes 786440 | tf_op jit(solution)/shard_map/ppermute | solution.py:60
  68.6 9.6 %collective-permute-start.7 = (f32[136,512]{1,0:T(8,128)S(1)}, f32[136,512]{1,0:T(8,128)S(1)}, u32[]{:S(2)}, u32[]{:S(2)}) collective-permute-start(f32[136,512]{1,0:T(8,128)S(1)} %get-tuple-element.73), channel_id=1, source_target_pairs={{0,32},{8,40},{16,48},{24,56},{32,0},{40,8},{48,16},{56,24},{64,96... | collective-permute-start | bytes 835592 | tf_op jit(solution)/shard_map/ppermute | solution.py:60
  68.7 13.4 %collective-permute-start.27 = (f32[128,512]{1,0:T(8,128)S(1)}, f32[128,512]{1,0:T(8,128)S(1)}, u32[]{:S(2)}, u32[]{:S(2)}) collective-permute-start(f32[128,512]{1,0:T(8,128)S(1)} %get-tuple-element.111), channel_id=1, source_target_pairs={{0,16},{8,24},{16,0},{24,8},{32,48},{40,56},{48,32},{56,40},{64,80... | collective-permute-start | bytes 786440 | tf_op jit(solution)/shard_map/ppermute | solution.py:60
  71.0 13.9 %collective-permute-start.22 = (f32[128,512]{1,0:T(8,128)S(1)}, f32[128,512]{1,0:T(8,128)S(1)}, u32[]{:S(2)}, u32[]{:S(2)}) collective-permute-start(f32[128,512]{1,0:T(8,128)S(1)} %get-tuple-element.100), channel_id=1, source_target_pairs={{0,96},{8,104},{16,112},{24,120},{32,64},{40,72},{48,80},{56,88},{... | collective-permute-start | bytes 786440 | tf_op jit(solution)/shard_map/ppermute | solution.py:60
  74.3 11.0 %collective-permute-start.17 = (f32[128,512]{1,0:T(8,128)S(1)}, f32[128,512]{1,0:T(8,128)S(1)}, u32[]{:S(2)}, u32[]{:S(2)}) collective-permute-start(f32[128,512]{1,0:T(8,128)S(1)} %get-tuple-element.92), channel_id=1, source_target_pairs={{0,96},{8,104},{16,112},{24,120},{32,64},{40,72},{48,80},{56,88},{... | collective-permute-start | bytes 786440 | tf_op jit(solution)/shard_map/ppermute | solution.py:60
  78.2 9.1 %collective-permute-start.12 = (f32[128,512]{1,0:T(8,128)S(1)}, f32[128,512]{1,0:T(8,128)S(1)}, u32[]{:S(2)}, u32[]{:S(2)}) collective-permute-start(f32[128,512]{1,0:T(8,128)S(1)} %get-tuple-element.81), channel_id=1, source_target_pairs={{0,32},{8,40},{16,48},{24,56},{32,0},{40,8},{48,16},{56,24},{64,96... | collective-permute-start | bytes 786440 | tf_op jit(solution)/shard_map/ppermute | solution.py:60
  78.3 9.3 %collective-permute-start.33 = (f32[64,512]{1,0:T(8,128)S(1)}, f32[64,512]{1,0:T(8,128)S(1)}, u32[]{:S(2)}, u32[]{:S(2)}) collective-permute-start(f32[64,512]{1,0:T(8,128)S(1)} %get-tuple-element.121), channel_id=1, source_target_pairs={{0,32},{8,40},{16,48},{24,56},{32,0},{40,8},{48,16},{56,24},{64,96... | collective-permute-start | bytes 393224 | tf_op jit(solution)/shard_map/ppermute | solution.py:60
  82.2 11.6 %collective-permute-start.8 = (f32[72,512]{1,0:T(8,128)S(1)}, f32[72,512]{1,0:T(8,128)S(1)}, u32[]{:S(2)}, u32[]{:S(2)}) collective-permute-start(f32[72,512]{1,0:T(8,128)S(1)} %get-tuple-element.75), channel_id=1, source_target_pairs={{0,96},{8,104},{16,112},{24,120},{32,64},{40,72},{48,80},{56,88},{... | collective-permute-start | bytes 442376 | tf_op jit(solution)/shard_map/ppermute | solution.py:60
  84.9 5.9 %collective-permute-start.28 = (f32[64,512]{1,0:T(8,128)S(1)}, f32[64,512]{1,0:T(8,128)S(1)}, u32[]{:S(2)}, u32[]{:S(2)}) collective-permute-start(f32[64,512]{1,0:T(8,128)S(1)} %get-tuple-element.113), channel_id=1, source_target_pairs={{0,32},{8,40},{16,48},{24,56},{32,0},{40,8},{48,16},{56,24},{64,96... | collective-permute-start | bytes 393224 | tf_op jit(solution)/shard_map/ppermute | solution.py:60
  85.3 5.5 %collective-permute-start.23 = (f32[64,512]{1,0:T(8,128)S(1)}, f32[64,512]{1,0:T(8,128)S(1)}, u32[]{:S(2)}, u32[]{:S(2)}) collective-permute-start(f32[64,512]{1,0:T(8,128)S(1)} %get-tuple-element.102), channel_id=1, source_target_pairs={{0,16},{8,24},{16,0},{24,8},{32,48},{40,56},{48,32},{56,40},{64,80... | collective-permute-start | bytes 393224 | tf_op jit(solution)/shard_map/ppermute | solution.py:60
  87.4 5.0 %collective-permute-start.18 = (f32[64,512]{1,0:T(8,128)S(1)}, f32[64,512]{1,0:T(8,128)S(1)}, u32[]{:S(2)}, u32[]{:S(2)}) collective-permute-start(f32[64,512]{1,0:T(8,128)S(1)} %get-tuple-element.94), channel_id=1, source_target_pairs={{0,16},{8,24},{16,0},{24,8},{32,48},{40,56},{48,32},{56,40},{64,80... | collective-permute-start | bytes 393224 | tf_op jit(solution)/shard_map/ppermute | solution.py:60
  87.5 6.3 %collective-permute-start.13 = (f32[64,512]{1,0:T(8,128)S(1)}, f32[64,512]{1,0:T(8,128)S(1)}, u32[]{:S(2)}, u32[]{:S(2)}) collective-permute-start(f32[64,512]{1,0:T(8,128)S(1)} %get-tuple-element.83), channel_id=1, source_target_pairs={{0,96},{8,104},{16,112},{24,120},{32,64},{40,72},{48,80},{56,88},{... | collective-permute-start | bytes 393224 | tf_op jit(solution)/shard_map/ppermute | solution.py:60

commit v5 on v4

--- a/solution.py
+++ b/solution.py
@@ -22,33 +22,33 @@
 SENDING, KEEPING, FIRST, SECOND, THIRD = "sending", "keeping", "first", "second", "third"
 PLAN = (
     (SENDING, 1, 0),
-    (SENDING, 0, 1),
+    (SENDING, 0, 0),
     (SENDING, 2, 1),
     (FIRST, 1, 0),
-    (FIRST, 0, 1),
+    (FIRST, 0, 0),
     (FIRST, 2, 1),
     (SENDING, 1, 1),
-    (SENDING, 0, 0),
+    (SENDING, 0, 1),
     (SENDING, 2, 0),
+    (KEEPING, 2, 1),
     (FIRST, 1, 1),
+    (FIRST, 0, 1),
     (FIRST, 2, 0),
-    (FIRST, 0, 0),
     (KEEPING, 1, 0),
+    (KEEPING, 0, 0),
+    (KEEPING, 0, 1),
+    (SECOND, 0, 0),
+    (SECOND, 1, 0),
     (KEEPING, 2, 0),
-    (KEEPING, 2, 1),
-    (KEEPING, 0, 1),
     (SECOND, 2, 1),
+    (KEEPING, 1, 1),
     (SECOND, 0, 1),
-    (SECOND, 1, 0),
-    (KEEPING, 0, 0),
-    (KEEPING, 1, 1),
-    (SECOND, 0, 0),
     (SECOND, 2, 0),
     (SECOND, 1, 1),
+    (THIRD, 0, 0),
     (THIRD, 2, 1),
     (THIRD, 1, 0),
     (THIRD, 0, 1),
-    (THIRD, 0, 0),
     (THIRD, 2, 0),
     (THIRD, 1, 1),
 )
@@ -84,13 +84,18 @@
 
 
 def unpack_kernel(where_ref, *refs):
-    word_refs, (dosage_ref, phase_ref, mixed_ref, margin_ref) = refs[:-4], refs[-4:]
+    word_refs = refs[:-6]
+    dosage_ref, phase_ref, mixed_ref, margin_ref, wide_ref, mask_ref = refs[-6:]
     samp, var = where_ref[0], where_ref[1]
     low = (1 << HALF) - 1
     words, block = word_refs[0].shape[1:]
     rows = block // 2
     samples = float(words * BITS)
     one, zero = jnp.bfloat16(1), jnp.bfloat16(0)
+    lane = lax.broadcasted_iota(jnp.int32, mask_ref.shape[1:], 1)
+    for step in range(mask_ref.shape[0]):
+        bits = jnp.where(lane < 2 * words, 1 << (2 * step), 2 << (2 * step))
+        mask_ref[step] = bits.astype(jnp.int16)
     pieces = [
         (flip + twin, word_ref, 2 * twin)
         for flip, word_ref in zip((0, *FAR), word_refs)
@@ -115,16 +120,14 @@
             relative = (2 * source + part) ^ samp
             starts = [pl.multiple_of(place_of(relative, order) * rows, rows) for order in ORDERS]
             mine = [t[part * rows : (part + 1) * rows] for t in turned]
-            wide = [jnp.concatenate([m, m], axis=1) for m in mine]
-            lane = lax.broadcasted_iota(jnp.int32, wide[0].shape, 1)
+            for hap, m in enumerate(mine):
+                wide_ref[hap] = jnp.concatenate([m, m], axis=1)
             for bit in range(0, HALF, 2):
                 both = min(2, HALF - bit)
-                used = wide if both == 2 else mine
-                mask = jnp.int16(1 << bit)
-                if both == 2:
-                    mask = jnp.where(lane < 2 * words, 1 << bit, 2 << bit).astype(jnp.int16)
-                hap_one = jnp.where((used[0] & mask) != 0, one, zero)
-                hap_two = jnp.where((used[1] & mask) != 0, one, zero)
+                used = slice(0, both * 2 * words)
+                mask = mask_ref[bit // 2, :, used]
+                hap_one = jnp.where((wide_ref[0, :, used] & mask) != 0, one, zero)
+                hap_two = jnp.where((wide_ref[1, :, used] & mask) != 0, one, zero)
                 phase = hap_one - hap_two
                 lanes = slice(bit * 2 * words, (bit + both) * 2 * words)
                 dosage_ref[pl.ds(starts[0], rows), lanes] = (hap_one + hap_two) - one
@@ -141,6 +144,10 @@
         unpack_kernel,
         out_shape=(design,) * 3 + (jax.ShapeDtypeStruct((count, 2, block), jnp.float32),),
         in_specs=[pl.BlockSpec(memory_space=pltpu.SMEM)] + whole(len(pairs)),
+        scratch_shapes=[
+            pltpu.VMEM((2, block // 2, 4 * words), jnp.int16),
+            pltpu.VMEM(((HALF + 1) // 2, block // 2, 4 * words), jnp.int16),
+        ],
         cost_estimate=pl.CostEstimate(
             flops=6_000_000_000, bytes_accessed=6 * variants * samples, transcendentals=0
         ),

time: 96 us -> 96 us (level)
  no operation moved by 1% of the time
where the time goes in v5:
time: 96 us; the launch traced here: 95.6 us
  starting transfers between devices  36.1 us (38%)
  Pallas kernels  30.9 us (32%)
  waiting for transfers between devices  27.3 us (28%)
  between operations  1.14 us (1%)
    ppermute x34, starting transfers between devices, swap(): return lax.ppermute(array, axis, [(d, d ^ flip) for d in range(size)])  36.1 us
    ppermute x34, waiting for transfers between devices, swap(): return lax.ppermute(array, axis, [(d, d ^ flip) for d in range(size)])  27.3 us
    pallas_call x12, Pallas kernels, cross(): pl.pallas_call(functools.partial(cross_kernel, spots, part, len(margins))...  15.1 us
    pallas_call x2, Pallas kernels, features(): pl.pallas_call(functools.partial(feature_kernel, first), out_shape=(featu...  10.8 us
    pallas_call x1, Pallas kernels, unpack(): pl.pallas_call(unpack_kernel, out_shape=(design,) * 3 + (jax.ShapeDtypeSt...  2.29 us
  transfers between devices with their start and end apart: 34, of which 9 were waited for; matrix products, arithmetic and copies ran while one was open for 0% of the time, Pallas kernels for 27%

profile of v5, /device:TPU:0, one launch (start us, length us, event | category | flops | bytes accessed | tf_op | source)
XLA Modules:
  0.0 95.6 jit_solution(11977723862437420378)
XLA Ops:
  0.6 3.4 %collective-permute-start = (s32[2,64,128]{2,1,0:T(8,128)}, s32[2,64,128]{2,1,0:T(8,128)S(1)}, u32[]{:S(2)}, u32[]{:S(2)}) collective-permute-start(s32[2,64,128]{2,1,0:T(8,128)} %own_ref.1), channel_id=1, source_target_pairs={{0,1},{1,0},{2,3},{3,2},{4,5},{5,4},{6,7},{7,6},{8,9},{9,8},{10,11... | collective-permute-start | bytes 196616 | tf_op jit(solution)/shard_map/ppermute | solution.py:60
  4.0 3.6 %features.2 = (bf16[2,1920,128]{2,1,0:T(8,128)(2,1)S(1)}, bf16[2,1920,128]{2,1,0:T(8,128)(2,1)S(1)}, bf16[2,1920,128]{2,1,0:T(8,128)(2,1)S(1)}, f32[2,256]{1,0:T(2,128)S(1)}) custom-call(s32[1920,1024]{1,0:T(8,128)} %total_hbm.3, s32[1920,1024]{1,0:T(8,128)} %one_hbm.3, s32[1920,1024]{1,0:T(8,128)} %two_hbm.3), custom_call_target="tpu_custom_call" | custom-call | flops 3072000000 | bytes 8847360 | tf_op jit(solution)/shard_map/features/pallas_call | solution.py:224
  7.6 0.1 pad_add_fusion.where_ref
  7.7 3.1 %collective-permute-start.1 = (s32[4,64,128]{2,1,0:T(8,128)S(1)}, s32[4,64,128]{2,1,0:T(8,128)S(1)}, u32[]{:S(2)}, u32[]{:S(2)}) collective-permute-start(s32[4,64,128]{2,1,0:T(8,128)S(1)} %paired.1.refs_0_), channel_id=1, source_target_pairs={{0,4},{1,5},{2,6},{3,7},{4,0},{5,1},{6,2},{7,3},{8,12},{9,13},{10,... | collective-permute-start | bytes 393224 | tf_op jit(solution)/shard_map/ppermute | solution.py:60
  10.8 0.6 collective-permute-start.2
  11.4 0.6 collective-permute-start.3
  12.0 7.2 %features.3 = (bf16[6,1920,128]{2,1,0:T(8,128)(2,1)S(1)}, bf16[6,1920,128]{2,1,0:T(8,128)(2,1)S(1)}, bf16[6,1920,128]{2,1,0:T(8,128)(2,1)S(1)}, f32[2,768]{1,0:T(2,128)S(1)}) custom-call(s32[1920,1024]{1,0:T(8,128)} %total_hbm.3, s32[1920,1024]{1,0:T(8,128)} %one_hbm.3, s32[1920,1024]{1,0:T(8,128)} %two_hbm.3, ...), custom_call_target="tpu_custom_call" | custom-call | flops 9216000000 | bytes 26542080 | tf_op jit(solution)/shard_map/features/pallas_call | solution.py:224
  19.2 2.3 %unpack.1 = (bf16[1024,1920]{1,0:T(8,128)(2,1)S(1)}, bf16[1024,1920]{1,0:T(8,128)(2,1)S(1)}, bf16[1024,1920]{1,0:T(8,128)(2,1)S(1)}, f32[8,2,128]{2,1,0:T(2,128)S(1)}) custom-call(s32[2]{0:T(128)S(1)} %pad_add_fusion.where_ref, s32[4,64,128]{2,1,0:T(8,128)S(1)} %paired.1.refs_0_, s32[4,64,128]{2,1,0:T(8,128)S(1)} %collective-permute-done.1.refs_1_, ...), custom_call_target="tpu_custom_call" | custom-call | flops 6000000000 | bytes 11796480 | tf_op jit(solution)/shard_map/unpack/pallas_call | solution.py:143
  21.5 1.3 %cross.23 = (f32[256,512]{1,0:T(8,128)S(1)}, f32[256,512]{1,0:T(8,128)S(1)}) custom-call(bf16[1024,1920]{1,0:T(8,128)(2,1)S(1)} %get-tuple-element.103.design_ref, bf16[2,1920,128]{2,1,0:T(8,128)(2,1)S(1)} %get-tuple-element.104.refs_0_, bf16[6,1920,128]{2,1,0:T(8,128)(2,1)S(1)} %get-tuple-element.105.refs_1_), custom_call_target="tpu_custom_call" | custom-call | flops 1006632960 | bytes 5898240 | tf_op jit(solution)/shard_map/cross/pallas_call | solution.py:290
  22.8 0.1 collective-permute-start.30
  22.9 1.3 %cross.22 = (f32[256,512]{1,0:T(8,128)S(1)}, f32[256,512]{1,0:T(8,128)S(1)}) custom-call(bf16[1024,1920]{1,0:T(8,128)(2,1)S(1)} %get-tuple-element.103.design_ref, bf16[2,1920,128]{2,1,0:T(8,128)(2,1)S(1)} %get-tuple-element.104.refs_0_, bf16[6,1920,128]{2,1,0:T(8,128)(2,1)S(1)} %get-tuple-element.105.refs_1_), custom_call_target="tpu_custom_call" | custom-call | flops 1006632960 | bytes 5898240 | tf_op jit(solution)/shard_map/cross/pallas_call | solution.py:290
  24.2 0.6 collective-permute-start.29
  24.7 1.3 %cross.21 = (f32[256,512]{1,0:T(8,128)S(1)}, f32[256,512]{1,0:T(8,128)S(1)}) custom-call(bf16[1024,1920]{1,0:T(8,128)(2,1)S(1)} %get-tuple-element.103.design_ref, bf16[2,1920,128]{2,1,0:T(8,128)(2,1)S(1)} %get-tuple-element.104.refs_0_, bf16[6,1920,128]{2,1,0:T(8,128)(2,1)S(1)} %get-tuple-element.105.refs_1_), custom_call_target="tpu_custom_call" | custom-call | flops 1006632960 | bytes 5898240 | tf_op jit(solution)/shard_map/cross/pallas_call | solution.py:290
  26.0 0.1 collective-permute-start.25
  26.1 1.3 %cross.20 = (f32[256,512]{1,0:T(8,128)S(1)}, f32[256,512]{1,0:T(8,128)S(1)}) custom-call(bf16[1024,1920]{1,0:T(8,128)(2,1)S(1)} %get-tuple-element.103.design_ref, bf16[2,1920,128]{2,1,0:T(8,128)(2,1)S(1)} %get-tuple-element.104.refs_0_, bf16[6,1920,128]{2,1,0:T(8,128)(2,1)S(1)} %get-tuple-element.105.refs_1_), custom_call_target="tpu_custom_call" | custom-call | flops 1006632960 | bytes 5898240 | tf_op jit(solution)/shard_map/cross/pallas_call | solution.py:290
  27.3 0.6 collective-permute-start.24
  27.9 1.3 %cross.19 = (f32[256,512]{1,0:T(8,128)S(1)}, f32[256,512]{1,0:T(8,128)S(1)}) custom-call(bf16[1024,1920]{1,0:T(8,128)(2,1)S(1)} %get-tuple-element.84.design_ref, bf16[2,1920,128]{2,1,0:T(8,128)(2,1)S(1)} %get-tuple-element.85.refs_0_, bf16[6,1920,128]{2,1,0:T(8,128)(2,1)S(1)} %get-tuple-element.86.refs_1_), custom_call_target="tpu_custom_call" | custom-call | flops 1006632960 | bytes 5898240 | tf_op jit(solution)/shard_map/cross/pallas_call | solution.py:290
  29.2 0.1 collective-permute-start.20
  29.3 1.3 %cross.18 = (f32[256,512]{1,0:T(8,128)S(1)}, f32[256,512]{1,0:T(8,128)S(1)}) custom-call(bf16[1024,1920]{1,0:T(8,128)(2,1)S(1)} %get-tuple-element.84.design_ref, bf16[2,1920,128]{2,1,0:T(8,128)(2,1)S(1)} %get-tuple-element.85.refs_0_, bf16[6,1920,128]{2,1,0:T(8,128)(2,1)S(1)} %get-tuple-element.86.refs_1_), custom_call_target="tpu_custom_call" | custom-call | flops 1006632960 | bytes 5898240 | tf_op jit(solution)/shard_map/cross/pallas_call | solution.py:290
  30.5 1.3 %cross.13 = (f32[264,512]{1,0:T(8,128)S(1)}, f32[264,512]{1,0:T(8,128)S(1)}) custom-call(bf16[1024,1920]{1,0:T(8,128)(2,1)S(1)} %get-tuple-element.62.design_ref, bf16[2,1920,128]{2,1,0:T(8,128)(2,1)S(1)} %get-tuple-element.63.refs_0_, bf16[6,1920,128]{2,1,0:T(8,128)(2,1)S(1)} %get-tuple-element.64.refs_1_, f32[2,256]{1,0:T(2,128)S(1)} %get-tuple-element.67.refs_2_, ...), custom_call_target="tpu_custom_call" | custom-call | flops 1006632960 | bytes 5898240 | tf_op jit(solution)/shard_map/cross/pallas_call | solution.py:290
  31.8 0.6 collective-permute-start.19
  32.4 0.1 collective-permute-start.5
  32.5 1.3 %cross.17 = (f32[256,512]{1,0:T(8,128)S(1)}, f32[256,512]{1,0:T(8,128)S(1)}) custom-call(bf16[1024,1920]{1,0:T(8,128)(2,1)S(1)} %get-tuple-element.84.design_ref, bf16[2,1920,128]{2,1,0:T(8,128)(2,1)S(1)} %get-tuple-element.85.refs_0_, bf16[6,1920,128]{2,1,0:T(8,128)(2,1)S(1)} %get-tuple-element.86.refs_1_), custom_call_target="tpu_custom_call" | custom-call | flops 1006632960 | bytes 5898240 | tf_op jit(solution)/shard_map/cross/pallas_call | solution.py:290
  33.8 0.7 collective-permute-start.15
  34.4 1.3 %cross.16 = (f32[256,512]{1,0:T(8,128)S(1)}, f32[256,512]{1,0:T(8,128)S(1)}) custom-call(bf16[1024,1920]{1,0:T(8,128)(2,1)S(1)} %get-tuple-element.84.design_ref, bf16[2,1920,128]{2,1,0:T(8,128)(2,1)S(1)} %get-tuple-element.85.refs_0_, bf16[6,1920,128]{2,1,0:T(8,128)(2,1)S(1)} %get-tuple-element.86.refs_1_), custom_call_target="tpu_custom_call" | custom-call | flops 1006632960 | bytes 5898240 | tf_op jit(solution)/shard_map/cross/pallas_call | solution.py:290
  35.7 0.2 collective-permute-start.14
  35.9 1.3 %cross.15 = (f32[256,512]{1,0:T(8,128)S(1)}, f32[256,512]{1,0:T(8,128)S(1)}) custom-call(bf16[1024,1920]{1,0:T(8,128)(2,1)S(1)} %get-tuple-element.62.design_ref, bf16[2,1920,128]{2,1,0:T(8,128)(2,1)S(1)} %get-tuple-element.63.refs_0_, bf16[6,1920,128]{2,1,0:T(8,128)(2,1)S(1)} %get-tuple-element.64.refs_1_), custom_call_target="tpu_custom_call" | custom-call | flops 1006632960 | bytes 5898240 | tf_op jit(solution)/shard_map/cross/pallas_call | solution.py:290
  37.2 0.5 collective-permute-start.10
  37.7 1.3 %cross.14 = (f32[256,512]{1,0:T(8,128)S(1)}, f32[256,512]{1,0:T(8,128)S(1)}) custom-call(bf16[1024,1920]{1,0:T(8,128)(2,1)S(1)} %get-tuple-element.62.design_ref, bf16[2,1920,128]{2,1,0:T(8,128)(2,1)S(1)} %get-tuple-element.63.refs_0_, bf16[6,1920,128]{2,1,0:T(8,128)(2,1)S(1)} %get-tuple-element.64.refs_1_), custom_call_target="tpu_custom_call" | custom-call | flops 1006632960 | bytes 5898240 | tf_op jit(solution)/shard_map/cross/pallas_call | solution.py:290
  38.9 0.2 collective-permute-start.9
  39.1 1.3 %cross.12 = (f32[256,512]{1,0:T(8,128)S(1)}, f32[256,512]{1,0:T(8,128)S(1)}) custom-call(bf16[1024,1920]{1,0:T(8,128)(2,1)S(1)} %get-tuple-element.62.design_ref, bf16[2,1920,128]{2,1,0:T(8,128)(2,1)S(1)} %get-tuple-element.63.refs_0_, bf16[6,1920,128]{2,1,0:T(8,128)(2,1)S(1)} %get-tuple-element.64.refs_1_), custom_call_target="tpu_custom_call" | custom-call | flops 1006632960 | bytes 5898240 | tf_op jit(solution)/shard_map/cross/pallas_call | solution.py:290
  40.4 0.5 collective-permute-start.4
  41.0 4.1 %collective-permute-start.31 = (f32[256,512]{1,0:T(8,128)S(1)}, f32[256,512]{1,0:T(8,128)S(1)}, u32[]{:S(2)}, u32[]{:S(2)}) collective-permute-start(f32[256,512]{1,0:T(8,128)S(1)} %meet.11), channel_id=1, source_target_pairs={{0,96},{8,104},{16,112},{24,120},{32,64},{40,72},{48,80},{56,88},{... | collective-permute-start | bytes 1572872 | tf_op jit(solution)/shard_map/ppermute | solution.py:60
  45.1 0.8 collective-permute-start.6
  46.0 0.1 collective-permute-start.26
  46.1 0.1 collective-permute-start.21
  46.3 2.1 %collective-permute-start.16 = (f32[256,512]{1,0:T(8,128)S(1)}, f32[256,512]{1,0:T(8,128)S(1)}, u32[]{:S(2)}, u32[]{:S(2)}) collective-permute-start(f32[256,512]{1,0:T(8,128)S(1)} %meet.8), channel_id=1, source_target_pairs={{0,32},{8,40},{16,48},{24,56},{32,0},{40,8},{48,16},{56,24},{64,96... | collective-permute-start | bytes 1572872 | tf_op jit(solution)/shard_map/ppermute | solution.py:60
  48.4 9.4 %collective-permute-done.31.refs_2_ = f32[256,512]{1,0:T(8,128)S(1)} collective-permute-done((f32[256,512]{1,0:T(8,128)S(1)}, f32[256,512]{1,0:T(8,128)S(1)}, u32[]{:S(2)}, u32[]{:S(2)}) %collective-permute-start.31) | collective-permute-done | bytes 524320 | tf_op jit(solution)/shard_map/ppermute | solution.py:60
  57.8 0.7 collective-permute-start.11
  58.5 0.1 fold.22
  58.6 0.6 collective-permute-done.6.refs_2_.refs_4_
  59.2 0.8 collective-permute-start.32
  60.1 0.1 fold.12
  60.1 8.4 %collective-permute-done.26.refs_2_ = f32[256,512]{1,0:T(8,128)S(1)} collective-permute-done((f32[256,512]{1,0:T(8,128)S(1)}, f32[256,512]{1,0:T(8,128)S(1)}, u32[]{:S(2)}, u32[]{:S(2)}) %collective-permute-start.26) | collective-permute-done | bytes 524320 | tf_op jit(solution)/shard_map/ppermute | solution.py:60
  68.5 0.1 fold.20
  68.6 0.8 collective-permute-start.27
  69.4 0.1 fold.18
  69.5 1.6 %collective-permute-done.16.refs_2_ = f32[256,512]{1,0:T(8,128)S(1)} collective-permute-done((f32[256,512]{1,0:T(8,128)S(1)}, f32[256,512]{1,0:T(8,128)S(1)}, u32[]{:S(2)}, u32[]{:S(2)}) %collective-permute-start.16) | collective-permute-done | bytes 524320 | tf_op jit(solution)/shard_map/ppermute | solution.py:60
  71.0 3.2 %collective-permute-start.22 = (f32[128,512]{1,0:T(8,128)S(1)}, f32[128,512]{1,0:T(8,128)S(1)}, u32[]{:S(2)}, u32[]{:S(2)}) collective-permute-start(f32[128,512]{1,0:T(8,128)S(1)} %get-tuple-element.100), channel_id=1, source_target_pairs={{0,96},{8,104},{16,112},{24,120},{32,64},{40,72},{48,80},{56,88},{... | collective-permute-start | bytes 786440 | tf_op jit(solution)/shard_map/ppermute | solution.py:60
  74.2 0.1 fold.16
  74.3 1.5 %collective-permute-start.17 = (f32[128,512]{1,0:T(8,128)S(1)}, f32[128,512]{1,0:T(8,128)S(1)}, u32[]{:S(2)}, u32[]{:S(2)}) collective-permute-start(f32[128,512]{1,0:T(8,128)S(1)} %get-tuple-element.92), channel_id=1, source_target_pairs={{0,96},{8,104},{16,112},{24,120},{32,64},{40,72},{48,80},{56,88},{... | collective-permute-start | bytes 786440 | tf_op jit(solution)/shard_map/ppermute | solution.py:60
  75.9 0.1 fold.14
  75.9 2.3 %collective-permute-done.32.refs_1_ = f32[128,512]{1,0:T(8,128)S(1)} collective-permute-done((f32[128,512]{1,0:T(8,128)S(1)}, f32[128,512]{1,0:T(8,128)S(1)}, u32[]{:S(2)}, u32[]{:S(2)}) %collective-permute-start.32) | collective-permute-done | bytes 262176 | tf_op jit(solution)/shard_map/ppermute | solution.py:60
  78.3 2.1 %collective-permute-start.33 = (f32[64,512]{1,0:T(8,128)S(1)}, f32[64,512]{1,0:T(8,128)S(1)}, u32[]{:S(2)}, u32[]{:S(2)}) collective-permute-start(f32[64,512]{1,0:T(8,128)S(1)} %get-tuple-element.121), channel_id=1, source_target_pairs={{0,32},{8,40},{16,48},{24,56},{32,0},{40,8},{48,16},{56,24},{64,96... | collective-permute-start | bytes 393224 | tf_op jit(solution)/shard_map/ppermute | solution.py:60
  80.4 1.4 %collective-permute-done.27.refs_1_ = f32[128,512]{1,0:T(8,128)S(1)} collective-permute-done((f32[128,512]{1,0:T(8,128)S(1)}, f32[128,512]{1,0:T(8,128)S(1)}, u32[]{:S(2)}, u32[]{:S(2)}) %collective-permute-start.27) | collective-permute-done | bytes 262176 | tf_op jit(solution)/shard_map/ppermute | solution.py:60
  81.8 2.7 %collective-permute-start.8 = (f32[72,512]{1,0:T(8,128)S(1)}, f32[72,512]{1,0:T(8,128)S(1)}, u32[]{:S(2)}, u32[]{:S(2)}) collective-permute-start(f32[72,512]{1,0:T(8,128)S(1)} %get-tuple-element.75), channel_id=1, source_target_pairs={{0,96},{8,104},{16,112},{24,120},{32,64},{40,72},{48,80},{56,88},{... | collective-permute-start | bytes 442376 | tf_op jit(solution)/shard_map/ppermute | solution.py:60
  84.6 0.1 collective-permute-start.28
  84.7 0.7 collective-permute-done.17.refs_1_
  85.3 2.0 %collective-permute-start.23 = (f32[64,512]{1,0:T(8,128)S(1)}, f32[64,512]{1,0:T(8,128)S(1)}, u32[]{:S(2)}, u32[]{:S(2)}) collective-permute-start(f32[64,512]{1,0:T(8,128)S(1)} %get-tuple-element.102), channel_id=1, source_target_pairs={{0,16},{8,24},{16,0},{24,8},{32,48},{40,56},{48,32},{56,40},{64,80... | collective-permute-start | bytes 393224 | tf_op jit(solution)/shard_map/ppermute | solution.py:60
  87.4 0.1 collective-permute-start.18
  87.6 3.3 %collective-permute-start.13 = (f32[64,512]{1,0:T(8,128)S(1)}, f32[64,512]{1,0:T(8,128)S(1)}, u32[]{:S(2)}, u32[]{:S(2)}) collective-permute-start(f32[64,512]{1,0:T(8,128)S(1)} %get-tuple-element.83), channel_id=1, source_target_pairs={{0,96},{8,104},{16,112},{24,120},{32,64},{40,72},{48,80},{56,88},{... | collective-permute-start | bytes 393224 | tf_op jit(solution)/shard_map/ppermute | solution.py:60
  90.8 1.6 %collective-permute-done.18.refs_5_ = f32[64,512]{1,0:T(8,128)S(1)} collective-permute-done((f32[64,512]{1,0:T(8,128)S(1)}, f32[64,512]{1,0:T(8,128)S(1)}, u32[]{:S(2)}, u32[]{:S(2)}) %collective-permute-start.18) | collective-permute-done | bytes 131104 | tf_op jit(solution)/shard_map/ppermute | solution.py:60
  92.5 1.4 %collective-permute-done.13.refs_3_ = f32[64,512]{1,0:T(8,128)S(1)} collective-permute-done((f32[64,512]{1,0:T(8,128)S(1)}, f32[64,512]{1,0:T(8,128)S(1)}, u32[]{:S(2)}, u32[]{:S(2)}) %collective-permute-start.13) | collective-permute-done | bytes 131104 | tf_op jit(solution)/shard_map/ppermute | solution.py:60
  93.8 1.6 %finish.1 = (f32[64,1024]{1,0:T(8,128)}, f32[64,1024]{1,0:T(8,128)}) custom-call(s32[2]{0:T(128)S(1)} %pad_add_fusion.where_ref, f32[72,512]{1,0:T(8,128)S(1)} %get-tuple-element.74.refs_0_, f32[72,512]{1,0:T(8,128)S(1)} %collective-permute-done.8.refs_1_, f32[64,512]{1,0:T(8,128)S(1)} %get-tuple-element.82.refs_2_, ...), custom_call_target="tpu_custom_call" | custom-call | tf_op jit(solution)/shard_map/finish/pallas_call | solution.py:409
  (42 shorter events, 0.6 us)
Async XLA Ops:
  0.6 7.1 %collective-permute-start = (s32[2,64,128]{2,1,0:T(8,128)}, s32[2,64,128]{2,1,0:T(8,128)S(1)}, u32[]{:S(2)}, u32[]{:S(2)}) collective-permute-start(s32[2,64,128]{2,1,0:T(8,128)} %own_ref.1), channel_id=1, source_target_pairs={{0,1},{1,0},{2,3},{3,2},{4,5},{5,4},{6,7},{7,6},{8,9},{9,8},{10,11... | collective-permute-start | bytes 196616 | tf_op jit(solution)/shard_map/ppermute | solution.py:60
  4.0 3.7 %copy-start = (s32[2,64,128]{2,1,0:T(8,128)S(1)}, s32[2,64,128]{2,1,0:T(8,128)}, u32[]{:S(2)}) copy-start(s32[2,64,128]{2,1,0:T(8,128)} %own_ref.1) | copy-start | bytes 196612
  7.7 11.5 %collective-permute-start.1 = (s32[4,64,128]{2,1,0:T(8,128)S(1)}, s32[4,64,128]{2,1,0:T(8,128)S(1)}, u32[]{:S(2)}, u32[]{:S(2)}) collective-permute-start(s32[4,64,128]{2,1,0:T(8,128)S(1)} %paired.1.refs_0_), channel_id=1, source_target_pairs={{0,4},{1,5},{2,6},{3,7},{4,0},{5,1},{6,2},{7,3},{8,12},{9,13},{10,... | collective-permute-start | bytes 393224 | tf_op jit(solution)/shard_map/ppermute | solution.py:60
  10.8 8.4 %collective-permute-start.2 = (s32[4,64,128]{2,1,0:T(8,128)S(1)}, s32[4,64,128]{2,1,0:T(8,128)S(1)}, u32[]{:S(2)}, u32[]{:S(2)}) collective-permute-start(s32[4,64,128]{2,1,0:T(8,128)S(1)} %paired.1.refs_0_), channel_id=1, source_target_pairs={{0,2},{1,3},{2,0},{3,1},{4,6},{5,7},{6,4},{7,5},{8,10},{9,11},{10,... | collective-permute-start | bytes 393224 | tf_op jit(solution)/shard_map/ppermute | solution.py:60
  11.4 7.8 %collective-permute-start.3 = (s32[4,64,128]{2,1,0:T(8,128)S(1)}, s32[4,64,128]{2,1,0:T(8,128)S(1)}, u32[]{:S(2)}, u32[]{:S(2)}) collective-permute-start(s32[4,64,128]{2,1,0:T(8,128)S(1)} %paired.1.refs_0_), channel_id=1, source_target_pairs={{0,6},{1,7},{2,4},{3,5},{4,2},{5,3},{6,0},{7,1},{8,14},{9,15},{10,... | collective-permute-start | bytes 393224 | tf_op jit(solution)/shard_map/ppermute | solution.py:60
  22.8 9.0 %collective-permute-start.30 = (f32[256,512]{1,0:T(8,128)S(1)}, f32[256,512]{1,0:T(8,128)S(1)}, u32[]{:S(2)}, u32[]{:S(2)}) collective-permute-start(f32[256,512]{1,0:T(8,128)S(1)} %get-tuple-element.117), channel_id=1, source_target_pairs={{0,8},{8,0},{16,24},{24,16},{32,40},{40,32},{48,56},{56,48},{64,72... | collective-permute-start | bytes 1572872 | tf_op jit(solution)/shard_map/ppermute | solution.py:60
  24.2 8.2 %collective-permute-start.29 = (f32[256,512]{1,0:T(8,128)S(1)}, f32[256,512]{1,0:T(8,128)S(1)}, u32[]{:S(2)}, u32[]{:S(2)}) collective-permute-start(f32[256,512]{1,0:T(8,128)S(1)} %get-tuple-element.115), channel_id=1, source_target_pairs={{0,8},{8,0},{16,24},{24,16},{32,40},{40,32},{48,56},{56,48},{64,72... | collective-permute-start | bytes 1572872 | tf_op jit(solution)/shard_map/ppermute | solution.py:60
  26.0 7.8 %collective-permute-start.25 = (f32[256,512]{1,0:T(8,128)S(1)}, f32[256,512]{1,0:T(8,128)S(1)}, u32[]{:S(2)}, u32[]{:S(2)}) collective-permute-start(f32[256,512]{1,0:T(8,128)S(1)} %get-tuple-element.109), channel_id=1, source_target_pairs={{0,8},{8,0},{16,24},{24,16},{32,40},{40,32},{48,56},{56,48},{64,72... | collective-permute-start | bytes 1572872 | tf_op jit(solution)/shard_map/ppermute | solution.py:60
  27.3 8.4 %collective-permute-start.24 = (f32[256,512]{1,0:T(8,128)S(1)}, f32[256,512]{1,0:T(8,128)S(1)}, u32[]{:S(2)}, u32[]{:S(2)}) collective-permute-start(f32[256,512]{1,0:T(8,128)S(1)} %get-tuple-element.107), channel_id=1, source_target_pairs={{0,8},{8,0},{16,24},{24,16},{32,40},{40,32},{48,56},{56,48},{64,72... | collective-permute-start | bytes 1572872 | tf_op jit(solution)/shard_map/ppermute | solution.py:60
  29.2 8.0 %collective-permute-start.20 = (f32[256,512]{1,0:T(8,128)S(1)}, f32[256,512]{1,0:T(8,128)S(1)}, u32[]{:S(2)}, u32[]{:S(2)}) collective-permute-start(f32[256,512]{1,0:T(8,128)S(1)} %get-tuple-element.98), channel_id=1, source_target_pairs={{0,8},{8,0},{16,24},{24,16},{32,40},{40,32},{48,56},{56,48},{64,72... | collective-permute-start | bytes 1572872 | tf_op jit(solution)/shard_map/ppermute | solution.py:60
  31.8 7.1 %collective-permute-start.19 = (f32[256,512]{1,0:T(8,128)S(1)}, f32[256,512]{1,0:T(8,128)S(1)}, u32[]{:S(2)}, u32[]{:S(2)}) collective-permute-start(f32[256,512]{1,0:T(8,128)S(1)} %get-tuple-element.96), channel_id=1, source_target_pairs={{0,8},{8,0},{16,24},{24,16},{32,40},{40,32},{48,56},{56,48},{64,72... | collective-permute-start | bytes 1572872 | tf_op jit(solution)/shard_map/ppermute | solution.py:60
  32.4 8.5 %collective-permute-start.5 = (f32[264,512]{1,0:T(8,128)S(1)}, f32[264,512]{1,0:T(8,128)S(1)}, u32[]{:S(2)}, u32[]{:S(2)}) collective-permute-start(f32[264,512]{1,0:T(8,128)S(1)} %get-tuple-element.71), channel_id=1, source_target_pairs={{0,8},{8,0},{16,24},{24,16},{32,40},{40,32},{48,56},{56,48},{64,72... | collective-permute-start | bytes 1622024 | tf_op jit(solution)/shard_map/ppermute | solution.py:60
  33.8 6.6 %collective-permute-start.15 = (f32[256,512]{1,0:T(8,128)S(1)}, f32[256,512]{1,0:T(8,128)S(1)}, u32[]{:S(2)}, u32[]{:S(2)}) collective-permute-start(f32[256,512]{1,0:T(8,128)S(1)} %get-tuple-element.90), channel_id=1, source_target_pairs={{0,8},{8,0},{16,24},{24,16},{32,40},{40,32},{48,56},{56,48},{64,72... | collective-permute-start | bytes 1572872 | tf_op jit(solution)/shard_map/ppermute | solution.py:60
  35.7 9.4 %collective-permute-start.14 = (f32[256,512]{1,0:T(8,128)S(1)}, f32[256,512]{1,0:T(8,128)S(1)}, u32[]{:S(2)}, u32[]{:S(2)}) collective-permute-start(f32[256,512]{1,0:T(8,128)S(1)} %get-tuple-element.88), channel_id=1, source_target_pairs={{0,8},{8,0},{16,24},{24,16},{32,40},{40,32},{48,56},{56,48},{64,72... | collective-permute-start | bytes 1572872 | tf_op jit(solution)/shard_map/ppermute | solution.py:60
  37.2 8.8 %collective-permute-start.10 = (f32[256,512]{1,0:T(8,128)S(1)}, f32[256,512]{1,0:T(8,128)S(1)}, u32[]{:S(2)}, u32[]{:S(2)}) collective-permute-start(f32[256,512]{1,0:T(8,128)S(1)} %get-tuple-element.79), channel_id=1, source_target_pairs={{0,8},{8,0},{16,24},{24,16},{32,40},{40,32},{48,56},{56,48},{64,72... | collective-permute-start | bytes 1572872 | tf_op jit(solution)/shard_map/ppermute | solution.py:60
  38.9 7.2 %collective-permute-start.9 = (f32[256,512]{1,0:T(8,128)S(1)}, f32[256,512]{1,0:T(8,128)S(1)}, u32[]{:S(2)}, u32[]{:S(2)}) collective-permute-start(f32[256,512]{1,0:T(8,128)S(1)} %get-tuple-element.77), channel_id=1, source_target_pairs={{0,8},{8,0},{16,24},{24,16},{32,40},{40,32},{48,56},{56,48},{64,72... | collective-permute-start | bytes 1572872 | tf_op jit(solution)/shard_map/ppermute | solution.py:60
  40.4 5.9 %collective-permute-start.4 = (f32[256,512]{1,0:T(8,128)S(1)}, f32[256,512]{1,0:T(8,128)S(1)}, u32[]{:S(2)}, u32[]{:S(2)}) collective-permute-start(f32[256,512]{1,0:T(8,128)S(1)} %get-tuple-element.66), channel_id=1, source_target_pairs={{0,8},{8,0},{16,24},{24,16},{32,40},{40,32},{48,56},{56,48},{64,72... | collective-permute-start | bytes 1572872 | tf_op jit(solution)/shard_map/ppermute | solution.py:60
  41.0 16.9 %collective-permute-start.31 = (f32[256,512]{1,0:T(8,128)S(1)}, f32[256,512]{1,0:T(8,128)S(1)}, u32[]{:S(2)}, u32[]{:S(2)}) collective-permute-start(f32[256,512]{1,0:T(8,128)S(1)} %meet.11), channel_id=1, source_target_pairs={{0,96},{8,104},{16,112},{24,120},{32,64},{40,72},{48,80},{56,88},{... | collective-permute-start | bytes 1572872 | tf_op jit(solution)/shard_map/ppermute | solution.py:60
  45.1 14.1 %collective-permute-start.6 = (f32[264,512]{1,0:T(8,128)S(1)}, f32[264,512]{1,0:T(8,128)S(1)}, u32[]{:S(2)}, u32[]{:S(2)}) collective-permute-start(f32[264,512]{1,0:T(8,128)S(1)} %meet.6.refs_3_), channel_id=1, source_target_pairs={{0,16},{8,24},{16,0},{24,8},{32,48},{40,56},{48,32},{56,40},{64,80... | collective-permute-start | bytes 1622024 | tf_op jit(solution)/shard_map/ppermute | solution.py:60
  46.0 22.5 %collective-permute-start.26 = (f32[256,512]{1,0:T(8,128)S(1)}, f32[256,512]{1,0:T(8,128)S(1)}, u32[]{:S(2)}, u32[]{:S(2)}) collective-permute-start(f32[256,512]{1,0:T(8,128)S(1)} %meet.10), channel_id=1, source_target_pairs={{0,96},{8,104},{16,112},{24,120},{32,64},{40,72},{48,80},{56,88},{... | collective-permute-start | bytes 1572872 | tf_op jit(solution)/shard_map/ppermute | solution.py:60
  46.1 22.5 %collective-permute-start.21 = (f32[256,512]{1,0:T(8,128)S(1)}, f32[256,512]{1,0:T(8,128)S(1)}, u32[]{:S(2)}, u32[]{:S(2)}) collective-permute-start(f32[256,512]{1,0:T(8,128)S(1)} %meet.9), channel_id=1, source_target_pairs={{0,32},{8,40},{16,48},{24,56},{32,0},{40,8},{48,16},{56,24},{64,96... | collective-permute-start | bytes 1572872 | tf_op jit(solution)/shard_map/ppermute | solution.py:60
  46.3 24.7 %collective-permute-start.16 = (f32[256,512]{1,0:T(8,128)S(1)}, f32[256,512]{1,0:T(8,128)S(1)}, u32[]{:S(2)}, u32[]{:S(2)}) collective-permute-start(f32[256,512]{1,0:T(8,128)S(1)} %meet.8), channel_id=1, source_target_pairs={{0,32},{8,40},{16,48},{24,56},{32,0},{40,8},{48,16},{56,24},{64,96... | collective-permute-start | bytes 1572872 | tf_op jit(solution)/shard_map/ppermute | solution.py:60
  57.8 16.5 %collective-permute-start.11 = (f32[256,512]{1,0:T(8,128)S(1)}, f32[256,512]{1,0:T(8,128)S(1)}, u32[]{:S(2)}, u32[]{:S(2)}) collective-permute-start(f32[256,512]{1,0:T(8,128)S(1)} %meet.7), channel_id=1, source_target_pairs={{0,16},{8,24},{16,0},{24,8},{32,48},{40,56},{48,32},{56,40},{64,80... | collective-permute-start | bytes 1572872 | tf_op jit(solution)/shard_map/ppermute | solution.py:60
  59.2 19.0 %collective-permute-start.32 = (f32[128,512]{1,0:T(8,128)S(1)}, f32[128,512]{1,0:T(8,128)S(1)}, u32[]{:S(2)}, u32[]{:S(2)}) collective-permute-start(f32[128,512]{1,0:T(8,128)S(1)} %get-tuple-element.119), channel_id=1, source_target_pairs={{0,16},{8,24},{16,0},{24,8},{32,48},{40,56},{48,32},{56,40},{64,80... | collective-permute-start | bytes 786440 | tf_op jit(solution)/shard_map/ppermute | solution.py:60
  68.5 9.8 %collective-permute-start.7 = (f32[136,512]{1,0:T(8,128)S(1)}, f32[136,512]{1,0:T(8,128)S(1)}, u32[]{:S(2)}, u32[]{:S(2)}) collective-permute-start(f32[136,512]{1,0:T(8,128)S(1)} %get-tuple-element.73), channel_id=1, source_target_pairs={{0,32},{8,40},{16,48},{24,56},{32,0},{40,8},{48,16},{56,24},{64,96... | collective-permute-start | bytes 835592 | tf_op jit(solution)/shard_map/ppermute | solution.py:60
  68.6 13.2 %collective-permute-start.27 = (f32[128,512]{1,0:T(8,128)S(1)}, f32[128,512]{1,0:T(8,128)S(1)}, u32[]{:S(2)}, u32[]{:S(2)}) collective-permute-start(f32[128,512]{1,0:T(8,128)S(1)} %get-tuple-element.111), channel_id=1, source_target_pairs={{0,16},{8,24},{16,0},{24,8},{32,48},{40,56},{48,32},{56,40},{64,80... | collective-permute-start | bytes 786440 | tf_op jit(solution)/shard_map/ppermute | solution.py:60
  71.0 13.5 %collective-permute-start.22 = (f32[128,512]{1,0:T(8,128)S(1)}, f32[128,512]{1,0:T(8,128)S(1)}, u32[]{:S(2)}, u32[]{:S(2)}) collective-permute-start(f32[128,512]{1,0:T(8,128)S(1)} %get-tuple-element.100), channel_id=1, source_target_pairs={{0,96},{8,104},{16,112},{24,120},{32,64},{40,72},{48,80},{56,88},{... | collective-permute-start | bytes 786440 | tf_op jit(solution)/shard_map/ppermute | solution.py:60
  74.3 11.0 %collective-permute-start.17 = (f32[128,512]{1,0:T(8,128)S(1)}, f32[128,512]{1,0:T(8,128)S(1)}, u32[]{:S(2)}, u32[]{:S(2)}) collective-permute-start(f32[128,512]{1,0:T(8,128)S(1)} %get-tuple-element.92), channel_id=1, source_target_pairs={{0,96},{8,104},{16,112},{24,120},{32,64},{40,72},{48,80},{56,88},{... | collective-permute-start | bytes 786440 | tf_op jit(solution)/shard_map/ppermute | solution.py:60
  78.3 9.2 %collective-permute-start.12 = (f32[128,512]{1,0:T(8,128)S(1)}, f32[128,512]{1,0:T(8,128)S(1)}, u32[]{:S(2)}, u32[]{:S(2)}) collective-permute-start(f32[128,512]{1,0:T(8,128)S(1)} %get-tuple-element.81), channel_id=1, source_target_pairs={{0,32},{8,40},{16,48},{24,56},{32,0},{40,8},{48,16},{56,24},{64,96... | collective-permute-start | bytes 786440 | tf_op jit(solution)/shard_map/ppermute | solution.py:60
  78.3 9.2 %collective-permute-start.33 = (f32[64,512]{1,0:T(8,128)S(1)}, f32[64,512]{1,0:T(8,128)S(1)}, u32[]{:S(2)}, u32[]{:S(2)}) collective-permute-start(f32[64,512]{1,0:T(8,128)S(1)} %get-tuple-element.121), channel_id=1, source_target_pairs={{0,32},{8,40},{16,48},{24,56},{32,0},{40,8},{48,16},{56,24},{64,96... | collective-permute-start | bytes 393224 | tf_op jit(solution)/shard_map/ppermute | solution.py:60
  81.8 12.0 %collective-permute-start.8 = (f32[72,512]{1,0:T(8,128)S(1)}, f32[72,512]{1,0:T(8,128)S(1)}, u32[]{:S(2)}, u32[]{:S(2)}) collective-permute-start(f32[72,512]{1,0:T(8,128)S(1)} %get-tuple-element.75), channel_id=1, source_target_pairs={{0,96},{8,104},{16,112},{24,120},{32,64},{40,72},{48,80},{56,88},{... | collective-permute-start | bytes 442376 | tf_op jit(solution)/shard_map/ppermute | solution.py:60
  84.6 6.3 %collective-permute-start.28 = (f32[64,512]{1,0:T(8,128)S(1)}, f32[64,512]{1,0:T(8,128)S(1)}, u32[]{:S(2)}, u32[]{:S(2)}) collective-permute-start(f32[64,512]{1,0:T(8,128)S(1)} %get-tuple-element.113), channel_id=1, source_target_pairs={{0,32},{8,40},{16,48},{24,56},{32,0},{40,8},{48,16},{56,24},{64,96... | collective-permute-start | bytes 393224 | tf_op jit(solution)/shard_map/ppermute | solution.py:60
  85.3 5.5 %collective-permute-start.23 = (f32[64,512]{1,0:T(8,128)S(1)}, f32[64,512]{1,0:T(8,128)S(1)}, u32[]{:S(2)}, u32[]{:S(2)}) collective-permute-start(f32[64,512]{1,0:T(8,128)S(1)} %get-tuple-element.102), channel_id=1, source_target_pairs={{0,16},{8,24},{16,0},{24,8},{32,48},{40,56},{48,32},{56,40},{64,80... | collective-permute-start | bytes 393224 | tf_op jit(solution)/shard_map/ppermute | solution.py:60
  87.4 5.0 %collective-permute-start.18 = (f32[64,512]{1,0:T(8,128)S(1)}, f32[64,512]{1,0:T(8,128)S(1)}, u32[]{:S(2)}, u32[]{:S(2)}) collective-permute-start(f32[64,512]{1,0:T(8,128)S(1)} %get-tuple-element.94), channel_id=1, source_target_pairs={{0,16},{8,24},{16,0},{24,8},{32,48},{40,56},{48,32},{56,40},{64,80... | collective-permute-start | bytes 393224 | tf_op jit(solution)/shard_map/ppermute | solution.py:60
  87.6 6.3 %collective-permute-start.13 = (f32[64,512]{1,0:T(8,128)S(1)}, f32[64,512]{1,0:T(8,128)S(1)}, u32[]{:S(2)}, u32[]{:S(2)}) collective-permute-start(f32[64,512]{1,0:T(8,128)S(1)} %get-tuple-element.83), channel_id=1, source_target_pairs={{0,96},{8,104},{16,112},{24,120},{32,64},{40,72},{48,80},{56,88},{... | collective-permute-start | bytes 393224 | tf_op jit(solution)/shard_map/ppermute | solution.py:60

commit v6 on v5

--- a/solution.py
+++ b/solution.py
@@ -375,8 +375,9 @@
         turned = jnp.broadcast_to(picked, (LANES, LANES)).T
         columns.append(jnp.where(samp & 1 == 0, turned[:own], turned[own:]))
     dos_sum, dos_sq = columns
-    dosage_var = dos_sq - dos_sum * dos_sum / sample_count
-    scale = jnp.sqrt(jnp.float32(sample_count))
+    dos_mean = dos_sum / sample_count
+    dosage_var = dos_sq - dos_sum * dos_mean
+    dos_scale = jnp.sqrt(jnp.float32(sample_count)) * lax.rsqrt(dosage_var + 1.0)
     first, copies = 0, []
     for chunk, blocks in enumerate(CHUNKS):
         for block in range(blocks):
@@ -389,11 +390,9 @@
                 pair_of[index][chunk][0][:own, lanes] + pair_of[index][chunk][1][:own, lanes]
                 for index in range(3)
             ]
-            covariance = pair_sums[0] - dos_sum * gene_sum / sample_count
-            total_ref[:, spot] = (
-                scale * covariance / jnp.sqrt((dosage_var + 1.0) * (gene_var + 1.0))
-            )
-            allelic_ref[:, spot] = pair_sums[1] / jnp.sqrt(pair_sums[2] + 1.0)
+            covariance = pair_sums[0] - dos_mean * gene_sum
+            total_ref[:, spot] = covariance * dos_scale * lax.rsqrt(gene_var + 1.0)
+            allelic_ref[:, spot] = pair_sums[1] * lax.rsqrt(pair_sums[2] + 1.0)
         lanes = pl.ds(first * LANES, blocks * LANES)
         for which, (ref, hbm) in enumerate(((total_ref, total_hbm), (allelic_ref, allelic_hbm))):
             copy = pltpu.make_async_copy(ref.at[:, lanes], hbm.at[:, lanes], sems.at[which, chunk])

time: 96 us -> 95.9 us (level)
  no operation moved by 1% of the time
where the time goes in v6:
time: 95.9 us; the launch traced here: 95.5 us
  starting transfers between devices  36.1 us (38%)
  Pallas kernels  30.8 us (32%)
  waiting for transfers between devices  27.3 us (28%)
  between operations  1.14 us (1%)
    ppermute x34, starting transfers between devices, swap(): return lax.ppermute(array, axis, [(d, d ^ flip) for d in range(size)])  36.1 us
    ppermute x34, waiting for transfers between devices, swap(): return lax.ppermute(array, axis, [(d, d ^ flip) for d in range(size)])  27.3 us
    pallas_call x12, Pallas kernels, cross(): pl.pallas_call(functools.partial(cross_kernel, spots, part, len(margins))...  15.1 us
    pallas_call x2, Pallas kernels, features(): pl.pallas_call(functools.partial(feature_kernel, first), out_shape=(featu...  10.8 us
    pallas_call x1, Pallas kernels, unpack(): pl.pallas_call(unpack_kernel, out_shape=(design,) * 3 + (jax.ShapeDtypeSt...  2.29 us
  transfers between devices with their start and end apart: 34, of which 9 were waited for; matrix products, arithmetic and copies ran while one was open for 0% of the time, Pallas kernels for 27%

profile of v6, /device:TPU:0, one launch (start us, length us, event | category | flops | bytes accessed | tf_op | source)
XLA Modules:
  0.0 95.5 jit_solution(16648082662260925015)
XLA Ops:
  0.6 3.4 %collective-permute-start = (s32[2,64,128]{2,1,0:T(8,128)}, s32[2,64,128]{2,1,0:T(8,128)S(1)}, u32[]{:S(2)}, u32[]{:S(2)}) collective-permute-start(s32[2,64,128]{2,1,0:T(8,128)} %own_ref.1), channel_id=1, source_target_pairs={{0,1},{1,0},{2,3},{3,2},{4,5},{5,4},{6,7},{7,6},{8,9},{9,8},{10,11... | collective-permute-start | bytes 196616 | tf_op jit(solution)/shard_map/ppermute | solution.py:60
  4.0 3.6 %features.2 = (bf16[2,1920,128]{2,1,0:T(8,128)(2,1)S(1)}, bf16[2,1920,128]{2,1,0:T(8,128)(2,1)S(1)}, bf16[2,1920,128]{2,1,0:T(8,128)(2,1)S(1)}, f32[2,256]{1,0:T(2,128)S(1)}) custom-call(s32[1920,1024]{1,0:T(8,128)} %total_hbm.3, s32[1920,1024]{1,0:T(8,128)} %one_hbm.3, s32[1920,1024]{1,0:T(8,128)} %two_hbm.3), custom_call_target="tpu_custom_call" | custom-call | flops 3072000000 | bytes 8847360 | tf_op jit(solution)/shard_map/features/pallas_call | solution.py:224
  7.6 0.1 pad_add_fusion.where_ref
  7.7 3.1 %collective-permute-start.1 = (s32[4,64,128]{2,1,0:T(8,128)S(1)}, s32[4,64,128]{2,1,0:T(8,128)S(1)}, u32[]{:S(2)}, u32[]{:S(2)}) collective-permute-start(s32[4,64,128]{2,1,0:T(8,128)S(1)} %paired.1.refs_0_), channel_id=1, source_target_pairs={{0,4},{1,5},{2,6},{3,7},{4,0},{5,1},{6,2},{7,3},{8,12},{9,13},{10,... | collective-permute-start | bytes 393224 | tf_op jit(solution)/shard_map/ppermute | solution.py:60
  10.8 0.6 collective-permute-start.2
  11.4 0.6 collective-permute-start.3
  12.0 7.2 %features.3 = (bf16[6,1920,128]{2,1,0:T(8,128)(2,1)S(1)}, bf16[6,1920,128]{2,1,0:T(8,128)(2,1)S(1)}, bf16[6,1920,128]{2,1,0:T(8,128)(2,1)S(1)}, f32[2,768]{1,0:T(2,128)S(1)}) custom-call(s32[1920,1024]{1,0:T(8,128)} %total_hbm.3, s32[1920,1024]{1,0:T(8,128)} %one_hbm.3, s32[1920,1024]{1,0:T(8,128)} %two_hbm.3, ...), custom_call_target="tpu_custom_call" | custom-call | flops 9216000000 | bytes 26542080 | tf_op jit(solution)/shard_map/features/pallas_call | solution.py:224
  19.2 2.3 %unpack.1 = (bf16[1024,1920]{1,0:T(8,128)(2,1)S(1)}, bf16[1024,1920]{1,0:T(8,128)(2,1)S(1)}, bf16[1024,1920]{1,0:T(8,128)(2,1)S(1)}, f32[8,2,128]{2,1,0:T(2,128)S(1)}) custom-call(s32[2]{0:T(128)S(1)} %pad_add_fusion.where_ref, s32[4,64,128]{2,1,0:T(8,128)S(1)} %paired.1.refs_0_, s32[4,64,128]{2,1,0:T(8,128)S(1)} %collective-permute-done.1.refs_1_, ...), custom_call_target="tpu_custom_call" | custom-call | flops 6000000000 | bytes 11796480 | tf_op jit(solution)/shard_map/unpack/pallas_call | solution.py:143
  21.5 1.3 %cross.23 = (f32[256,512]{1,0:T(8,128)S(1)}, f32[256,512]{1,0:T(8,128)S(1)}) custom-call(bf16[1024,1920]{1,0:T(8,128)(2,1)S(1)} %get-tuple-element.103.design_ref, bf16[2,1920,128]{2,1,0:T(8,128)(2,1)S(1)} %get-tuple-element.104.refs_0_, bf16[6,1920,128]{2,1,0:T(8,128)(2,1)S(1)} %get-tuple-element.105.refs_1_), custom_call_target="tpu_custom_call" | custom-call | flops 1006632960 | bytes 5898240 | tf_op jit(solution)/shard_map/cross/pallas_call | solution.py:290
  22.8 0.1 collective-permute-start.30
  22.9 1.3 %cross.22 = (f32[256,512]{1,0:T(8,128)S(1)}, f32[256,512]{1,0:T(8,128)S(1)}) custom-call(bf16[1024,1920]{1,0:T(8,128)(2,1)S(1)} %get-tuple-element.103.design_ref, bf16[2,1920,128]{2,1,0:T(8,128)(2,1)S(1)} %get-tuple-element.104.refs_0_, bf16[6,1920,128]{2,1,0:T(8,128)(2,1)S(1)} %get-tuple-element.105.refs_1_), custom_call_target="tpu_custom_call" | custom-call | flops 1006632960 | bytes 5898240 | tf_op jit(solution)/shard_map/cross/pallas_call | solution.py:290
  24.2 0.6 collective-permute-start.29
  24.7 1.3 %cross.21 = (f32[256,512]{1,0:T(8,128)S(1)}, f32[256,512]{1,0:T(8,128)S(1)}) custom-call(bf16[1024,1920]{1,0:T(8,128)(2,1)S(1)} %get-tuple-element.103.design_ref, bf16[2,1920,128]{2,1,0:T(8,128)(2,1)S(1)} %get-tuple-element.104.refs_0_, bf16[6,1920,128]{2,1,0:T(8,128)(2,1)S(1)} %get-tuple-element.105.refs_1_), custom_call_target="tpu_custom_call" | custom-call | flops 1006632960 | bytes 5898240 | tf_op jit(solution)/shard_map/cross/pallas_call | solution.py:290
  26.0 0.1 collective-permute-start.25
  26.1 1.3 %cross.20 = (f32[256,512]{1,0:T(8,128)S(1)}, f32[256,512]{1,0:T(8,128)S(1)}) custom-call(bf16[1024,1920]{1,0:T(8,128)(2,1)S(1)} %get-tuple-element.103.design_ref, bf16[2,1920,128]{2,1,0:T(8,128)(2,1)S(1)} %get-tuple-element.104.refs_0_, bf16[6,1920,128]{2,1,0:T(8,128)(2,1)S(1)} %get-tuple-element.105.refs_1_), custom_call_target="tpu_custom_call" | custom-call | flops 1006632960 | bytes 5898240 | tf_op jit(solution)/shard_map/cross/pallas_call | solution.py:290
  27.3 0.6 collective-permute-start.24
  27.9 1.3 %cross.19 = (f32[256,512]{1,0:T(8,128)S(1)}, f32[256,512]{1,0:T(8,128)S(1)}) custom-call(bf16[1024,1920]{1,0:T(8,128)(2,1)S(1)} %get-tuple-element.84.design_ref, bf16[2,1920,128]{2,1,0:T(8,128)(2,1)S(1)} %get-tuple-element.85.refs_0_, bf16[6,1920,128]{2,1,0:T(8,128)(2,1)S(1)} %get-tuple-element.86.refs_1_), custom_call_target="tpu_custom_call" | custom-call | flops 1006632960 | bytes 5898240 | tf_op jit(solution)/shard_map/cross/pallas_call | solution.py:290
  29.2 0.1 collective-permute-start.20
  29.3 1.3 %cross.18 = (f32[256,512]{1,0:T(8,128)S(1)}, f32[256,512]{1,0:T(8,128)S(1)}) custom-call(bf16[1024,1920]{1,0:T(8,128)(2,1)S(1)} %get-tuple-element.84.design_ref, bf16[2,1920,128]{2,1,0:T(8,128)(2,1)S(1)} %get-tuple-element.85.refs_0_, bf16[6,1920,128]{2,1,0:T(8,128)(2,1)S(1)} %get-tuple-element.86.refs_1_), custom_call_target="tpu_custom_call" | custom-call | flops 1006632960 | bytes 5898240 | tf_op jit(solution)/shard_map/cross/pallas_call | solution.py:290
  30.5 1.3 %cross.13 = (f32[264,512]{1,0:T(8,128)S(1)}, f32[264,512]{1,0:T(8,128)S(1)}) custom-call(bf16[1024,1920]{1,0:T(8,128)(2,1)S(1)} %get-tuple-element.62.design_ref, bf16[2,1920,128]{2,1,0:T(8,128)(2,1)S(1)} %get-tuple-element.63.refs_0_, bf16[6,1920,128]{2,1,0:T(8,128)(2,1)S(1)} %get-tuple-element.64.refs_1_, f32[2,256]{1,0:T(2,128)S(1)} %get-tuple-element.67.refs_2_, ...), custom_call_target="tpu_custom_call" | custom-call | flops 1006632960 | bytes 5898240 | tf_op jit(solution)/shard_map/cross/pallas_call | solution.py:290
  31.8 0.6 collective-permute-start.19
  32.4 0.1 collective-permute-start.5
  32.5 1.3 %cross.17 = (f32[256,512]{1,0:T(8,128)S(1)}, f32[256,512]{1,0:T(8,128)S(1)}) custom-call(bf16[1024,1920]{1,0:T(8,128)(2,1)S(1)} %get-tuple-element.84.design_ref, bf16[2,1920,128]{2,1,0:T(8,128)(2,1)S(1)} %get-tuple-element.85.refs_0_, bf16[6,1920,128]{2,1,0:T(8,128)(2,1)S(1)} %get-tuple-element.86.refs_1_), custom_call_target="tpu_custom_call" | custom-call | flops 1006632960 | bytes 5898240 | tf_op jit(solution)/shard_map/cross/pallas_call | solution.py:290
  33.8 0.7 collective-permute-start.15
  34.4 1.3 %cross.16 = (f32[256,512]{1,0:T(8,128)S(1)}, f32[256,512]{1,0:T(8,128)S(1)}) custom-call(bf16[1024,1920]{1,0:T(8,128)(2,1)S(1)} %get-tuple-element.84.design_ref, bf16[2,1920,128]{2,1,0:T(8,128)(2,1)S(1)} %get-tuple-element.85.refs_0_, bf16[6,1920,128]{2,1,0:T(8,128)(2,1)S(1)} %get-tuple-element.86.refs_1_), custom_call_target="tpu_custom_call" | custom-call | flops 1006632960 | bytes 5898240 | tf_op jit(solution)/shard_map/cross/pallas_call | solution.py:290
  35.7 0.2 collective-permute-start.14
  35.9 1.3 %cross.15 = (f32[256,512]{1,0:T(8,128)S(1)}, f32[256,512]{1,0:T(8,128)S(1)}) custom-call(bf16[1024,1920]{1,0:T(8,128)(2,1)S(1)} %get-tuple-element.62.design_ref, bf16[2,1920,128]{2,1,0:T(8,128)(2,1)S(1)} %get-tuple-element.63.refs_0_, bf16[6,1920,128]{2,1,0:T(8,128)(2,1)S(1)} %get-tuple-element.64.refs_1_), custom_call_target="tpu_custom_call" | custom-call | flops 1006632960 | bytes 5898240 | tf_op jit(solution)/shard_map/cross/pallas_call | solution.py:290
  37.2 0.5 collective-permute-start.10
  37.7 1.3 %cross.14 = (f32[256,512]{1,0:T(8,128)S(1)}, f32[256,512]{1,0:T(8,128)S(1)}) custom-call(bf16[1024,1920]{1,0:T(8,128)(2,1)S(1)} %get-tuple-element.62.design_ref, bf16[2,1920,128]{2,1,0:T(8,128)(2,1)S(1)} %get-tuple-element.63.refs_0_, bf16[6,1920,128]{2,1,0:T(8,128)(2,1)S(1)} %get-tuple-element.64.refs_1_), custom_call_target="tpu_custom_call" | custom-call | flops 1006632960 | bytes 5898240 | tf_op jit(solution)/shard_map/cross/pallas_call | solution.py:290
  38.9 0.2 collective-permute-start.9
  39.1 1.3 %cross.12 = (f32[256,512]{1,0:T(8,128)S(1)}, f32[256,512]{1,0:T(8,128)S(1)}) custom-call(bf16[1024,1920]{1,0:T(8,128)(2,1)S(1)} %get-tuple-element.62.design_ref, bf16[2,1920,128]{2,1,0:T(8,128)(2,1)S(1)} %get-tuple-element.63.refs_0_, bf16[6,1920,128]{2,1,0:T(8,128)(2,1)S(1)} %get-tuple-element.64.refs_1_), custom_call_target="tpu_custom_call" | custom-call | flops 1006632960 | bytes 5898240 | tf_op jit(solution)/shard_map/cross/pallas_call | solution.py:290
  40.4 0.5 collective-permute-start.4
  41.0 4.1 %collective-permute-start.31 = (f32[256,512]{1,0:T(8,128)S(1)}, f32[256,512]{1,0:T(8,128)S(1)}, u32[]{:S(2)}, u32[]{:S(2)}) collective-permute-start(f32[256,512]{1,0:T(8,128)S(1)} %meet.11), channel_id=1, source_target_pairs={{0,96},{8,104},{16,112},{24,120},{32,64},{40,72},{48,80},{56,88},{... | collective-permute-start | bytes 1572872 | tf_op jit(solution)/shard_map/ppermute | solution.py:60
  45.1 0.8 collective-permute-start.6
  46.0 0.1 collective-permute-start.26
  46.1 0.1 collective-permute-start.21
  46.3 2.1 %collective-permute-start.16 = (f32[256,512]{1,0:T(8,128)S(1)}, f32[256,512]{1,0:T(8,128)S(1)}, u32[]{:S(2)}, u32[]{:S(2)}) collective-permute-start(f32[256,512]{1,0:T(8,128)S(1)} %meet.8), channel_id=1, source_target_pairs={{0,32},{8,40},{16,48},{24,56},{32,0},{40,8},{48,16},{56,24},{64,96... | collective-permute-start | bytes 1572872 | tf_op jit(solution)/shard_map/ppermute | solution.py:60
  48.4 9.4 %collective-permute-done.31.refs_2_ = f32[256,512]{1,0:T(8,128)S(1)} collective-permute-done((f32[256,512]{1,0:T(8,128)S(1)}, f32[256,512]{1,0:T(8,128)S(1)}, u32[]{:S(2)}, u32[]{:S(2)}) %collective-permute-start.31) | collective-permute-done | bytes 524320 | tf_op jit(solution)/shard_map/ppermute | solution.py:60
  57.8 0.7 collective-permute-start.11
  58.5 0.1 fold.22
  58.6 0.6 collective-permute-done.6.refs_2_.refs_4_
  59.2 0.8 collective-permute-start.32
  60.1 0.1 fold.12
  60.1 8.4 %collective-permute-done.26.refs_2_ = f32[256,512]{1,0:T(8,128)S(1)} collective-permute-done((f32[256,512]{1,0:T(8,128)S(1)}, f32[256,512]{1,0:T(8,128)S(1)}, u32[]{:S(2)}, u32[]{:S(2)}) %collective-permute-start.26) | collective-permute-done | bytes 524320 | tf_op jit(solution)/shard_map/ppermute | solution.py:60
  68.5 0.1 fold.20
  68.6 0.8 collective-permute-start.27
  69.4 0.1 fold.18
  69.5 1.6 %collective-permute-done.16.refs_2_ = f32[256,512]{1,0:T(8,128)S(1)} collective-permute-done((f32[256,512]{1,0:T(8,128)S(1)}, f32[256,512]{1,0:T(8,128)S(1)}, u32[]{:S(2)}, u32[]{:S(2)}) %collective-permute-start.16) | collective-permute-done | bytes 524320 | tf_op jit(solution)/shard_map/ppermute | solution.py:60
  71.0 3.2 %collective-permute-start.22 = (f32[128,512]{1,0:T(8,128)S(1)}, f32[128,512]{1,0:T(8,128)S(1)}, u32[]{:S(2)}, u32[]{:S(2)}) collective-permute-start(f32[128,512]{1,0:T(8,128)S(1)} %get-tuple-element.100), channel_id=1, source_target_pairs={{0,96},{8,104},{16,112},{24,120},{32,64},{40,72},{48,80},{56,88},{... | collective-permute-start | bytes 786440 | tf_op jit(solution)/shard_map/ppermute | solution.py:60
  74.2 0.1 fold.16
  74.3 1.5 %collective-permute-start.17 = (f32[128,512]{1,0:T(8,128)S(1)}, f32[128,512]{1,0:T(8,128)S(1)}, u32[]{:S(2)}, u32[]{:S(2)}) collective-permute-start(f32[128,512]{1,0:T(8,128)S(1)} %get-tuple-element.92), channel_id=1, source_target_pairs={{0,96},{8,104},{16,112},{24,120},{32,64},{40,72},{48,80},{56,88},{... | collective-permute-start | bytes 786440 | tf_op jit(solution)/shard_map/ppermute | solution.py:60
  75.9 0.1 fold.14
  75.9 2.3 %collective-permute-done.32.refs_1_ = f32[128,512]{1,0:T(8,128)S(1)} collective-permute-done((f32[128,512]{1,0:T(8,128)S(1)}, f32[128,512]{1,0:T(8,128)S(1)}, u32[]{:S(2)}, u32[]{:S(2)}) %collective-permute-start.32) | collective-permute-done | bytes 262176 | tf_op jit(solution)/shard_map/ppermute | solution.py:60
  78.3 2.1 %collective-permute-start.33 = (f32[64,512]{1,0:T(8,128)S(1)}, f32[64,512]{1,0:T(8,128)S(1)}, u32[]{:S(2)}, u32[]{:S(2)}) collective-permute-start(f32[64,512]{1,0:T(8,128)S(1)} %get-tuple-element.121), channel_id=1, source_target_pairs={{0,32},{8,40},{16,48},{24,56},{32,0},{40,8},{48,16},{56,24},{64,96... | collective-permute-start | bytes 393224 | tf_op jit(solution)/shard_map/ppermute | solution.py:60
  80.4 1.4 %collective-permute-done.27.refs_1_ = f32[128,512]{1,0:T(8,128)S(1)} collective-permute-done((f32[128,512]{1,0:T(8,128)S(1)}, f32[128,512]{1,0:T(8,128)S(1)}, u32[]{:S(2)}, u32[]{:S(2)}) %collective-permute-start.27) | collective-permute-done | bytes 262176 | tf_op jit(solution)/shard_map/ppermute | solution.py:60
  81.8 2.7 %collective-permute-start.8 = (f32[72,512]{1,0:T(8,128)S(1)}, f32[72,512]{1,0:T(8,128)S(1)}, u32[]{:S(2)}, u32[]{:S(2)}) collective-permute-start(f32[72,512]{1,0:T(8,128)S(1)} %get-tuple-element.75), channel_id=1, source_target_pairs={{0,96},{8,104},{16,112},{24,120},{32,64},{40,72},{48,80},{56,88},{... | collective-permute-start | bytes 442376 | tf_op jit(solution)/shard_map/ppermute | solution.py:60
  84.6 0.1 collective-permute-start.28
  84.7 0.7 collective-permute-done.17.refs_1_
  85.3 2.0 %collective-permute-start.23 = (f32[64,512]{1,0:T(8,128)S(1)}, f32[64,512]{1,0:T(8,128)S(1)}, u32[]{:S(2)}, u32[]{:S(2)}) collective-permute-start(f32[64,512]{1,0:T(8,128)S(1)} %get-tuple-element.102), channel_id=1, source_target_pairs={{0,16},{8,24},{16,0},{24,8},{32,48},{40,56},{48,32},{56,40},{64,80... | collective-permute-start | bytes 393224 | tf_op jit(solution)/shard_map/ppermute | solution.py:60
  87.4 0.1 collective-permute-start.18
  87.6 3.3 %collective-permute-start.13 = (f32[64,512]{1,0:T(8,128)S(1)}, f32[64,512]{1,0:T(8,128)S(1)}, u32[]{:S(2)}, u32[]{:S(2)}) collective-permute-start(f32[64,512]{1,0:T(8,128)S(1)} %get-tuple-element.83), channel_id=1, source_target_pairs={{0,96},{8,104},{16,112},{24,120},{32,64},{40,72},{48,80},{56,88},{... | collective-permute-start | bytes 393224 | tf_op jit(solution)/shard_map/ppermute | solution.py:60
  90.8 1.6 %collective-permute-done.18.refs_5_ = f32[64,512]{1,0:T(8,128)S(1)} collective-permute-done((f32[64,512]{1,0:T(8,128)S(1)}, f32[64,512]{1,0:T(8,128)S(1)}, u32[]{:S(2)}, u32[]{:S(2)}) %collective-permute-start.18) | collective-permute-done | bytes 131104 | tf_op jit(solution)/shard_map/ppermute | solution.py:60
  92.5 1.4 %collective-permute-done.13.refs_3_ = f32[64,512]{1,0:T(8,128)S(1)} collective-permute-done((f32[64,512]{1,0:T(8,128)S(1)}, f32[64,512]{1,0:T(8,128)S(1)}, u32[]{:S(2)}, u32[]{:S(2)}) %collective-permute-start.13) | collective-permute-done | bytes 131104 | tf_op jit(solution)/shard_map/ppermute | solution.py:60
  93.8 1.5 %finish.1 = (f32[64,1024]{1,0:T(8,128)}, f32[64,1024]{1,0:T(8,128)}) custom-call(s32[2]{0:T(128)S(1)} %pad_add_fusion.where_ref, f32[72,512]{1,0:T(8,128)S(1)} %get-tuple-element.74.refs_0_, f32[72,512]{1,0:T(8,128)S(1)} %collective-permute-done.8.refs_1_, f32[64,512]{1,0:T(8,128)S(1)} %get-tuple-element.82.refs_2_, ...), custom_call_target="tpu_custom_call" | custom-call | tf_op jit(solution)/shard_map/finish/pallas_call | solution.py:408
  (42 shorter events, 0.6 us)
Async XLA Ops:
  0.6 7.1 %collective-permute-start = (s32[2,64,128]{2,1,0:T(8,128)}, s32[2,64,128]{2,1,0:T(8,128)S(1)}, u32[]{:S(2)}, u32[]{:S(2)}) collective-permute-start(s32[2,64,128]{2,1,0:T(8,128)} %own_ref.1), channel_id=1, source_target_pairs={{0,1},{1,0},{2,3},{3,2},{4,5},{5,4},{6,7},{7,6},{8,9},{9,8},{10,11... | collective-permute-start | bytes 196616 | tf_op jit(solution)/shard_map/ppermute | solution.py:60
  4.0 3.7 %copy-start = (s32[2,64,128]{2,1,0:T(8,128)S(1)}, s32[2,64,128]{2,1,0:T(8,128)}, u32[]{:S(2)}) copy-start(s32[2,64,128]{2,1,0:T(8,128)} %own_ref.1) | copy-start | bytes 196612
  7.7 11.5 %collective-permute-start.1 = (s32[4,64,128]{2,1,0:T(8,128)S(1)}, s32[4,64,128]{2,1,0:T(8,128)S(1)}, u32[]{:S(2)}, u32[]{:S(2)}) collective-permute-start(s32[4,64,128]{2,1,0:T(8,128)S(1)} %paired.1.refs_0_), channel_id=1, source_target_pairs={{0,4},{1,5},{2,6},{3,7},{4,0},{5,1},{6,2},{7,3},{8,12},{9,13},{10,... | collective-permute-start | bytes 393224 | tf_op jit(solution)/shard_map/ppermute | solution.py:60
  10.8 8.4 %collective-permute-start.2 = (s32[4,64,128]{2,1,0:T(8,128)S(1)}, s32[4,64,128]{2,1,0:T(8,128)S(1)}, u32[]{:S(2)}, u32[]{:S(2)}) collective-permute-start(s32[4,64,128]{2,1,0:T(8,128)S(1)} %paired.1.refs_0_), channel_id=1, source_target_pairs={{0,2},{1,3},{2,0},{3,1},{4,6},{5,7},{6,4},{7,5},{8,10},{9,11},{10,... | collective-permute-start | bytes 393224 | tf_op jit(solution)/shard_map/ppermute | solution.py:60
  11.4 7.8 %collective-permute-start.3 = (s32[4,64,128]{2,1,0:T(8,128)S(1)}, s32[4,64,128]{2,1,0:T(8,128)S(1)}, u32[]{:S(2)}, u32[]{:S(2)}) collective-permute-start(s32[4,64,128]{2,1,0:T(8,128)S(1)} %paired.1.refs_0_), channel_id=1, source_target_pairs={{0,6},{1,7},{2,4},{3,5},{4,2},{5,3},{6,0},{7,1},{8,14},{9,15},{10,... | collective-permute-start | bytes 393224 | tf_op jit(solution)/shard_map/ppermute | solution.py:60
  22.8 9.0 %collective-permute-start.30 = (f32[256,512]{1,0:T(8,128)S(1)}, f32[256,512]{1,0:T(8,128)S(1)}, u32[]{:S(2)}, u32[]{:S(2)}) collective-permute-start(f32[256,512]{1,0:T(8,128)S(1)} %get-tuple-element.117), channel_id=1, source_target_pairs={{0,8},{8,0},{16,24},{24,16},{32,40},{40,32},{48,56},{56,48},{64,72... | collective-permute-start | bytes 1572872 | tf_op jit(solution)/shard_map/ppermute | solution.py:60
  24.2 8.2 %collective-permute-start.29 = (f32[256,512]{1,0:T(8,128)S(1)}, f32[256,512]{1,0:T(8,128)S(1)}, u32[]{:S(2)}, u32[]{:S(2)}) collective-permute-start(f32[256,512]{1,0:T(8,128)S(1)} %get-tuple-element.115), channel_id=1, source_target_pairs={{0,8},{8,0},{16,24},{24,16},{32,40},{40,32},{48,56},{56,48},{64,72... | collective-permute-start | bytes 1572872 | tf_op jit(solution)/shard_map/ppermute | solution.py:60
  26.0 7.8 %collective-permute-start.25 = (f32[256,512]{1,0:T(8,128)S(1)}, f32[256,512]{1,0:T(8,128)S(1)}, u32[]{:S(2)}, u32[]{:S(2)}) collective-permute-start(f32[256,512]{1,0:T(8,128)S(1)} %get-tuple-element.109), channel_id=1, source_target_pairs={{0,8},{8,0},{16,24},{24,16},{32,40},{40,32},{48,56},{56,48},{64,72... | collective-permute-start | bytes 1572872 | tf_op jit(solution)/shard_map/ppermute | solution.py:60
  27.3 8.4 %collective-permute-start.24 = (f32[256,512]{1,0:T(8,128)S(1)}, f32[256,512]{1,0:T(8,128)S(1)}, u32[]{:S(2)}, u32[]{:S(2)}) collective-permute-start(f32[256,512]{1,0:T(8,128)S(1)} %get-tuple-element.107), channel_id=1, source_target_pairs={{0,8},{8,0},{16,24},{24,16},{32,40},{40,32},{48,56},{56,48},{64,72... | collective-permute-start | bytes 1572872 | tf_op jit(solution)/shard_map/ppermute | solution.py:60
  29.2 8.0 %collective-permute-start.20 = (f32[256,512]{1,0:T(8,128)S(1)}, f32[256,512]{1,0:T(8,128)S(1)}, u32[]{:S(2)}, u32[]{:S(2)}) collective-permute-start(f32[256,512]{1,0:T(8,128)S(1)} %get-tuple-element.98), channel_id=1, source_target_pairs={{0,8},{8,0},{16,24},{24,16},{32,40},{40,32},{48,56},{56,48},{64,72... | collective-permute-start | bytes 1572872 | tf_op jit(solution)/shard_map/ppermute | solution.py:60
  31.8 7.1 %collective-permute-start.19 = (f32[256,512]{1,0:T(8,128)S(1)}, f32[256,512]{1,0:T(8,128)S(1)}, u32[]{:S(2)}, u32[]{:S(2)}) collective-permute-start(f32[256,512]{1,0:T(8,128)S(1)} %get-tuple-element.96), channel_id=1, source_target_pairs={{0,8},{8,0},{16,24},{24,16},{32,40},{40,32},{48,56},{56,48},{64,72... | collective-permute-start | bytes 1572872 | tf_op jit(solution)/shard_map/ppermute | solution.py:60
  32.4 8.5 %collective-permute-start.5 = (f32[264,512]{1,0:T(8,128)S(1)}, f32[264,512]{1,0:T(8,128)S(1)}, u32[]{:S(2)}, u32[]{:S(2)}) collective-permute-start(f32[264,512]{1,0:T(8,128)S(1)} %get-tuple-element.71), channel_id=1, source_target_pairs={{0,8},{8,0},{16,24},{24,16},{32,40},{40,32},{48,56},{56,48},{64,72... | collective-permute-start | bytes 1622024 | tf_op jit(solution)/shard_map/ppermute | solution.py:60
  33.8 6.6 %collective-permute-start.15 = (f32[256,512]{1,0:T(8,128)S(1)}, f32[256,512]{1,0:T(8,128)S(1)}, u32[]{:S(2)}, u32[]{:S(2)}) collective-permute-start(f32[256,512]{1,0:T(8,128)S(1)} %get-tuple-element.90), channel_id=1, source_target_pairs={{0,8},{8,0},{16,24},{24,16},{32,40},{40,32},{48,56},{56,48},{64,72... | collective-permute-start | bytes 1572872 | tf_op jit(solution)/shard_map/ppermute | solution.py:60
  35.7 9.4 %collective-permute-start.14 = (f32[256,512]{1,0:T(8,128)S(1)}, f32[256,512]{1,0:T(8,128)S(1)}, u32[]{:S(2)}, u32[]{:S(2)}) collective-permute-start(f32[256,512]{1,0:T(8,128)S(1)} %get-tuple-element.88), channel_id=1, source_target_pairs={{0,8},{8,0},{16,24},{24,16},{32,40},{40,32},{48,56},{56,48},{64,72... | collective-permute-start | bytes 1572872 | tf_op jit(solution)/shard_map/ppermute | solution.py:60
  37.2 8.8 %collective-permute-start.10 = (f32[256,512]{1,0:T(8,128)S(1)}, f32[256,512]{1,0:T(8,128)S(1)}, u32[]{:S(2)}, u32[]{:S(2)}) collective-permute-start(f32[256,512]{1,0:T(8,128)S(1)} %get-tuple-element.79), channel_id=1, source_target_pairs={{0,8},{8,0},{16,24},{24,16},{32,40},{40,32},{48,56},{56,48},{64,72... | collective-permute-start | bytes 1572872 | tf_op jit(solution)/shard_map/ppermute | solution.py:60
  38.9 7.2 %collective-permute-start.9 = (f32[256,512]{1,0:T(8,128)S(1)}, f32[256,512]{1,0:T(8,128)S(1)}, u32[]{:S(2)}, u32[]{:S(2)}) collective-permute-start(f32[256,512]{1,0:T(8,128)S(1)} %get-tuple-element.77), channel_id=1, source_target_pairs={{0,8},{8,0},{16,24},{24,16},{32,40},{40,32},{48,56},{56,48},{64,72... | collective-permute-start | bytes 1572872 | tf_op jit(solution)/shard_map/ppermute | solution.py:60
  40.4 5.9 %collective-permute-start.4 = (f32[256,512]{1,0:T(8,128)S(1)}, f32[256,512]{1,0:T(8,128)S(1)}, u32[]{:S(2)}, u32[]{:S(2)}) collective-permute-start(f32[256,512]{1,0:T(8,128)S(1)} %get-tuple-element.66), channel_id=1, source_target_pairs={{0,8},{8,0},{16,24},{24,16},{32,40},{40,32},{48,56},{56,48},{64,72... | collective-permute-start | bytes 1572872 | tf_op jit(solution)/shard_map/ppermute | solution.py:60
  41.0 16.9 %collective-permute-start.31 = (f32[256,512]{1,0:T(8,128)S(1)}, f32[256,512]{1,0:T(8,128)S(1)}, u32[]{:S(2)}, u32[]{:S(2)}) collective-permute-start(f32[256,512]{1,0:T(8,128)S(1)} %meet.11), channel_id=1, source_target_pairs={{0,96},{8,104},{16,112},{24,120},{32,64},{40,72},{48,80},{56,88},{... | collective-permute-start | bytes 1572872 | tf_op jit(solution)/shard_map/ppermute | solution.py:60
  45.1 14.1 %collective-permute-start.6 = (f32[264,512]{1,0:T(8,128)S(1)}, f32[264,512]{1,0:T(8,128)S(1)}, u32[]{:S(2)}, u32[]{:S(2)}) collective-permute-start(f32[264,512]{1,0:T(8,128)S(1)} %meet.6.refs_3_), channel_id=1, source_target_pairs={{0,16},{8,24},{16,0},{24,8},{32,48},{40,56},{48,32},{56,40},{64,80... | collective-permute-start | bytes 1622024 | tf_op jit(solution)/shard_map/ppermute | solution.py:60
  46.0 22.5 %collective-permute-start.26 = (f32[256,512]{1,0:T(8,128)S(1)}, f32[256,512]{1,0:T(8,128)S(1)}, u32[]{:S(2)}, u32[]{:S(2)}) collective-permute-start(f32[256,512]{1,0:T(8,128)S(1)} %meet.10), channel_id=1, source_target_pairs={{0,96},{8,104},{16,112},{24,120},{32,64},{40,72},{48,80},{56,88},{... | collective-permute-start | bytes 1572872 | tf_op jit(solution)/shard_map/ppermute | solution.py:60
  46.1 22.5 %collective-permute-start.21 = (f32[256,512]{1,0:T(8,128)S(1)}, f32[256,512]{1,0:T(8,128)S(1)}, u32[]{:S(2)}, u32[]{:S(2)}) collective-permute-start(f32[256,512]{1,0:T(8,128)S(1)} %meet.9), channel_id=1, source_target_pairs={{0,32},{8,40},{16,48},{24,56},{32,0},{40,8},{48,16},{56,24},{64,96... | collective-permute-start | bytes 1572872 | tf_op jit(solution)/shard_map/ppermute | solution.py:60
  46.3 24.7 %collective-permute-start.16 = (f32[256,512]{1,0:T(8,128)S(1)}, f32[256,512]{1,0:T(8,128)S(1)}, u32[]{:S(2)}, u32[]{:S(2)}) collective-permute-start(f32[256,512]{1,0:T(8,128)S(1)} %meet.8), channel_id=1, source_target_pairs={{0,32},{8,40},{16,48},{24,56},{32,0},{40,8},{48,16},{56,24},{64,96... | collective-permute-start | bytes 1572872 | tf_op jit(solution)/shard_map/ppermute | solution.py:60
  57.8 16.5 %collective-permute-start.11 = (f32[256,512]{1,0:T(8,128)S(1)}, f32[256,512]{1,0:T(8,128)S(1)}, u32[]{:S(2)}, u32[]{:S(2)}) collective-permute-start(f32[256,512]{1,0:T(8,128)S(1)} %meet.7), channel_id=1, source_target_pairs={{0,16},{8,24},{16,0},{24,8},{32,48},{40,56},{48,32},{56,40},{64,80... | collective-permute-start | bytes 1572872 | tf_op jit(solution)/shard_map/ppermute | solution.py:60
  59.2 19.0 %collective-permute-start.32 = (f32[128,512]{1,0:T(8,128)S(1)}, f32[128,512]{1,0:T(8,128)S(1)}, u32[]{:S(2)}, u32[]{:S(2)}) collective-permute-start(f32[128,512]{1,0:T(8,128)S(1)} %get-tuple-element.119), channel_id=1, source_target_pairs={{0,16},{8,24},{16,0},{24,8},{32,48},{40,56},{48,32},{56,40},{64,80... | collective-permute-start | bytes 786440 | tf_op jit(solution)/shard_map/ppermute | solution.py:60
  68.5 9.8 %collective-permute-start.7 = (f32[136,512]{1,0:T(8,128)S(1)}, f32[136,512]{1,0:T(8,128)S(1)}, u32[]{:S(2)}, u32[]{:S(2)}) collective-permute-start(f32[136,512]{1,0:T(8,128)S(1)} %get-tuple-element.73), channel_id=1, source_target_pairs={{0,32},{8,40},{16,48},{24,56},{32,0},{40,8},{48,16},{56,24},{64,96... | collective-permute-start | bytes 835592 | tf_op jit(solution)/shard_map/ppermute | solution.py:60
  68.6 13.2 %collective-permute-start.27 = (f32[128,512]{1,0:T(8,128)S(1)}, f32[128,512]{1,0:T(8,128)S(1)}, u32[]{:S(2)}, u32[]{:S(2)}) collective-permute-start(f32[128,512]{1,0:T(8,128)S(1)} %get-tuple-element.111), channel_id=1, source_target_pairs={{0,16},{8,24},{16,0},{24,8},{32,48},{40,56},{48,32},{56,40},{64,80... | collective-permute-start | bytes 786440 | tf_op jit(solution)/shard_map/ppermute | solution.py:60
  71.0 13.5 %collective-permute-start.22 = (f32[128,512]{1,0:T(8,128)S(1)}, f32[128,512]{1,0:T(8,128)S(1)}, u32[]{:S(2)}, u32[]{:S(2)}) collective-permute-start(f32[128,512]{1,0:T(8,128)S(1)} %get-tuple-element.100), channel_id=1, source_target_pairs={{0,96},{8,104},{16,112},{24,120},{32,64},{40,72},{48,80},{56,88},{... | collective-permute-start | bytes 786440 | tf_op jit(solution)/shard_map/ppermute | solution.py:60
  74.3 11.0 %collective-permute-start.17 = (f32[128,512]{1,0:T(8,128)S(1)}, f32[128,512]{1,0:T(8,128)S(1)}, u32[]{:S(2)}, u32[]{:S(2)}) collective-permute-start(f32[128,512]{1,0:T(8,128)S(1)} %get-tuple-element.92), channel_id=1, source_target_pairs={{0,96},{8,104},{16,112},{24,120},{32,64},{40,72},{48,80},{56,88},{... | collective-permute-start | bytes 786440 | tf_op jit(solution)/shard_map/ppermute | solution.py:60
  78.3 9.2 %collective-permute-start.12 = (f32[128,512]{1,0:T(8,128)S(1)}, f32[128,512]{1,0:T(8,128)S(1)}, u32[]{:S(2)}, u32[]{:S(2)}) collective-permute-start(f32[128,512]{1,0:T(8,128)S(1)} %get-tuple-element.81), channel_id=1, source_target_pairs={{0,32},{8,40},{16,48},{24,56},{32,0},{40,8},{48,16},{56,24},{64,96... | collective-permute-start | bytes 786440 | tf_op jit(solution)/shard_map/ppermute | solution.py:60
  78.3 9.2 %collective-permute-start.33 = (f32[64,512]{1,0:T(8,128)S(1)}, f32[64,512]{1,0:T(8,128)S(1)}, u32[]{:S(2)}, u32[]{:S(2)}) collective-permute-start(f32[64,512]{1,0:T(8,128)S(1)} %get-tuple-element.121), channel_id=1, source_target_pairs={{0,32},{8,40},{16,48},{24,56},{32,0},{40,8},{48,16},{56,24},{64,96... | collective-permute-start | bytes 393224 | tf_op jit(solution)/shard_map/ppermute | solution.py:60
  81.8 12.0 %collective-permute-start.8 = (f32[72,512]{1,0:T(8,128)S(1)}, f32[72,512]{1,0:T(8,128)S(1)}, u32[]{:S(2)}, u32[]{:S(2)}) collective-permute-start(f32[72,512]{1,0:T(8,128)S(1)} %get-tuple-element.75), channel_id=1, source_target_pairs={{0,96},{8,104},{16,112},{24,120},{32,64},{40,72},{48,80},{56,88},{... | collective-permute-start | bytes 442376 | tf_op jit(solution)/shard_map/ppermute | solution.py:60
  84.6 6.3 %collective-permute-start.28 = (f32[64,512]{1,0:T(8,128)S(1)}, f32[64,512]{1,0:T(8,128)S(1)}, u32[]{:S(2)}, u32[]{:S(2)}) collective-permute-start(f32[64,512]{1,0:T(8,128)S(1)} %get-tuple-element.113), channel_id=1, source_target_pairs={{0,32},{8,40},{16,48},{24,56},{32,0},{40,8},{48,16},{56,24},{64,96... | collective-permute-start | bytes 393224 | tf_op jit(solution)/shard_map/ppermute | solution.py:60
  85.3 5.5 %collective-permute-start.23 = (f32[64,512]{1,0:T(8,128)S(1)}, f32[64,512]{1,0:T(8,128)S(1)}, u32[]{:S(2)}, u32[]{:S(2)}) collective-permute-start(f32[64,512]{1,0:T(8,128)S(1)} %get-tuple-element.102), channel_id=1, source_target_pairs={{0,16},{8,24},{16,0},{24,8},{32,48},{40,56},{48,32},{56,40},{64,80... | collective-permute-start | bytes 393224 | tf_op jit(solution)/shard_map/ppermute | solution.py:60
  87.4 5.0 %collective-permute-start.18 = (f32[64,512]{1,0:T(8,128)S(1)}, f32[64,512]{1,0:T(8,128)S(1)}, u32[]{:S(2)}, u32[]{:S(2)}) collective-permute-start(f32[64,512]{1,0:T(8,128)S(1)} %get-tuple-element.94), channel_id=1, source_target_pairs={{0,16},{8,24},{16,0},{24,8},{32,48},{40,56},{48,32},{56,40},{64,80... | collective-permute-start | bytes 393224 | tf_op jit(solution)/shard_map/ppermute | solution.py:60
  87.6 6.3 %collective-permute-start.13 = (f32[64,512]{1,0:T(8,128)S(1)}, f32[64,512]{1,0:T(8,128)S(1)}, u32[]{:S(2)}, u32[]{:S(2)}) collective-permute-start(f32[64,512]{1,0:T(8,128)S(1)} %get-tuple-element.83), channel_id=1, source_target_pairs={{0,96},{8,104},{16,112},{24,120},{32,64},{40,72},{48,80},{56,88},{... | collective-permute-start | bytes 393224 | tf_op jit(solution)/shard_map/ppermute | solution.py:60

commit v7 on v6

--- a/solution.py
+++ b/solution.py
@@ -177,25 +177,33 @@
     blocks, samples = total_out.shape[:2]
     words = samples // BITS
 
-    def copies(block):
+    pieces = [(block, 0, words) for block in range(blocks - 1)]
+    pieces += [(blocks - 1, at, words // 2) for at in (0, words // 2)]
+
+    def copies(piece):
+        block, at, count = pieces[piece]
         lanes = pl.ds((first + block) * LANES, LANES)
+        rows = pl.ds(at * BITS, count * BITS)
         return [
-            pltpu.make_async_copy(ref.at[:, lanes], buffer.at[spot, block], sems.at[spot, block])
+            pltpu.make_async_copy(
+                ref.at[rows, lanes], buffer.at[spot, block, rows], sems.at[spot, piece]
+            )
             for spot, ref in enumerate((total_hbm, one_hbm, two_hbm))
         ]
 
-    for block in range(blocks):
-        for copy in copies(block):
+    for piece in range(len(pieces)):
+        for copy in copies(piece):
             copy.start()
-    for block in range(blocks):
-        for copy in copies(block):
+    for piece, (block, at, count) in enumerate(pieces):
+        for copy in copies(piece):
             copy.wait()
 
-        def step(bit, sums, block=block):
+        def step(bit, sums, block=block, at=at, count=count):
             log_sum, log_sq = sums
             for half in range(2):
-                rows = pl.ds(bit + half * HALF, words, stride=BITS)
-                spot = pl.ds(pl.multiple_of((2 * bit + half) * words, words), words)
+                rows = pl.ds(bit + half * HALF + at * BITS, count, stride=BITS)
+                start = (2 * bit + half) * words + at
+                spot = pl.ds(pl.multiple_of(start, count), count)
                 log_total = jnp.log(buffer[0, block, rows, :].astype(jnp.float32) + 1.0)
                 one_plus = buffer[1, block, rows, :].astype(jnp.float32) + 1.0
                 two_plus = buffer[2, block, rows, :].astype(jnp.float32) + 1.0
@@ -204,7 +212,7 @@
                 total_out[block, spot, :] = log_total.astype(jnp.bfloat16)
                 weighted_out[block, spot, :] = (weight * log_ratio).astype(jnp.bfloat16)
                 weight_out[block, spot, :] = weight.astype(jnp.bfloat16)
-                folded = log_total.reshape(words // 8, 8, LANES)
+                folded = log_total.reshape(count // 8, 8, LANES)
                 log_sum = log_sum + jnp.sum(folded, axis=0)
                 log_sq = log_sq + jnp.sum(folded * folded, axis=0)
             return log_sum, log_sq
@@ -212,9 +220,9 @@
         blank = jnp.zeros((8, LANES), jnp.float32)
         sums = lax.fori_loop(0, HALF, step, (blank, blank), unroll=3)
         for kind in range(2):
-            margin_ref[kind : kind + 1, block * LANES : (block + 1) * LANES] = jnp.sum(
-                sums[kind], axis=0, keepdims=True
-            )
+            spot = (slice(kind, kind + 1), slice(block * LANES, (block + 1) * LANES))
+            total = jnp.sum(sums[kind], axis=0, keepdims=True)
+            margin_ref[spot] = total + margin_ref[spot] if at else total
 
 
 def features(total_counts, allele_one, allele_two, first, blocks, after):
@@ -229,7 +237,7 @@
         out_specs=tuple(whole(4)),
         scratch_shapes=[
             pltpu.VMEM((3, blocks, samples, LANES), jnp.int32),
-            pltpu.SemaphoreType.DMA((3, blocks)),
+            pltpu.SemaphoreType.DMA((3, blocks + 1)),
         ],
         cost_estimate=pl.CostEstimate(
             flops=12_000_000 * width, bytes_accessed=18 * samples * width, transcendentals=0

time: 95.9 us -> 95.8 us (level)
  no operation moved by 1% of the time
where the time goes in v7:
time: 95.8 us; the launch traced here: 95.5 us
  starting transfers between devices  36.2 us (38%)
  Pallas kernels  30.7 us (32%)
  waiting for transfers between devices  27.4 us (29%)
  between operations  1.13 us (1%)
    ppermute x34, starting transfers between devices, swap(): return lax.ppermute(array, axis, [(d, d ^ flip) for d in range(size)])  36.2 us
    ppermute x34, waiting for transfers between devices, swap(): return lax.ppermute(array, axis, [(d, d ^ flip) for d in range(size)])  27.4 us
    pallas_call x12, Pallas kernels, cross(): pl.pallas_call(functools.partial(cross_kernel, spots, part, len(margins))...  15.1 us
    pallas_call x2, Pallas kernels, features(): pl.pallas_call(functools.partial(feature_kernel, first), out_shape=(featu...  10.7 us
    pallas_call x1, Pallas kernels, unpack(): pl.pallas_call(unpack_kernel, out_shape=(design,) * 3 + (jax.ShapeDtypeSt...  2.29 us
  transfers between devices with their start and end apart: 34, of which 9 were waited for; matrix products, arithmetic and copies ran while one was open for 0% of the time, Pallas kernels for 27%

profile of v7, /device:TPU:0, one launch (start us, length us, event | category | flops | bytes accessed | tf_op | source)
XLA Modules:
  0.0 95.5 jit_solution(10900203519613475928)
XLA Ops:
  0.6 3.4 %collective-permute-start = (s32[2,64,128]{2,1,0:T(8,128)}, s32[2,64,128]{2,1,0:T(8,128)S(1)}, u32[]{:S(2)}, u32[]{:S(2)}) collective-permute-start(s32[2,64,128]{2,1,0:T(8,128)} %own_ref.1), channel_id=1, source_target_pairs={{0,1},{1,0},{2,3},{3,2},{4,5},{5,4},{6,7},{7,6},{8,9},{9,8},{10,11... | collective-permute-start | bytes 196616 | tf_op jit(solution)/shard_map/ppermute | solution.py:60
  4.0 3.5 %features.2 = (bf16[2,1920,128]{2,1,0:T(8,128)(2,1)S(1)}, bf16[2,1920,128]{2,1,0:T(8,128)(2,1)S(1)}, bf16[2,1920,128]{2,1,0:T(8,128)(2,1)S(1)}, f32[2,256]{1,0:T(2,128)S(1)}) custom-call(s32[1920,1024]{1,0:T(8,128)} %total_hbm.3, s32[1920,1024]{1,0:T(8,128)} %one_hbm.3, s32[1920,1024]{1,0:T(8,128)} %two_hbm.3), custom_call_target="tpu_custom_call" | custom-call | flops 3072000000 | bytes 8847360 | tf_op jit(solution)/shard_map/features/pallas_call | solution.py:232
  7.5 0.1 pad_add_fusion.where_ref
  7.6 3.1 %collective-permute-start.1 = (s32[4,64,128]{2,1,0:T(8,128)S(1)}, s32[4,64,128]{2,1,0:T(8,128)S(1)}, u32[]{:S(2)}, u32[]{:S(2)}) collective-permute-start(s32[4,64,128]{2,1,0:T(8,128)S(1)} %paired.1.refs_0_), channel_id=1, source_target_pairs={{0,4},{1,5},{2,6},{3,7},{4,0},{5,1},{6,2},{7,3},{8,12},{9,13},{10,... | collective-permute-start | bytes 393224 | tf_op jit(solution)/shard_map/ppermute | solution.py:60
  10.7 0.6 collective-permute-start.2
  11.3 0.6 collective-permute-start.3
  11.9 7.2 %features.3 = (bf16[6,1920,128]{2,1,0:T(8,128)(2,1)S(1)}, bf16[6,1920,128]{2,1,0:T(8,128)(2,1)S(1)}, bf16[6,1920,128]{2,1,0:T(8,128)(2,1)S(1)}, f32[2,768]{1,0:T(2,128)S(1)}) custom-call(s32[1920,1024]{1,0:T(8,128)} %total_hbm.3, s32[1920,1024]{1,0:T(8,128)} %one_hbm.3, s32[1920,1024]{1,0:T(8,128)} %two_hbm.3, ...), custom_call_target="tpu_custom_call" | custom-call | flops 9216000000 | bytes 26542080 | tf_op jit(solution)/shard_map/features/pallas_call | solution.py:232
  19.1 2.3 %unpack.1 = (bf16[1024,1920]{1,0:T(8,128)(2,1)S(1)}, bf16[1024,1920]{1,0:T(8,128)(2,1)S(1)}, bf16[1024,1920]{1,0:T(8,128)(2,1)S(1)}, f32[8,2,128]{2,1,0:T(2,128)S(1)}) custom-call(s32[2]{0:T(128)S(1)} %pad_add_fusion.where_ref, s32[4,64,128]{2,1,0:T(8,128)S(1)} %paired.1.refs_0_, s32[4,64,128]{2,1,0:T(8,128)S(1)} %collective-permute-done.1.refs_1_, ...), custom_call_target="tpu_custom_call" | custom-call | flops 6000000000 | bytes 11796480 | tf_op jit(solution)/shard_map/unpack/pallas_call | solution.py:143
  21.4 1.3 %cross.23 = (f32[256,512]{1,0:T(8,128)S(1)}, f32[256,512]{1,0:T(8,128)S(1)}) custom-call(bf16[1024,1920]{1,0:T(8,128)(2,1)S(1)} %get-tuple-element.103.design_ref, bf16[2,1920,128]{2,1,0:T(8,128)(2,1)S(1)} %get-tuple-element.104.refs_0_, bf16[6,1920,128]{2,1,0:T(8,128)(2,1)S(1)} %get-tuple-element.105.refs_1_), custom_call_target="tpu_custom_call" | custom-call | flops 1006632960 | bytes 5898240 | tf_op jit(solution)/shard_map/cross/pallas_call | solution.py:298
  22.7 0.1 collective-permute-start.30
  22.7 1.3 %cross.22 = (f32[256,512]{1,0:T(8,128)S(1)}, f32[256,512]{1,0:T(8,128)S(1)}) custom-call(bf16[1024,1920]{1,0:T(8,128)(2,1)S(1)} %get-tuple-element.103.design_ref, bf16[2,1920,128]{2,1,0:T(8,128)(2,1)S(1)} %get-tuple-element.104.refs_0_, bf16[6,1920,128]{2,1,0:T(8,128)(2,1)S(1)} %get-tuple-element.105.refs_1_), custom_call_target="tpu_custom_call" | custom-call | flops 1006632960 | bytes 5898240 | tf_op jit(solution)/shard_map/cross/pallas_call | solution.py:298
  24.0 0.6 collective-permute-start.29
  24.6 1.3 %cross.21 = (f32[256,512]{1,0:T(8,128)S(1)}, f32[256,512]{1,0:T(8,128)S(1)}) custom-call(bf16[1024,1920]{1,0:T(8,128)(2,1)S(1)} %get-tuple-element.103.design_ref, bf16[2,1920,128]{2,1,0:T(8,128)(2,1)S(1)} %get-tuple-element.104.refs_0_, bf16[6,1920,128]{2,1,0:T(8,128)(2,1)S(1)} %get-tuple-element.105.refs_1_), custom_call_target="tpu_custom_call" | custom-call | flops 1006632960 | bytes 5898240 | tf_op jit(solution)/shard_map/cross/pallas_call | solution.py:298
  25.8 0.1 collective-permute-start.25
  25.9 1.3 %cross.20 = (f32[256,512]{1,0:T(8,128)S(1)}, f32[256,512]{1,0:T(8,128)S(1)}) custom-call(bf16[1024,1920]{1,0:T(8,128)(2,1)S(1)} %get-tuple-element.103.design_ref, bf16[2,1920,128]{2,1,0:T(8,128)(2,1)S(1)} %get-tuple-element.104.refs_0_, bf16[6,1920,128]{2,1,0:T(8,128)(2,1)S(1)} %get-tuple-element.105.refs_1_), custom_call_target="tpu_custom_call" | custom-call | flops 1006632960 | bytes 5898240 | tf_op jit(solution)/shard_map/cross/pallas_call | solution.py:298
  27.2 0.6 collective-permute-start.24
  27.8 1.3 %cross.19 = (f32[256,512]{1,0:T(8,128)S(1)}, f32[256,512]{1,0:T(8,128)S(1)}) custom-call(bf16[1024,1920]{1,0:T(8,128)(2,1)S(1)} %get-tuple-element.84.design_ref, bf16[2,1920,128]{2,1,0:T(8,128)(2,1)S(1)} %get-tuple-element.85.refs_0_, bf16[6,1920,128]{2,1,0:T(8,128)(2,1)S(1)} %get-tuple-element.86.refs_1_), custom_call_target="tpu_custom_call" | custom-call | flops 1006632960 | bytes 5898240 | tf_op jit(solution)/shard_map/cross/pallas_call | solution.py:298
  29.0 0.1 collective-permute-start.20
  29.1 1.3 %cross.18 = (f32[256,512]{1,0:T(8,128)S(1)}, f32[256,512]{1,0:T(8,128)S(1)}) custom-call(bf16[1024,1920]{1,0:T(8,128)(2,1)S(1)} %get-tuple-element.84.design_ref, bf16[2,1920,128]{2,1,0:T(8,128)(2,1)S(1)} %get-tuple-element.85.refs_0_, bf16[6,1920,128]{2,1,0:T(8,128)(2,1)S(1)} %get-tuple-element.86.refs_1_), custom_call_target="tpu_custom_call" | custom-call | flops 1006632960 | bytes 5898240 | tf_op jit(solution)/shard_map/cross/pallas_call | solution.py:298
  30.4 1.3 %cross.13 = (f32[264,512]{1,0:T(8,128)S(1)}, f32[264,512]{1,0:T(8,128)S(1)}) custom-call(bf16[1024,1920]{1,0:T(8,128)(2,1)S(1)} %get-tuple-element.62.design_ref, bf16[2,1920,128]{2,1,0:T(8,128)(2,1)S(1)} %get-tuple-element.63.refs_0_, bf16[6,1920,128]{2,1,0:T(8,128)(2,1)S(1)} %get-tuple-element.64.refs_1_, f32[2,256]{1,0:T(2,128)S(1)} %get-tuple-element.67.refs_2_, ...), custom_call_target="tpu_custom_call" | custom-call | flops 1006632960 | bytes 5898240 | tf_op jit(solution)/shard_map/cross/pallas_call | solution.py:298
  31.7 0.6 collective-permute-start.19
  32.3 0.1 collective-permute-start.5
  32.4 1.3 %cross.17 = (f32[256,512]{1,0:T(8,128)S(1)}, f32[256,512]{1,0:T(8,128)S(1)}) custom-call(bf16[1024,1920]{1,0:T(8,128)(2,1)S(1)} %get-tuple-element.84.design_ref, bf16[2,1920,128]{2,1,0:T(8,128)(2,1)S(1)} %get-tuple-element.85.refs_0_, bf16[6,1920,128]{2,1,0:T(8,128)(2,1)S(1)} %get-tuple-element.86.refs_1_), custom_call_target="tpu_custom_call" | custom-call | flops 1006632960 | bytes 5898240 | tf_op jit(solution)/shard_map/cross/pallas_call | solution.py:298
  33.6 0.7 collective-permute-start.15
  34.3 1.3 %cross.16 = (f32[256,512]{1,0:T(8,128)S(1)}, f32[256,512]{1,0:T(8,128)S(1)}) custom-call(bf16[1024,1920]{1,0:T(8,128)(2,1)S(1)} %get-tuple-element.84.design_ref, bf16[2,1920,128]{2,1,0:T(8,128)(2,1)S(1)} %get-tuple-element.85.refs_0_, bf16[6,1920,128]{2,1,0:T(8,128)(2,1)S(1)} %get-tuple-element.86.refs_1_), custom_call_target="tpu_custom_call" | custom-call | flops 1006632960 | bytes 5898240 | tf_op jit(solution)/shard_map/cross/pallas_call | solution.py:298
  35.6 0.2 collective-permute-start.14
  35.8 1.3 %cross.15 = (f32[256,512]{1,0:T(8,128)S(1)}, f32[256,512]{1,0:T(8,128)S(1)}) custom-call(bf16[1024,1920]{1,0:T(8,128)(2,1)S(1)} %get-tuple-element.62.design_ref, bf16[2,1920,128]{2,1,0:T(8,128)(2,1)S(1)} %get-tuple-element.63.refs_0_, bf16[6,1920,128]{2,1,0:T(8,128)(2,1)S(1)} %get-tuple-element.64.refs_1_), custom_call_target="tpu_custom_call" | custom-call | flops 1006632960 | bytes 5898240 | tf_op jit(solution)/shard_map/cross/pallas_call | solution.py:298
  37.0 0.5 collective-permute-start.10
  37.5 1.3 %cross.14 = (f32[256,512]{1,0:T(8,128)S(1)}, f32[256,512]{1,0:T(8,128)S(1)}) custom-call(bf16[1024,1920]{1,0:T(8,128)(2,1)S(1)} %get-tuple-element.62.design_ref, bf16[2,1920,128]{2,1,0:T(8,128)(2,1)S(1)} %get-tuple-element.63.refs_0_, bf16[6,1920,128]{2,1,0:T(8,128)(2,1)S(1)} %get-tuple-element.64.refs_1_), custom_call_target="tpu_custom_call" | custom-call | flops 1006632960 | bytes 5898240 | tf_op jit(solution)/shard_map/cross/pallas_call | solution.py:298
  38.8 0.2 collective-permute-start.9
  39.0 1.3 %cross.12 = (f32[256,512]{1,0:T(8,128)S(1)}, f32[256,512]{1,0:T(8,128)S(1)}) custom-call(bf16[1024,1920]{1,0:T(8,128)(2,1)S(1)} %get-tuple-element.62.design_ref, bf16[2,1920,128]{2,1,0:T(8,128)(2,1)S(1)} %get-tuple-element.63.refs_0_, bf16[6,1920,128]{2,1,0:T(8,128)(2,1)S(1)} %get-tuple-element.64.refs_1_), custom_call_target="tpu_custom_call" | custom-call | flops 1006632960 | bytes 5898240 | tf_op jit(solution)/shard_map/cross/pallas_call | solution.py:298
  40.2 0.5 collective-permute-start.4
  40.8 4.1 %collective-permute-start.31 = (f32[256,512]{1,0:T(8,128)S(1)}, f32[256,512]{1,0:T(8,128)S(1)}, u32[]{:S(2)}, u32[]{:S(2)}) collective-permute-start(f32[256,512]{1,0:T(8,128)S(1)} %meet.11), channel_id=1, source_target_pairs={{0,96},{8,104},{16,112},{24,120},{32,64},{40,72},{48,80},{56,88},{... | collective-permute-start | bytes 1572872 | tf_op jit(solution)/shard_map/ppermute | solution.py:60
  45.0 0.9 collective-permute-start.6
  45.9 0.1 collective-permute-start.26
  46.1 0.1 collective-permute-start.21
  46.3 2.1 %collective-permute-start.16 = (f32[256,512]{1,0:T(8,128)S(1)}, f32[256,512]{1,0:T(8,128)S(1)}, u32[]{:S(2)}, u32[]{:S(2)}) collective-permute-start(f32[256,512]{1,0:T(8,128)S(1)} %meet.8), channel_id=1, source_target_pairs={{0,32},{8,40},{16,48},{24,56},{32,0},{40,8},{48,16},{56,24},{64,96... | collective-permute-start | bytes 1572872 | tf_op jit(solution)/shard_map/ppermute | solution.py:60
  48.4 9.3 %collective-permute-done.31.refs_2_ = f32[256,512]{1,0:T(8,128)S(1)} collective-permute-done((f32[256,512]{1,0:T(8,128)S(1)}, f32[256,512]{1,0:T(8,128)S(1)}, u32[]{:S(2)}, u32[]{:S(2)}) %collective-permute-start.31) | collective-permute-done | bytes 524320 | tf_op jit(solution)/shard_map/ppermute | solution.py:60
  57.7 0.8 collective-permute-start.11
  58.5 0.1 fold.22
  58.6 0.5 collective-permute-done.6.refs_2_.refs_4_
  59.1 0.8 collective-permute-start.32
  59.9 0.1 fold.12
  60.0 8.4 %collective-permute-done.26.refs_2_ = f32[256,512]{1,0:T(8,128)S(1)} collective-permute-done((f32[256,512]{1,0:T(8,128)S(1)}, f32[256,512]{1,0:T(8,128)S(1)}, u32[]{:S(2)}, u32[]{:S(2)}) %collective-permute-start.26) | collective-permute-done | bytes 524320 | tf_op jit(solution)/shard_map/ppermute | solution.py:60
  68.3 0.1 fold.20
  68.5 0.9 collective-permute-start.27
  69.3 0.1 fold.18
  69.4 1.6 %collective-permute-done.16.refs_2_ = f32[256,512]{1,0:T(8,128)S(1)} collective-permute-done((f32[256,512]{1,0:T(8,128)S(1)}, f32[256,512]{1,0:T(8,128)S(1)}, u32[]{:S(2)}, u32[]{:S(2)}) %collective-permute-start.16) | collective-permute-done | bytes 524320 | tf_op jit(solution)/shard_map/ppermute | solution.py:60
  71.1 3.2 %collective-permute-start.22 = (f32[128,512]{1,0:T(8,128)S(1)}, f32[128,512]{1,0:T(8,128)S(1)}, u32[]{:S(2)}, u32[]{:S(2)}) collective-permute-start(f32[128,512]{1,0:T(8,128)S(1)} %get-tuple-element.100), channel_id=1, source_target_pairs={{0,96},{8,104},{16,112},{24,120},{32,64},{40,72},{48,80},{56,88},{... | collective-permute-start | bytes 786440 | tf_op jit(solution)/shard_map/ppermute | solution.py:60
  74.3 0.1 fold.16
  74.4 1.3 %collective-permute-start.17 = (f32[128,512]{1,0:T(8,128)S(1)}, f32[128,512]{1,0:T(8,128)S(1)}, u32[]{:S(2)}, u32[]{:S(2)}) collective-permute-start(f32[128,512]{1,0:T(8,128)S(1)} %get-tuple-element.92), channel_id=1, source_target_pairs={{0,96},{8,104},{16,112},{24,120},{32,64},{40,72},{48,80},{56,88},{... | collective-permute-start | bytes 786440 | tf_op jit(solution)/shard_map/ppermute | solution.py:60
  75.7 0.1 fold.14
  75.8 2.3 %collective-permute-done.32.refs_1_ = f32[128,512]{1,0:T(8,128)S(1)} collective-permute-done((f32[128,512]{1,0:T(8,128)S(1)}, f32[128,512]{1,0:T(8,128)S(1)}, u32[]{:S(2)}, u32[]{:S(2)}) %collective-permute-start.32) | collective-permute-done | bytes 262176 | tf_op jit(solution)/shard_map/ppermute | solution.py:60
  78.2 2.1 %collective-permute-start.33 = (f32[64,512]{1,0:T(8,128)S(1)}, f32[64,512]{1,0:T(8,128)S(1)}, u32[]{:S(2)}, u32[]{:S(2)}) collective-permute-start(f32[64,512]{1,0:T(8,128)S(1)} %get-tuple-element.121), channel_id=1, source_target_pairs={{0,32},{8,40},{16,48},{24,56},{32,0},{40,8},{48,16},{56,24},{64,96... | collective-permute-start | bytes 393224 | tf_op jit(solution)/shard_map/ppermute | solution.py:60
  80.3 1.4 %collective-permute-done.27.refs_1_ = f32[128,512]{1,0:T(8,128)S(1)} collective-permute-done((f32[128,512]{1,0:T(8,128)S(1)}, f32[128,512]{1,0:T(8,128)S(1)}, u32[]{:S(2)}, u32[]{:S(2)}) %collective-permute-start.27) | collective-permute-done | bytes 262176 | tf_op jit(solution)/shard_map/ppermute | solution.py:60
  81.7 2.7 %collective-permute-start.8 = (f32[72,512]{1,0:T(8,128)S(1)}, f32[72,512]{1,0:T(8,128)S(1)}, u32[]{:S(2)}, u32[]{:S(2)}) collective-permute-start(f32[72,512]{1,0:T(8,128)S(1)} %get-tuple-element.75), channel_id=1, source_target_pairs={{0,96},{8,104},{16,112},{24,120},{32,64},{40,72},{48,80},{56,88},{... | collective-permute-start | bytes 442376 | tf_op jit(solution)/shard_map/ppermute | solution.py:60
  84.4 0.1 collective-permute-start.28
  84.5 0.9 collective-permute-done.17.refs_1_
  85.4 1.7 %collective-permute-start.23 = (f32[64,512]{1,0:T(8,128)S(1)}, f32[64,512]{1,0:T(8,128)S(1)}, u32[]{:S(2)}, u32[]{:S(2)}) collective-permute-start(f32[64,512]{1,0:T(8,128)S(1)} %get-tuple-element.102), channel_id=1, source_target_pairs={{0,16},{8,24},{16,0},{24,8},{32,48},{40,56},{48,32},{56,40},{64,80... | collective-permute-start | bytes 393224 | tf_op jit(solution)/shard_map/ppermute | solution.py:60
  87.2 0.4 collective-permute-start.18
  87.6 3.3 %collective-permute-start.13 = (f32[64,512]{1,0:T(8,128)S(1)}, f32[64,512]{1,0:T(8,128)S(1)}, u32[]{:S(2)}, u32[]{:S(2)}) collective-permute-start(f32[64,512]{1,0:T(8,128)S(1)} %get-tuple-element.83), channel_id=1, source_target_pairs={{0,96},{8,104},{16,112},{24,120},{32,64},{40,72},{48,80},{56,88},{... | collective-permute-start | bytes 393224 | tf_op jit(solution)/shard_map/ppermute | solution.py:60
  90.9 1.3 %collective-permute-done.18.refs_5_ = f32[64,512]{1,0:T(8,128)S(1)} collective-permute-done((f32[64,512]{1,0:T(8,128)S(1)}, f32[64,512]{1,0:T(8,128)S(1)}, u32[]{:S(2)}, u32[]{:S(2)}) %collective-permute-start.18) | collective-permute-done | bytes 131104 | tf_op jit(solution)/shard_map/ppermute | solution.py:60
  92.2 1.6 %collective-permute-done.13.refs_3_ = f32[64,512]{1,0:T(8,128)S(1)} collective-permute-done((f32[64,512]{1,0:T(8,128)S(1)}, f32[64,512]{1,0:T(8,128)S(1)}, u32[]{:S(2)}, u32[]{:S(2)}) %collective-permute-start.13) | collective-permute-done | bytes 131104 | tf_op jit(solution)/shard_map/ppermute | solution.py:60
  93.9 1.5 %finish.1 = (f32[64,1024]{1,0:T(8,128)}, f32[64,1024]{1,0:T(8,128)}) custom-call(s32[2]{0:T(128)S(1)} %pad_add_fusion.where_ref, f32[72,512]{1,0:T(8,128)S(1)} %get-tuple-element.74.refs_0_, f32[72,512]{1,0:T(8,128)S(1)} %collective-permute-done.8.refs_1_, f32[64,512]{1,0:T(8,128)S(1)} %get-tuple-element.82.refs_2_, ...), custom_call_target="tpu_custom_call" | custom-call | tf_op jit(solution)/shard_map/finish/pallas_call | solution.py:416
  (42 shorter events, 0.6 us)
Async XLA Ops:
  0.6 7.0 %collective-permute-start = (s32[2,64,128]{2,1,0:T(8,128)}, s32[2,64,128]{2,1,0:T(8,128)S(1)}, u32[]{:S(2)}, u32[]{:S(2)}) collective-permute-start(s32[2,64,128]{2,1,0:T(8,128)} %own_ref.1), channel_id=1, source_target_pairs={{0,1},{1,0},{2,3},{3,2},{4,5},{5,4},{6,7},{7,6},{8,9},{9,8},{10,11... | collective-permute-start | bytes 196616 | tf_op jit(solution)/shard_map/ppermute | solution.py:60
  4.0 3.6 %copy-start = (s32[2,64,128]{2,1,0:T(8,128)S(1)}, s32[2,64,128]{2,1,0:T(8,128)}, u32[]{:S(2)}) copy-start(s32[2,64,128]{2,1,0:T(8,128)} %own_ref.1) | copy-start | bytes 196612
  7.6 11.4 %collective-permute-start.1 = (s32[4,64,128]{2,1,0:T(8,128)S(1)}, s32[4,64,128]{2,1,0:T(8,128)S(1)}, u32[]{:S(2)}, u32[]{:S(2)}) collective-permute-start(s32[4,64,128]{2,1,0:T(8,128)S(1)} %paired.1.refs_0_), channel_id=1, source_target_pairs={{0,4},{1,5},{2,6},{3,7},{4,0},{5,1},{6,2},{7,3},{8,12},{9,13},{10,... | collective-permute-start | bytes 393224 | tf_op jit(solution)/shard_map/ppermute | solution.py:60
  10.7 8.3 %collective-permute-start.2 = (s32[4,64,128]{2,1,0:T(8,128)S(1)}, s32[4,64,128]{2,1,0:T(8,128)S(1)}, u32[]{:S(2)}, u32[]{:S(2)}) collective-permute-start(s32[4,64,128]{2,1,0:T(8,128)S(1)} %paired.1.refs_0_), channel_id=1, source_target_pairs={{0,2},{1,3},{2,0},{3,1},{4,6},{5,7},{6,4},{7,5},{8,10},{9,11},{10,... | collective-permute-start | bytes 393224 | tf_op jit(solution)/shard_map/ppermute | solution.py:60
  11.3 7.8 %collective-permute-start.3 = (s32[4,64,128]{2,1,0:T(8,128)S(1)}, s32[4,64,128]{2,1,0:T(8,128)S(1)}, u32[]{:S(2)}, u32[]{:S(2)}) collective-permute-start(s32[4,64,128]{2,1,0:T(8,128)S(1)} %paired.1.refs_0_), channel_id=1, source_target_pairs={{0,6},{1,7},{2,4},{3,5},{4,2},{5,3},{6,0},{7,1},{8,14},{9,15},{10,... | collective-permute-start | bytes 393224 | tf_op jit(solution)/shard_map/ppermute | solution.py:60
  22.7 9.0 %collective-permute-start.30 = (f32[256,512]{1,0:T(8,128)S(1)}, f32[256,512]{1,0:T(8,128)S(1)}, u32[]{:S(2)}, u32[]{:S(2)}) collective-permute-start(f32[256,512]{1,0:T(8,128)S(1)} %get-tuple-element.117), channel_id=1, source_target_pairs={{0,8},{8,0},{16,24},{24,16},{32,40},{40,32},{48,56},{56,48},{64,72... | collective-permute-start | bytes 1572872 | tf_op jit(solution)/shard_map/ppermute | solution.py:60
  24.0 8.2 %collective-permute-start.29 = (f32[256,512]{1,0:T(8,128)S(1)}, f32[256,512]{1,0:T(8,128)S(1)}, u32[]{:S(2)}, u32[]{:S(2)}) collective-permute-start(f32[256,512]{1,0:T(8,128)S(1)} %get-tuple-element.115), channel_id=1, source_target_pairs={{0,8},{8,0},{16,24},{24,16},{32,40},{40,32},{48,56},{56,48},{64,72... | collective-permute-start | bytes 1572872 | tf_op jit(solution)/shard_map/ppermute | solution.py:60
  25.8 7.8 %collective-permute-start.25 = (f32[256,512]{1,0:T(8,128)S(1)}, f32[256,512]{1,0:T(8,128)S(1)}, u32[]{:S(2)}, u32[]{:S(2)}) collective-permute-start(f32[256,512]{1,0:T(8,128)S(1)} %get-tuple-element.109), channel_id=1, source_target_pairs={{0,8},{8,0},{16,24},{24,16},{32,40},{40,32},{48,56},{56,48},{64,72... | collective-permute-start | bytes 1572872 | tf_op jit(solution)/shard_map/ppermute | solution.py:60
  27.2 8.4 %collective-permute-start.24 = (f32[256,512]{1,0:T(8,128)S(1)}, f32[256,512]{1,0:T(8,128)S(1)}, u32[]{:S(2)}, u32[]{:S(2)}) collective-permute-start(f32[256,512]{1,0:T(8,128)S(1)} %get-tuple-element.107), channel_id=1, source_target_pairs={{0,8},{8,0},{16,24},{24,16},{32,40},{40,32},{48,56},{56,48},{64,72... | collective-permute-start | bytes 1572872 | tf_op jit(solution)/shard_map/ppermute | solution.py:60
  29.0 8.0 %collective-permute-start.20 = (f32[256,512]{1,0:T(8,128)S(1)}, f32[256,512]{1,0:T(8,128)S(1)}, u32[]{:S(2)}, u32[]{:S(2)}) collective-permute-start(f32[256,512]{1,0:T(8,128)S(1)} %get-tuple-element.98), channel_id=1, source_target_pairs={{0,8},{8,0},{16,24},{24,16},{32,40},{40,32},{48,56},{56,48},{64,72... | collective-permute-start | bytes 1572872 | tf_op jit(solution)/shard_map/ppermute | solution.py:60
  31.7 7.1 %collective-permute-start.19 = (f32[256,512]{1,0:T(8,128)S(1)}, f32[256,512]{1,0:T(8,128)S(1)}, u32[]{:S(2)}, u32[]{:S(2)}) collective-permute-start(f32[256,512]{1,0:T(8,128)S(1)} %get-tuple-element.96), channel_id=1, source_target_pairs={{0,8},{8,0},{16,24},{24,16},{32,40},{40,32},{48,56},{56,48},{64,72... | collective-permute-start | bytes 1572872 | tf_op jit(solution)/shard_map/ppermute | solution.py:60
  32.3 8.5 %collective-permute-start.5 = (f32[264,512]{1,0:T(8,128)S(1)}, f32[264,512]{1,0:T(8,128)S(1)}, u32[]{:S(2)}, u32[]{:S(2)}) collective-permute-start(f32[264,512]{1,0:T(8,128)S(1)} %get-tuple-element.71), channel_id=1, source_target_pairs={{0,8},{8,0},{16,24},{24,16},{32,40},{40,32},{48,56},{56,48},{64,72... | collective-permute-start | bytes 1622024 | tf_op jit(solution)/shard_map/ppermute | solution.py:60
  33.6 6.6 %collective-permute-start.15 = (f32[256,512]{1,0:T(8,128)S(1)}, f32[256,512]{1,0:T(8,128)S(1)}, u32[]{:S(2)}, u32[]{:S(2)}) collective-permute-start(f32[256,512]{1,0:T(8,128)S(1)} %get-tuple-element.90), channel_id=1, source_target_pairs={{0,8},{8,0},{16,24},{24,16},{32,40},{40,32},{48,56},{56,48},{64,72... | collective-permute-start | bytes 1572872 | tf_op jit(solution)/shard_map/ppermute | solution.py:60
  35.6 9.4 %collective-permute-start.14 = (f32[256,512]{1,0:T(8,128)S(1)}, f32[256,512]{1,0:T(8,128)S(1)}, u32[]{:S(2)}, u32[]{:S(2)}) collective-permute-start(f32[256,512]{1,0:T(8,128)S(1)} %get-tuple-element.88), channel_id=1, source_target_pairs={{0,8},{8,0},{16,24},{24,16},{32,40},{40,32},{48,56},{56,48},{64,72... | collective-permute-start | bytes 1572872 | tf_op jit(solution)/shard_map/ppermute | solution.py:60
  37.0 8.9 %collective-permute-start.10 = (f32[256,512]{1,0:T(8,128)S(1)}, f32[256,512]{1,0:T(8,128)S(1)}, u32[]{:S(2)}, u32[]{:S(2)}) collective-permute-start(f32[256,512]{1,0:T(8,128)S(1)} %get-tuple-element.79), channel_id=1, source_target_pairs={{0,8},{8,0},{16,24},{24,16},{32,40},{40,32},{48,56},{56,48},{64,72... | collective-permute-start | bytes 1572872 | tf_op jit(solution)/shard_map/ppermute | solution.py:60
  38.8 7.3 %collective-permute-start.9 = (f32[256,512]{1,0:T(8,128)S(1)}, f32[256,512]{1,0:T(8,128)S(1)}, u32[]{:S(2)}, u32[]{:S(2)}) collective-permute-start(f32[256,512]{1,0:T(8,128)S(1)} %get-tuple-element.77), channel_id=1, source_target_pairs={{0,8},{8,0},{16,24},{24,16},{32,40},{40,32},{48,56},{56,48},{64,72... | collective-permute-start | bytes 1572872 | tf_op jit(solution)/shard_map/ppermute | solution.py:60
  40.2 6.0 %collective-permute-start.4 = (f32[256,512]{1,0:T(8,128)S(1)}, f32[256,512]{1,0:T(8,128)S(1)}, u32[]{:S(2)}, u32[]{:S(2)}) collective-permute-start(f32[256,512]{1,0:T(8,128)S(1)} %get-tuple-element.66), channel_id=1, source_target_pairs={{0,8},{8,0},{16,24},{24,16},{32,40},{40,32},{48,56},{56,48},{64,72... | collective-permute-start | bytes 1572872 | tf_op jit(solution)/shard_map/ppermute | solution.py:60
  40.8 16.9 %collective-permute-start.31 = (f32[256,512]{1,0:T(8,128)S(1)}, f32[256,512]{1,0:T(8,128)S(1)}, u32[]{:S(2)}, u32[]{:S(2)}) collective-permute-start(f32[256,512]{1,0:T(8,128)S(1)} %meet.11), channel_id=1, source_target_pairs={{0,96},{8,104},{16,112},{24,120},{32,64},{40,72},{48,80},{56,88},{... | collective-permute-start | bytes 1572872 | tf_op jit(solution)/shard_map/ppermute | solution.py:60
  45.0 14.1 %collective-permute-start.6 = (f32[264,512]{1,0:T(8,128)S(1)}, f32[264,512]{1,0:T(8,128)S(1)}, u32[]{:S(2)}, u32[]{:S(2)}) collective-permute-start(f32[264,512]{1,0:T(8,128)S(1)} %meet.6.refs_3_), channel_id=1, source_target_pairs={{0,16},{8,24},{16,0},{24,8},{32,48},{40,56},{48,32},{56,40},{64,80... | collective-permute-start | bytes 1622024 | tf_op jit(solution)/shard_map/ppermute | solution.py:60
  45.9 22.4 %collective-permute-start.26 = (f32[256,512]{1,0:T(8,128)S(1)}, f32[256,512]{1,0:T(8,128)S(1)}, u32[]{:S(2)}, u32[]{:S(2)}) collective-permute-start(f32[256,512]{1,0:T(8,128)S(1)} %meet.10), channel_id=1, source_target_pairs={{0,96},{8,104},{16,112},{24,120},{32,64},{40,72},{48,80},{56,88},{... | collective-permute-start | bytes 1572872 | tf_op jit(solution)/shard_map/ppermute | solution.py:60
  46.1 22.4 %collective-permute-start.21 = (f32[256,512]{1,0:T(8,128)S(1)}, f32[256,512]{1,0:T(8,128)S(1)}, u32[]{:S(2)}, u32[]{:S(2)}) collective-permute-start(f32[256,512]{1,0:T(8,128)S(1)} %meet.9), channel_id=1, source_target_pairs={{0,32},{8,40},{16,48},{24,56},{32,0},{40,8},{48,16},{56,24},{64,96... | collective-permute-start | bytes 1572872 | tf_op jit(solution)/shard_map/ppermute | solution.py:60
  46.3 24.8 %collective-permute-start.16 = (f32[256,512]{1,0:T(8,128)S(1)}, f32[256,512]{1,0:T(8,128)S(1)}, u32[]{:S(2)}, u32[]{:S(2)}) collective-permute-start(f32[256,512]{1,0:T(8,128)S(1)} %meet.8), channel_id=1, source_target_pairs={{0,32},{8,40},{16,48},{24,56},{32,0},{40,8},{48,16},{56,24},{64,96... | collective-permute-start | bytes 1572872 | tf_op jit(solution)/shard_map/ppermute | solution.py:60
  57.7 16.7 %collective-permute-start.11 = (f32[256,512]{1,0:T(8,128)S(1)}, f32[256,512]{1,0:T(8,128)S(1)}, u32[]{:S(2)}, u32[]{:S(2)}) collective-permute-start(f32[256,512]{1,0:T(8,128)S(1)} %meet.7), channel_id=1, source_target_pairs={{0,16},{8,24},{16,0},{24,8},{32,48},{40,56},{48,32},{56,40},{64,80... | collective-permute-start | bytes 1572872 | tf_op jit(solution)/shard_map/ppermute | solution.py:60
  59.1 19.0 %collective-permute-start.32 = (f32[128,512]{1,0:T(8,128)S(1)}, f32[128,512]{1,0:T(8,128)S(1)}, u32[]{:S(2)}, u32[]{:S(2)}) collective-permute-start(f32[128,512]{1,0:T(8,128)S(1)} %get-tuple-element.119), channel_id=1, source_target_pairs={{0,16},{8,24},{16,0},{24,8},{32,48},{40,56},{48,32},{56,40},{64,80... | collective-permute-start | bytes 786440 | tf_op jit(solution)/shard_map/ppermute | solution.py:60
  68.3 9.8 %collective-permute-start.7 = (f32[136,512]{1,0:T(8,128)S(1)}, f32[136,512]{1,0:T(8,128)S(1)}, u32[]{:S(2)}, u32[]{:S(2)}) collective-permute-start(f32[136,512]{1,0:T(8,128)S(1)} %get-tuple-element.73), channel_id=1, source_target_pairs={{0,32},{8,40},{16,48},{24,56},{32,0},{40,8},{48,16},{56,24},{64,96... | collective-permute-start | bytes 835592 | tf_op jit(solution)/shard_map/ppermute | solution.py:60
  68.5 13.2 %collective-permute-start.27 = (f32[128,512]{1,0:T(8,128)S(1)}, f32[128,512]{1,0:T(8,128)S(1)}, u32[]{:S(2)}, u32[]{:S(2)}) collective-permute-start(f32[128,512]{1,0:T(8,128)S(1)} %get-tuple-element.111), channel_id=1, source_target_pairs={{0,16},{8,24},{16,0},{24,8},{32,48},{40,56},{48,32},{56,40},{64,80... | collective-permute-start | bytes 786440 | tf_op jit(solution)/shard_map/ppermute | solution.py:60
  71.1 13.3 %collective-permute-start.22 = (f32[128,512]{1,0:T(8,128)S(1)}, f32[128,512]{1,0:T(8,128)S(1)}, u32[]{:S(2)}, u32[]{:S(2)}) collective-permute-start(f32[128,512]{1,0:T(8,128)S(1)} %get-tuple-element.100), channel_id=1, source_target_pairs={{0,96},{8,104},{16,112},{24,120},{32,64},{40,72},{48,80},{56,88},{... | collective-permute-start | bytes 786440 | tf_op jit(solution)/shard_map/ppermute | solution.py:60
  74.4 11.0 %collective-permute-start.17 = (f32[128,512]{1,0:T(8,128)S(1)}, f32[128,512]{1,0:T(8,128)S(1)}, u32[]{:S(2)}, u32[]{:S(2)}) collective-permute-start(f32[128,512]{1,0:T(8,128)S(1)} %get-tuple-element.92), channel_id=1, source_target_pairs={{0,96},{8,104},{16,112},{24,120},{32,64},{40,72},{48,80},{56,88},{... | collective-permute-start | bytes 786440 | tf_op jit(solution)/shard_map/ppermute | solution.py:60
  78.1 9.1 %collective-permute-start.12 = (f32[128,512]{1,0:T(8,128)S(1)}, f32[128,512]{1,0:T(8,128)S(1)}, u32[]{:S(2)}, u32[]{:S(2)}) collective-permute-start(f32[128,512]{1,0:T(8,128)S(1)} %get-tuple-element.81), channel_id=1, source_target_pairs={{0,32},{8,40},{16,48},{24,56},{32,0},{40,8},{48,16},{56,24},{64,96... | collective-permute-start | bytes 786440 | tf_op jit(solution)/shard_map/ppermute | solution.py:60
  78.2 9.4 %collective-permute-start.33 = (f32[64,512]{1,0:T(8,128)S(1)}, f32[64,512]{1,0:T(8,128)S(1)}, u32[]{:S(2)}, u32[]{:S(2)}) collective-permute-start(f32[64,512]{1,0:T(8,128)S(1)} %get-tuple-element.121), channel_id=1, source_target_pairs={{0,32},{8,40},{16,48},{24,56},{32,0},{40,8},{48,16},{56,24},{64,96... | collective-permute-start | bytes 393224 | tf_op jit(solution)/shard_map/ppermute | solution.py:60
  81.7 12.2 %collective-permute-start.8 = (f32[72,512]{1,0:T(8,128)S(1)}, f32[72,512]{1,0:T(8,128)S(1)}, u32[]{:S(2)}, u32[]{:S(2)}) collective-permute-start(f32[72,512]{1,0:T(8,128)S(1)} %get-tuple-element.75), channel_id=1, source_target_pairs={{0,96},{8,104},{16,112},{24,120},{32,64},{40,72},{48,80},{56,88},{... | collective-permute-start | bytes 442376 | tf_op jit(solution)/shard_map/ppermute | solution.py:60
  84.4 6.5 %collective-permute-start.28 = (f32[64,512]{1,0:T(8,128)S(1)}, f32[64,512]{1,0:T(8,128)S(1)}, u32[]{:S(2)}, u32[]{:S(2)}) collective-permute-start(f32[64,512]{1,0:T(8,128)S(1)} %get-tuple-element.113), channel_id=1, source_target_pairs={{0,32},{8,40},{16,48},{24,56},{32,0},{40,8},{48,16},{56,24},{64,96... | collective-permute-start | bytes 393224 | tf_op jit(solution)/shard_map/ppermute | solution.py:60
  85.4 5.5 %collective-permute-start.23 = (f32[64,512]{1,0:T(8,128)S(1)}, f32[64,512]{1,0:T(8,128)S(1)}, u32[]{:S(2)}, u32[]{:S(2)}) collective-permute-start(f32[64,512]{1,0:T(8,128)S(1)} %get-tuple-element.102), channel_id=1, source_target_pairs={{0,16},{8,24},{16,0},{24,8},{32,48},{40,56},{48,32},{56,40},{64,80... | collective-permute-start | bytes 393224 | tf_op jit(solution)/shard_map/ppermute | solution.py:60
  87.2 5.0 %collective-permute-start.18 = (f32[64,512]{1,0:T(8,128)S(1)}, f32[64,512]{1,0:T(8,128)S(1)}, u32[]{:S(2)}, u32[]{:S(2)}) collective-permute-start(f32[64,512]{1,0:T(8,128)S(1)} %get-tuple-element.94), channel_id=1, source_target_pairs={{0,16},{8,24},{16,0},{24,8},{32,48},{40,56},{48,32},{56,40},{64,80... | collective-permute-start | bytes 393224 | tf_op jit(solution)/shard_map/ppermute | solution.py:60
  87.6 6.3 %collective-permute-start.13 = (f32[64,512]{1,0:T(8,128)S(1)}, f32[64,512]{1,0:T(8,128)S(1)}, u32[]{:S(2)}, u32[]{:S(2)}) collective-permute-start(f32[64,512]{1,0:T(8,128)S(1)} %get-tuple-element.83), channel_id=1, source_target_pairs={{0,96},{8,104},{16,112},{24,120},{32,64},{40,72},{48,80},{56,88},{... | collective-permute-start | bytes 393224 | tf_op jit(solution)/shard_map/ppermute | solution.py:60
